TPU v7x, 16 devices: a whole 2x2x2 slice. The times are simulated.
16 devices in a mesh: dp: 4 (over z, y), cp: 4 (over x, core).
Axes of the slice: x: 2, y: 2, z: 2, core: 2. Of those that a mesh axis runs over, the one named last changes fastest.
Arguments:
- x: bfloat16 [4, 4096, 2048], P('dp', 'cp')
- grad_out: bfloat16 [4, 4096, 2048], P('dp', 'cp')
- w_q: bfloat16 [2048, 16, 128], replicated
- w_k: bfloat16 [2048, 2, 128], replicated
- w_v: bfloat16 [2048, 2, 128], replicated
- w_o: bfloat16 [2048, 16, 128], replicated
- w_up: bfloat16 [2048, 11008], replicated
- w_down: bfloat16 [11008, 2048], replicated
Outputs:
- output 1: bfloat16 [4, 4096, 2048], P('dp', 'cp')
- output 2: float32 [2048, 16, 128], P(('dp', 'cp'))
- output 3: float32 [2048, 2, 128], P(('dp', 'cp'))
- output 4: float32 [2048, 2, 128], P(('dp', 'cp'))
- output 5: float32 [2048, 16, 128], P(('dp', 'cp'))
- output 6: float32 [2048, 11008], P(('dp', 'cp'))
- output 7: float32 [11008, 2048], P(('dp', 'cp'))
All inputs are finite; a program needn't handle non-finite values.
Results may differ from a plain program's by a relative error of at most 0.0141916.
Values are sent between devices in bfloat16 or wider.
A program may use at most 1 GiB of HBM per device.

v0:
```python
import jax
import jax.numpy as jnp
from jax import lax
from jax.sharding import PartitionSpec as P

NEG_BIG = -1e30


def gelu_tanh(values):
    return jax.nn.gelu(values, approximate=True)


def solution(mesh):
    cp_size = mesh.shape['cp']
    dev_count = cp_size * mesh.shape['dp']
    send_perm = [(sender, (sender + 1) % cp_size) for sender in range(cp_size)]

    def reduce_grad(grad):
        return lax.psum_scatter(grad, ('dp', 'cp'), scatter_dimension=0, tiled=True) / dev_count

    def per_device(x_loc, cot_loc, w_q, w_k, w_v, w_o, w_up, w_down):
        batch, seq_len, d_model = x_loc.shape
        kv_heads, head_dim = w_k.shape[1], w_k.shape[2]
        group = w_q.shape[1] // kv_heads
        half = seq_len // 2
        scale = head_dim ** -0.5
        my_idx = lax.axis_index('cp')
        w_q_heads = w_q.reshape(d_model, kv_heads, group, head_dim)
        w_o_heads = w_o.reshape(d_model, kv_heads, group, head_dim)
        offsets = jnp.arange(half)
        local_pos = jnp.concatenate([my_idx * half + offsets, (2 * cp_size - 1 - my_idx) * half + offsets])
        diag_keep = local_pos[None, :] <= local_pos[:, None]

        def fwd_block(q_blk, k_blk, v_blk, state, keep):
            row_max, row_sum, out_sum = state
            scores = jnp.einsum('bkgqe,bkte->bkgqt', q_blk, k_blk, preferred_element_type=jnp.float32) * scale
            if keep is not None:
                scores = jnp.where(keep, scores, NEG_BIG)
            new_max = jnp.maximum(row_max, scores.max(axis=-1))
            alpha = jnp.exp(row_max - new_max)
            exp_scores = jnp.exp(scores - new_max[..., None])
            new_sum = alpha * row_sum + exp_scores.sum(axis=-1)
            new_out = alpha[..., None] * out_sum + jnp.einsum('bkgqt,bkte->bkgqe', exp_scores.astype(jnp.bfloat16), v_blk, preferred_element_type=jnp.float32)
            return new_max, new_sum, new_out

        def bwd_block(q_blk, k_blk, v_blk, grad_o, log_norm, delta, keep):
            scores = jnp.einsum('bkgqe,bkte->bkgqt', q_blk, k_blk, preferred_element_type=jnp.float32) * scale
            if keep is not None:
                scores = jnp.where(keep, scores, NEG_BIG)
            attn_prob = jnp.exp(scores - log_norm[..., None])
            grad_v = jnp.einsum('bkgqt,bkgqe->bkte', attn_prob.astype(jnp.bfloat16), grad_o, preferred_element_type=jnp.float32)
            grad_p = jnp.einsum('bkgqe,bkte->bkgqt', grad_o, v_blk, preferred_element_type=jnp.float32)
            grad_s = (attn_prob * (grad_p - delta[..., None]) * scale).astype(jnp.bfloat16)
            grad_q = jnp.einsum('bkgqt,bkte->bkgqe', grad_s, k_blk, preferred_element_type=jnp.float32)
            grad_k = jnp.einsum('bkgqt,bkgqe->bkte', grad_s, q_blk, preferred_element_type=jnp.float32)
            return grad_q, grad_k, grad_v

        q_heads = jnp.einsum('bsd,dkge->bkgse', x_loc, w_q_heads, preferred_element_type=jnp.float32).astype(jnp.bfloat16)
        k_heads = jnp.einsum('bsd,dke->bkse', x_loc, w_k, preferred_element_type=jnp.float32).astype(jnp.bfloat16)
        v_heads = jnp.einsum('bsd,dke->bkse', x_loc, w_v, preferred_element_type=jnp.float32).astype(jnp.bfloat16)
        kv_own = jnp.stack([k_heads, v_heads])

        stat_shape = (batch, kv_heads, group, seq_len)
        init = (jnp.full(stat_shape, NEG_BIG, jnp.float32), jnp.zeros(stat_shape, jnp.float32),
                jnp.zeros(stat_shape + (head_dim,), jnp.float32))
        state = fwd_block(q_heads, k_heads, v_heads, init, diag_keep)

        def fwd_step(step, carry):
            kv_cur = lax.ppermute(carry[0], 'cp', send_perm)
            src_idx = (my_idx - step) % cp_size

            def lower(args):
                return fwd_block(q_heads, kv_cur[0][:, :, :half], kv_cur[1][:, :, :half], args, None)

            def upper(args):
                part = fwd_block(q_heads[:, :, :, half:], kv_cur[0], kv_cur[1], tuple(piece[:, :, :, half:] for piece in args), None)
                return tuple(lax.dynamic_update_slice_in_dim(full, piece, half, axis=3) for full, piece in zip(args, part))

            return (kv_cur,) + tuple(lax.cond(src_idx < my_idx, lower, upper, carry[1:]))

        _, row_max, row_sum, out_sum = lax.fori_loop(1, cp_size, fwd_step, (kv_own,) + tuple(state))
        o_f32 = out_sum / row_sum[..., None]
        o_heads = o_f32.astype(jnp.bfloat16)
        log_norm = row_max + jnp.log(row_sum)

        h_act = (x_loc + jnp.einsum('bkgse,dkge->bsd', o_heads, w_o_heads, preferred_element_type=jnp.float32)).astype(jnp.bfloat16)
        act_f, gelu_back = jax.vjp(gelu_tanh, jnp.einsum('bsd,df->bsf', h_act, w_up, preferred_element_type=jnp.float32))
        act_out = act_f.astype(jnp.bfloat16)

        grad_w_down = reduce_grad(jnp.einsum('bsf,bsd->fd', act_out, cot_loc, preferred_element_type=jnp.float32))
        grad_act = jnp.einsum('bsd,fd->bsf', cot_loc, w_down, preferred_element_type=jnp.float32).astype(jnp.bfloat16)
        grad_u = gelu_back(grad_act.astype(jnp.float32))[0].astype(jnp.bfloat16)
        grad_w_up = reduce_grad(jnp.einsum('bsd,bsf->df', h_act, grad_u, preferred_element_type=jnp.float32))
        grad_h = cot_loc + jnp.einsum('bsf,df->bsd', grad_u, w_up, preferred_element_type=jnp.float32)
        grad_h_bf = grad_h.astype(jnp.bfloat16)
        grad_w_o = reduce_grad(jnp.einsum('bsd,bkgse->dkge', grad_h_bf, o_heads, preferred_element_type=jnp.float32).reshape(d_model, -1, head_dim))
        grad_o = jnp.einsum('bsd,dkge->bkgse', grad_h_bf, w_o_heads, preferred_element_type=jnp.float32).astype(jnp.bfloat16)
        delta = jnp.sum(grad_o.astype(jnp.float32) * o_f32, axis=-1)

        dq_own, dk_own, dv_own = bwd_block(q_heads, k_heads, v_heads, grad_o, log_norm, delta, diag_keep)

        def bwd_step(step, carry):
            kv_cur = lax.ppermute(carry[0], 'cp', send_perm)
            dkv_cur = lax.ppermute(carry[1], 'cp', send_perm)
            src_idx = (my_idx - step) % cp_size

            def lower(args):
                dkv_acc, grad_q = args
                part_q, part_k, part_v = bwd_block(q_heads, kv_cur[0][:, :, :half], kv_cur[1][:, :, :half], grad_o, log_norm, delta, None)
                new_dkv = lax.dynamic_update_slice_in_dim(dkv_acc, dkv_acc[:, :, :, :half] + jnp.stack([part_k, part_v]), 0, axis=3)
                return new_dkv, grad_q + part_q

            def upper(args):
                dkv_acc, grad_q = args
                part_q, part_k, part_v = bwd_block(q_heads[:, :, :, half:], kv_cur[0], kv_cur[1], grad_o[:, :, :, half:],
                                                   log_norm[:, :, :, half:], delta[:, :, :, half:], None)
                new_q = lax.dynamic_update_slice_in_dim(grad_q, grad_q[:, :, :, half:] + part_q, half, axis=3)
                return dkv_acc + jnp.stack([part_k, part_v]), new_q

            dkv_cur, grad_q = lax.cond(src_idx < my_idx, lower, upper, (dkv_cur, carry[2]))
            return kv_cur, dkv_cur, grad_q

        _, dkv_acc, grad_q = lax.fori_loop(1, cp_size, bwd_step, (kv_own, jnp.stack([dk_own, dv_own]), dq_own))
        dkv_acc = lax.ppermute(dkv_acc, 'cp', send_perm)

        grad_q_bf = grad_q.astype(jnp.bfloat16)
        grad_k_bf = dkv_acc[0].astype(jnp.bfloat16)
        grad_v_bf = dkv_acc[1].astype(jnp.bfloat16)
        grad_w_q = reduce_grad(jnp.einsum('bsd,bkgse->dkge', x_loc, grad_q_bf, preferred_element_type=jnp.float32).reshape(d_model, -1, head_dim))
        grad_w_k = reduce_grad(jnp.einsum('bsd,bkse->dke', x_loc, grad_k_bf, preferred_element_type=jnp.float32))
        grad_w_v = reduce_grad(jnp.einsum('bsd,bkse->dke', x_loc, grad_v_bf, preferred_element_type=jnp.float32))
        grad_x = (grad_h
                  + jnp.einsum('bkgse,dkge->bsd', grad_q_bf, w_q_heads, preferred_element_type=jnp.float32)
                  + jnp.einsum('bkse,dke->bsd', grad_k_bf, w_k, preferred_element_type=jnp.float32)
                  + jnp.einsum('bkse,dke->bsd', grad_v_bf, w_v, preferred_element_type=jnp.float32))
        return grad_x.astype(jnp.bfloat16), grad_w_q, grad_w_k, grad_w_v, grad_w_o, grad_w_up, grad_w_down

    act_spec = P('dp', 'cp', None)
    rep_three = P(None, None, None)
    rep_two = P(None, None)
    grad_three = P(('dp', 'cp'), None, None)
    grad_two = P(('dp', 'cp'), None)
    return jax.shard_map(per_device, mesh=mesh,
                         in_specs=(act_spec, act_spec, rep_three, rep_three, rep_three, rep_three, rep_two, rep_two),
                         out_specs=(act_spec, grad_three, grad_three, grad_three, grad_three, grad_two, grad_two),
                         check_vma=False)
```

profile of v0, /device:TPU:0, one launch (start us, length us, event | category | flops | bytes accessed | tf_op | source)
XLA Modules:
  0.0 3385.6 jit_solution(9050828345596341808)
XLA Ops:
  16.3 14.3 fusion.153
  49.1 26.0 fusion.92
  75.1 21.6 fusion.80
  96.7 29.5 add_bitcast_fusion
  126.2 182.4 %while.40 = (s32[]{:T(128)}, bf16[2,1,2,1024,128]{4,3,2,1,0:T(8,128)(2,1)S(1)}, f32[1,2,8,1024]{3,2,1,0:T(8,128)S(1)}, f32[1,2,8,1024]{3,2,1,0:T(8,128)S(1)}, f3...) while((s32[]{:T(128)}, ...), condition=%wide.region_9.10_spmd, body=%wide.region_2.9_spmd.sunk | while | flops 4366319616 | bytes 190317008 | solution.py:81
  126.9 14.4 collective-permute-done
  141.3 46.1 %conditional.4 = (f32[1,2,8,1024]{3,2,1,0:T(8,128)S(1)}, f32[1,2,8,1024]{3,2,1,0:T(8,128)S(1)}, f32[1,2,8,1024,128]{4,3,2,1,0:T(8,128)}) conditional(s32[]{:T(128)} %convert_element_type.294, (f32[1,2,8,1024]{3,2,1,0:T(8,128)S(1)}, bf16[1,2,8,1024,128]{4,3,2,1,0:T(8,128)(2,1)}, bf16[2,1,2,1024,128]{4,3,2,1,0:T(8,128)(2,1)S(1)}, ...), branch_computations={%region_3.5_spmd, %region_6.8_spmd} | conditional | flops 4366319616 | bytes 184025184 | solution.py:79
  141.3 14.8 multiply_reduce_fusion
  170.4 17.0 fusion.6
  201.8 46.1 %conditional.4 = (f32[1,2,8,1024]{3,2,1,0:T(8,128)S(1)}, f32[1,2,8,1024]{3,2,1,0:T(8,128)S(1)}, f32[1,2,8,1024,128]{4,3,2,1,0:T(8,128)}) conditional(s32[]{:T(128)} %convert_element_type.294, (f32[1,2,8,1024]{3,2,1,0:T(8,128)S(1)}, bf16[1,2,8,1024,128]{4,3,2,1,0:T(8,128)(2,1)}, bf16[2,1,2,1024,128]{4,3,2,1,0:T(8,128)(2,1)S(1)}, ...), branch_computations={%region_3.5_spmd, %region_6.8_spmd} | conditional | flops 4366319616 | bytes 184025184 | solution.py:79
  201.8 14.8 multiply_reduce_fusion
  230.8 17.0 fusion.6
  262.2 46.1 %conditional.4 = (f32[1,2,8,1024]{3,2,1,0:T(8,128)S(1)}, f32[1,2,8,1024]{3,2,1,0:T(8,128)S(1)}, f32[1,2,8,1024,128]{4,3,2,1,0:T(8,128)}) conditional(s32[]{:T(128)} %convert_element_type.294, (f32[1,2,8,1024]{3,2,1,0:T(8,128)S(1)}, bf16[1,2,8,1024,128]{4,3,2,1,0:T(8,128)(2,1)}, bf16[2,1,2,1024,128]{4,3,2,1,0:T(8,128)(2,1)S(1)}, ...), branch_computations={%region_3.5_spmd, %region_6.8_spmd} | conditional | flops 4366319616 | bytes 184025184 | solution.py:79
  262.2 14.8 multiply_reduce_fusion
  291.3 17.0 fusion.6
  317.9 14.9 fusion.115
  334.8 53.6 %fusion.200 = f32[1024,11008]{1,0:T(8,128)} fusion(bf16[1024,2048]{1,0:T(8,128)(2,1)S(1)} %fusion.115, bf16[2048,11008]{1,0:T(8,128)(2,1)} %param.22), kind=kOutput, calls=%fused_computation.213 | convolution fusion | flops 46170898432 | bytes 94371840 | tf_op jit(solution)/shard_map/bsd,df->bsf/dot_general | solution.py:87
  388.4 82.8 %fusion.84 = bf16[1024,11008]{1,0:T(8,128)(2,1)} fusion(f32[1024,11008]{1,0:T(8,128)} %fusion.200, bf16[11008,2048]{1,0:T(8,128)(2,1)} %param.23, bf16[1,1024,2048]{2,1,0:T(8,128)(2,1)S(1)} %copy-done.11), kind=kOutput, calls=%fused_computation.103 | convolution fusion | flops 46418886656 | bytes 116916224 | tf_op jit(solution)/shard_map/bsd,fd->bsf/dot_general | solution.py:91
  471.2 56.1 %fusion.201 = f32[1024,2048]{1,0:T(8,128)} fusion(bf16[1024,11008]{1,0:T(8,128)(2,1)} %fusion.84, bf16[2048,11008]{1,0:T(8,128)(2,1)} %param.22), kind=kOutput, calls=%fused_computation.214 | convolution fusion | flops 46170898432 | bytes 76021760 | tf_op jit(solution)/shard_map/bsf,df->bsd/dot_general | solution.py:94
  527.3 16.9 multiply_reduce_fusion.2
  544.3 25.3 fusion.161
  569.6 41.9 %multiply_convert_fusion.2 = bf16[2,8,1024,1024]{2,3,1,0:T(8,128)(2,1)} fusion(f32[2,8,1024,1024]{2,3,1,0:T(8,128)} %get-tuple-element.590, f32[2,8,1024]{2,1,0:T(8,128)S(1)} %get-tuple-element.591, f32[2,8,1024]{2,1,0:T(8,128)S(1)} %bitcast.396, pred[1024,1024]{0,1:T(8,128)(4,1)S(1)} %copy-done.6, bf16[1024,2,8,128]{0,3,2,1:T(8,128)(2,1)} %get-tuple-element.592, ...), kind=kOutput, calls=%fused_computation.90 | convolution fusion | flops 4412407808 | bytes 106561536 | tf_op jit(solution)/shard_map/bkgqe,bkte->bkgqt/dot_general | solution.py:52
  611.5 16.0 fusion.158
  627.6 20.2 convolution_bitcast_fusion.1
  655.5 383.1 %while.41 = (s32[]{:T(128)}, bf16[2,1,2,1024,128]{4,3,2,1,0:T(8,128)(2,1)}, f32[2,1,2,1024,128]{4,3,2,1,0:T(8,128)}, f32[1,2,8,1024,128]{4,3,2,1,0:T(8,128)}, s3...) while((s32[]{:T(128)}, ...), condition=%wide.region_14.15_spmd, body=%wide.region_11.14_spmd.sunk | while | flops 10815537152 | bytes 242156144 | solution.py:123
  683.7 31.7 collective-permute-done.1
  716.4 74.6 %conditional.5 = (f32[2,1,2,1024,128]{4,3,2,1,0:T(8,128)S(1)}, f32[1,2,8,1024,128]{4,3,2,1,0:T(8,128)}) conditional(s32[]{:T(128)} %convert_element_type.295, (bf16[1,2,8,1024,128]{4,3,2,1,0:T(8,128)(2,1)}, bf16[2,1,2,1024,128]{4,3,2,1,0:T(8,128)(2,1)S(1)}, f32[1,2,8,1024]{3,2,1,0:T(8,128)S(1)}, bf16[1,2,8,1024,128]{4,3,2,1,0:T(8,128)(2,1)}, ...), branch_computations={%region_12.12_spmd, %region_13.13_spmd} | conditional | flops 10815537152 | bytes 219086992 | solution.py:120
  716.4 14.7 fusion.39
  731.2 16.2 fusion.45
  747.4 19.5 multiply_convert_fusion
  805.5 29.2 collective-permute-done.1
  835.7 74.6 %conditional.5 = (f32[2,1,2,1024,128]{4,3,2,1,0:T(8,128)S(1)}, f32[1,2,8,1024,128]{4,3,2,1,0:T(8,128)}) conditional(s32[]{:T(128)} %convert_element_type.295, (bf16[1,2,8,1024,128]{4,3,2,1,0:T(8,128)(2,1)}, bf16[2,1,2,1024,128]{4,3,2,1,0:T(8,128)(2,1)S(1)}, f32[1,2,8,1024]{3,2,1,0:T(8,128)S(1)}, bf16[1,2,8,1024,128]{4,3,2,1,0:T(8,128)(2,1)}, ...), branch_computations={%region_12.12_spmd, %region_13.13_spmd} | conditional | flops 10815537152 | bytes 219086992 | solution.py:120
  835.7 14.7 fusion.39
  850.5 16.2 fusion.45
  866.7 19.6 multiply_convert_fusion
  927.3 26.7 collective-permute-done.1
  955.0 74.6 %conditional.5 = (f32[2,1,2,1024,128]{4,3,2,1,0:T(8,128)S(1)}, f32[1,2,8,1024,128]{4,3,2,1,0:T(8,128)}) conditional(s32[]{:T(128)} %convert_element_type.295, (bf16[1,2,8,1024,128]{4,3,2,1,0:T(8,128)(2,1)}, bf16[2,1,2,1024,128]{4,3,2,1,0:T(8,128)(2,1)S(1)}, f32[1,2,8,1024]{3,2,1,0:T(8,128)S(1)}, bf16[1,2,8,1024,128]{4,3,2,1,0:T(8,128)(2,1)}, ...), branch_computations={%region_12.12_spmd, %region_13.13_spmd} | conditional | flops 10815537152 | bytes 219086992 | solution.py:120
  955.0 14.7 fusion.39
  969.8 16.2 fusion.45
  986.0 19.6 multiply_convert_fusion
  1075.3 14.5 fusion.116
  1106.1 66.6 %fusion.99 = f32[11008,2048]{1,0:T(8,128)} fusion(f32[1024,11008]{1,0:T(8,128)} %fusion.200, bf16[1,1024,2048]{2,1,0:T(8,128)(2,1)} %param.17), kind=kOutput, calls=%fused_computation.117 | convolution fusion | flops 46272348160 | bytes 139460608 | tf_op jit(solution)/shard_map/bsf,bsd->fd/dot_general | solution.py:90
  1172.8 58.0 %fusion.202 = f32[2048,11008]{1,0:T(8,128)} fusion(bf16[1024,2048]{1,0:T(8,128)(2,1)} %copy-done.29, bf16[1024,11008]{1,0:T(8,128)(2,1)} %fusion.84), kind=kOutput, calls=%fused_computation.215 | convolution fusion | flops 46170898432 | bytes 116916224 | tf_op jit(solution)/shard_map/bsd,bsf->df/dot_general | solution.py:93
  1230.8 16.2 fusion.108
  1262.0 102.6 %reduce-scatter.13.cloned.1.call-done = f32[128,16,128]{0,2,1:T(8,128)} async-done(((f32[2048,16,128]{0,2,1:T(8,128)}), f32[128,16,128]{0,2,1:T(8,128)}) %reduce-scatter.13.cloned.1.call-update) | async-done | bytes 1048592 | tf_op jit(solution)/shard_map/reduce_scatter | solution.py:19
  1367.4 175.0 %reduce-scatter.7.cloned.1.call-done = f32[128,16,128]{0,2,1:T(8,128)} async-done(((f32[2048,16,128]{0,2,1:T(8,128)}), f32[128,16,128]{0,2,1:T(8,128)}) %reduce-scatter.7.cloned.1.call-update) | async-done | bytes 1048592 | tf_op jit(solution)/shard_map/reduce_scatter | solution.py:19
  1545.0 912.5 %reduce-scatter.17.cloned.1.call-done = f32[688,2048]{1,0:T(8,128)} async-done(((f32[11008,2048]{1,0:T(8,128)}), f32[688,2048]{1,0:T(8,128)}) %reduce-scatter.17.cloned.1.call-update) | async-done | bytes 5636112 | tf_op jit(solution)/shard_map/reduce_scatter | solution.py:19
  2463.6 909.2 %reduce-scatter.15.cloned.1.call-done = f32[128,11008]{1,0:T(8,128)} async-done(((f32[2048,11008]{1,0:T(8,128)}), f32[128,11008]{1,0:T(8,128)}) %reduce-scatter.15.cloned.1.call-update) | async-done | bytes 5636112 | tf_op jit(solution)/shard_map/reduce_scatter | solution.py:19
  (152 shorter events, 316.7 us)
Async XLA Ops:
  7.2 4.0 copy-start.26
  7.2 1251.5 %reduce-scatter.9.cloned.1.call-start = ((), (), s32[]{:S(2)}) async-start(), calls=%async_computation.7 | async-start | bytes 2228224 | tf_op jit(solution)/shard_map/reduce_scatter | solution.py:19
  7.2 4.0 copy-start.9
  11.3 37.8 %copy-start.21 = (bf16[2,128,1024]{2,1,0:T(8,128)(2,1)}, bf16[2,128,1024]{2,1,0:T(8,128)(2,1)S(1)}, u32[]{:S(2)}) copy-start(bf16[2,128,1024]{2,1,0:T(8,128)(2,1)S(1)} %fusion.166) | copy-start | bytes 1572868
  12.6 84.1 %copy-start.27 = (bf16[2,128,1024]{2,1,0:T(8,128)(2,1)}, bf16[2,128,1024]{2,1,0:T(8,128)(2,1)S(1)}, u32[]{:S(2)}) copy-start(bf16[2,128,1024]{2,1,0:T(8,128)(2,1)S(1)} %fusion.169) | copy-start | bytes 1572868
  13.3 83.4 %copy-start.5 = (pred[1024,1024]{0,1:T(8,128)(4,1)}, pred[1024,1024]{0,1:T(8,128)(4,1)S(1)}, u32[]{:S(2)}) copy-start(pred[1024,1024]{0,1:T(8,128)(4,1)S(1)} %broadcast_compare_fusion) | copy-start | bytes 3145732
  16.3 14.3 copy-start.23
  96.7 29.5 copy-start.24
  126.2 15.1 collective-permute-start
  187.5 14.3 collective-permute-start
  248.0 14.3 collective-permute-start
  308.6 9.4 copy-start.15
  332.8 1.9 copy-start.29
  334.8 53.6 %copy-start.11 = (bf16[1,1024,2048]{2,1,0:T(8,128)(2,1)S(1)}, bf16[1,1024,2048]{2,1,0:T(8,128)(2,1)}, u32[]{:S(2)}) copy-start(bf16[1,1024,2048]{2,1,0:T(8,128)(2,1)} %param.17) | copy-start | bytes 12582916
  471.2 56.1 %copy-start.4 = (f32[1,2,8,1024,128]{3,4,2,1,0:T(8,128)S(1)}, f32[1,2,8,1024,128]{3,4,2,1,0:T(8,128)}, u32[]{:S(2)}) copy-start(f32[1,2,8,1024,128]{3,4,2,1,0:T(8,128)} %copy.29) | copy-start | bytes 25165828
  471.2 56.1 %copy-start.16 = (f32[1,2,8,1024]{3,2,1,0:T(8,128)S(1)}, f32[1,2,8,1024]{3,2,1,0:T(8,128)}, u32[]{:S(2)}) copy-start(f32[1,2,8,1024]{3,2,1,0:T(8,128)} %copy-done.15) | copy-start | bytes 196612
  527.3 16.9 copy-start.6
  527.3 16.9 copy-start.14
  544.3 25.3 copy-start.28
  611.5 16.0 copy-start.22
  678.7 37.7 %collective-permute-start.2 = (f32[2,1,2,1024,128]{4,3,2,1,0:T(8,128)}, f32[2,1,2,1024,128]{4,3,2,1,0:T(8,128)S(1)}, u32[]{:S(2)}, u32[]{:S(2)}) collective-permute-start(f32[2,1,2,1024,128]{4,3,2,1,0:T(8,128)} %get-tuple-element.761), channel_id=1, source_target_pairs={{0,1},{1,2},{2,3},{3,0},{4,5},{5,6},{6,7},{7,4},{8,9},{9,10},{10,1... | collective-permute-start | bytes 6291464 | tf_op jit(solution)/shard_map/while/body/eval_jaxpr/ppermute | solution.py:104
  681.2 34.2 %collective-permute-start.1 = (bf16[2,1,2,1024,128]{4,3,2,1,0:T(8,128)(2,1)}, bf16[2,1,2,1024,128]{4,3,2,1,0:T(8,128)(2,1)S(1)}, u32[]{:S(2)}, u32[]{:S(2)}) collective-permute-start(bf16[2,1,2,1024,128]{4,3,2,1,0:T(8,128)(2,1)} %get-tuple-element.760), channel_id=1, source_target_pairs={{0,1},{1,2},{2,3},{3,0},{4,5},{5,6},{6,7},{7,4},{8,9},{9,10},{10,1... | collective-permute-start | bytes 3145736 | tf_op jit(solution)/shard_map/while/body/eval_jaxpr/ppermute | solution.py:103
  747.4 19.6 copy-start
  777.1 13.5 copy-start.3
  791.0 1.3 copy-start.18
  792.3 43.4 %collective-permute-start.2 = (f32[2,1,2,1024,128]{4,3,2,1,0:T(8,128)}, f32[2,1,2,1024,128]{4,3,2,1,0:T(8,128)S(1)}, u32[]{:S(2)}, u32[]{:S(2)}) collective-permute-start(f32[2,1,2,1024,128]{4,3,2,1,0:T(8,128)} %get-tuple-element.761), channel_id=1, source_target_pairs={{0,1},{1,2},{2,3},{3,0},{4,5},{5,6},{6,7},{7,4},{8,9},{9,10},{10,1... | collective-permute-start | bytes 6291464 | tf_op jit(solution)/shard_map/while/body/eval_jaxpr/ppermute | solution.py:104
  803.0 31.7 collective-permute-start.1
  866.7 19.6 copy-start
  896.4 13.5 copy-start.3
  910.3 1.3 copy-start.18
  911.6 43.4 %collective-permute-start.2 = (f32[2,1,2,1024,128]{4,3,2,1,0:T(8,128)}, f32[2,1,2,1024,128]{4,3,2,1,0:T(8,128)S(1)}, u32[]{:S(2)}, u32[]{:S(2)}) collective-permute-start(f32[2,1,2,1024,128]{4,3,2,1,0:T(8,128)} %get-tuple-element.761), channel_id=1, source_target_pairs={{0,1},{1,2},{2,3},{3,0},{4,5},{5,6},{6,7},{7,4},{8,9},{9,10},{10,1... | collective-permute-start | bytes 6291464 | tf_op jit(solution)/shard_map/while/body/eval_jaxpr/ppermute | solution.py:104
  916.6 37.4 %collective-permute-start.1 = (bf16[2,1,2,1024,128]{4,3,2,1,0:T(8,128)(2,1)}, bf16[2,1,2,1024,128]{4,3,2,1,0:T(8,128)(2,1)S(1)}, u32[]{:S(2)}, u32[]{:S(2)}) collective-permute-start(bf16[2,1,2,1024,128]{4,3,2,1,0:T(8,128)(2,1)} %get-tuple-element.760), channel_id=1, source_target_pairs={{0,1},{1,2},{2,3},{3,0},{4,5},{5,6},{6,7},{7,4},{8,9},{9,10},{10,1... | collective-permute-start | bytes 3145736 | tf_op jit(solution)/shard_map/while/body/eval_jaxpr/ppermute | solution.py:103
  986.0 19.6 copy-start
  1015.7 13.5 copy-start.3
  1029.6 1.3 copy-start.18
  1040.4 30.1 copy-start.17
  1040.4 20.0 collective-permute-start.3
  1060.3 10.0 copy-start.19
  1065.5 194.8 %reduce-scatter.11.cloned.1.call-start = ((), (), s32[]{:S(2)}) async-start(), calls=%async_computation.8 | async-start | bytes 2228224 | tf_op jit(solution)/shard_map/reduce_scatter | solution.py:19
  1070.4 294.3 %reduce-scatter.13.cloned.1.call-start = ((), (), s32[]{:S(2)}) async-start(), calls=%async_computation.9 | async-start | bytes 17825792 | tf_op jit(solution)/shard_map/reduce_scatter | solution.py:19
  1070.4 4.9 copy-start.12
  1089.8 452.5 %reduce-scatter.7.cloned.1.call-start = ((), (), s32[]{:S(2)}) async-start(), calls=%async_computation.6 | async-start | bytes 17825792 | tf_op jit(solution)/shard_map/reduce_scatter | solution.py:19
  1089.9 4.6 copy-start.10
  1106.1 1351.4 %reduce-scatter.17.cloned.1.call-start = ((), (), s32[]{:S(2)}) async-start(), calls=%async_computation.11 | async-start | bytes 95813632 | tf_op jit(solution)/shard_map/reduce_scatter | solution.py:19
  1172.8 2200.0 %reduce-scatter.15.cloned.1.call-start = ((), (), s32[]{:S(2)}) async-start(), calls=%async_computation.10 | async-start | bytes 95813632 | tf_op jit(solution)/shard_map/reduce_scatter | solution.py:19
  1230.8 16.3 copy-start.20
  1230.8 16.3 copy-start.25
Sparse Core Ops, SparseCore 0:
  1065.6 61.6 reduce-scatter.8
  1130.1 56.4 reduce-scatter.10
  1188.9 175.7 reduce-scatter.12
  1366.8 175.4 reduce-scatter.6
  1544.5 912.9 reduce-scatter.16
  2459.7 912.9 reduce-scatter.14
where the time goes:
time: 3390 us
  waiting for transfers between devices  2240 us (66%)
  matrix products  909 us (27%)
  other arithmetic  96.3 us (3%)
  local copies, waits for them, and re-layouts  49 us (1%)
  starting transfers between devices  45 us (1%)
    reduce_scatter x6, waiting for transfers between devices, reduce_grad(): lax.psum_scatter(grad, ('dp', 'cp'), scatter_dimension=0, tiled=True)  2100 us
    dot_general x4, matrix products, bwd_block(): jnp.einsum('bkgqe,bkte->bkgqt', grad_o, v_blk, preferred_element_type=jnp...  101 us
    ppermute x3, waiting for transfers between devices, bwd_step(): kv_cur = lax.ppermute(carry[0], 'cp', send_perm)  87.6 us
    dot_general x1, matrix products, per_device(): jnp.einsum('bsd,fd->bsf', cot_loc, w_down, preferred_element_type=jnp.flo...  82.8 us
    dot_general x4, matrix products, fwd_block(): jnp.einsum('bkgqt,bkte->bkgqe', exp_scores.astype(jnp.bfloat16), v_blk, p...  80.4 us
    dot_general x4, matrix products, bwd_block(): jnp.einsum('bkgqt,bkgqe->bkte', attn_prob.astype(jnp.bfloat16), grad_o, p...  74 us
    dot_general x4, matrix products, fwd_block(): jnp.einsum('bkgqe,bkte->bkgqt', q_blk, k_blk, preferred_element_type=jnp....  70.2 us
  transfers between devices with their start and end apart: 16, of which 11 were waited for; matrix products, arithmetic and copies ran while one was open for 6% of the time, Pallas kernels for 0%

commit v1 on v0

v1 whole, which is shorter than its diff:
```python
import functools
import math

import jax
import jax.numpy as jnp
from jax import lax
from jax.experimental import pallas as pl
from jax.experimental.pallas import tpu as pltpu
from jax.experimental.layout import Layout, with_layout_constraint
from jax.sharding import PartitionSpec as P


NEG_BIG = -1e30
LOG2E = math.log2(math.e)
F32 = jnp.float32
FF_TILE = 256
BF16 = jnp.bfloat16


def row_major(values):
    return with_layout_constraint(values, Layout(major_to_minor=(0, 1)))


def dot_nn(lhs, rhs):
    return lax.dot_general(lhs, rhs, (((1,), (0,)), ((), ())), preferred_element_type=F32)


def dot_nt(lhs, rhs):
    return lax.dot_general(lhs, rhs, (((1,), (1,)), ((), ())), preferred_element_type=F32)


def dot_tn(lhs, rhs):
    return lax.dot_general(lhs, rhs, (((0,), (0,)), ((), ())), preferred_element_type=F32)


def dot_tt(lhs, rhs):
    return lax.dot_general(lhs, rhs, (((0,), (1,)), ((), ())), preferred_element_type=F32)


def pair_table(my_idx, cp_size):
    steps = jnp.arange(2 * cp_size + 1)
    late = steps > my_idx
    key_block = jnp.where(late, steps - my_idx - 1, steps)
    key_slot = jnp.where(key_block < cp_size, 2 * key_block, 2 * (2 * cp_size - 1 - key_block) + 1)
    last = (steps == my_idx) | (steps == 2 * cp_size)
    first = (steps == 0) | (steps == my_idx + 1)
    return jnp.stack([late, key_slot, last, first]).astype(jnp.int32)


def causal_keep(half):
    keys = lax.broadcasted_iota(jnp.int32, (half, half), 0)
    queries = lax.broadcasted_iota(jnp.int32, (half, half), 1)
    return keys <= queries


def attn_fwd_kernel(group, scale, tab, q_ref, k_ref, v_ref, of_ref, ob_ref, lse_ref, m_ref, l_ref, acc_ref):
    pair = pl.program_id(1)
    half, dim = k_ref.shape
    factor = scale * LOG2E

    @pl.when(tab[3, pair] == 1)
    def _():
        m_ref[...] = jnp.full(m_ref.shape, NEG_BIG, F32)
        l_ref[...] = jnp.zeros(l_ref.shape, F32)
        acc_ref[...] = jnp.zeros(acc_ref.shape, F32)

    def run(masked):
        keys = k_ref[...]
        vals_t = v_ref[...].T
        for head in range(group):
            rows = slice(head * dim, (head + 1) * dim)
            scores = dot_nn(keys, q_ref[rows, :])
            if masked:
                scores = jnp.where(causal_keep(half), scores, NEG_BIG)
            old_max = m_ref[head:head + 1, :]
            new_max = jnp.maximum(old_max, jnp.max(scores, axis=0, keepdims=True))
            probs = jnp.exp2((scores - new_max) * factor)
            alpha = jnp.exp2((old_max - new_max) * factor)
            m_ref[head:head + 1, :] = new_max
            l_ref[head:head + 1, :] = alpha * l_ref[head:head + 1, :] + jnp.sum(probs, axis=0, keepdims=True)
            acc_ref[rows, :] = alpha * acc_ref[rows, :] + dot_nn(vals_t, probs.astype(BF16))

    @pl.when(tab[2, pair] == 0)
    def _():
        run(False)

    @pl.when(tab[2, pair] == 1)
    def _():
        run(True)
        lse_ref[0] = m_ref[...] * factor + jnp.log2(l_ref[...])
        for head in range(group):
            rows = slice(head * dim, (head + 1) * dim)
            out = acc_ref[rows, :] / l_ref[head:head + 1, :]
            of_ref[rows, :] = out
            ob_ref[rows, :] = out.astype(BF16)


def attn_forward(tab, q_t, kv_all, kv_heads, head_dim):
    width, seq = q_t.shape
    half = seq // 2
    group = width // (kv_heads * head_dim)
    rows = group * head_dim
    n_pairs = tab.shape[1]
    q_spec = pl.BlockSpec((rows, half), lambda k, p, t: (k, t[0, p]))
    return pl.pallas_call(
        functools.partial(attn_fwd_kernel, group, head_dim ** -0.5),
        grid_spec=pltpu.PrefetchScalarGridSpec(
            num_scalar_prefetch=1,
            grid=(kv_heads, n_pairs),
            in_specs=[q_spec,
                      pl.BlockSpec((half, head_dim), lambda k, p, t: (t[1, p], k)),
                      pl.BlockSpec((half, head_dim), lambda k, p, t: (t[1, p], kv_heads + k))],
            out_specs=[q_spec, q_spec,
                       pl.BlockSpec((1, group, half), lambda k, p, t: (k, 0, t[0, p]))],
            scratch_shapes=[pltpu.VMEM((group, half), F32), pltpu.VMEM((group, half), F32),
                            pltpu.VMEM((rows, half), F32)]),
        out_shape=[jax.ShapeDtypeStruct((width, seq), F32), jax.ShapeDtypeStruct((width, seq), BF16),
                   jax.ShapeDtypeStruct((kv_heads, group, seq), F32)],
        compiler_params=pltpu.CompilerParams(vmem_limit_bytes=48 * 2 ** 20),
        cost_estimate=pl.CostEstimate(flops=4 * width * half * half * n_pairs,
                                      bytes_accessed=12 * width * seq, transcendentals=width // head_dim * half * half * n_pairs),
        name='attn_fwd',
    )(tab, q_t, kv_all, kv_all)


def attn_bwd_kernel(group, scale, tab, q_ref, do_ref, of_ref, lse_ref, k_ref, v_ref, dq_ref, dkv_ref, delta_ref, acc_ref):
    pair = pl.program_id(0)
    half, dim = k_ref.shape
    factor = scale * LOG2E
    slot = tab[1, pair]

    @pl.when(pair == 0)
    def _():
        dkv_ref[...] = jnp.zeros(dkv_ref.shape, F32)

    @pl.when(tab[3, pair] == 1)
    def _():
        acc_ref[...] = jnp.zeros(acc_ref.shape, F32)
        for head in range(group):
            rows = slice(head * dim, (head + 1) * dim)
            delta_ref[head:head + 1, :] = jnp.sum(do_ref[rows, :].astype(F32) * of_ref[rows, :], axis=0, keepdims=True)

    def run(masked):
        keys = k_ref[...]
        vals = v_ref[...]
        keys_t = keys.T
        for head in range(group):
            rows = slice(head * dim, (head + 1) * dim)
            q_head = q_ref[rows, :]
            do_head = do_ref[rows, :]
            scores = dot_nn(keys, q_head)
            if masked:
                scores = jnp.where(causal_keep(half), scores, NEG_BIG)
            probs = jnp.exp2(scores * factor - lse_ref[0, head:head + 1, :])
            grad_p = dot_nn(vals, do_head)
            grad_s = (probs * (grad_p - delta_ref[head:head + 1, :])).astype(BF16)
            dkv_ref[slot, 1] += dot_nt(do_head, probs.astype(BF16))
            dkv_ref[slot, 0] += scale * dot_nt(q_head, grad_s)
            acc_ref[rows, :] += dot_nn(keys_t, grad_s)

    @pl.when(tab[2, pair] == 0)
    def _():
        run(False)

    @pl.when(tab[2, pair] == 1)
    def _():
        run(True)
        dq_ref[...] = (scale * acc_ref[...]).astype(BF16)


def attn_backward(tab, q_t, do_t, o_f32, lse, kv_all, kv_heads, head_dim, kv_head):
    width, seq = q_t.shape
    half = seq // 2
    group = width // (kv_heads * head_dim)
    rows = group * head_dim
    n_slots = kv_all.shape[0] // half
    n_pairs = tab.shape[1]
    q_spec = pl.BlockSpec((rows, half), lambda p, t: (kv_head, t[0, p]))
    return pl.pallas_call(
        functools.partial(attn_bwd_kernel, group, head_dim ** -0.5),
        grid_spec=pltpu.PrefetchScalarGridSpec(
            num_scalar_prefetch=1,
            grid=(n_pairs,),
            in_specs=[q_spec, q_spec, q_spec,
                      pl.BlockSpec((1, group, half), lambda p, t: (kv_head, 0, t[0, p])),
                      pl.BlockSpec((half, head_dim), lambda p, t: (t[1, p], kv_head)),
                      pl.BlockSpec((half, head_dim), lambda p, t: (t[1, p], kv_heads + kv_head))],
            out_specs=[pl.BlockSpec((rows, half), lambda p, t: (0, t[0, p])),
                       pl.BlockSpec((n_slots, 2, head_dim, half), lambda p, t: (0, 0, 0, 0))],
            scratch_shapes=[pltpu.VMEM((group, half), F32), pltpu.VMEM((rows, half), F32)]),
        out_shape=[jax.ShapeDtypeStruct((rows, seq), BF16),
                   jax.ShapeDtypeStruct((n_slots, 2, head_dim, half), F32)],
        compiler_params=pltpu.CompilerParams(vmem_limit_bytes=56 * 2 ** 20),
        cost_estimate=pl.CostEstimate(flops=10 * rows * half * half * n_pairs,
                                      bytes_accessed=12 * rows * seq, transcendentals=group * half * half * n_pairs),
        name='attn_bwd',
    )(tab, q_t, do_t, o_f32, lse, kv_all, kv_all)


def gelu_parts(values):
    curve = math.sqrt(2 / math.pi)
    square = values * values
    tanh = jnp.tanh(values * (curve + (curve * 0.044715) * square))
    cdf = 0.5 + 0.5 * tanh
    slope = cdf + (0.5 * values) * (1.0 - tanh * tanh) * (curve + (3 * curve * 0.044715) * square)
    return values * cdf, slope


def ff_kernel(step_rows, h_ref, cot_ref, up_ref, down_ref, *rest):
    act_ref, du_ref, h_out, cot_out = rest[-4:]

    @pl.when(pl.program_id(0) == 0)
    def _():
        h_out[...] = h_ref[...]
        cot_out[...] = cot_ref[...]

    for first in range(0, h_ref.shape[0], step_rows):
        rows = slice(first, first + step_rows)
        hidden = dot_nn(h_ref[rows, :], up_ref[...])
        grad_act = dot_nt(cot_ref[rows, :], down_ref[...]).astype(BF16).astype(F32)
        act, slope = gelu_parts(hidden)
        act_ref[rows, :] = act.astype(BF16)
        du_ref[rows, :] = (grad_act * slope).astype(BF16)


def ff_forward(index, count, h_blk, cot_blk, up, down, carry):
    tokens, d_model = h_blk.shape
    width = up.shape[1]
    tile = FF_TILE
    whole = pl.BlockSpec((tokens, d_model), lambda n: (0, 0))
    shapes = [jax.ShapeDtypeStruct((count * tokens, width), BF16)] * 2 + [jax.ShapeDtypeStruct((count * tokens, d_model), BF16)] * 2
    carry = list(carry)
    return pl.pallas_call(
        functools.partial(ff_kernel, 256),
        grid=(pl.cdiv(width, tile),),
        in_specs=[whole, whole, pl.BlockSpec((d_model, tile), lambda n: (0, n)),
                  pl.BlockSpec((tile, d_model), lambda n: (n, 0))] + [pl.BlockSpec(memory_space=pl.ANY)] * len(carry),
        out_specs=[pl.BlockSpec((tokens, tile), lambda n: (index, n))] * 2 + [pl.BlockSpec((tokens, d_model), lambda n: (index, 0))] * 2,
        out_shape=shapes,
        input_output_aliases={4 + pos: pos for pos in range(len(carry))},
        compiler_params=pltpu.CompilerParams(vmem_limit_bytes=56 * 2 ** 20),
        cost_estimate=pl.CostEstimate(flops=4 * tokens * d_model * width, bytes_accessed=4 * d_model * (width + 2 * tokens),
                                      transcendentals=tokens * width),
        name='ff_forward',
    )(h_blk, cot_blk, up, down, *carry)


def grad_h_kernel(du_ref, up_ref, *rest):
    total = dot_nt(du_ref[...], up_ref[...])
    for extra in rest[:-1]:
        total = total + extra[...]
    rest[-1][...] = total.astype(rest[-1].dtype)


def grad_h_block(index, grad_u, up, extras, dtype):
    d_model, width = up.shape
    tokens = grad_u.shape[0] // 4
    tile = 256
    out_spec = pl.BlockSpec((tokens, tile), lambda n: (0, n))
    return pl.pallas_call(
        grad_h_kernel,
        grid=(d_model // tile,),
        in_specs=[pl.BlockSpec((tokens, width), lambda n: (index, 0)), pl.BlockSpec((tile, width), lambda n: (n, 0))]
        + [out_spec] * len(extras),
        out_specs=out_spec,
        out_shape=jax.ShapeDtypeStruct((tokens, d_model), dtype),
        compiler_params=pltpu.CompilerParams(vmem_limit_bytes=48 * 2 ** 20),
        cost_estimate=pl.CostEstimate(flops=2 * tokens * d_model * width, bytes_accessed=2 * width * (d_model + tokens) + 4 * tokens * d_model,
                                      transcendentals=0),
        name='grad_h',
    )(grad_u, up, *extras)


def spread_kernel(part, scale, idx_ref, got_ref, out_ref):
    count = got_ref.shape[0]
    for blk in range(out_ref.shape[1] // part):
        row, src = blk // count, blk % count
        out_ref[:, blk * part:(blk + 1) * part] = scale * got_ref[idx_ref[0] ^ src, :, row * part:(row + 1) * part]


def spread_columns(my_idx, got, part, scale):
    count, rows, width = got.shape
    return pl.pallas_call(
        functools.partial(spread_kernel, part, scale),
        in_specs=[pl.BlockSpec(memory_space=pltpu.SMEM), pl.BlockSpec(memory_space=pltpu.VMEM)],
        out_specs=pl.BlockSpec(memory_space=pltpu.VMEM),
        out_shape=jax.ShapeDtypeStruct((rows, count * width), F32),
        cost_estimate=pl.CostEstimate(flops=count * rows * width, bytes_accessed=8 * count * rows * width, transcendentals=0),
        name='spread',
    )(my_idx.reshape(1), got)


def solution(mesh):
    cp_size = mesh.shape['cp']
    dp_size = mesh.shape['dp']
    dev_count = cp_size * dp_size

    def swap(values, bits):
        return lax.ppermute(values, 'cp', [(src, src ^ bits) for src in range(cp_size)])

    def dp_reduce(grad):
        return lax.psum_scatter(grad, 'dp', scatter_dimension=0, tiled=True)

    def after(value, *earlier):
        return lax.optimization_barrier((value,) + earlier)[0]

    def per_device(x_loc, cot_loc, w_q, w_k, w_v, w_o, w_up, w_down):
        d_model = x_loc.shape[2]
        kv_heads, head_dim = w_k.shape[1], w_k.shape[2]
        n_heads = w_q.shape[1]
        kv_width = kv_heads * head_dim
        ff_dim = w_up.shape[1]
        ff_part = ff_dim // dev_count
        my_idx = lax.axis_index('cp')
        x = x_loc[0]
        cot = cot_loc[0]
        w_q = w_q.reshape(d_model, n_heads * head_dim)
        w_o = w_o.reshape(d_model, n_heads * head_dim)
        w_kv = jnp.concatenate([w_k.reshape(d_model, kv_width), w_v.reshape(d_model, kv_width)], axis=1)
        tab = pair_table(my_idx, cp_size)

        inv_count = 1.0 / dev_count

        def own_cols(values, bits):
            width = d_model // dev_count
            return jnp.concatenate([lax.dynamic_slice_in_dim(values, (part * cp_size + (my_idx ^ bits)) * width, width, axis=1)
                                    for part in range(dp_size)], axis=1)

        kv_own = dot_nn(x, w_kv).astype(BF16)
        kv_all = lax.all_gather(kv_own, 'cp', axis=0, tiled=True)
        q_t = dot_tt(w_q, x).astype(BF16)

        starts = [(part * cp_size + my_idx) * ff_part for part in range(dp_size)]
        extra = -(dp_size * ff_part) % FF_TILE
        w_up_own = jnp.concatenate([lax.dynamic_slice_in_dim(w_up, start, ff_part, axis=1) for start in starts]
                                   + [jnp.zeros((d_model, extra), BF16)], axis=1)
        w_down_own = jnp.concatenate([lax.dynamic_slice_in_dim(w_down, start, ff_part, axis=0) for start in starts]
                                     + [jnp.zeros((extra, d_model), BF16)], axis=0)

        cot_far = swap(after(cot, kv_all), 2)
        cot_near = swap(cot, 1)
        o_f32, o_t, lse = attn_forward(tab, q_t, kv_all, kv_heads, head_dim)
        o_t = after(o_t, cot_far)

        h_act = (x + dot_tt(o_t, w_o)).astype(BF16)
        h_far = swap(h_act, 2)
        h_near = swap(h_act, 1)
        state = ff_forward(0, cp_size, h_act, cot, w_up_own, w_down_own, ())
        state = ff_forward(1, cp_size, h_near, cot_near, w_up_own, w_down_own, state)
        cot_last = swap(cot_far, 1)
        h_last = swap(after(h_far, state[0]), 1)
        state = ff_forward(2, cp_size, h_far, cot_far, w_up_own, w_down_own, state)
        act_out, grad_u, h_all, cot_all = ff_forward(3, cp_size, h_last, cot_last, w_up_own, w_down_own, state)

        part_up = row_major(inv_count * dot_tn(h_all, grad_u[:, :dp_size * ff_part]))
        up_rows = dp_reduce(part_up)
        grad_u = after(grad_u, part_up)
        part = grad_h_block(3, grad_u, w_up_own, [], F32)
        near = swap(part, 1)
        part = grad_h_block(1, after(grad_u, part), w_up_own, [], F32)
        side = swap(part, 1)
        part = grad_h_block(2, after(grad_u, part), w_up_own, [near], F32)
        far = swap(part, 2)
        part_down = inv_count * dot_tn(after(act_out, part)[:, :dp_size * ff_part], cot_all)
        grad_w_down = dp_reduce(part_down)
        grad_h_bf = grad_h_block(0, after(grad_u, part_down), w_up_own, [cot, side, far], BF16)

        up_got = [lax.dynamic_slice_in_dim(up_rows, (my_idx ^ bits) * (d_model // dev_count), d_model // dev_count, axis=0)
                  for bits in range(cp_size)]
        up_got = jnp.stack([up_got[0]] + [row_major(swap(row_major(up_got[bits]), bits)) for bits in range(1, cp_size)])
        grad_w_up = spread_columns(my_idx, up_got, ff_part, 1.0)

        def block_sum(left, right_t):
            def block(bits):
                return inv_count * dot_tt(own_cols(left, bits), right_t)

            return block

        def first_sends(block):
            parts = block(3), block(1)
            return (swap(parts[0], 1), swap(parts[1], 1)), parts

        def second_send(block, sent):
            part = block(2) + sent[0]
            return swap(part, 2), part

        do_t = dot_tt(w_o, grad_h_bf).astype(BF16)
        o_block = block_sum(grad_h_bf, o_t)
        o_sent, parts = first_sends(o_block)
        do_t = after(do_t, *parts)

        def kv_block(dkv):
            blocks = dkv.reshape((cp_size, 2) + dkv.shape[1:])
            return lambda bits: lax.dynamic_index_in_dim(blocks, my_idx ^ bits, axis=0, keepdims=False)

        dq0_t, dkv0 = attn_backward(tab, q_t, do_t, o_f32, lse, kv_all, kv_heads, head_dim, 0)
        kv0_block, q0_block = kv_block(dkv0), block_sum(x, dq0_t)
        kv0_sent, parts_kv = first_sends(kv0_block)
        q0_sent, parts_q = first_sends(q0_block)
        o_far, part = second_send(o_block, o_sent)
        do_t = after(do_t, part, *parts_kv, *parts_q)
        dq1_t, dkv1 = attn_backward(tab, q_t, do_t, o_f32, lse, kv_all, kv_heads, head_dim, 1)
        kv1_block, q1_block = kv_block(dkv1), block_sum(x, dq1_t)
        kv1_sent, _ = first_sends(kv1_block)
        kv0_far, _ = second_send(kv0_block, kv0_sent)
        q0_far, _ = second_send(q0_block, q0_sent)
        q1_sent, _ = first_sends(q1_block)
        kv1_far, _ = second_send(kv1_block, kv1_sent)
        q1_far, part = second_send(q1_block, q1_sent)
        grad_w_o = dp_reduce(o_block(0) + o_sent[1] + o_far)
        grad_x = grad_h_bf + dot_tt(after(jnp.concatenate([dq0_t, dq1_t], axis=0), part), w_q)
        dkv_parts = [(kv0_block(0) + kv0_sent[1] + kv0_far).astype(BF16), (kv1_block(0) + kv1_sent[1] + kv1_far).astype(BF16)]
        dkv_t = jnp.concatenate([jnp.concatenate([part[0, which], part[1, which]], axis=1)
                                 for which in range(2) for part in dkv_parts], axis=0)
        w_block = block_sum(x, dkv_t)
        w_sent, _ = first_sends(w_block)
        grad_q0 = dp_reduce(q0_block(0) + q0_sent[1] + q0_far)
        w_far, _ = second_send(w_block, w_sent)
        grad_x = grad_x + dot_tt(dkv_t, w_kv)
        grad_q1 = dp_reduce(q1_block(0) + q1_sent[1] + q1_far)
        grad_kv = dp_reduce(w_block(0) + w_sent[1] + w_far)

        own_rows = d_model // dev_count
        grad_w_q = jnp.concatenate([grad_q0, grad_q1], axis=1).reshape(own_rows, n_heads, head_dim)
        grad_w_k = grad_kv[:, :kv_width].reshape(own_rows, kv_heads, head_dim)
        grad_w_v = grad_kv[:, kv_width:].reshape(own_rows, kv_heads, head_dim)
        grad_w_o = grad_w_o.reshape(own_rows, n_heads, head_dim)
        return grad_x.astype(BF16)[None], grad_w_q, grad_w_k, grad_w_v, grad_w_o, grad_w_up, grad_w_down

    act_spec = P('dp', 'cp', None)
    rep_three = P(None, None, None)
    rep_two = P(None, None)
    grad_three = P(('dp', 'cp'), None, None)
    grad_two = P(('dp', 'cp'), None)
    return jax.shard_map(per_device, mesh=mesh,
                         in_specs=(act_spec, act_spec, rep_three, rep_three, rep_three, rep_three, rep_two, rep_two),
                         out_specs=(act_spec, grad_three, grad_three, grad_three, grad_three, grad_two, grad_two),
                         check_vma=False)
```

time: 3390 us -> 1410 us (0.42)
  waiting for transfers between devices: 2240 us -> 575 us
  matrix products: 909 us -> 239 us
  Pallas kernels: 0 us -> 423 us
  other arithmetic: 96.3 us -> 33.2 us
  local copies, waits for them, and re-layouts: 49 us -> 99.4 us
    reduce_scatter x6, waiting for transfers between devices: 2100 us -> 156 us  [dp_reduce(): return lax.psum_scatter(grad, 'dp', scatter_dimension=0, tiled=True)]
    dot_general x43 -> x24, matrix products: 892 us -> 239 us  [the longest x2 125 us: dot_tn(): lax.dot_general(lhs, rhs, (((0,), (0,)), ((), ())), preferred_element_typ...]
    pallas_call x0 -> x12, Pallas kernels: none -> 423 us  [the longest x4 146 us: ff_forward(): pl.pallas_call(functools.partial(ff_kernel, 256), grid=(pl.cdiv(width, ti...]
    ppermute x10 -> x30, waiting for transfers between devices: 140 us -> 385 us  [swap(): lax.ppermute(values, 'cp', [(src, src ^ bits) for src in range(cp_size)])]
    reduce_sum x4 -> x0, other arithmetic: 64.3 us -> none  [fwd_block(): new_sum = alpha * row_sum + exp_scores.sum(axis=-1)]
    all_gather x0 -> x1, waiting for transfers between devices: none -> 34.2 us  [per_device(): kv_all = lax.all_gather(kv_own, 'cp', axis=0, tiled=True)]
  transfers between devices with their start and end apart: 16 -> 37, of which waited for: 11 -> 15; matrix products, arithmetic and copies ran while one was open for 6% -> 21% of each run, Pallas kernels for 0% -> 28%
where the time goes in v1:
time: 1410 us; the launch traced here: 1400 us
  waiting for transfers between devices  575 us (41%)
  Pallas kernels  423 us (30%)
  matrix products  239 us (17%)
  local copies, waits for them, and re-layouts  99.4 us (7%)
  other arithmetic  33.2 us (2%)
  starting transfers between devices  17.3 us (1%)
  between operations  15.3 us (1%)
    ppermute x30, waiting for transfers between devices, swap(): lax.ppermute(values, 'cp', [(src, src ^ bits) for src in range(cp_size)])  385 us
    reduce_scatter x6, waiting for transfers between devices, dp_reduce(): return lax.psum_scatter(grad, 'dp', scatter_dimension=0, tiled=True)  156 us
    pallas_call x4, Pallas kernels, ff_forward(): pl.pallas_call(functools.partial(ff_kernel, 256), grid=(pl.cdiv(width, ti...  146 us
    dot_general x2, matrix products, dot_tn(): lax.dot_general(lhs, rhs, (((0,), (0,)), ((), ())), preferred_element_typ...  125 us
    pallas_call x2, Pallas kernels, attn_backward(): pl.pallas_call(functools.partial(attn_bwd_kernel, group, head_dim ** (-0....  114 us
    dot_general x21, matrix products, dot_tt(): lax.dot_general(lhs, rhs, (((0,), (1,)), ((), ())), preferred_element_typ...  110 us
    pallas_call x1, Pallas kernels, attn_forward(): pl.pallas_call(functools.partial(attn_fwd_kernel, group, head_dim ** (-0....  79.9 us
    pallas_call x4, Pallas kernels, grad_h_block(): pl.pallas_call(grad_h_kernel, grid=(d_model // tile,), in_specs=[pl.Block...  76.4 us
  transfers between devices with their start and end apart: 37, of which 15 were waited for; matrix products, arithmetic and copies ran while one was open for 21% of the time, Pallas kernels for 28%

profile of v1, /device:TPU:0, one launch (start us, length us, event | category | flops | bytes accessed | tf_op | source)
XLA Modules:
  0.0 1402.9 jit_solution(16608026880890927238)
XLA Ops:
  16.2 34.2 %all-gather.2.cloned.1.call-done.k_ref.v_ref = bf16[4096,512]{1,0:T(8,128)(2,1)} async-done(((bf16[1024,512]{1,0:T(8,128)(2,1)}), bf16[4096,512]{1,0:T(8,128)(2,1)}) %all-gather.2.cloned.1.call-update) | async-done | bytes 4194320 | tf_op jit(solution)/shard_map/all_gather | solution.py:330
  50.7 13.9 fusion.26.q_ref
  64.6 79.9 %attn_fwd.1 = (f32[2048,1024]{1,0:T(8,128)}, bf16[2048,1024]{1,0:T(8,128)(2,1)S(1)}, f32[2,8,1024]{2,1,0:T(8,128)S(1)}) custom-call(s32[4,9]{1,0:T(4,128)S(1)} %pad_add_fusion.tab, bf16[2048,1024]{1,0:T(8,128)(2,1)} %fusion.26.q_ref, bf16[4096,512]{1,0:T(8,128)(2,1)} %all-gather.2.cloned.1.call-done.k_ref.v_ref, ...), custom_call_target="tpu_custom_call" | custom-call | flops 19327352832 | bytes 25165824 | tf_op jit(solution)/shard_map/attn_fwd/pallas_call | solution.py:105
  144.6 15.6 %add_convert_fusion.1.h_ref = bf16[1024,2048]{1,0:T(8,128)(2,1)} fusion(bf16[1,1024,2048]{2,1,0:T(8,128)(2,1)S(1)} %copy-done.8, bf16[2048,1024]{1,0:T(8,128)(2,1)S(1)} %get-tuple-element.43, bf16[256,8,16,128]{3,2,1,0:T(8,128)(2,1)} %bitcast.169), kind=kOutput, calls=%fused_computation.15 | convolution fusion | flops 8596226048 | bytes 20971520 | tf_op jit(solution)/shard_map/dot_general | solution.py:37
  160.3 13.1 constant_dynamic-slice_fusion.19
  174.2 20.6 %concatenate.63.up_ref = bf16[2048,2816]{1,0:T(8,128)(2,1)} concatenate(bf16[2048,688]{1,0:T(8,128)(2,1)} %get-tuple-element.77, bf16[2048,688]{1,0:T(8,128)(2,1)} %get-tuple-element.76, bf16[2048,688]{1,0:T(8,128)(2,1)} %get-tuple-element.78, bf16[2048,688]{1,0:T(8,128)(2,1)S(1)} %get-tuple-element.75, bf16[2048,64]{1,0:T(8,128)(2,1)} %broadcast_in_dim.9), dimensions={1} | concatenate | bytes 23068672 | tf_op jit(solution)/shard_map/concatenate | solution.py:335
  194.8 3.7 dynamic-slice_dynamic-update-slice_fusion.3
  198.5 3.7 dynamic-slice_dynamic-update-slice_fusion.2
  202.2 3.8 dynamic-slice_dynamic-update-slice_fusion.1
  206.0 3.9 dynamic-slice_dynamic-update-slice_fusion
  212.4 36.7 %ff_forward.4 = (bf16[4096,2816]{1,0:T(8,128)(2,1)}, bf16[4096,2816]{1,0:T(8,128)(2,1)}, bf16[4096,2048]{1,0:T(8,128)(2,1)}, bf16[4096,2048]{1,0:T(8,128)(2,1)}) custom-call(bf16[1024,2048]{1,0:T(8,128)(2,1)} %add_convert_fusion.1.h_ref, bf16[1024,2048]{1,0:T(8,128)(2,1)} %bitcast.156, bf16[2048,2816]{1,0:T(8,128)(2,1)} %concatenate.63.up_ref, ...), custom_call_target="tpu_custom_call" | custom-call | flops 23622320128 | bytes 39845888 | tf_op jit(solution)/shard_map/ff_forward/pallas_call | solution.py:233
  249.1 36.5 %ff_forward.5 = (bf16[4096,2816]{1,0:T(8,128)(2,1)}, bf16[4096,2816]{1,0:T(8,128)(2,1)}, bf16[4096,2048]{1,0:T(8,128)(2,1)}, bf16[4096,2048]{1,0:T(8,128)(2,1)}) custom-call(bf16[1024,2048]{1,0:T(8,128)(2,1)} %collective-permute-done.2.h_ref, ...), custom_call_target="tpu_custom_call", output_to_operand_aliasing={{0}: (4, {}), {1}: (5, {}), {2}: (6, {}), {3}: (7, {})} | custom-call | flops 23622320128 | bytes 39845888 | tf_op jit(solution)/shard_map/ff_forward/pallas_call | solution.py:233
  285.5 18.4 %collective-permute-done.1.h_ref = bf16[1024,2048]{1,0:T(8,128)(2,1)} collective-permute-done((bf16[1024,2048]{1,0:T(8,128)(2,1)}, bf16[1024,2048]{1,0:T(8,128)(2,1)}, u32[]{:S(2)}, u32[]{:S(2)}) %collective-permute-start.1) | collective-permute-done | bytes 4194336 | tf_op jit(solution)/shard_map/ppermute | solution.py:299
  303.9 36.4 %ff_forward.6 = (bf16[4096,2816]{1,0:T(8,128)(2,1)}, bf16[4096,2816]{1,0:T(8,128)(2,1)}, bf16[4096,2048]{1,0:T(8,128)(2,1)}, bf16[4096,2048]{1,0:T(8,128)(2,1)}) custom-call(bf16[1024,2048]{1,0:T(8,128)(2,1)} %collective-permute-done.1.h_ref, bf16[1024,2048]{1,0:T(8,128)(2,1)} %copy-done.9, ...), custom_call_target="tpu_custom_call", output_to_operand_aliasing={{0}: (4, {}), {1}: (5, {}), {2}: (6, {}), {3}: (7, {})} | custom-call | flops 23622320128 | bytes 39845888 | tf_op jit(solution)/shard_map/ff_forward/pallas_call | solution.py:233
  340.3 36.9 %ff_forward.7 = (bf16[4096,2816]{1,0:T(8,128)(2,1)}, bf16[4096,2816]{1,0:T(8,128)(2,1)}, bf16[4096,2048]{1,0:T(8,128)(2,1)}, bf16[4096,2048]{1,0:T(8,128)(2,1)}) custom-call(bf16[1024,2048]{1,0:T(8,128)(2,1)} %collective-permute-done.4.h_ref, ...), custom_call_target="tpu_custom_call", output_to_operand_aliasing={{0}: (4, {}), {1}: (5, {}), {2}: (6, {}), {3}: (7, {})} | custom-call | flops 23622320128 | bytes 39845888 | tf_op jit(solution)/shard_map/ff_forward/pallas_call | solution.py:233
  377.3 62.4 %fusion.7 = f32[2048,2752]{1,0:T(8,128)} fusion(bf16[4096,2048]{1,0:T(8,128)(2,1)} %get-tuple-element.58, bf16[4096,2816]{1,0:T(8,128)(2,1)} %get-tuple-element.65.du_ref), kind=kOutput, calls=%fused_computation.5 | convolution fusion | flops 46176534528 | bytes 62390272 | tf_op jit(solution)/shard_map/dot_general | solution.py:33
  439.7 18.4 %grad_h.4 = f32[1024,2048]{1,0:T(8,128)} custom-call(bf16[4096,2816]{1,0:T(8,128)(2,1)} %get-tuple-element.65.du_ref, bf16[2048,2816]{1,0:T(8,128)(2,1)} %concatenate.63.up_ref), custom_call_target="tpu_custom_call" | custom-call | flops 11811160064 | bytes 25690112 | tf_op jit(solution)/shard_map/grad_h/pallas_call | solution.py:260
  458.6 18.4 %grad_h.5 = f32[1024,2048]{1,0:T(8,128)} custom-call(bf16[4096,2816]{1,0:T(8,128)(2,1)} %get-tuple-element.65.du_ref, bf16[2048,2816]{1,0:T(8,128)(2,1)} %concatenate.63.up_ref), custom_call_target="tpu_custom_call" | custom-call | flops 11811160064 | bytes 25690112 | tf_op jit(solution)/shard_map/grad_h/pallas_call | solution.py:260
  480.5 19.6 %grad_h.6 = f32[1024,2048]{1,0:T(8,128)} custom-call(bf16[4096,2816]{1,0:T(8,128)(2,1)} %get-tuple-element.65.du_ref, bf16[2048,2816]{1,0:T(8,128)(2,1)} %concatenate.63.up_ref, f32[1024,2048]{1,0:T(8,128)} %copy-done.5), custom_call_target="tpu_custom_call" | custom-call | flops 11811160064 | bytes 25690112 | tf_op jit(solution)/shard_map/grad_h/pallas_call | solution.py:260
  501.7 4.5 dynamic-slice_bitcast_fusion.8
  506.1 62.6 %fusion.4 = f32[2752,2048]{1,0:T(8,128)} fusion(bf16[4096,2048]{1,0:T(8,128)(2,1)} %get-tuple-element.64, bf16[4096,2816]{1,0:T(8,128)(2,1)} %get-tuple-element.63), kind=kOutput, calls=%fused_computation.4 | convolution fusion | flops 46176534528 | bytes 62390272 | tf_op jit(solution)/shard_map/dot_general | solution.py:33
  568.7 114.8 %collective-permute-done.8.rest_2_ = f32[1024,2048]{1,0:T(8,128)} collective-permute-done((f32[1024,2048]{1,0:T(8,128)}, f32[1024,2048]{1,0:T(8,128)}, u32[]{:S(2)}, u32[]{:S(2)}) %collective-permute-start.8) | collective-permute-done | bytes 8388640 | tf_op jit(solution)/shard_map/ppermute | solution.py:299
  683.5 20.0 %grad_h.7 = bf16[1024,2048]{1,0:T(8,128)(2,1)S(1)} custom-call(bf16[4096,2816]{1,0:T(8,128)(2,1)} %get-tuple-element.65.du_ref, bf16[2048,2816]{1,0:T(8,128)(2,1)} %concatenate.63.up_ref, bf16[1024,2048]{1,0:T(8,128)(2,1)} %bitcast.157, f32[1024,2048]{1,0:T(8,128)} %collective-permute-done.7.rest_1_, f32[1024,2048]{1,0:T(8,128)} %collective-permute-done.8.rest_2_), custom_call_target="tpu_custom_call" | custom-call | flops 11811160064 | bytes 25690112 | tf_op jit(solution)/shard_map/grad_h/pallas_call | solution.py:260
  707.8 4.4 convolution_multiply_fusion.1
  712.2 12.8 convert_bitcast_fusion.do_ref
  725.0 4.4 convolution_multiply_fusion
  729.4 56.7 %attn_bwd.2 = (bf16[1024,1024]{1,0:T(8,128)(2,1)}, f32[8,2,128,512]{3,2,1,0:T(8,128)}) custom-call(s32[4,9]{1,0:T(4,128)} %copy-done.1, bf16[2048,1024]{1,0:T(8,128)(2,1)} %fusion.26.q_ref, bf16[2048,1024]{1,0:T(8,128)(2,1)} %convert_bitcast_fusion.do_ref, f32[2048,1024]{1,0:T(8,128)} %get-tuple-element.67.of_ref, f32[2,8,1024]{2,1,0:T(8,128)} %copy-done.4, ...), custom_call_target="tpu_custom_call" | custom-call | flops 24159191040 | bytes 12582912 | tf_op jit(solution)/shard_map/attn_bwd/pallas_call | solution.py:179
  794.9 6.6 multiply_add_fusion
  801.5 57.0 %attn_bwd.3 = (bf16[1024,1024]{1,0:T(8,128)(2,1)}, f32[8,2,128,512]{3,2,1,0:T(8,128)}) custom-call(s32[4,9]{1,0:T(4,128)} %copy-done.1, bf16[2048,1024]{1,0:T(8,128)(2,1)} %fusion.26.q_ref, bf16[2048,1024]{1,0:T(8,128)(2,1)} %convert_bitcast_fusion.do_ref, f32[2048,1024]{1,0:T(8,128)} %get-tuple-element.67.of_ref, f32[2,8,1024]{2,1,0:T(8,128)} %copy-done.4, ...), custom_call_target="tpu_custom_call" | custom-call | flops 24159191040 | bytes 12582912 | tf_op jit(solution)/shard_map/attn_bwd/pallas_call | solution.py:179
  869.5 21.6 %collective-permute-done.13 = f32[2,2,128,512]{3,2,1,0:T(8,128)} collective-permute-done((f32[2,2,128,512]{3,2,1,0:T(8,128)}, f32[2,2,128,512]{3,2,1,0:T(8,128)}, u32[]{:S(2)}, u32[]{:S(2)}) %collective-permute-start.13) | collective-permute-done | bytes 1048608 | tf_op jit(solution)/shard_map/ppermute | solution.py:299
  893.4 19.3 %collective-permute-done.16 = f32[2,2,128,512]{3,2,1,0:T(8,128)} collective-permute-done((f32[2,2,128,512]{3,2,1,0:T(8,128)}, f32[2,2,128,512]{3,2,1,0:T(8,128)}, u32[]{:S(2)}, u32[]{:S(2)}) %collective-permute-start.16) | collective-permute-done | bytes 1048608 | tf_op jit(solution)/shard_map/ppermute | solution.py:299
  925.7 19.7 %collective-permute-done.24 = f32[512,512]{1,0:T(8,128)S(1)} collective-permute-done((f32[512,512]{1,0:T(8,128)S(1)}, f32[512,512]{1,0:T(8,128)S(1)}, u32[]{:S(2)}, u32[]{:S(2)}) %collective-permute-start.24) | collective-permute-done | bytes 1048608 | tf_op jit(solution)/shard_map/ppermute | solution.py:299
  947.3 4.5 convolution_multiply_fusion.3
  953.2 36.4 %collective-permute-done.19 = f32[512,1024]{1,0:T(8,128)} collective-permute-done((f32[512,1024]{1,0:T(8,128)}, f32[512,1024]{1,0:T(8,128)}, u32[]{:S(2)}, u32[]{:S(2)}) %collective-permute-start.19) | collective-permute-done | bytes 2097184 | tf_op jit(solution)/shard_map/ppermute | solution.py:299
  989.6 4.2 add_add_fusion.2
  1004.1 44.9 %collective-permute-done.21 = f32[512,1024]{1,0:T(8,128)S(1)} collective-permute-done((f32[512,1024]{1,0:T(8,128)S(1)}, f32[512,1024]{1,0:T(8,128)S(1)}, u32[]{:S(2)}, u32[]{:S(2)}) %collective-permute-start.21) | collective-permute-done | bytes 2097184 | tf_op jit(solution)/shard_map/ppermute | solution.py:299
  1052.2 4.6 fusion.67
  1056.7 81.8 %collective-permute-done.26 = f32[512,2048]{1,0:T(8,128)} collective-permute-done((f32[512,2048]{1,0:T(8,128)}, f32[512,2048]{1,0:T(8,128)}, u32[]{:S(2)}, u32[]{:S(2)}) %collective-permute-start.26) | collective-permute-done | bytes 4194336 | tf_op jit(solution)/shard_map/ppermute | solution.py:299
  1138.5 6.9 add_add_fusion
  1146.4 4.2 pad_maximum_fusion.1
  1150.6 5.6 fusion.85
  1156.3 5.1 dynamic-slice_bitcast_fusion
  1169.1 17.2 %fusion.22 = bf16[1,1024,2048]{2,1,0:T(8,128)(2,1)} fusion(f32[1024,2048]{1,0:T(8,128)} %fusion.85, bf16[1024,2048]{1,0:T(8,128)(2,1)} %copy-done, bf16[2048,1024]{1,0:T(8,128)(2,1)} %pad_maximum_fusion.1, bf16[256,8,16,128]{3,2,1,0:T(8,128)(2,1)} %bitcast.172), kind=kOutput, calls=%fused_computation.21 | convolution fusion | flops 8598323200 | bytes 29360128 | tf_op jit(solution)/shard_map/dot_general | solution.py:37
  1191.3 4.1 reduce-scatter.13.cloned.1.call-done
  1202.7 26.4 %collective-permute-done.29 = f32[128,2752]{0,1:T(8,128)} collective-permute-done((f32[128,2752]{0,1:T(8,128)}, f32[128,2752]{0,1:T(8,128)}, u32[]{:S(2)}, u32[]{:S(2)}) %collective-permute-start.29) | collective-permute-done | bytes 1409056 | tf_op jit(solution)/shard_map/ppermute | solution.py:299
  1232.0 4.8 pad_maximum_fusion.got_ref
  1236.8 7.0 spread.1
  1243.8 152.0 %reduce-scatter.17.cloned.1.call-done = f32[688,2048]{1,0:T(8,128)} async-done(((f32[2752,2048]{1,0:T(8,128)}), f32[688,2048]{1,0:T(8,128)}) %reduce-scatter.17.cloned.1.call-update) | async-done | bytes 5636112 | tf_op jit(solution)/shard_map/reduce_scatter | solution.py:302
  (241 shorter events, 97.6 us)
Async XLA Ops:
  7.2 43.2 %all-gather.2.cloned.1.call-start = ((), (), s32[]{:S(2)}) async-start(), calls=%async_computation.6 | async-start | bytes 5242880 | tf_op jit(solution)/shard_map/all_gather | solution.py:330
  14.8 1141.4 %reduce-scatter.15.cloned.1.call-start = ((), (), s32[]{:S(2)}) async-start(), calls=%async_computation.11 | async-start | bytes 28835840 | tf_op jit(solution)/shard_map/reduce_scatter | solution.py:302
  15.4 233.7 %collective-permute-start.3 = (bf16[1024,2048]{1,0:T(8,128)(2,1)}, bf16[1024,2048]{1,0:T(8,128)(2,1)}, u32[]{:S(2)}, u32[]{:S(2)}) collective-permute-start(bf16[1024,2048]{1,0:T(8,128)(2,1)} %bitcast.154), channel_id=1, source_target_pairs={{0,1},{1,0},{2,3},{3,2},{4,5},{5,4},{6,7},{7,6},{8,9},{9,8},{10,11... | collective-permute-start | bytes 12582920 | tf_op jit(solution)/shard_map/ppermute | solution.py:299
  50.3 94.2 %collective-permute-start = (bf16[1024,2048]{1,0:T(8,128)(2,1)}, bf16[1024,2048]{1,0:T(8,128)(2,1)S(1)}, u32[]{:S(2)}, u32[]{:S(2)}) collective-permute-start(bf16[1024,2048]{1,0:T(8,128)(2,1)} %bitcast.155), channel_id=1, source_target_pairs={{0,2},{1,3},{2,0},{3,1},{4,6},{5,7},{6,4},{7,5},{8,10},{9,11},{10,... | collective-permute-start | bytes 12582920 | tf_op jit(solution)/shard_map/ppermute | solution.py:299
  64.6 80.0 %copy-start.8 = (bf16[1,1024,2048]{2,1,0:T(8,128)(2,1)S(1)}, bf16[1,1024,2048]{2,1,0:T(8,128)(2,1)}, u32[]{:S(2)}) copy-start(bf16[1,1024,2048]{2,1,0:T(8,128)(2,1)} %param.8) | copy-start | bytes 12582916
  160.2 88.8 %collective-permute-start.2 = (bf16[1024,2048]{1,0:T(8,128)(2,1)}, bf16[1024,2048]{1,0:T(8,128)(2,1)}, u32[]{:S(2)}, u32[]{:S(2)}) collective-permute-start(bf16[1024,2048]{1,0:T(8,128)(2,1)} %add_convert_fusion.1.h_ref), channel_id=1, source_target_pairs={{0,1},{1,0},{2,3},{3,2},{4,5},{5,4},{6,7},{7,6},{8,9},{9,8},{10,11... | collective-permute-start | bytes 12582920 | tf_op jit(solution)/shard_map/ppermute | solution.py:299
  210.6 93.3 %collective-permute-start.1 = (bf16[1024,2048]{1,0:T(8,128)(2,1)}, bf16[1024,2048]{1,0:T(8,128)(2,1)}, u32[]{:S(2)}, u32[]{:S(2)}) collective-permute-start(bf16[1024,2048]{1,0:T(8,128)(2,1)} %add_convert_fusion.1.h_ref), channel_id=1, source_target_pairs={{0,2},{1,3},{2,0},{3,1},{4,6},{5,7},{6,4},{7,5},{8,10},{9,11},{10,... | collective-permute-start | bytes 12582920 | tf_op jit(solution)/shard_map/ppermute | solution.py:299
  212.3 128.0 %collective-permute-start.5 = (bf16[1024,2048]{1,0:T(8,128)(2,1)S(1)}, bf16[1024,2048]{1,0:T(8,128)(2,1)}, u32[]{:S(2)}, u32[]{:S(2)}) collective-permute-start(bf16[1024,2048]{1,0:T(8,128)(2,1)S(1)} %copy-done.10), channel_id=1, source_target_pairs={{0,1},{1,0},{2,3},{3,2},{4,5},{5,4},{6,7},{7,6},{8,9},{9,8},{10,11... | collective-permute-start | bytes 12582920 | tf_op jit(solution)/shard_map/ppermute | solution.py:299
  303.9 36.4 %collective-permute-start.4 = (bf16[1024,2048]{1,0:T(8,128)(2,1)}, bf16[1024,2048]{1,0:T(8,128)(2,1)}, u32[]{:S(2)}, u32[]{:S(2)}) collective-permute-start(bf16[1024,2048]{1,0:T(8,128)(2,1)} %collective-permute-done.1.h_ref), channel_id=1, source_target_pairs={{0,1},{1,0},{2,3},{3,2},{4,5},{5,4},{6,7},{7,6},{8,9},{9,8},{10,11... | collective-permute-start | bytes 12582920 | tf_op jit(solution)/shard_map/ppermute | solution.py:299
  439.6 746.7 %reduce-scatter.11.cloned.1.call-start = ((), (), s32[]{:S(2)}) async-start(), calls=%async_computation.9 | async-start | bytes 1310720 | tf_op jit(solution)/shard_map/reduce_scatter | solution.py:302
  458.1 19.2 %collective-permute-start.6 = (f32[1024,2048]{1,0:T(8,128)}, f32[1024,2048]{1,0:T(8,128)S(1)}, u32[]{:S(2)}, u32[]{:S(2)}) collective-permute-start(f32[1024,2048]{1,0:T(8,128)} %grad_h.4), channel_id=1, source_target_pairs={{0,1},{1,0},{2,3},{3,2},{4,5},{5,4},{6,7},{7,6},{8,9},{9,8},{10,11... | collective-permute-start | bytes 25165832 | tf_op jit(solution)/shard_map/ppermute | solution.py:299
  477.0 91.8 %collective-permute-start.7 = (f32[1024,2048]{1,0:T(8,128)}, f32[1024,2048]{1,0:T(8,128)}, u32[]{:S(2)}, u32[]{:S(2)}) collective-permute-start(f32[1024,2048]{1,0:T(8,128)} %grad_h.5), channel_id=1, source_target_pairs={{0,1},{1,0},{2,3},{3,2},{4,5},{5,4},{6,7},{7,6},{8,9},{9,8},{10,11... | collective-permute-start | bytes 25165832 | tf_op jit(solution)/shard_map/ppermute | solution.py:299
  500.2 183.3 %collective-permute-start.8 = (f32[1024,2048]{1,0:T(8,128)}, f32[1024,2048]{1,0:T(8,128)}, u32[]{:S(2)}, u32[]{:S(2)}) collective-permute-start(f32[1024,2048]{1,0:T(8,128)} %grad_h.6), channel_id=1, source_target_pairs={{0,2},{1,3},{2,0},{3,1},{4,6},{5,7},{6,4},{7,5},{8,10},{9,11},{10,... | collective-permute-start | bytes 25165832 | tf_op jit(solution)/shard_map/ppermute | solution.py:299
  712.2 82.7 %collective-permute-start.9 = (f32[512,2048]{1,0:T(8,128)}, f32[512,2048]{1,0:T(8,128)}, u32[]{:S(2)}, u32[]{:S(2)}) collective-permute-start(f32[512,2048]{1,0:T(8,128)} %convolution_multiply_fusion.1), channel_id=1, source_target_pairs={{0,1},{1,0},{2,3},{3,2},{4,5},{5,4},{6,7},{7,6},{8,9},{9,8},{10,11... | collective-permute-start | bytes 12582920 | tf_op jit(solution)/shard_map/ppermute | solution.py:299
  789.0 73.1 %collective-permute-start.12 = (f32[2,2,128,512]{3,2,1,0:T(8,128)}, f32[2,2,128,512]{3,2,1,0:T(8,128)}, u32[]{:S(2)}, u32[]{:S(2)}) collective-permute-start(f32[2,2,128,512]{3,2,1,0:T(8,128)} %get-tuple-element.118), channel_id=1, source_target_pairs={{0,1},{1,0},{2,3},{3,2},{4,5},{5,4},{6,7},{7,6},{8,9},{9,8},{10,11... | collective-permute-start | bytes 3145736 | tf_op jit(solution)/shard_map/ppermute | solution.py:299
  861.6 4.8 collective-permute-start.15
  861.6 8.0 collective-permute-start.11
  864.8 26.3 %collective-permute-start.13 = (f32[2,2,128,512]{3,2,1,0:T(8,128)}, f32[2,2,128,512]{3,2,1,0:T(8,128)}, u32[]{:S(2)}, u32[]{:S(2)}) collective-permute-start(f32[2,2,128,512]{3,2,1,0:T(8,128)} %bitcast_add_fusion.2), channel_id=1, source_target_pairs={{0,2},{1,3},{2,0},{3,1},{4,6},{5,7},{6,4},{7,5},{8,10},{9,11},{10,... | collective-permute-start | bytes 3145736 | tf_op jit(solution)/shard_map/ppermute | solution.py:299
  866.4 27.0 %collective-permute-start.14 = (f32[2,2,128,512]{3,2,1,0:T(8,128)}, f32[2,2,128,512]{3,2,1,0:T(8,128)}, u32[]{:S(2)}, u32[]{:S(2)}) collective-permute-start(f32[2,2,128,512]{3,2,1,0:T(8,128)} %get-tuple-element.115), channel_id=1, source_target_pairs={{0,1},{1,0},{2,3},{3,2},{4,5},{5,4},{6,7},{7,6},{8,9},{9,8},{10,11... | collective-permute-start | bytes 3145736 | tf_op jit(solution)/shard_map/ppermute | solution.py:299
  869.1 43.6 %collective-permute-start.16 = (f32[2,2,128,512]{3,2,1,0:T(8,128)}, f32[2,2,128,512]{3,2,1,0:T(8,128)}, u32[]{:S(2)}, u32[]{:S(2)}) collective-permute-start(f32[2,2,128,512]{3,2,1,0:T(8,128)} %bitcast_add_fusion), channel_id=1, source_target_pairs={{0,2},{1,3},{2,0},{3,1},{4,6},{5,7},{6,4},{7,5},{8,10},{9,11},{10,... | collective-permute-start | bytes 3145736 | tf_op jit(solution)/shard_map/ppermute | solution.py:299
  893.3 52.1 %copy-start.50 = (bf16[128,512]{1,0:T(8,128)(2,1)}, bf16[128,512]{1,0:T(8,128)(2,1)S(1)}, u32[]{:S(2)}) copy-start(bf16[128,512]{1,0:T(8,128)(2,1)S(1)} %get-tuple-element.120) | copy-start | bytes 393220
  893.3 52.1 %copy-start.52 = (bf16[128,512]{1,0:T(8,128)(2,1)}, bf16[128,512]{1,0:T(8,128)(2,1)S(1)}, u32[]{:S(2)}) copy-start(bf16[128,512]{1,0:T(8,128)(2,1)S(1)} %get-tuple-element.121) | copy-start | bytes 393220
  893.3 52.1 %copy-start.54 = (bf16[128,512]{1,0:T(8,128)(2,1)}, bf16[128,512]{1,0:T(8,128)(2,1)S(1)}, u32[]{:S(2)}) copy-start(bf16[128,512]{1,0:T(8,128)(2,1)S(1)} %get-tuple-element.122) | copy-start | bytes 393220
  914.8 30.6 %copy-start.56 = (bf16[128,512]{1,0:T(8,128)(2,1)}, bf16[128,512]{1,0:T(8,128)(2,1)S(1)}, u32[]{:S(2)}) copy-start(bf16[128,512]{1,0:T(8,128)(2,1)S(1)} %get-tuple-element.123) | copy-start | bytes 393220
  914.9 30.6 %copy-start.58 = (bf16[128,512]{1,0:T(8,128)(2,1)}, bf16[128,512]{1,0:T(8,128)(2,1)S(1)}, u32[]{:S(2)}) copy-start(bf16[128,512]{1,0:T(8,128)(2,1)S(1)} %get-tuple-element.124) | copy-start | bytes 393220
  914.9 30.6 %copy-start.60 = (bf16[128,512]{1,0:T(8,128)(2,1)}, bf16[128,512]{1,0:T(8,128)(2,1)S(1)}, u32[]{:S(2)}) copy-start(bf16[128,512]{1,0:T(8,128)(2,1)S(1)} %get-tuple-element.125) | copy-start | bytes 393220
  914.9 30.6 %copy-start.62 = (bf16[128,512]{1,0:T(8,128)(2,1)}, bf16[128,512]{1,0:T(8,128)(2,1)S(1)}, u32[]{:S(2)}) copy-start(bf16[128,512]{1,0:T(8,128)(2,1)S(1)} %get-tuple-element.126) | copy-start | bytes 393220
  915.8 2.7 collective-permute-start.23
  916.6 4.9 collective-permute-start.18
  917.6 8.1 collective-permute-start.22
  919.3 26.2 %copy-start.15 = (bf16[1024,128]{1,0:T(8,128)(2,1)S(1)}, bf16[1024,128]{1,0:T(8,128)(2,1)}, u32[]{:S(2)}) copy-start(bf16[1024,128]{1,0:T(8,128)(2,1)} %get-tuple-element.99) | copy-start | bytes 786436
  919.3 26.2 %copy-start.16 = (bf16[1024,128]{1,0:T(8,128)(2,1)S(1)}, bf16[1024,128]{1,0:T(8,128)(2,1)}, u32[]{:S(2)}) copy-start(bf16[1024,128]{1,0:T(8,128)(2,1)} %get-tuple-element.100) | copy-start | bytes 786436
  919.3 26.1 %collective-permute-start.24 = (f32[512,512]{1,0:T(8,128)S(1)}, f32[512,512]{1,0:T(8,128)S(1)}, u32[]{:S(2)}, u32[]{:S(2)}) collective-permute-start(f32[512,512]{1,0:T(8,128)S(1)} %fusion.43), channel_id=1, source_target_pairs={{0,2},{1,3},{2,0},{3,1},{4,6},{5,7},{6,4},{7,5},{8,10},{9,11},{10,... | collective-permute-start | bytes 3145736 | tf_op jit(solution)/shard_map/ppermute | solution.py:299
  920.9 32.2 %collective-permute-start.17 = (f32[512,1024]{1,0:T(8,128)}, f32[512,1024]{1,0:T(8,128)}, u32[]{:S(2)}, u32[]{:S(2)}) collective-permute-start(f32[512,1024]{1,0:T(8,128)} %convolution_multiply_fusion.4), channel_id=1, source_target_pairs={{0,1},{1,0},{2,3},{3,2},{4,5},{5,4},{6,7},{7,6},{8,9},{9,8},{10,11... | collective-permute-start | bytes 6291464 | tf_op jit(solution)/shard_map/ppermute | solution.py:299
  924.1 65.5 %collective-permute-start.19 = (f32[512,1024]{1,0:T(8,128)}, f32[512,1024]{1,0:T(8,128)}, u32[]{:S(2)}, u32[]{:S(2)}) collective-permute-start(f32[512,1024]{1,0:T(8,128)} %multiply_add_fusion.1), channel_id=1, source_target_pairs={{0,2},{1,3},{2,0},{3,1},{4,6},{5,7},{6,4},{7,5},{8,10},{9,11},{10,... | collective-permute-start | bytes 6291464 | tf_op jit(solution)/shard_map/ppermute | solution.py:299
  947.2 241.6 %reduce-scatter.7.cloned.1.call-start = ((), (), s32[]{:S(2)}) async-start(), calls=%async_computation.7 | async-start | bytes 2621440 | tf_op jit(solution)/shard_map/reduce_scatter | solution.py:302
  951.8 45.7 %collective-permute-start.10 = (f32[512,1024]{1,0:T(8,128)}, f32[512,1024]{1,0:T(8,128)}, u32[]{:S(2)}, u32[]{:S(2)}) collective-permute-start(f32[512,1024]{1,0:T(8,128)} %convolution_multiply_fusion.3), channel_id=1, source_target_pairs={{0,1},{1,0},{2,3},{3,2},{4,5},{5,4},{6,7},{7,6},{8,9},{9,8},{10,11... | collective-permute-start | bytes 6291464 | tf_op jit(solution)/shard_map/ppermute | solution.py:299
  993.8 195.0 %reduce-scatter.9.cloned.1.call-start = ((), (), s32[]{:S(2)}) async-start(), calls=%async_computation.8 | async-start | bytes 2621440 | tf_op jit(solution)/shard_map/reduce_scatter | solution.py:302
  997.5 6.6 collective-permute-start.20
  1000.5 48.5 %collective-permute-start.21 = (f32[512,1024]{1,0:T(8,128)S(1)}, f32[512,1024]{1,0:T(8,128)S(1)}, u32[]{:S(2)}, u32[]{:S(2)}) collective-permute-start(f32[512,1024]{1,0:T(8,128)S(1)} %multiply_add_fusion.2), channel_id=1, source_target_pairs={{0,2},{1,3},{2,0},{3,1},{4,6},{5,7},{6,4},{7,5},{8,10},{9,11},{10,... | collective-permute-start | bytes 6291464 | tf_op jit(solution)/shard_map/ppermute | solution.py:299
  1002.1 54.6 %collective-permute-start.25 = (f32[512,2048]{1,0:T(8,128)}, f32[512,2048]{1,0:T(8,128)}, u32[]{:S(2)}, u32[]{:S(2)}) collective-permute-start(f32[512,2048]{1,0:T(8,128)} %convolution_multiply_fusion), channel_id=1, source_target_pairs={{0,1},{1,0},{2,3},{3,2},{4,5},{5,4},{6,7},{7,6},{8,9},{9,8},{10,11... | collective-permute-start | bytes 12582920 | tf_op jit(solution)/shard_map/ppermute | solution.py:299
  1002.3 136.2 %collective-permute-start.26 = (f32[512,2048]{1,0:T(8,128)}, f32[512,2048]{1,0:T(8,128)}, u32[]{:S(2)}, u32[]{:S(2)}) collective-permute-start(f32[512,2048]{1,0:T(8,128)} %multiply_add_fusion), channel_id=1, source_target_pairs={{0,2},{1,3},{2,0},{3,1},{4,6},{5,7},{6,4},{7,5},{8,10},{9,11},{10,... | collective-permute-start | bytes 12582920 | tf_op jit(solution)/shard_map/ppermute | solution.py:299
  1051.1 144.3 %reduce-scatter.13.cloned.1.call-start = ((), (), s32[]{:S(2)}) async-start(), calls=%async_computation.10 | async-start | bytes 5242880 | tf_op jit(solution)/shard_map/reduce_scatter | solution.py:302
  1145.5 250.3 %reduce-scatter.17.cloned.1.call-start = ((), (), s32[]{:S(2)}) async-start(), calls=%async_computation.12 | async-start | bytes 28180480 | tf_op jit(solution)/shard_map/reduce_scatter | solution.py:302
  1164.2 33.5 %collective-permute-start.27 = (f32[128,2752]{0,1:T(8,128)}, f32[128,2752]{0,1:T(8,128)}, u32[]{:S(2)}, u32[]{:S(2)}) collective-permute-start(f32[128,2752]{0,1:T(8,128)} %copy.31), channel_id=1, source_target_pairs={{0,1},{1,0},{2,3},{3,2},{4,5},{5,4},{6,7},{7,6},{8,9},{9,8},{10,11... | collective-permute-start | bytes 4227080 | tf_op jit(solution)/shard_map/ppermute | solution.py:299
  1165.7 34.1 %collective-permute-start.28 = (f32[128,2752]{0,1:T(8,128)}, f32[128,2752]{0,1:T(8,128)}, u32[]{:S(2)}, u32[]{:S(2)}) collective-permute-start(f32[128,2752]{0,1:T(8,128)} %copy.33), channel_id=1, source_target_pairs={{0,2},{1,3},{2,0},{3,1},{4,6},{5,7},{6,4},{7,5},{8,10},{9,11},{10,... | collective-permute-start | bytes 4227080 | tf_op jit(solution)/shard_map/ppermute | solution.py:299
  1168.8 60.2 %collective-permute-start.29 = (f32[128,2752]{0,1:T(8,128)}, f32[128,2752]{0,1:T(8,128)}, u32[]{:S(2)}, u32[]{:S(2)}) collective-permute-start(f32[128,2752]{0,1:T(8,128)} %copy.35), channel_id=1, source_target_pairs={{0,3},{1,2},{2,1},{3,0},{4,7},{5,6},{6,5},{7,4},{8,11},{9,10},{10,... | collective-permute-start | bytes 4227080 | tf_op jit(solution)/shard_map/ppermute | solution.py:299
  1202.7 29.3 %copy-start.6 = (f32[1,128,2752]{2,1,0:T(8,128)S(1)}, f32[1,128,2752]{2,1,0:T(8,128)}, u32[]{:S(2)}) copy-start(f32[1,128,2752]{2,1,0:T(8,128)} %get-tuple-element.79) | copy-start | bytes 4227076
  (54 other events, 340.5 us)
Sparse Core Ops, SparseCore 0:
  14.9 35.3 all-gather.1
  439.8 202.0 reduce-scatter.14
  947.4 25.0 reduce-scatter.10
  993.9 32.2 reduce-scatter.6
  1051.2 32.2 reduce-scatter.8
  1145.6 49.6 reduce-scatter.12
  1199.1 196.7 reduce-scatter.16

commit v2 on v1

v2 whole, which is shorter than its diff:
```python
import functools
import math

import jax
import jax.numpy as jnp
from jax import lax
from jax.experimental import pallas as pl
from jax.experimental.pallas import tpu as pltpu
from jax.experimental.layout import Layout, with_layout_constraint
from jax.sharding import PartitionSpec as P


NEG_BIG = -1e30
LOG2E = math.log2(math.e)
F32 = jnp.float32
FF_TILE = 256
BF16 = jnp.bfloat16


def row_major(values):
    return with_layout_constraint(values, Layout(major_to_minor=(0, 1)))


def dot_nn(lhs, rhs):
    return lax.dot_general(lhs, rhs, (((1,), (0,)), ((), ())), preferred_element_type=F32)


def dot_nt(lhs, rhs):
    return lax.dot_general(lhs, rhs, (((1,), (1,)), ((), ())), preferred_element_type=F32)


def dot_tn(lhs, rhs):
    return lax.dot_general(lhs, rhs, (((0,), (0,)), ((), ())), preferred_element_type=F32)


def dot_tt(lhs, rhs):
    return lax.dot_general(lhs, rhs, (((0,), (1,)), ((), ())), preferred_element_type=F32)


def pair_table(my_idx, cp_size):
    steps = jnp.arange(2 * cp_size + 1)
    late = steps > my_idx
    key_block = jnp.where(late, steps - my_idx - 1, steps)
    key_slot = jnp.where(key_block < cp_size, 2 * key_block, 2 * (2 * cp_size - 1 - key_block) + 1)
    last = (steps == my_idx) | (steps == 2 * cp_size)
    first = (steps == 0) | (steps == my_idx + 1)
    return jnp.stack([late, key_slot, last, first]).astype(jnp.int32)


def causal_keep(half):
    keys = lax.broadcasted_iota(jnp.int32, (half, half), 0)
    queries = lax.broadcasted_iota(jnp.int32, (half, half), 1)
    return keys <= queries


def attn_fwd_kernel(group, scale, tab, q_ref, k_ref, v_ref, of_ref, ob_ref, lse_ref, m_ref, l_ref):
    dim = k_ref.shape[1]
    half = q_ref.shape[1] // 2
    factor = scale * LOG2E

    def pair_step(pair, carry):
        cols = pl.ds(pl.multiple_of(tab[0, pair] * half, half), half)
        slot = pl.ds(pl.multiple_of(tab[1, pair] * half, half), half)

        @pl.when(tab[3, pair] == 1)
        def _():
            m_ref[...] = jnp.full(m_ref.shape, NEG_BIG, F32)
            l_ref[...] = jnp.zeros(l_ref.shape, F32)
            of_ref[:, cols] = jnp.zeros((of_ref.shape[0], half), F32)

        def run(masked):
            keys = k_ref[slot, :]
            vals_t = v_ref[slot, :].T
            for head in range(group):
                rows = slice(head * dim, (head + 1) * dim)
                scores = dot_nn(keys, q_ref[rows, cols])
                if masked:
                    scores = jnp.where(causal_keep(half), scores, NEG_BIG)
                old_max = m_ref[head:head + 1, :]
                new_max = jnp.maximum(old_max, jnp.max(scores, axis=0, keepdims=True))
                probs = jnp.exp2((scores - new_max) * factor)
                alpha = jnp.exp2((old_max - new_max) * factor)
                m_ref[head:head + 1, :] = new_max
                l_ref[head:head + 1, :] = alpha * l_ref[head:head + 1, :] + jnp.sum(probs, axis=0, keepdims=True)
                of_ref[rows, cols] = alpha * of_ref[rows, cols] + dot_nn(vals_t, probs.astype(BF16))

        @pl.when(tab[2, pair] == 0)
        def _():
            run(False)

        @pl.when(tab[2, pair] == 1)
        def _():
            run(True)
            lse_ref[0, :, cols] = m_ref[...] * factor + jnp.log2(l_ref[...])
            for head in range(group):
                rows = slice(head * dim, (head + 1) * dim)
                out = of_ref[rows, cols] / l_ref[head:head + 1, :]
                of_ref[rows, cols] = out
                ob_ref[rows, cols] = out.astype(BF16)

        return carry

    lax.fori_loop(0, tab.shape[1], pair_step, 0)


def attn_forward(tab, q_t, kv_all, kv_heads, head_dim):
    width, seq = q_t.shape
    half = seq // 2
    group = width // (kv_heads * head_dim)
    rows = group * head_dim
    n_pairs = tab.shape[1]
    q_spec = pl.BlockSpec((rows, seq), lambda k, t: (k, 0))
    return pl.pallas_call(
        functools.partial(attn_fwd_kernel, group, head_dim ** -0.5),
        grid_spec=pltpu.PrefetchScalarGridSpec(
            num_scalar_prefetch=1,
            grid=(kv_heads,),
            in_specs=[q_spec,
                      pl.BlockSpec((kv_all.shape[0], head_dim), lambda k, t: (0, k)),
                      pl.BlockSpec((kv_all.shape[0], head_dim), lambda k, t: (0, kv_heads + k))],
            out_specs=[q_spec, q_spec,
                       pl.BlockSpec((1, group, seq), lambda k, t: (k, 0, 0))],
            scratch_shapes=[pltpu.VMEM((group, half), F32), pltpu.VMEM((group, half), F32)]),
        out_shape=[jax.ShapeDtypeStruct((width, seq), F32), jax.ShapeDtypeStruct((width, seq), BF16),
                   jax.ShapeDtypeStruct((kv_heads, group, seq), F32)],
        compiler_params=pltpu.CompilerParams(vmem_limit_bytes=56 * 2 ** 20),
        cost_estimate=pl.CostEstimate(flops=4 * width * half * half * n_pairs,
                                      bytes_accessed=12 * width * seq, transcendentals=width // head_dim * half * half * n_pairs),
        name='attn_fwd',
    )(tab, q_t, kv_all, kv_all)


def attn_bwd_kernel(group, scale, tab, q_ref, do_ref, of_ref, lse_ref, k_ref, v_ref, dq_ref, dkv_ref, delta_ref, acc_ref):
    dim = k_ref.shape[1]
    half = q_ref.shape[1] // 2
    factor = scale * LOG2E
    dkv_ref[...] = jnp.zeros(dkv_ref.shape, F32)

    def pair_step(pair, carry):
        cols = pl.ds(pl.multiple_of(tab[0, pair] * half, half), half)
        slot = tab[1, pair]
        slot_rows = pl.ds(pl.multiple_of(slot * half, half), half)

        @pl.when(tab[3, pair] == 1)
        def _():
            acc_ref[...] = jnp.zeros(acc_ref.shape, F32)
            for head in range(group):
                rows = slice(head * dim, (head + 1) * dim)
                delta_ref[head:head + 1, :] = jnp.sum(do_ref[rows, cols].astype(F32) * of_ref[rows, cols], axis=0, keepdims=True)

        def run(masked):
            keys = k_ref[slot_rows, :]
            vals = v_ref[slot_rows, :]
            keys_t = keys.T
            for head in range(group):
                rows = slice(head * dim, (head + 1) * dim)
                q_head = q_ref[rows, cols]
                do_head = do_ref[rows, cols]
                scores = dot_nn(keys, q_head)
                if masked:
                    scores = jnp.where(causal_keep(half), scores, NEG_BIG)
                probs = jnp.exp2(scores * factor - lse_ref[0, head:head + 1, cols])
                grad_p = dot_nn(vals, do_head)
                grad_s = (probs * (grad_p - delta_ref[head:head + 1, :])).astype(BF16)
                dkv_ref[slot, 1] += dot_nt(do_head, probs.astype(BF16))
                dkv_ref[slot, 0] += scale * dot_nt(q_head, grad_s)
                acc_ref[rows, :] += dot_nn(keys_t, grad_s)

        @pl.when(tab[2, pair] == 0)
        def _():
            run(False)

        @pl.when(tab[2, pair] == 1)
        def _():
            run(True)
            dq_ref[:, cols] = (scale * acc_ref[...]).astype(BF16)

        return carry

    lax.fori_loop(0, tab.shape[1], pair_step, 0)


def attn_backward(tab, q_t, do_t, o_f32, lse, kv_all, kv_heads, head_dim, kv_head):
    width, seq = q_t.shape
    half = seq // 2
    group = width // (kv_heads * head_dim)
    rows = group * head_dim
    n_slots = kv_all.shape[0] // half
    n_pairs = tab.shape[1]
    q_spec = pl.BlockSpec((rows, seq), lambda p, t: (kv_head, 0))
    return pl.pallas_call(
        functools.partial(attn_bwd_kernel, group, head_dim ** -0.5),
        grid_spec=pltpu.PrefetchScalarGridSpec(
            num_scalar_prefetch=1,
            grid=(1,),
            in_specs=[q_spec, q_spec, q_spec,
                      pl.BlockSpec((1, group, seq), lambda p, t: (kv_head, 0, 0)),
                      pl.BlockSpec((kv_all.shape[0], head_dim), lambda p, t: (0, kv_head)),
                      pl.BlockSpec((kv_all.shape[0], head_dim), lambda p, t: (0, kv_heads + kv_head))],
            out_specs=[pl.BlockSpec((rows, seq), lambda p, t: (0, 0)),
                       pl.BlockSpec((n_slots, 2, head_dim, half), lambda p, t: (0, 0, 0, 0))],
            scratch_shapes=[pltpu.VMEM((group, half), F32), pltpu.VMEM((rows, half), F32)]),
        out_shape=[jax.ShapeDtypeStruct((rows, seq), BF16),
                   jax.ShapeDtypeStruct((n_slots, 2, head_dim, half), F32)],
        compiler_params=pltpu.CompilerParams(vmem_limit_bytes=56 * 2 ** 20),
        cost_estimate=pl.CostEstimate(flops=10 * rows * half * half * n_pairs,
                                      bytes_accessed=12 * rows * seq, transcendentals=group * half * half * n_pairs),
        name='attn_bwd',
    )(tab, q_t, do_t, o_f32, lse, kv_all, kv_all)


def gelu_parts(values):
    curve = math.sqrt(2 / math.pi)
    square = values * values
    tanh = jnp.tanh(values * (curve + (curve * 0.044715) * square))
    cdf = 0.5 + 0.5 * tanh
    slope = cdf + (0.5 * values) * (1.0 - tanh * tanh) * (curve + (3 * curve * 0.044715) * square)
    return values * cdf, slope


def prep_kernel(segs, parts, idx_ref, *refs):
    n_blocks = sum(seg['tiles'] + 1 for seg in segs)
    blocks, down_ref = refs[:n_blocks], refs[n_blocks]
    n_parts = len(parts)
    up_refs, down_refs = refs[n_blocks + 1:n_blocks + 1 + n_parts], refs[n_blocks + 1 + n_parts:n_blocks + 1 + 2 * n_parts]
    buf_ref, zero_ref, in_sem, out_sem = refs[n_blocks + 1 + 2 * n_parts:]
    step = pl.program_id(0)
    n_own, own_rows = buf_ref.shape[0], buf_ref.shape[1]
    ins = [pltpu.make_async_copy(down_ref.at[pl.ds(pl.multiple_of(idx_ref[0, own], 16), own_rows)], buf_ref.at[own], in_sem.at[own])
           for own in range(n_own)]
    outs = []
    for part, down_out in zip(parts, down_refs):
        for own in range(n_own):
            outs.append(pltpu.make_async_copy(buf_ref.at[own, pl.ds(part['first'], part['rows'])],
                                              down_out.at[pl.ds(own * part['rows'], part['rows'])], out_sem.at[len(outs)]))
        if part['pad']:
            outs.append(pltpu.make_async_copy(zero_ref.at[pl.ds(0, part['pad'])],
                                              down_out.at[pl.ds(n_own * part['rows'], part['pad'])], out_sem.at[len(outs)]))

    @pl.when(step == 0)
    def _():
        zero_ref[...] = jnp.zeros(zero_ref.shape, BF16)
        for copy in ins:
            copy.start()

    @pl.when(step == 1)
    def _():
        for copy in ins:
            copy.wait()
        for copy in outs:
            copy.start()

    rows = blocks[0].shape[0]
    lanes = lax.broadcasted_iota(jnp.int32, (rows, 128), 1)
    cover = [{} for _ in parts]
    pos = 0
    for number, seg in enumerate(segs):
        shift = idx_ref[1, number]
        turned = [pltpu.roll(blocks[pos + tile][...].astype(F32), (128 - shift) % 128, 1) for tile in range(seg['tiles'] + 1)]
        pos += seg['tiles'] + 1
        for tile in range(seg['tiles']):
            cover[seg['part']].setdefault(seg['tile'] + tile, []).append(
                (seg['start'], jnp.where(lanes < 128 - shift, turned[tile], turned[tile + 1])))
    for part, tiles, up_ref in zip(parts, cover, up_refs):
        used = n_own * part['rows']
        for tile in range(up_ref.shape[1] // 128):
            value = jnp.zeros((rows, 128), F32)
            for start, piece in tiles.get(tile, []):
                value = piece if start <= tile * 128 else jnp.where(lanes >= start - tile * 128, piece, value)
            if used < (tile + 1) * 128:
                value = jnp.where(lanes < used - tile * 128, value, 0.0)
            up_ref[:, tile * 128:(tile + 1) * 128] = value.astype(BF16)

    @pl.when(step == pl.num_programs(0) - 1)
    def _():
        for copy in outs:
            copy.wait()


def prepare(starts, splits, w_up, w_down):
    d_model, own_rows = w_up.shape[0], splits[-1][0] + splits[-1][1]
    n_own = starts.shape[0]
    parts = [{'first': first, 'rows': count, 'pad': -(n_own * count) % FF_TILE} for first, count in splits]
    segs, shifts, bases = [], [], []
    for number, part in enumerate(parts):
        for own in range(n_own):
            dest = own * part['rows']
            segs.append({'part': number, 'start': dest, 'tile': dest // 128, 'tiles': -(-(dest % 128 + part['rows']) // 128)})
            source = starts[own] + part['first'] - dest % 128
            shifts.append(source % 128)
            bases.append(source // 128)
    table = jnp.stack([jnp.pad(starts, (0, len(segs) - n_own)), jnp.stack(shifts), jnp.stack(bases)]).astype(jnp.int32)
    rows = 512
    last = w_up.shape[1] // 128 - 1
    in_specs = []
    for number, seg in enumerate(segs):
        for tile in range(seg['tiles'] + 1):
            in_specs.append(pl.BlockSpec((rows, 128), lambda i, t, number=number, tile=tile:
                                         (i, jnp.clip(t[2, number] + tile, 0, last))))
    widths = [n_own * part['rows'] + part['pad'] for part in parts]
    outs = pl.pallas_call(
        functools.partial(prep_kernel, segs, parts),
        grid_spec=pltpu.PrefetchScalarGridSpec(
            num_scalar_prefetch=1,
            grid=(d_model // rows,),
            in_specs=in_specs + [pl.BlockSpec(memory_space=pl.ANY)],
            out_specs=[pl.BlockSpec((rows, width), lambda i, t: (i, 0)) for width in widths]
            + [pl.BlockSpec(memory_space=pl.ANY) for _ in widths],
            scratch_shapes=[pltpu.VMEM((n_own, own_rows, d_model), BF16), pltpu.VMEM((64, d_model), BF16),
                            pltpu.SemaphoreType.DMA((n_own,)), pltpu.SemaphoreType.DMA((n_own * len(parts) + len(parts),))]),
        out_shape=[jax.ShapeDtypeStruct((d_model, width), BF16) for width in widths]
        + [jax.ShapeDtypeStruct((width, d_model), BF16) for width in widths],
        compiler_params=pltpu.CompilerParams(vmem_limit_bytes=56 * 2 ** 20),
        cost_estimate=pl.CostEstimate(flops=8 * d_model * sum(widths), bytes_accessed=9 * d_model * sum(widths), transcendentals=0),
        name='prepare',
    )(table, *([w_up] * len(in_specs)), w_down)
    return outs[:len(parts)], outs[len(parts):]


def ff_kernel(step_rows, copies, index, h_ref, cot_ref, up_ref, down_ref, *rest):
    if copies:
        act_ref, du_ref, h_out, cot_out, sem = rest[-5:]
        rows = pl.ds(index * h_ref.shape[0], h_ref.shape[0])
        moves = [pltpu.make_async_copy(h_ref, h_out.at[rows], sem.at[0]), pltpu.make_async_copy(cot_ref, cot_out.at[rows], sem.at[1])]

        @pl.when(pl.program_id(0) == 0)
        def _():
            for move in moves:
                move.start()
    else:
        act_ref, du_ref = rest[-2:]

    for first in range(0, h_ref.shape[0], step_rows):
        rows = slice(first, first + step_rows)
        hidden = dot_nn(h_ref[rows, :], up_ref[...])
        grad_act = dot_nt(cot_ref[rows, :], down_ref[...]).astype(BF16).astype(F32)
        act, slope = gelu_parts(hidden)
        act_ref[rows, :] = act.astype(BF16)
        du_ref[rows, :] = (grad_act * slope).astype(BF16)

    if copies:
        @pl.when(pl.program_id(0) == pl.num_programs(0) - 1)
        def _():
            for move in moves:
                move.wait()


def ff_forward(index, count, h_blk, cot_blk, up, down, copies, carry):
    tokens, d_model = h_blk.shape
    width = up.shape[1]
    tile = FF_TILE
    whole = pl.BlockSpec((tokens, d_model), lambda n: (0, 0))
    shapes = [jax.ShapeDtypeStruct((count * tokens, width), BF16)] * 2
    specs = [pl.BlockSpec((tokens, tile), lambda n: (index, n))] * 2
    if copies:
        shapes = shapes + [jax.ShapeDtypeStruct((count * tokens, d_model), BF16)] * 2
        specs = specs + [pl.BlockSpec(memory_space=pl.ANY)] * 2
    carry = list(carry)
    return pl.pallas_call(
        functools.partial(ff_kernel, 256, copies, index),
        grid=(width // tile,),
        in_specs=[whole, whole, pl.BlockSpec((d_model, tile), lambda n: (0, n)),
                  pl.BlockSpec((tile, d_model), lambda n: (n, 0))] + [pl.BlockSpec(memory_space=pl.ANY)] * len(carry),
        out_specs=specs,
        out_shape=shapes,
        input_output_aliases={4 + pos: pos for pos in range(len(carry))},
        scratch_shapes=[pltpu.SemaphoreType.DMA((2,))] if copies else [],
        compiler_params=pltpu.CompilerParams(vmem_limit_bytes=56 * 2 ** 20),
        cost_estimate=pl.CostEstimate(flops=4 * tokens * d_model * width, bytes_accessed=4 * d_model * (width + 2 * tokens),
                                      transcendentals=tokens * width),
        name='ff_forward',
    )(h_blk, cot_blk, up, down, *carry)


def grad_h_kernel(n_parts, *refs):
    total = sum(dot_nt(refs[2 * part][...], refs[2 * part + 1][...]) for part in range(n_parts))
    for extra in refs[2 * n_parts:-1]:
        total = total + extra[...]
    refs[-1][...] = total.astype(refs[-1].dtype)


def grad_h_block(index, grad_u, up, extras, dtype):
    d_model = up[0].shape[0]
    tokens = grad_u[0].shape[0] // 4
    width = sum(part.shape[1] for part in up)
    tile = 256
    out_spec = pl.BlockSpec((tokens, tile), lambda n: (0, n))
    in_specs, args = [], []
    for left, right in zip(grad_u, up):
        in_specs += [pl.BlockSpec((tokens, left.shape[1]), lambda n: (index, 0)), pl.BlockSpec((tile, right.shape[1]), lambda n: (n, 0))]
        args += [left, right]
    return pl.pallas_call(
        functools.partial(grad_h_kernel, len(up)),
        grid=(d_model // tile,),
        in_specs=in_specs + [out_spec] * len(extras),
        out_specs=out_spec,
        out_shape=jax.ShapeDtypeStruct((tokens, d_model), dtype),
        compiler_params=pltpu.CompilerParams(vmem_limit_bytes=48 * 2 ** 20),
        cost_estimate=pl.CostEstimate(flops=2 * tokens * d_model * width, bytes_accessed=2 * width * (d_model + tokens) + 4 * tokens * d_model,
                                      transcendentals=0),
        name='grad_h',
    )(*args, *extras)


def spread_kernel(splits, idx_ref, *refs):
    got_refs, out_ref = refs[:-1], refs[-1]
    count = got_refs[0].shape[0]
    block = splits[-1][0] + splits[-1][1]
    for dest in range(out_ref.shape[1] // block):
        row, src = dest // count, dest % count
        for (first, cols), got_ref in zip(splits, got_refs):
            out_ref[:, dest * block + first:dest * block + first + cols] = got_ref[idx_ref[0] ^ src, :, row * cols:(row + 1) * cols]


def spread_columns(my_idx, got, splits):
    count, rows = got[0].shape[:2]
    width = count * sum(part.shape[2] for part in got)
    return pl.pallas_call(
        functools.partial(spread_kernel, splits),
        in_specs=[pl.BlockSpec(memory_space=pltpu.SMEM)] + [pl.BlockSpec(memory_space=pltpu.VMEM)] * len(got),
        out_specs=pl.BlockSpec(memory_space=pltpu.VMEM),
        out_shape=jax.ShapeDtypeStruct((rows, width), F32),
        cost_estimate=pl.CostEstimate(flops=rows * width, bytes_accessed=8 * rows * width, transcendentals=0),
        name='spread',
    )(my_idx.reshape(1), *got)


def solution(mesh):
    cp_size = mesh.shape['cp']
    dp_size = mesh.shape['dp']
    dev_count = cp_size * dp_size

    def swap(values, bits):
        return lax.ppermute(values, 'cp', [(src, src ^ bits) for src in range(cp_size)])

    def dp_reduce(grad):
        return lax.psum_scatter(grad, 'dp', scatter_dimension=0, tiled=True)

    def after(value, *earlier):
        return lax.optimization_barrier((value,) + earlier)[0]

    def per_device(x_loc, cot_loc, w_q, w_k, w_v, w_o, w_up, w_down):
        d_model = x_loc.shape[2]
        kv_heads, head_dim = w_k.shape[1], w_k.shape[2]
        n_heads = w_q.shape[1]
        kv_width = kv_heads * head_dim
        ff_dim = w_up.shape[1]
        ff_part = ff_dim // dev_count
        my_idx = lax.axis_index('cp')
        x = x_loc[0]
        cot = cot_loc[0]
        w_q = w_q.reshape(d_model, n_heads * head_dim)
        w_o = w_o.reshape(d_model, n_heads * head_dim)
        w_kv = jnp.concatenate([w_k.reshape(d_model, kv_width), w_v.reshape(d_model, kv_width)], axis=1)
        tab = pair_table(my_idx, cp_size)

        inv_count = 1.0 / dev_count

        def own_cols(values, bits):
            width = d_model // dev_count
            return jnp.concatenate([lax.dynamic_slice_in_dim(values, (part * cp_size + (my_idx ^ bits)) * width, width, axis=1)
                                    for part in range(dp_size)], axis=1)

        kv_own = dot_nn(x, w_kv).astype(BF16)
        kv_all = lax.all_gather(kv_own, 'cp', axis=0, tiled=True)
        cot_near = swap(cot, 1)
        q_t = dot_tt(w_q, x).astype(BF16)

        first_part = FF_TILE * (dp_size * ff_part // (2 * FF_TILE)) // dp_size
        splits = ((0, first_part), (first_part, ff_part - first_part))
        used = [dp_size * count for _, count in splits]
        starts = (jnp.arange(dp_size) * cp_size + my_idx) * ff_part
        w_up_own, w_down_own = prepare(starts, splits, w_up, w_down)

        kv_all = after(kv_all, q_t, w_up_own[0])
        cot_far = swap(after(cot, kv_all), 2)
        o_f32, o_t, lse = attn_forward(tab, q_t, kv_all, kv_heads, head_dim)
        o_t = after(o_t, cot_far)

        h_act = (x + dot_tt(o_t, w_o)).astype(BF16)
        h_far = swap(h_act, 2)
        h_near = swap(h_act, 1)
        cot_last = swap(cot_far, 1)
        state = ff_forward(0, cp_size, h_act, cot, w_up_own[0], w_down_own[0], True, ())
        state = ff_forward(1, cp_size, h_near, cot_near, w_up_own[0], w_down_own[0], True, state)
        more = ff_forward(0, cp_size, after(h_act, state[0]), cot, w_up_own[1], w_down_own[1], False, ())
        more = ff_forward(1, cp_size, h_near, cot_near, w_up_own[1], w_down_own[1], False, more)
        h_far = after(h_far, more[0])
        h_last = swap(h_far, 1)
        state = ff_forward(2, cp_size, h_far, cot_far, w_up_own[0], w_down_own[0], True, state)
        act0, grad_u0, h_all, cot_all = ff_forward(3, cp_size, h_last, cot_last, w_up_own[0], w_down_own[0], True, state)
        part = row_major(inv_count * dot_tn(h_all, grad_u0))
        up_rows = [dp_reduce(part)]
        later = after(h_far, part)
        more = ff_forward(2, cp_size, later, cot_far, w_up_own[1], w_down_own[1], False, more)
        act1, grad_u1 = ff_forward(3, cp_size, h_last, cot_last, w_up_own[1], w_down_own[1], False, more)

        part = grad_h_block(3, (grad_u0, grad_u1), w_up_own, [], F32)
        near = swap(part, 1)
        later = after(grad_u1, part)
        part = row_major(inv_count * dot_tn(h_all, later[:, :used[1]]))
        up_rows.append(dp_reduce(part))
        later = after(grad_u1, part)
        part = grad_h_block(2, (grad_u0, later), w_up_own, [near], F32)
        far = swap(part, 2)
        later = after(act0, part)
        part = row_major(inv_count * dot_tn(later, cot_all))
        down_rows = [dp_reduce(part)]
        later = after(act1, part)
        part = row_major(inv_count * dot_tn(later[:, :used[1]], cot_all))
        down_rows.append(dp_reduce(part))
        later = after(grad_u1, part)
        part = grad_h_block(1, (grad_u0, later), w_up_own, [], F32)
        side = swap(part, 1)
        far = after(far, part)

        own_rows = d_model // dev_count
        up_got = []
        for rows_of in up_rows:
            blocks = [lax.dynamic_slice_in_dim(rows_of, (my_idx ^ bits) * own_rows, own_rows, axis=0) for bits in range(cp_size)]
            up_got.append(jnp.stack([blocks[0]] + [row_major(swap(row_major(blocks[bits]), bits))
                                                   for bits in range(1, cp_size)]))
        later = after(grad_u1, part)
        grad_h_bf = grad_h_block(0, (grad_u0, later), w_up_own, [cot, side, far], BF16)
        grad_w_up = spread_columns(my_idx, up_got, splits)

        def block_sum(left, right_t):
            def block(bits):
                return inv_count * dot_tt(own_cols(left, bits), right_t)

            return block

        def first_sends(block):
            parts = block(3), block(1)
            return (swap(parts[0], 1), swap(parts[1], 1)), parts

        def second_send(block, sent):
            part = block(2) + sent[0]
            return swap(part, 2), part

        o_block = block_sum(grad_h_bf, o_t)
        o_sent, parts = first_sends(o_block)
        later = after(grad_h_bf, *parts)
        do_t = dot_tt(w_o, later).astype(BF16)
        o_sent = (after(o_sent[0], do_t), o_sent[1])
        o_far, part = second_send(o_block, o_sent)
        do_t = after(do_t, part)

        def kv_block(dkv):
            blocks = dkv.reshape((cp_size, 2) + dkv.shape[1:])
            return lambda bits: lax.dynamic_index_in_dim(blocks, my_idx ^ bits, axis=0, keepdims=False)

        dq0_t, dkv0 = attn_backward(tab, q_t, do_t, o_f32, lse, kv_all, kv_heads, head_dim, 0)
        kv0_block, q0_block = kv_block(dkv0), block_sum(x, dq0_t)
        kv0_sent, _ = first_sends(kv0_block)
        q0_sent, parts_q = first_sends(q0_block)
        kv0_far, part_kv = second_send(kv0_block, (after(kv0_sent[0], *parts_q), kv0_sent[1]))
        q0_far, part_q = second_send(q0_block, q0_sent)
        do_t = after(do_t, part_kv, part_q)
        dq1_t, dkv1 = attn_backward(tab, q_t, do_t, o_f32, lse, kv_all, kv_heads, head_dim, 1)
        kv1_block, q1_block = kv_block(dkv1), block_sum(x, dq1_t)
        kv1_sent, _ = first_sends(kv1_block)
        q1_sent, parts_q = first_sends(q1_block)
        grad_w_o = dp_reduce(after(o_block(0), *parts_q) + o_sent[1] + o_far)
        kv1_far, part_kv = second_send(kv1_block, kv1_sent)
        q1_far, part_q = second_send(q1_block, q1_sent)
        grad_q0 = dp_reduce(q0_block(0) + q0_sent[1] + q0_far)
        later = after(jnp.concatenate([dq0_t, dq1_t], axis=0), part_q, part_kv)
        grad_x = dot_tt(later, w_q)
        grad_x = grad_h_bf + grad_x
        dkv_parts = [(kv0_block(0) + kv0_sent[1] + kv0_far).astype(BF16), (kv1_block(0) + kv1_sent[1] + kv1_far).astype(BF16)]
        dkv_t = jnp.concatenate([jnp.concatenate([part[0, which], part[1, which]], axis=1)
                                 for which in range(2) for part in dkv_parts], axis=0)
        w_block = block_sum(x, dkv_t)
        w_sent, _ = first_sends(w_block)
        w_far, _ = second_send(w_block, w_sent)
        grad_q1 = dp_reduce(q1_block(0) + q1_sent[1] + q1_far)
        grad_x = grad_x + dot_tt(dkv_t, w_kv)
        grad_kv = dp_reduce(w_block(0) + w_sent[1] + w_far)
        grad_w_down = jnp.concatenate(down_rows, axis=0)

        grad_w_q = jnp.concatenate([grad_q0, grad_q1], axis=1).reshape(own_rows, n_heads, head_dim)
        grad_w_k = grad_kv[:, :kv_width].reshape(own_rows, kv_heads, head_dim)
        grad_w_v = grad_kv[:, kv_width:].reshape(own_rows, kv_heads, head_dim)
        grad_w_o = grad_w_o.reshape(own_rows, n_heads, head_dim)
        return grad_x.astype(BF16)[None], grad_w_q, grad_w_k, grad_w_v, grad_w_o, grad_w_up, grad_w_down

    act_spec = P('dp', 'cp', None)
    rep_three = P(None, None, None)
    rep_two = P(None, None)
    grad_three = P(('dp', 'cp'), None, None)
    grad_two = P(('dp', 'cp'), None)
    return jax.shard_map(per_device, mesh=mesh,
                         in_specs=(act_spec, act_spec, rep_three, rep_three, rep_three, rep_three, rep_two, rep_two),
                         out_specs=(act_spec, grad_three, grad_three, grad_three, grad_three, grad_two, grad_two),
                         check_vma=False)
```

time: 1410 us -> 1330 us (0.943)
  waiting for transfers between devices: 575 us -> 489 us
  local copies, waits for them, and re-layouts: 99.4 us -> 45.9 us
  Pallas kernels: 423 us -> 466 us
    reduce_scatter x6 -> x8, waiting for transfers between devices: 156 us -> 94.6 us  [dp_reduce(): return lax.psum_scatter(grad, 'dp', scatter_dimension=0, tiled=True)]
    pallas_call x9 -> x14, Pallas kernels: 230 us -> 268 us  [the longest x8 165 us: ff_forward(): pl.pallas_call(functools.partial(ff_kernel, 256, copies, index), grid=(wi...]
    all_gather x1, waiting for transfers between devices: 34.2 us -> 0.01 us  [per_device(): kv_all = lax.all_gather(kv_own, 'cp', axis=0, tiled=True)]
    concatenate x2 -> x0, local copies, waits for them, and re-layouts: 21.3 us -> none  [the longest x1 20.6 us: per_device(): jnp.concatenate([lax.dynamic_slice_in_dim(w_up, start, ff_part, axis=1) f...]
    unnamed x137 -> x133, local copies, waits for them, and re-layouts: 29.2 us -> 17.7 us
    ppermute x30 -> x33, waiting for transfers between devices: 385 us -> 393 us  [swap(): lax.ppermute(values, 'cp', [(src, src ^ bits) for src in range(cp_size)])]
    dot_general x2 -> x4, matrix products: 125 us -> 128 us  [dot_tn(): lax.dot_general(lhs, rhs, (((0,), (0,)), ((), ())), preferred_element_typ...]
  transfers between devices with their start and end apart: 37 -> 42, of which waited for: 15 -> 18; matrix products, arithmetic and copies ran while one was open for 21% -> 21% of each run, Pallas kernels for 28% -> 29%
where the time goes in v2:
time: 1330 us; the launch traced here: 1320 us
  waiting for transfers between devices  489 us (37%)
  Pallas kernels  466 us (35%)
  matrix products  238 us (18%)
  local copies, waits for them, and re-layouts  45.9 us (3%)
  other arithmetic  38.3 us (3%)
  between operations  24.7 us (2%)
  starting transfers between devices  22.1 us (2%)
    ppermute x33, waiting for transfers between devices, swap(): lax.ppermute(values, 'cp', [(src, src ^ bits) for src in range(cp_size)])  393 us
    pallas_call x8, Pallas kernels, ff_forward(): pl.pallas_call(functools.partial(ff_kernel, 256, copies, index), grid=(wi...  165 us
    dot_general x4, matrix products, dot_tn(): lax.dot_general(lhs, rhs, (((0,), (0,)), ((), ())), preferred_element_typ...  128 us
    pallas_call x2, Pallas kernels, attn_backward(): pl.pallas_call(functools.partial(attn_bwd_kernel, group, head_dim ** (-0....  115 us
    dot_general x21, matrix products, dot_tt(): lax.dot_general(lhs, rhs, (((0,), (1,)), ((), ())), preferred_element_typ...  107 us
    reduce_scatter x8, waiting for transfers between devices, dp_reduce(): return lax.psum_scatter(grad, 'dp', scatter_dimension=0, tiled=True)  94.6 us
    pallas_call x1, Pallas kernels, attn_forward(): pl.pallas_call(functools.partial(attn_fwd_kernel, group, head_dim ** (-0....  81.9 us
    pallas_call x4, Pallas kernels, grad_h_block(): pl.pallas_call(functools.partial(grad_h_kernel, len(up)), grid=(d_model /...  75.3 us
  transfers between devices with their start and end apart: 42, of which 18 were waited for; matrix products, arithmetic and copies ran while one was open for 21% of the time, Pallas kernels for 29%

profile of v2, /device:TPU:0, one launch (start us, length us, event | category | flops | bytes accessed | tf_op | source)
XLA Modules:
  0.0 1324.2 jit_solution(17462594635308108099)
XLA Ops:
  25.7 21.3 %prepare.1 = (bf16[2048,1280]{1,0:T(8,128)(2,1)}, bf16[2048,1536]{1,0:T(8,128)(2,1)}, bf16[1280,2048]{1,0:T(8,128)(2,1)}, bf16[1536,2048]{1,0:T(8,128)(2,1)}) custom-call(s32[3,8]{1,0:T(4,128)} %pad_add_fusion.1.idx_ref, bf16[2048,11008]{1,0:T(8,128)(2,1)} %refs_34_.1, bf16[2048,11008]{1,0:T(8,128)(2,1)} %refs_34_.1, bf16[2048,11008]{1,0:T(8,128)(2,1)} %refs_34_.1, ...), custom_call_target="tpu_custom_call" | custom-call | flops 46137344 | bytes 51904512 | tf_op jit(solution)/shard_map/prepare/pallas_call | solution.py:301
  47.0 12.6 fusion.26.q_ref
  63.5 81.9 %attn_fwd.1 = (f32[2048,1024]{1,0:T(8,128)}, bf16[2048,1024]{1,0:T(8,128)(2,1)}, f32[2,8,1024]{2,1,0:T(8,128)}) custom-call(s32[4,9]{1,0:T(4,128)} %pad_add_fusion.tab, bf16[2048,1024]{1,0:T(8,128)(2,1)} %fusion.26.q_ref, bf16[4096,512]{1,0:T(8,128)(2,1)} %all-gather.2.cloned.1.call-done.k_ref.v_ref, bf16[4096,512]{1,0:T(8,128)(2,1)} %all-gather.2.cloned.1.call-done.k_ref.v_ref), custom_call_target="tpu_custom_call" | custom-call | flops 19327352832 | bytes 25165824 | tf_op jit(solution)/shard_map/attn_fwd/pallas_call | solution.py:113
  145.4 8.4 collective-permute-done.cot_ref
  153.7 14.0 %add_convert_fusion.1.h_ref = bf16[1024,2048]{1,0:T(8,128)(2,1)} fusion(bf16[1,1024,2048]{2,1,0:T(8,128)(2,1)S(1)} %copy-done.7, bf16[2048,1024]{1,0:T(8,128)(2,1)} %get-tuple-element.66, bf16[256,8,16,128]{3,2,1,0:T(8,128)(2,1)} %bitcast.207), kind=kOutput, calls=%fused_computation.17 | convolution fusion | flops 8596226048 | bytes 20971520 | tf_op jit(solution)/shard_map/dot_general | solution.py:37
  169.7 19.2 %ff_forward.8 = (bf16[4096,1280]{1,0:T(8,128)(2,1)}, bf16[4096,1280]{1,0:T(8,128)(2,1)}, bf16[4096,2048]{1,0:T(8,128)(2,1)}, bf16[4096,2048]{1,0:T(8,128)(2,1)}) custom-call(bf16[1024,2048]{1,0:T(8,128)(2,1)} %add_convert_fusion.1.h_ref, bf16[1024,2048]{1,0:T(8,128)(2,1)} %bitcast.188, bf16[2048,1280]{1,0:T(8,128)(2,1)} %get-tuple-element.62.up_ref.refs_1_, ...), custom_call_target="tpu_custom_call" | custom-call | flops 10737418240 | bytes 27262976 | tf_op jit(solution)/shard_map/ff_forward/pallas_call | solution.py:359
  189.0 19.1 %ff_forward.9 = (bf16[4096,1280]{1,0:T(8,128)(2,1)}, bf16[4096,1280]{1,0:T(8,128)(2,1)}, bf16[4096,2048]{1,0:T(8,128)(2,1)}, bf16[4096,2048]{1,0:T(8,128)(2,1)}) custom-call(bf16[1024,2048]{1,0:T(8,128)(2,1)} %collective-permute-done.2.h_ref, ...), custom_call_target="tpu_custom_call", output_to_operand_aliasing={{0}: (4, {}), {1}: (5, {}), {2}: (6, {}), {3}: (7, {})} | custom-call | flops 10737418240 | bytes 27262976 | tf_op jit(solution)/shard_map/ff_forward/pallas_call | solution.py:359
  208.1 21.9 %ff_forward.10 = (bf16[4096,1536]{1,0:T(8,128)(2,1)}, bf16[4096,1536]{1,0:T(8,128)(2,1)}) custom-call(bf16[1024,2048]{1,0:T(8,128)(2,1)} %add_convert_fusion.1.h_ref, bf16[1024,2048]{1,0:T(8,128)(2,1)} %bitcast.189, bf16[2048,1536]{1,0:T(8,128)(2,1)} %get-tuple-element.67.up_ref.refs_3_, bf16[1536,2048]{1,0:T(8,128)(2,1)} %get-tuple-element.68.down_ref), custom_call_target="tpu_custom_call" | custom-call | flops 12884901888 | bytes 29360128 | tf_op jit(solution)/shard_map/ff_forward/pallas_call | solution.py:359
  230.0 21.8 %ff_forward.11 = (bf16[4096,1536]{1,0:T(8,128)(2,1)}, bf16[4096,1536]{1,0:T(8,128)(2,1)}) custom-call(bf16[1024,2048]{1,0:T(8,128)(2,1)} %collective-permute-done.2.h_ref, bf16[1024,2048]{1,0:T(8,128)(2,1)} %collective-permute-done.3.cot_ref, bf16[2048,1536]{1,0:T(8,128)(2,1)} %get-tuple-element.67.up_ref.refs_3_, ...), custom_call_target="tpu_custom_call", output_to_operand_aliasing={{0}: (4, {}), {1}: (5, {})} | custom-call | flops 12884901888 | bytes 29360128 | tf_op jit(solution)/shard_map/ff_forward/pallas_call | solution.py:359
  251.8 9.3 collective-permute-done.1.h_ref
  261.1 19.5 %ff_forward.12 = (bf16[4096,1280]{1,0:T(8,128)(2,1)}, bf16[4096,1280]{1,0:T(8,128)(2,1)}, bf16[4096,2048]{1,0:T(8,128)(2,1)}, bf16[4096,2048]{1,0:T(8,128)(2,1)}) custom-call(bf16[1024,2048]{1,0:T(8,128)(2,1)} %collective-permute-done.1.h_ref, ...), custom_call_target="tpu_custom_call", output_to_operand_aliasing={{0}: (4, {}), {1}: (5, {}), {2}: (6, {}), {3}: (7, {})} | custom-call | flops 10737418240 | bytes 27262976 | tf_op jit(solution)/shard_map/ff_forward/pallas_call | solution.py:359
  282.7 19.1 %ff_forward.13 = (bf16[4096,1280]{1,0:T(8,128)(2,1)}, bf16[4096,1280]{1,0:T(8,128)(2,1)}, bf16[4096,2048]{1,0:T(8,128)(2,1)}, bf16[4096,2048]{1,0:T(8,128)(2,1)}) custom-call(bf16[1024,2048]{1,0:T(8,128)(2,1)} %collective-permute-done.4.h_ref, bf16[1024,2048]{1,0:T(8,128)(2,1)} %copy-done.4, ...), custom_call_target="tpu_custom_call", output_to_operand_aliasing={{0}: (4, {}), {1}: (5, {}), {2}: (6, {}), {3}: (7, {})} | custom-call | flops 10737418240 | bytes 27262976 | tf_op jit(solution)/shard_map/ff_forward/pallas_call | solution.py:359
  301.8 29.6 %convolution_multiply_fusion.1 = f32[2048,1280]{1,0:T(8,128)} fusion(bf16[4096,2048]{1,0:T(8,128)(2,1)} %get-tuple-element.88, bf16[4096,1280]{1,0:T(8,128)(2,1)} %get-tuple-element.87.refs_0_), kind=kOutput, calls=%fused_computation.6 | convolution fusion | flops 21477457920 | bytes 37748736 | tf_op jit(solution)/shard_map/dot_general | solution.py:33
  331.4 22.1 %ff_forward.14 = (bf16[4096,1536]{1,0:T(8,128)(2,1)}, bf16[4096,1536]{1,0:T(8,128)(2,1)}) custom-call(bf16[1024,2048]{1,0:T(8,128)(2,1)} %collective-permute-done.1.h_ref, bf16[1024,2048]{1,0:T(8,128)(2,1)} %collective-permute-done.cot_ref, bf16[2048,1536]{1,0:T(8,128)(2,1)} %get-tuple-element.67.up_ref.refs_3_, ...), custom_call_target="tpu_custom_call", output_to_operand_aliasing={{0}: (4, {}), {1}: (5, {})} | custom-call | flops 12884901888 | bytes 29360128 | tf_op jit(solution)/shard_map/ff_forward/pallas_call | solution.py:359
  353.5 21.9 %ff_forward.15 = (bf16[4096,1536]{1,0:T(8,128)(2,1)}, bf16[4096,1536]{1,0:T(8,128)(2,1)}) custom-call(bf16[1024,2048]{1,0:T(8,128)(2,1)} %collective-permute-done.4.h_ref, bf16[1024,2048]{1,0:T(8,128)(2,1)} %copy-done.4, bf16[2048,1536]{1,0:T(8,128)(2,1)} %get-tuple-element.67.up_ref.refs_3_, ...), custom_call_target="tpu_custom_call", output_to_operand_aliasing={{0}: (4, {}), {1}: (5, {})} | custom-call | flops 12884901888 | bytes 29360128 | tf_op jit(solution)/shard_map/ff_forward/pallas_call | solution.py:359
  375.4 17.6 %grad_h.4 = f32[1024,2048]{1,0:T(8,128)} custom-call(bf16[4096,1280]{1,0:T(8,128)(2,1)} %get-tuple-element.87.refs_0_, bf16[2048,1280]{1,0:T(8,128)(2,1)S(1)} %bitcast.185, bf16[4096,1536]{1,0:T(8,128)(2,1)} %get-tuple-element.102.refs_2_, bf16[2048,1536]{1,0:T(8,128)(2,1)} %get-tuple-element.67.up_ref.refs_3_), custom_call_target="tpu_custom_call" | custom-call | flops 11811160064 | bytes 25690112 | tf_op jit(solution)/shard_map/grad_h/pallas_call | solution.py:392
  393.6 34.8 %fusion.7 = f32[2048,1472]{1,0:T(8,128)} fusion(bf16[4096,2048]{1,0:T(8,128)(2,1)} %get-tuple-element.88, bf16[4096,1536]{1,0:T(8,128)(2,1)} %get-tuple-element.102.refs_2_), kind=kOutput, calls=%fused_computation.7 | convolution fusion | flops 24699076608 | bytes 41418752 | tf_op jit(solution)/shard_map/dot_general | solution.py:33
  430.9 19.0 %grad_h.5 = f32[1024,2048]{1,0:T(8,128)} custom-call(bf16[4096,1280]{1,0:T(8,128)(2,1)} %get-tuple-element.87.refs_0_, bf16[2048,1280]{1,0:T(8,128)(2,1)S(1)} %copy-done, bf16[4096,1536]{1,0:T(8,128)(2,1)} %get-tuple-element.102.refs_2_, bf16[2048,1536]{1,0:T(8,128)(2,1)} %get-tuple-element.67.up_ref.refs_3_, f32[1024,2048]{1,0:T(8,128)} %collective-permute-done.6.refs_4_), custom_call_target="tpu_custom_call" | custom-call | flops 11811160064 | bytes 25690112 | tf_op jit(solution)/shard_map/grad_h/pallas_call | solution.py:392
  451.5 29.5 %convolution_multiply_fusion = f32[1280,2048]{1,0:T(8,128)} fusion(bf16[4096,1280]{1,0:T(8,128)(2,1)} %get-tuple-element.98, bf16[4096,2048]{1,0:T(8,128)(2,1)} %get-tuple-element.99), kind=kOutput, calls=%fused_computation.5 | convolution fusion | flops 21477457920 | bytes 37748736 | tf_op jit(solution)/shard_map/dot_general | solution.py:33
  481.0 33.8 %fusion.4 = f32[1472,2048]{1,0:T(8,128)} fusion(bf16[4096,2048]{1,0:T(8,128)(2,1)} %get-tuple-element.99, bf16[4096,1536]{1,0:T(8,128)(2,1)} %get-tuple-element.100), kind=kOutput, calls=%fused_computation.4 | convolution fusion | flops 24699076608 | bytes 41418752 | tf_op jit(solution)/shard_map/dot_general | solution.py:33
  517.3 17.7 %grad_h.6 = f32[1024,2048]{1,0:T(8,128)} custom-call(bf16[4096,1280]{1,0:T(8,128)(2,1)} %get-tuple-element.87.refs_0_, bf16[2048,1280]{1,0:T(8,128)(2,1)S(1)} %copy-done.1, bf16[4096,1536]{1,0:T(8,128)(2,1)} %get-tuple-element.102.refs_2_, bf16[2048,1536]{1,0:T(8,128)(2,1)} %get-tuple-element.67.up_ref.refs_3_), custom_call_target="tpu_custom_call" | custom-call | flops 11811160064 | bytes 25690112 | tf_op jit(solution)/shard_map/grad_h/pallas_call | solution.py:392
  535.1 97.1 %collective-permute-done.8.refs_6_ = f32[1024,2048]{1,0:T(8,128)} collective-permute-done((f32[1024,2048]{1,0:T(8,128)}, f32[1024,2048]{1,0:T(8,128)}, u32[]{:S(2)}, u32[]{:S(2)}) %collective-permute-start.8) | collective-permute-done | bytes 8388640 | tf_op jit(solution)/shard_map/ppermute | solution.py:434
  632.2 21.0 %grad_h.7 = bf16[1024,2048]{1,0:T(8,128)(2,1)S(1)} custom-call(bf16[4096,1280]{1,0:T(8,128)(2,1)} %get-tuple-element.87.refs_0_, bf16[2048,1280]{1,0:T(8,128)(2,1)} %get-tuple-element.62.up_ref.refs_1_, bf16[4096,1536]{1,0:T(8,128)(2,1)} %get-tuple-element.102.refs_2_, bf16[2048,1536]{1,0:T(8,128)(2,1)} %get-tuple-element.67.up_ref.refs_3_, ...), custom_call_target="tpu_custom_call" | custom-call | flops 11811160064 | bytes 25690112 | tf_op jit(solution)/shard_map/grad_h/pallas_call | solution.py:392
  657.2 4.4 convolution_multiply_fusion.4
  664.0 4.4 convolution_multiply_fusion.3
  670.8 13.0 convert_bitcast_fusion.do_ref
  686.9 57.7 %attn_bwd.2 = (bf16[1024,1024]{1,0:T(8,128)(2,1)}, f32[8,2,128,512]{3,2,1,0:T(8,128)}) custom-call(s32[4,9]{1,0:T(4,128)} %pad_add_fusion.tab, bf16[2048,1024]{1,0:T(8,128)(2,1)} %fusion.26.q_ref, bf16[2048,1024]{1,0:T(8,128)(2,1)} %convert_bitcast_fusion.do_ref, f32[2048,1024]{1,0:T(8,128)} %get-tuple-element.107.of_ref, ...), custom_call_target="tpu_custom_call" | custom-call | flops 24159191040 | bytes 12582912 | tf_op jit(solution)/shard_map/attn_bwd/pallas_call | solution.py:191
  759.0 4.2 multiply_add_fusion.2
  763.2 57.7 %attn_bwd.3 = (bf16[1024,1024]{1,0:T(8,128)(2,1)}, f32[8,2,128,512]{3,2,1,0:T(8,128)}) custom-call(s32[4,9]{1,0:T(4,128)} %pad_add_fusion.tab, bf16[2048,1024]{1,0:T(8,128)(2,1)} %fusion.26.q_ref, bf16[2048,1024]{1,0:T(8,128)(2,1)} %convert_bitcast_fusion.do_ref, f32[2048,1024]{1,0:T(8,128)} %get-tuple-element.107.of_ref, ...), custom_call_target="tpu_custom_call" | custom-call | flops 24159191040 | bytes 12582912 | tf_op jit(solution)/shard_map/attn_bwd/pallas_call | solution.py:191
  830.5 20.0 %collective-permute-done.15 = f32[2,2,128,512]{3,2,1,0:T(8,128)} collective-permute-done((f32[2,2,128,512]{3,2,1,0:T(8,128)}, f32[2,2,128,512]{3,2,1,0:T(8,128)}, u32[]{:S(2)}, u32[]{:S(2)}) %collective-permute-start.15) | collective-permute-done | bytes 1048608 | tf_op jit(solution)/shard_map/ppermute | solution.py:434
  852.7 19.7 %collective-permute-done.17 = f32[2,2,128,512]{3,2,1,0:T(8,128)} collective-permute-done((f32[2,2,128,512]{3,2,1,0:T(8,128)}, f32[2,2,128,512]{3,2,1,0:T(8,128)}, u32[]{:S(2)}, u32[]{:S(2)}) %collective-permute-start.17) | collective-permute-done | bytes 1048608 | tf_op jit(solution)/shard_map/ppermute | solution.py:434
  881.1 24.0 %collective-permute-done.24 = f32[512,512]{1,0:T(8,128)S(1)} collective-permute-done((f32[512,512]{1,0:T(8,128)S(1)}, f32[512,512]{1,0:T(8,128)S(1)}, u32[]{:S(2)}, u32[]{:S(2)}) %collective-permute-start.24) | collective-permute-done | bytes 1048608 | tf_op jit(solution)/shard_map/ppermute | solution.py:434
  907.0 4.6 convolution_multiply_fusion.6
  912.9 36.5 %collective-permute-done.19 = f32[512,1024]{1,0:T(8,128)} collective-permute-done((f32[512,1024]{1,0:T(8,128)}, f32[512,1024]{1,0:T(8,128)}, u32[]{:S(2)}, u32[]{:S(2)}) %collective-permute-start.19) | collective-permute-done | bytes 2097184 | tf_op jit(solution)/shard_map/ppermute | solution.py:434
  949.3 4.3 add_add_fusion.2
  963.8 45.0 %collective-permute-done.21 = f32[512,1024]{1,0:T(8,128)S(1)} collective-permute-done((f32[512,1024]{1,0:T(8,128)S(1)}, f32[512,1024]{1,0:T(8,128)S(1)}, u32[]{:S(2)}, u32[]{:S(2)}) %collective-permute-start.21) | collective-permute-done | bytes 2097184 | tf_op jit(solution)/shard_map/ppermute | solution.py:434
  1014.4 4.6 convolution_multiply_fusion.2
  1020.0 85.8 %collective-permute-done.26 = f32[512,2048]{1,0:T(8,128)S(1)} collective-permute-done((f32[512,2048]{1,0:T(8,128)}, f32[512,2048]{1,0:T(8,128)S(1)}, u32[]{:S(2)}, u32[]{:S(2)}) %collective-permute-start.26) | collective-permute-done | bytes 4194336 | tf_op jit(solution)/shard_map/ppermute | solution.py:434
  1122.7 7.8 collective-permute-done.28
  1130.5 13.3 %collective-permute-done.29 = f32[128,1280]{1,0:T(8,128)} collective-permute-done((f32[128,1280]{1,0:T(8,128)}, f32[128,1280]{1,0:T(8,128)}, u32[]{:S(2)}, u32[]{:S(2)}) %collective-permute-start.29) | collective-permute-done | bytes 655392 | tf_op jit(solution)/shard_map/ppermute | solution.py:434
  1151.0 9.7 collective-permute-done.31
  1162.1 13.8 %collective-permute-done.32 = f32[128,1472]{0,1:T(8,128)} collective-permute-done((f32[128,1472]{0,1:T(8,128)}, f32[128,1472]{0,1:T(8,128)}, u32[]{:S(2)}, u32[]{:S(2)}) %collective-permute-start.32) | collective-permute-done | bytes 753696 | tf_op jit(solution)/shard_map/ppermute | solution.py:434
  1179.2 7.0 spread.1
  1186.3 6.1 fusion.85
  1192.4 17.1 %fusion.22 = bf16[1,1024,2048]{2,1,0:T(8,128)(2,1)} fusion(f32[1024,2048]{1,0:T(8,128)} %fusion.85, bf16[1024,2048]{1,0:T(8,128)(2,1)S(1)} %copy-done.3, bf16[2048,1024]{1,0:T(8,128)(2,1)S(1)} %copy-done.9, bf16[256,8,16,128]{3,2,1,0:T(8,128)(2,1)} %bitcast.210), kind=kOutput, calls=%fused_computation.23 | convolution fusion | flops 8598323200 | bytes 29360128 | tf_op jit(solution)/shard_map/dot_general | solution.py:37
  1214.4 48.6 %reduce-scatter.23.cloned.1.call-done = f32[368,2048]{1,0:T(8,128)} async-done(((f32[1472,2048]{1,0:T(8,128)}), f32[368,2048]{1,0:T(8,128)}) %reduce-scatter.23.cloned.1.call-update) | async-done | bytes 3014672 | tf_op jit(solution)/shard_map/reduce_scatter | solution.py:437
  1263.0 5.8 pad_maximum_fusion
  1268.8 46.0 %reduce-scatter.15.cloned.1.call-done = f32[128,2048]{1,0:T(8,128)} async-done(((f32[512,2048]{1,0:T(8,128)}), f32[128,2048]{1,0:T(8,128)}) %reduce-scatter.15.cloned.1.call-update) | async-done | bytes 1048592 | tf_op jit(solution)/shard_map/reduce_scatter | solution.py:437
  (263 shorter events, 126.3 us)
Async XLA Ops:
  7.2 52.5 %all-gather.2.cloned.1.call-start = ((), (), s32[]{:S(2)}) async-start(), calls=%async_computation.8 | async-start | bytes 5242880 | tf_op jit(solution)/shard_map/all_gather | solution.py:465
  14.9 1094.5 %reduce-scatter.17.cloned.1.call-start = ((), (), s32[]{:S(2)}) async-start(), calls=%async_computation.13 | async-start | bytes 13107200 | tf_op jit(solution)/shard_map/reduce_scatter | solution.py:437
  59.6 94.1 %collective-permute-start = (bf16[1024,2048]{1,0:T(8,128)(2,1)}, bf16[1024,2048]{1,0:T(8,128)(2,1)}, u32[]{:S(2)}, u32[]{:S(2)}) collective-permute-start(bf16[1024,2048]{1,0:T(8,128)(2,1)} %bitcast.186), channel_id=1, source_target_pairs={{0,2},{1,3},{2,0},{3,1},{4,6},{5,7},{6,4},{7,5},{8,10},{9,11},{10,... | collective-permute-start | bytes 12582920 | tf_op jit(solution)/shard_map/ppermute | solution.py:434
  62.9 126.1 %collective-permute-start.3 = (bf16[1024,2048]{1,0:T(8,128)(2,1)}, bf16[1024,2048]{1,0:T(8,128)(2,1)}, u32[]{:S(2)}, u32[]{:S(2)}) collective-permute-start(bf16[1024,2048]{1,0:T(8,128)(2,1)} %bitcast.187), channel_id=1, source_target_pairs={{0,1},{1,0},{2,3},{3,2},{4,5},{5,4},{6,7},{7,6},{8,9},{9,8},{10,11... | collective-permute-start | bytes 12582920 | tf_op jit(solution)/shard_map/ppermute | solution.py:434
  63.5 90.3 %copy-start.7 = (bf16[1,1024,2048]{2,1,0:T(8,128)(2,1)S(1)}, bf16[1,1024,2048]{2,1,0:T(8,128)(2,1)}, u32[]{:S(2)}) copy-start(bf16[1,1024,2048]{2,1,0:T(8,128)(2,1)} %param.8) | copy-start | bytes 12582916
  167.8 21.3 %collective-permute-start.2 = (bf16[1024,2048]{1,0:T(8,128)(2,1)}, bf16[1024,2048]{1,0:T(8,128)(2,1)}, u32[]{:S(2)}, u32[]{:S(2)}) collective-permute-start(bf16[1024,2048]{1,0:T(8,128)(2,1)} %add_convert_fusion.1.h_ref), channel_id=1, source_target_pairs={{0,1},{1,0},{2,3},{3,2},{4,5},{5,4},{6,7},{7,6},{8,9},{9,8},{10,11... | collective-permute-start | bytes 12582920 | tf_op jit(solution)/shard_map/ppermute | solution.py:434
  167.8 93.3 %collective-permute-start.1 = (bf16[1024,2048]{1,0:T(8,128)(2,1)}, bf16[1024,2048]{1,0:T(8,128)(2,1)}, u32[]{:S(2)}, u32[]{:S(2)}) collective-permute-start(bf16[1024,2048]{1,0:T(8,128)(2,1)} %add_convert_fusion.1.h_ref), channel_id=1, source_target_pairs={{0,2},{1,3},{2,0},{3,1},{4,6},{5,7},{6,4},{7,5},{8,10},{9,11},{10,... | collective-permute-start | bytes 12582920 | tf_op jit(solution)/shard_map/ppermute | solution.py:434
  169.5 111.1 %collective-permute-start.5 = (bf16[1024,2048]{1,0:T(8,128)(2,1)}, bf16[1024,2048]{1,0:T(8,128)(2,1)S(1)}, u32[]{:S(2)}, u32[]{:S(2)}) collective-permute-start(bf16[1024,2048]{1,0:T(8,128)(2,1)} %collective-permute-done.cot_ref), channel_id=1, source_target_pairs={{0,1},{1,0},{2,3},{3,2},{4,5},{5,4},{6,7},{7,6},{8,9},{9,8},{10,11... | collective-permute-start | bytes 12582920 | tf_op jit(solution)/shard_map/ppermute | solution.py:434
  261.1 19.5 %collective-permute-start.4 = (bf16[1024,2048]{1,0:T(8,128)(2,1)}, bf16[1024,2048]{1,0:T(8,128)(2,1)}, u32[]{:S(2)}, u32[]{:S(2)}) collective-permute-start(bf16[1024,2048]{1,0:T(8,128)(2,1)} %collective-permute-done.1.h_ref), channel_id=1, source_target_pairs={{0,1},{1,0},{2,3},{3,2},{4,5},{5,4},{6,7},{7,6},{8,9},{9,8},{10,11... | collective-permute-start | bytes 12582920 | tf_op jit(solution)/shard_map/ppermute | solution.py:434
  393.0 35.4 %collective-permute-start.6 = (f32[1024,2048]{1,0:T(8,128)}, f32[1024,2048]{1,0:T(8,128)}, u32[]{:S(2)}, u32[]{:S(2)}) collective-permute-start(f32[1024,2048]{1,0:T(8,128)} %grad_h.4), channel_id=1, source_target_pairs={{0,1},{1,0},{2,3},{3,2},{4,5},{5,4},{6,7},{7,6},{8,9},{9,8},{10,11... | collective-permute-start | bytes 25165832 | tf_op jit(solution)/shard_map/ppermute | solution.py:434
  393.6 720.9 %reduce-scatter.19.cloned.1.call-start = ((), (), s32[]{:S(2)}) async-start(), calls=%async_computation.14 | async-start | bytes 15728640 | tf_op jit(solution)/shard_map/reduce_scatter | solution.py:437
  450.0 182.2 %collective-permute-start.8 = (f32[1024,2048]{1,0:T(8,128)}, f32[1024,2048]{1,0:T(8,128)}, u32[]{:S(2)}, u32[]{:S(2)}) collective-permute-start(f32[1024,2048]{1,0:T(8,128)} %grad_h.5), channel_id=1, source_target_pairs={{0,2},{1,3},{2,0},{3,1},{4,6},{5,7},{6,4},{7,5},{8,10},{9,11},{10,... | collective-permute-start | bytes 25165832 | tf_op jit(solution)/shard_map/ppermute | solution.py:434
  534.9 97.3 %collective-permute-start.7 = (f32[1024,2048]{1,0:T(8,128)}, f32[1024,2048]{1,0:T(8,128)}, u32[]{:S(2)}, u32[]{:S(2)}) collective-permute-start(f32[1024,2048]{1,0:T(8,128)} %grad_h.6), channel_id=1, source_target_pairs={{0,1},{1,0},{2,3},{3,2},{4,5},{5,4},{6,7},{7,6},{8,9},{9,8},{10,11... | collective-permute-start | bytes 25165832 | tf_op jit(solution)/shard_map/ppermute | solution.py:434
  535.0 674.6 %reduce-scatter.13.cloned.1.call-start = ((), (), s32[]{:S(2)}) async-start(), calls=%async_computation.11 | async-start | bytes 1310720 | tf_op jit(solution)/shard_map/reduce_scatter | solution.py:437
  661.6 22.2 %collective-permute-start.9 = (f32[512,2048]{1,0:T(8,128)}, f32[512,2048]{1,0:T(8,128)S(1)}, u32[]{:S(2)}, u32[]{:S(2)}) collective-permute-start(f32[512,2048]{1,0:T(8,128)} %convolution_multiply_fusion.4), channel_id=1, source_target_pairs={{0,1},{1,0},{2,3},{3,2},{4,5},{5,4},{6,7},{7,6},{8,9},{9,8},{10,11... | collective-permute-start | bytes 12582920 | tf_op jit(solution)/shard_map/ppermute | solution.py:434
  663.9 80.7 %copy-start.40 = (bf16[1024,128]{1,0:T(8,128)(2,1)}, bf16[1024,128]{1,0:T(8,128)(2,1)S(1)}, u32[]{:S(2)}) copy-start(bf16[1024,128]{1,0:T(8,128)(2,1)S(1)} %get-tuple-element.143) | copy-start | bytes 786436
  663.9 80.7 %copy-start.42 = (bf16[1024,128]{1,0:T(8,128)(2,1)}, bf16[1024,128]{1,0:T(8,128)(2,1)S(1)}, u32[]{:S(2)}) copy-start(bf16[1024,128]{1,0:T(8,128)(2,1)S(1)} %get-tuple-element.144) | copy-start | bytes 786436
  663.9 80.7 %copy-start.44 = (bf16[1024,128]{1,0:T(8,128)(2,1)}, bf16[1024,128]{1,0:T(8,128)(2,1)S(1)}, u32[]{:S(2)}) copy-start(bf16[1024,128]{1,0:T(8,128)(2,1)S(1)} %get-tuple-element.145) | copy-start | bytes 786436
  664.0 80.7 %copy-start.46 = (bf16[1024,128]{1,0:T(8,128)(2,1)}, bf16[1024,128]{1,0:T(8,128)(2,1)S(1)}, u32[]{:S(2)}) copy-start(bf16[1024,128]{1,0:T(8,128)(2,1)S(1)} %get-tuple-element.146) | copy-start | bytes 786436
  748.8 10.1 collective-permute-start.11
  752.2 3.9 collective-permute-start.10
  823.6 2.8 collective-permute-start.13
  824.1 6.4 collective-permute-start.14
  824.1 26.3 %collective-permute-start.15 = (f32[2,2,128,512]{3,2,1,0:T(8,128)}, f32[2,2,128,512]{3,2,1,0:T(8,128)}, u32[]{:S(2)}, u32[]{:S(2)}) collective-permute-start(f32[2,2,128,512]{3,2,1,0:T(8,128)} %bitcast_add_fusion.3), channel_id=1, source_target_pairs={{0,2},{1,3},{2,0},{3,1},{4,6},{5,7},{6,4},{7,5},{8,10},{9,11},{10,... | collective-permute-start | bytes 3145736 | tf_op jit(solution)/shard_map/ppermute | solution.py:434
  825.8 26.9 %collective-permute-start.16 = (f32[2,2,128,512]{3,2,1,0:T(8,128)}, f32[2,2,128,512]{3,2,1,0:T(8,128)}, u32[]{:S(2)}, u32[]{:S(2)}) collective-permute-start(f32[2,2,128,512]{3,2,1,0:T(8,128)} %get-tuple-element.151), channel_id=1, source_target_pairs={{0,1},{1,0},{2,3},{3,2},{4,5},{5,4},{6,7},{7,6},{8,9},{9,8},{10,11... | collective-permute-start | bytes 3145736 | tf_op jit(solution)/shard_map/ppermute | solution.py:434
  828.8 43.7 %collective-permute-start.17 = (f32[2,2,128,512]{3,2,1,0:T(8,128)}, f32[2,2,128,512]{3,2,1,0:T(8,128)}, u32[]{:S(2)}, u32[]{:S(2)}) collective-permute-start(f32[2,2,128,512]{3,2,1,0:T(8,128)} %bitcast_add_fusion.2), channel_id=1, source_target_pairs={{0,2},{1,3},{2,0},{3,1},{4,6},{5,7},{6,4},{7,5},{8,10},{9,11},{10,... | collective-permute-start | bytes 3145736 | tf_op jit(solution)/shard_map/ppermute | solution.py:434
  852.6 52.5 %copy-start.48 = (bf16[128,512]{1,0:T(8,128)(2,1)}, bf16[128,512]{1,0:T(8,128)(2,1)S(1)}, u32[]{:S(2)}) copy-start(bf16[128,512]{1,0:T(8,128)(2,1)S(1)} %get-tuple-element.162) | copy-start | bytes 393220
  875.5 2.7 collective-permute-start.23
  876.8 4.3 collective-permute-start.22
  879.0 26.1 %collective-permute-start.24 = (f32[512,512]{1,0:T(8,128)S(1)}, f32[512,512]{1,0:T(8,128)S(1)}, u32[]{:S(2)}, u32[]{:S(2)}) collective-permute-start(f32[512,512]{1,0:T(8,128)S(1)} %fusion.43), channel_id=1, source_target_pairs={{0,2},{1,3},{2,0},{3,1},{4,6},{5,7},{6,4},{7,5},{8,10},{9,11},{10,... | collective-permute-start | bytes 3145736 | tf_op jit(solution)/shard_map/ppermute | solution.py:434
  880.8 32.1 %collective-permute-start.18 = (f32[512,1024]{1,0:T(8,128)}, f32[512,1024]{1,0:T(8,128)}, u32[]{:S(2)}, u32[]{:S(2)}) collective-permute-start(f32[512,1024]{1,0:T(8,128)} %convolution_multiply_fusion.7), channel_id=1, source_target_pairs={{0,1},{1,0},{2,3},{3,2},{4,5},{5,4},{6,7},{7,6},{8,9},{9,8},{10,11... | collective-permute-start | bytes 6291464 | tf_op jit(solution)/shard_map/ppermute | solution.py:434
  880.8 68.5 %collective-permute-start.19 = (f32[512,1024]{1,0:T(8,128)}, f32[512,1024]{1,0:T(8,128)}, u32[]{:S(2)}, u32[]{:S(2)}) collective-permute-start(f32[512,1024]{1,0:T(8,128)} %multiply_add_fusion.2), channel_id=1, source_target_pairs={{0,2},{1,3},{2,0},{3,1},{4,6},{5,7},{6,4},{7,5},{8,10},{9,11},{10,... | collective-permute-start | bytes 6291464 | tf_op jit(solution)/shard_map/ppermute | solution.py:434
  906.9 305.0 %reduce-scatter.9.cloned.1.call-start = ((), (), s32[]{:S(2)}) async-start(), calls=%async_computation.9 | async-start | bytes 2621440 | tf_op jit(solution)/shard_map/reduce_scatter | solution.py:437
  911.5 46.3 %collective-permute-start.12 = (f32[512,1024]{1,0:T(8,128)}, f32[512,1024]{1,0:T(8,128)}, u32[]{:S(2)}, u32[]{:S(2)}) collective-permute-start(f32[512,1024]{1,0:T(8,128)} %convolution_multiply_fusion.6), channel_id=1, source_target_pairs={{0,1},{1,0},{2,3},{3,2},{4,5},{5,4},{6,7},{7,6},{8,9},{9,8},{10,11... | collective-permute-start | bytes 6291464 | tf_op jit(solution)/shard_map/ppermute | solution.py:434
  953.6 258.4 %reduce-scatter.11.cloned.1.call-start = ((), (), s32[]{:S(2)}) async-start(), calls=%async_computation.10 | async-start | bytes 2621440 | tf_op jit(solution)/shard_map/reduce_scatter | solution.py:437
  957.8 6.1 collective-permute-start.20
  960.8 48.0 %collective-permute-start.21 = (f32[512,1024]{1,0:T(8,128)S(1)}, f32[512,1024]{1,0:T(8,128)S(1)}, u32[]{:S(2)}, u32[]{:S(2)}) collective-permute-start(f32[512,1024]{1,0:T(8,128)S(1)} %multiply_add_fusion.1), channel_id=1, source_target_pairs={{0,2},{1,3},{2,0},{3,1},{4,6},{5,7},{6,4},{7,5},{8,10},{9,11},{10,... | collective-permute-start | bytes 6291464 | tf_op jit(solution)/shard_map/ppermute | solution.py:434
  1010.8 203.6 %reduce-scatter.21.cloned.1.call-start = ((), (), s32[]{:S(2)}) async-start(), calls=%async_computation.15 | async-start | bytes 13107200 | tf_op jit(solution)/shard_map/reduce_scatter | solution.py:437
  1011.6 251.4 %reduce-scatter.23.cloned.1.call-start = ((), (), s32[]{:S(2)}) async-start(), calls=%async_computation.16 | async-start | bytes 15073280 | tf_op jit(solution)/shard_map/reduce_scatter | solution.py:437
  1012.4 302.4 %reduce-scatter.15.cloned.1.call-start = ((), (), s32[]{:S(2)}) async-start(), calls=%async_computation.12 | async-start | bytes 5242880 | tf_op jit(solution)/shard_map/reduce_scatter | solution.py:437
  1012.6 7.4 collective-permute-start.25
  1012.7 93.2 %collective-permute-start.26 = (f32[512,2048]{1,0:T(8,128)}, f32[512,2048]{1,0:T(8,128)S(1)}, u32[]{:S(2)}, u32[]{:S(2)}) collective-permute-start(f32[512,2048]{1,0:T(8,128)} %multiply_add_fusion), channel_id=1, source_target_pairs={{0,2},{1,3},{2,0},{3,1},{4,6},{5,7},{6,4},{7,5},{8,10},{9,11},{10,... | collective-permute-start | bytes 12582920 | tf_op jit(solution)/shard_map/ppermute | solution.py:434
  1112.6 10.2 collective-permute-start.27
  1112.6 17.9 %collective-permute-start.28 = (f32[128,1280]{1,0:T(8,128)}, f32[128,1280]{1,0:T(8,128)}, u32[]{:S(2)}, u32[]{:S(2)}) collective-permute-start(f32[128,1280]{1,0:T(8,128)} %get-tuple-element.159), channel_id=1, source_target_pairs={{0,2},{1,3},{2,0},{3,1},{4,6},{5,7},{6,4},{7,5},{8,10},{9,11},{10,... | collective-permute-start | bytes 1966088 | tf_op jit(solution)/shard_map/ppermute | solution.py:434
  1114.3 29.5 %collective-permute-start.29 = (f32[128,1280]{1,0:T(8,128)}, f32[128,1280]{1,0:T(8,128)}, u32[]{:S(2)}, u32[]{:S(2)}) collective-permute-start(f32[128,1280]{1,0:T(8,128)} %get-tuple-element.158), channel_id=1, source_target_pairs={{0,3},{1,2},{2,1},{3,0},{4,7},{5,6},{6,5},{7,4},{8,11},{9,10},{10,... | collective-permute-start | bytes 1966088 | tf_op jit(solution)/shard_map/ppermute | solution.py:434
  1118.5 31.2 %collective-permute-start.30 = (f32[128,1472]{0,1:T(8,128)}, f32[128,1472]{0,1:T(8,128)}, u32[]{:S(2)}, u32[]{:S(2)}) collective-permute-start(f32[128,1472]{0,1:T(8,128)} %copy.37), channel_id=1, source_target_pairs={{0,1},{1,0},{2,3},{3,2},{4,5},{5,4},{6,7},{7,6},{8,9},{9,8},{10,11... | collective-permute-start | bytes 2261000 | tf_op jit(solution)/shard_map/ppermute | solution.py:434
  1119.8 40.9 %collective-permute-start.31 = (f32[128,1472]{0,1:T(8,128)}, f32[128,1472]{0,1:T(8,128)}, u32[]{:S(2)}, u32[]{:S(2)}) collective-permute-start(f32[128,1472]{0,1:T(8,128)} %copy.39), channel_id=1, source_target_pairs={{0,2},{1,3},{2,0},{3,1},{4,6},{5,7},{6,4},{7,5},{8,10},{9,11},{10,... | collective-permute-start | bytes 2261000 | tf_op jit(solution)/shard_map/ppermute | solution.py:434
  1122.7 53.2 %collective-permute-start.32 = (f32[128,1472]{0,1:T(8,128)}, f32[128,1472]{0,1:T(8,128)}, u32[]{:S(2)}, u32[]{:S(2)}) collective-permute-start(f32[128,1472]{0,1:T(8,128)} %copy.41), channel_id=1, source_target_pairs={{0,3},{1,2},{2,1},{3,0},{4,7},{5,6},{6,5},{7,4},{8,11},{9,10},{10,... | collective-permute-start | bytes 2261000 | tf_op jit(solution)/shard_map/ppermute | solution.py:434
  (59 other events, 706.1 us)
Sparse Core Ops, SparseCore 0:
  15.0 35.3 all-gather.1
  393.7 101.0 reduce-scatter.16
  535.1 117.6 reduce-scatter.18
  907.1 26.1 reduce-scatter.12
  953.7 33.4 reduce-scatter.8
  1011.0 33.4 reduce-scatter.10
  1047.5 99.7 reduce-scatter.20
  1150.4 112.5 reduce-scatter.22
  1265.9 48.8 reduce-scatter.14

commit v3 on v2

--- a/solution.py
+++ b/solution.py
@@ -317,26 +317,36 @@
     return outs[:len(parts)], outs[len(parts):]
 
 
-def ff_kernel(step_rows, copies, index, h_ref, cot_ref, up_ref, down_ref, *rest):
+def ff_kernel(step_rows, copies, first_row, n_pieces, *refs):
+    pieces = [(refs[2 * piece], refs[2 * piece + 1]) for piece in range(n_pieces)]
+    up_ref, down_ref = refs[2 * n_pieces:2 * n_pieces + 2]
     if copies:
-        act_ref, du_ref, h_out, cot_out, sem = rest[-5:]
-        rows = pl.ds(index * h_ref.shape[0], h_ref.shape[0])
-        moves = [pltpu.make_async_copy(h_ref, h_out.at[rows], sem.at[0]), pltpu.make_async_copy(cot_ref, cot_out.at[rows], sem.at[1])]
+        act_ref, du_ref, h_out, cot_out, sem = refs[-5:]
+        moves, row = [], first_row
+        for h_ref, cot_ref in pieces:
+            rows = pl.ds(row, h_ref.shape[0])
+            moves.append(pltpu.make_async_copy(h_ref, h_out.at[rows], sem.at[len(moves)]))
+            moves.append(pltpu.make_async_copy(cot_ref, cot_out.at[rows], sem.at[len(moves)]))
+            row += h_ref.shape[0]
 
         @pl.when(pl.program_id(0) == 0)
         def _():
             for move in moves:
                 move.start()
     else:
-        act_ref, du_ref = rest[-2:]
-
-    for first in range(0, h_ref.shape[0], step_rows):
-        rows = slice(first, first + step_rows)
-        hidden = dot_nn(h_ref[rows, :], up_ref[...])
-        grad_act = dot_nt(cot_ref[rows, :], down_ref[...]).astype(BF16).astype(F32)
-        act, slope = gelu_parts(hidden)
-        act_ref[rows, :] = act.astype(BF16)
-        du_ref[rows, :] = (grad_act * slope).astype(BF16)
+        act_ref, du_ref = refs[-2:]
+
+    base = 0
+    for h_ref, cot_ref in pieces:
+        for first in range(0, h_ref.shape[0], step_rows):
+            rows = slice(first, first + step_rows)
+            out_rows = slice(base + first, base + first + step_rows)
+            hidden = dot_nn(h_ref[rows, :], up_ref[...])
+            grad_act = dot_nt(cot_ref[rows, :], down_ref[...]).astype(BF16).astype(F32)
+            act, slope = gelu_parts(hidden)
+            act_ref[out_rows, :] = act.astype(BF16)
+            du_ref[out_rows, :] = (grad_act * slope).astype(BF16)
+        base += h_ref.shape[0]
 
     if copies:
         @pl.when(pl.program_id(0) == pl.num_programs(0) - 1)
@@ -345,46 +355,54 @@
                 move.wait()
 
 
-def ff_forward(index, count, h_blk, cot_blk, up, down, copies, carry):
-    tokens, d_model = h_blk.shape
-    width = up.shape[1]
+def ff_forward(index, count, pieces, up, down, copies, carry):
+    tokens = sum(piece[0].shape[0] for piece in pieces)
+    d_model, width = up.shape
     tile = FF_TILE
-    whole = pl.BlockSpec((tokens, d_model), lambda n: (0, 0))
     shapes = [jax.ShapeDtypeStruct((count * tokens, width), BF16)] * 2
     specs = [pl.BlockSpec((tokens, tile), lambda n: (index, n))] * 2
     if copies:
         shapes = shapes + [jax.ShapeDtypeStruct((count * tokens, d_model), BF16)] * 2
         specs = specs + [pl.BlockSpec(memory_space=pl.ANY)] * 2
+    in_specs, args = [], []
+    for h_blk, cot_blk, row_blk in pieces:
+        in_specs += [pl.BlockSpec(h_blk.shape, lambda n: (0, 0)),
+                     pl.BlockSpec(h_blk.shape, lambda n, row_blk=row_blk: (row_blk, 0))]
+        args += [h_blk, cot_blk]
     carry = list(carry)
     return pl.pallas_call(
-        functools.partial(ff_kernel, 256, copies, index),
+        functools.partial(ff_kernel, 512, copies, index * tokens, len(pieces)),
         grid=(width // tile,),
-        in_specs=[whole, whole, pl.BlockSpec((d_model, tile), lambda n: (0, n)),
-                  pl.BlockSpec((tile, d_model), lambda n: (n, 0))] + [pl.BlockSpec(memory_space=pl.ANY)] * len(carry),
+        in_specs=in_specs + [pl.BlockSpec((d_model, tile), lambda n: (0, n)), pl.BlockSpec((tile, d_model), lambda n: (n, 0))]
+        + [pl.BlockSpec(memory_space=pl.ANY)] * len(carry),
         out_specs=specs,
         out_shape=shapes,
-        input_output_aliases={4 + pos: pos for pos in range(len(carry))},
-        scratch_shapes=[pltpu.SemaphoreType.DMA((2,))] if copies else [],
+        input_output_aliases={len(args) + 2 + pos: pos for pos in range(len(carry))},
+        scratch_shapes=[pltpu.SemaphoreType.DMA((2 * len(pieces),))] if copies else [],
         compiler_params=pltpu.CompilerParams(vmem_limit_bytes=56 * 2 ** 20),
         cost_estimate=pl.CostEstimate(flops=4 * tokens * d_model * width, bytes_accessed=4 * d_model * (width + 2 * tokens),
                                       transcendentals=tokens * width),
         name='ff_forward',
-    )(h_blk, cot_blk, up, down, *carry)
+    )(*args, up, down, *carry)
 
 
 def grad_h_kernel(n_parts, *refs):
     total = sum(dot_nt(refs[2 * part][...], refs[2 * part + 1][...]) for part in range(n_parts))
+    halves = []
     for extra in refs[2 * n_parts:-1]:
-        total = total + extra[...]
+        if extra.shape == total.shape:
+            total = total + extra[...]
+        else:
+            halves.append(extra[...])
+    if halves:
+        total = total + jnp.concatenate(halves, axis=0)
     refs[-1][...] = total.astype(refs[-1].dtype)
 
 
-def grad_h_block(index, grad_u, up, extras, dtype):
+def grad_h_block(index, tokens, grad_u, up, extras, dtype):
     d_model = up[0].shape[0]
-    tokens = grad_u[0].shape[0] // 4
     width = sum(part.shape[1] for part in up)
     tile = 256
-    out_spec = pl.BlockSpec((tokens, tile), lambda n: (0, n))
     in_specs, args = [], []
     for left, right in zip(grad_u, up):
         in_specs += [pl.BlockSpec((tokens, left.shape[1]), lambda n: (index, 0)), pl.BlockSpec((tile, right.shape[1]), lambda n: (n, 0))]
@@ -392,8 +410,8 @@
     return pl.pallas_call(
         functools.partial(grad_h_kernel, len(up)),
         grid=(d_model // tile,),
-        in_specs=in_specs + [out_spec] * len(extras),
-        out_specs=out_spec,
+        in_specs=in_specs + [pl.BlockSpec((extra.shape[0], tile), lambda n: (0, n)) for extra in extras],
+        out_specs=pl.BlockSpec((tokens, tile), lambda n: (0, n)),
         out_shape=jax.ShapeDtypeStruct((tokens, d_model), dtype),
         compiler_params=pltpu.CompilerParams(vmem_limit_bytes=48 * 2 ** 20),
         cost_estimate=pl.CostEstimate(flops=2 * tokens * d_model * width, bytes_accessed=2 * width * (d_model + tokens) + 4 * tokens * d_model,
@@ -441,9 +459,13 @@
 
     def per_device(x_loc, cot_loc, w_q, w_k, w_v, w_o, w_up, w_down):
         d_model = x_loc.shape[2]
+        seq_len = x_loc.shape[1]
         kv_heads, head_dim = w_k.shape[1], w_k.shape[2]
         n_heads = w_q.shape[1]
+        group = n_heads // kv_heads
+        half = seq_len // 2
         kv_width = kv_heads * head_dim
+        rows = group * head_dim
         ff_dim = w_up.shape[1]
         ff_part = ff_dim // dev_count
         my_idx = lax.axis_index('cp')
@@ -478,41 +500,59 @@
         o_t = after(o_t, cot_far)
 
         h_act = (x + dot_tt(o_t, w_o)).astype(BF16)
-        h_far = swap(h_act, 2)
+        h_far = [swap(h_act[:half], 2), swap(h_act[half:], 2)]
         h_near = swap(h_act, 1)
         cot_last = swap(cot_far, 1)
-        state = ff_forward(0, cp_size, h_act, cot, w_up_own[0], w_down_own[0], True, ())
-        state = ff_forward(1, cp_size, h_near, cot_near, w_up_own[0], w_down_own[0], True, state)
-        more = ff_forward(0, cp_size, after(h_act, state[0]), cot, w_up_own[1], w_down_own[1], False, ())
-        more = ff_forward(1, cp_size, h_near, cot_near, w_up_own[1], w_down_own[1], False, more)
-        h_far = after(h_far, more[0])
-        h_last = swap(h_far, 1)
-        state = ff_forward(2, cp_size, h_far, cot_far, w_up_own[0], w_down_own[0], True, state)
-        act0, grad_u0, h_all, cot_all = ff_forward(3, cp_size, h_last, cot_last, w_up_own[0], w_down_own[0], True, state)
-        part = row_major(inv_count * dot_tn(h_all, grad_u0))
+
+        def ff_call(index, part, pieces, carry, *earlier):
+            first = after(pieces[0][0], *earlier) if earlier else pieces[0][0]
+            pieces = [(first,) + pieces[0][1:]] + pieces[1:]
+            return ff_forward(index, cp_size, pieces, w_up_own[part], w_down_own[part], part == 0, carry)
+
+        own, near = [(h_act, cot, 0)], [(h_near, cot_near, 0)]
+        state = ff_call(0, 0, own, ())
+        state = ff_call(1, 0, near, state)
+        more = ff_call(0, 1, own, (), state[0])
+
+        def remote(piece, *earlier):
+            far_piece = after(h_far[piece], *earlier)
+            return [(far_piece, cot_far, piece), (swap(far_piece, 1), cot_last, piece)]
+
+        remote0 = remote(0, more[0])
+        state = ff_call(2, 0, remote0, state)
+        more = ff_call(2, 1, remote0, more, state[0])
+        remote1 = remote(1, more[0])
+
+        def grad_h(index, tokens, grads, earlier, extras, dtype):
+            later = after(grads[1], earlier)
+            return grad_h_block(index, tokens, (grads[0], later), w_up_own, extras, dtype)
+
+        gh_last0 = grad_h(5, half, (state[1], more[1]), more[0], [], F32)
+        near0 = swap(gh_last0, 1)
+        act0, grad_u0, h_all, cot_all = ff_call(3, 0, remote1, state, gh_last0)
+        part = grad_h(4, half, (grad_u0, more[1]), act0, [near0], F32)
+        far0 = swap(part, 2)
+        later = after(grad_u0, part)
+        part = row_major(inv_count * dot_tn(h_all, later))
         up_rows = [dp_reduce(part)]
-        later = after(h_far, part)
-        more = ff_forward(2, cp_size, later, cot_far, w_up_own[1], w_down_own[1], False, more)
-        act1, grad_u1 = ff_forward(3, cp_size, h_last, cot_last, w_up_own[1], w_down_own[1], False, more)
-
-        part = grad_h_block(3, (grad_u0, grad_u1), w_up_own, [], F32)
-        near = swap(part, 1)
+        more = ff_call(3, 1, remote1, more, part)
+        gh_last1 = grad_h(7, half, (grad_u0, more[1]), more[0], [], F32)
+        near1 = swap(gh_last1, 1)
+        act1, grad_u1 = ff_call(1, 1, near, more, gh_last1)
+        part = grad_h(6, half, (grad_u0, grad_u1), act1, [near1], F32)
+        far1 = swap(part, 2)
         later = after(grad_u1, part)
         part = row_major(inv_count * dot_tn(h_all, later[:, :used[1]]))
         up_rows.append(dp_reduce(part))
-        later = after(grad_u1, part)
-        part = grad_h_block(2, (grad_u0, later), w_up_own, [near], F32)
-        far = swap(part, 2)
         later = after(act0, part)
         part = row_major(inv_count * dot_tn(later, cot_all))
         down_rows = [dp_reduce(part)]
+        part = grad_h(1, seq_len, (grad_u0, grad_u1), part, [], F32)
+        side = swap(part, 1)
         later = after(act1, part)
         part = row_major(inv_count * dot_tn(later[:, :used[1]], cot_all))
         down_rows.append(dp_reduce(part))
-        later = after(grad_u1, part)
-        part = grad_h_block(1, (grad_u0, later), w_up_own, [], F32)
-        side = swap(part, 1)
-        far = after(far, part)
+        far0 = after(far0, part)
 
         own_rows = d_model // dev_count
         up_got = []
@@ -520,8 +560,7 @@
             blocks = [lax.dynamic_slice_in_dim(rows_of, (my_idx ^ bits) * own_rows, own_rows, axis=0) for bits in range(cp_size)]
             up_got.append(jnp.stack([blocks[0]] + [row_major(swap(row_major(blocks[bits]), bits))
                                                    for bits in range(1, cp_size)]))
-        later = after(grad_u1, part)
-        grad_h_bf = grad_h_block(0, (grad_u0, later), w_up_own, [cot, side, far], BF16)
+        grad_h_bf = grad_h(0, seq_len, (grad_u0, grad_u1), part, [cot, side, far0, far1], BF16)
         grad_w_up = spread_columns(my_idx, up_got, splits)
 
         def block_sum(left, right_t):
@@ -561,10 +600,10 @@
         kv1_block, q1_block = kv_block(dkv1), block_sum(x, dq1_t)
         kv1_sent, _ = first_sends(kv1_block)
         q1_sent, parts_q = first_sends(q1_block)
-        grad_w_o = dp_reduce(after(o_block(0), *parts_q) + o_sent[1] + o_far)
+        sum_o = after(o_block(0), *parts_q) + o_sent[1] + o_far
         kv1_far, part_kv = second_send(kv1_block, kv1_sent)
         q1_far, part_q = second_send(q1_block, q1_sent)
-        grad_q0 = dp_reduce(q0_block(0) + q0_sent[1] + q0_far)
+        grad_oq = dp_reduce(jnp.concatenate([sum_o, q0_block(0) + q0_sent[1] + q0_far], axis=1))
         later = after(jnp.concatenate([dq0_t, dq1_t], axis=0), part_q, part_kv)
         grad_x = dot_tt(later, w_q)
         grad_x = grad_h_bf + grad_x
@@ -574,15 +613,16 @@
         w_block = block_sum(x, dkv_t)
         w_sent, _ = first_sends(w_block)
         w_far, _ = second_send(w_block, w_sent)
-        grad_q1 = dp_reduce(q1_block(0) + q1_sent[1] + q1_far)
+        sum_q1 = q1_block(0) + q1_sent[1] + q1_far
         grad_x = grad_x + dot_tt(dkv_t, w_kv)
-        grad_kv = dp_reduce(w_block(0) + w_sent[1] + w_far)
+        grad_qk = dp_reduce(jnp.concatenate([sum_q1, w_block(0) + w_sent[1] + w_far], axis=1))
+        o_width = n_heads * head_dim
         grad_w_down = jnp.concatenate(down_rows, axis=0)
 
-        grad_w_q = jnp.concatenate([grad_q0, grad_q1], axis=1).reshape(own_rows, n_heads, head_dim)
-        grad_w_k = grad_kv[:, :kv_width].reshape(own_rows, kv_heads, head_dim)
-        grad_w_v = grad_kv[:, kv_width:].reshape(own_rows, kv_heads, head_dim)
-        grad_w_o = grad_w_o.reshape(own_rows, n_heads, head_dim)
+        grad_w_q = jnp.concatenate([grad_oq[:, o_width:], grad_qk[:, :rows]], axis=1).reshape(own_rows, n_heads, head_dim)
+        grad_w_k = grad_qk[:, rows:rows + kv_width].reshape(own_rows, kv_heads, head_dim)
+        grad_w_v = grad_qk[:, rows + kv_width:].reshape(own_rows, kv_heads, head_dim)
+        grad_w_o = grad_oq[:, :o_width].reshape(own_rows, n_heads, head_dim)
         return grad_x.astype(BF16)[None], grad_w_q, grad_w_k, grad_w_v, grad_w_o, grad_w_up, grad_w_down
 
     act_spec = P('dp', 'cp', None)

time: 1330 us -> 1270 us (0.955)
  waiting for transfers between devices: 489 us -> 413 us
  Pallas kernels: 466 us -> 481 us
    reduce_scatter x8 -> x6, waiting for transfers between devices: 94.6 us -> 0.03 us  [dp_reduce(): return lax.psum_scatter(grad, 'dp', scatter_dimension=0, tiled=True)]
    ppermute x33 -> x37, waiting for transfers between devices: 393 us -> 413 us  [swap(): lax.ppermute(values, 'cp', [(src, src ^ bits) for src in range(cp_size)])]
    pallas_call x4 -> x6, Pallas kernels: 75.3 us -> 90.8 us  [grad_h_block(): pl.pallas_call(functools.partial(grad_h_kernel, len(up)), grid=(d_model /...]
  transfers between devices with their start and end apart: 42 -> 44, of which waited for: 18 -> 13; matrix products, arithmetic and copies ran while one was open for 21% -> 22% of each run, Pallas kernels for 29% -> 37%
where the time goes in v3:
time: 1270 us; the launch traced here: 1260 us
  Pallas kernels  481 us (38%)
  waiting for transfers between devices  413 us (33%)
  matrix products  236 us (19%)
  local copies, waits for them, and re-layouts  45.7 us (4%)
  other arithmetic  40.7 us (3%)
  between operations  25.1 us (2%)
  starting transfers between devices  20.9 us (2%)
    ppermute x37, waiting for transfers between devices, swap(): lax.ppermute(values, 'cp', [(src, src ^ bits) for src in range(cp_size)])  413 us
    pallas_call x8, Pallas kernels, ff_forward(): pl.pallas_call(functools.partial(ff_kernel, 512, copies, index * tokens,...  165 us
    dot_general x4, matrix products, dot_tn(): lax.dot_general(lhs, rhs, (((0,), (0,)), ((), ())), preferred_element_typ...  126 us
    pallas_call x2, Pallas kernels, attn_backward(): pl.pallas_call(functools.partial(attn_bwd_kernel, group, head_dim ** (-0....  116 us
    dot_general x21, matrix products, dot_tt(): lax.dot_general(lhs, rhs, (((0,), (1,)), ((), ())), preferred_element_typ...  107 us
    pallas_call x6, Pallas kernels, grad_h_block(): pl.pallas_call(functools.partial(grad_h_kernel, len(up)), grid=(d_model /...  90.8 us
    pallas_call x1, Pallas kernels, attn_forward(): pl.pallas_call(functools.partial(attn_fwd_kernel, group, head_dim ** (-0....  81.9 us
  transfers between devices with their start and end apart: 44, of which 13 were waited for; matrix products, arithmetic and copies ran while one was open for 22% of the time, Pallas kernels for 37%

profile of v3, /device:TPU:0, one launch (start us, length us, event | category | flops | bytes accessed | tf_op | source)
XLA Modules:
  0.0 1262.8 jit_solution(17898999886159944681)
XLA Ops:
  25.6 21.3 %prepare.1 = (bf16[2048,1280]{1,0:T(8,128)(2,1)}, bf16[2048,1536]{1,0:T(8,128)(2,1)}, bf16[1280,2048]{1,0:T(8,128)(2,1)}, bf16[1536,2048]{1,0:T(8,128)(2,1)}) custom-call(s32[3,8]{1,0:T(4,128)} %pad_add_fusion.1.idx_ref, bf16[2048,11008]{1,0:T(8,128)(2,1)} %refs_34_.1, bf16[2048,11008]{1,0:T(8,128)(2,1)} %refs_34_.1, bf16[2048,11008]{1,0:T(8,128)(2,1)} %refs_34_.1, ...), custom_call_target="tpu_custom_call" | custom-call | flops 46137344 | bytes 51904512 | tf_op jit(solution)/shard_map/prepare/pallas_call | solution.py:301
  47.0 12.6 %fusion.26.q_ref = bf16[2048,1024]{1,0:T(8,128)(2,1)} fusion(bf16[1,1024,2048]{2,1,0:T(8,128)(2,1)S(1)} %copy-done.7, bf16[256,8,16,128]{3,2,1,0:T(8,128)(2,1)} %bitcast.207), kind=kOutput, calls=%fused_computation.32 | convolution fusion | flops 8592031744 | bytes 16777216 | tf_op jit(solution)/shard_map/dot_general | solution.py:37
  63.4 81.9 %attn_fwd.1 = (f32[2048,1024]{1,0:T(8,128)}, bf16[2048,1024]{1,0:T(8,128)(2,1)}, f32[2,8,1024]{2,1,0:T(8,128)}) custom-call(s32[4,9]{1,0:T(4,128)} %pad_add_fusion.tab, bf16[2048,1024]{1,0:T(8,128)(2,1)} %fusion.26.q_ref, bf16[4096,512]{1,0:T(8,128)(2,1)} %all-gather.2.cloned.1.call-done.k_ref.v_ref, bf16[4096,512]{1,0:T(8,128)(2,1)} %all-gather.2.cloned.1.call-done.k_ref.v_ref), custom_call_target="tpu_custom_call" | custom-call | flops 19327352832 | bytes 25165824 | tf_op jit(solution)/shard_map/attn_fwd/pallas_call | solution.py:113
  145.3 8.3 collective-permute-done.refs_1_
  153.7 14.0 %add_convert_fusion.1.refs_0_ = bf16[1024,2048]{1,0:T(8,128)(2,1)} fusion(bf16[1,1024,2048]{2,1,0:T(8,128)(2,1)S(1)} %copy-done.8, bf16[2048,1024]{1,0:T(8,128)(2,1)} %get-tuple-element.74, bf16[256,8,16,128]{3,2,1,0:T(8,128)(2,1)} %bitcast.205), kind=kOutput, calls=%fused_computation.17 | convolution fusion | flops 8596226048 | bytes 20971520 | tf_op jit(solution)/shard_map/dot_general | solution.py:37
  167.7 4.2 fusion.86
  173.8 19.2 %ff_forward.8 = (bf16[4096,1280]{1,0:T(8,128)(2,1)}, bf16[4096,1280]{1,0:T(8,128)(2,1)}, bf16[4096,2048]{1,0:T(8,128)(2,1)}, bf16[4096,2048]{1,0:T(8,128)(2,1)}) custom-call(bf16[1024,2048]{1,0:T(8,128)(2,1)} %add_convert_fusion.1.refs_0_, bf16[1024,2048]{1,0:T(8,128)(2,1)} %bitcast.187, bf16[2048,1280]{1,0:T(8,128)(2,1)} %get-tuple-element.70.refs_2_.refs_4_.refs_1_, ...), custom_call_target="tpu_custom_call" | custom-call | flops 10737418240 | bytes 27262976 | tf_op jit(solution)/shard_map/ff_forward/pallas_call | solution.py:373
  193.0 19.1 %ff_forward.9 = (bf16[4096,1280]{1,0:T(8,128)(2,1)}, bf16[4096,1280]{1,0:T(8,128)(2,1)}, bf16[4096,2048]{1,0:T(8,128)(2,1)}, bf16[4096,2048]{1,0:T(8,128)(2,1)}) custom-call(bf16[1024,2048]{1,0:T(8,128)(2,1)} %collective-permute-done.3.refs_0_, ...), custom_call_target="tpu_custom_call", output_to_operand_aliasing={{0}: (4, {}), {1}: (5, {}), {2}: (6, {}), {3}: (7, {})} | custom-call | flops 10737418240 | bytes 27262976 | tf_op jit(solution)/shard_map/ff_forward/pallas_call | solution.py:373
  212.1 21.7 %ff_forward.10 = (bf16[4096,1536]{1,0:T(8,128)(2,1)}, bf16[4096,1536]{1,0:T(8,128)(2,1)}) custom-call(bf16[1024,2048]{1,0:T(8,128)(2,1)} %add_convert_fusion.1.refs_0_, bf16[1024,2048]{1,0:T(8,128)(2,1)} %bitcast.188, bf16[2048,1536]{1,0:T(8,128)(2,1)} %get-tuple-element.82.refs_2_.refs_4_.refs_3_, bf16[1536,2048]{1,0:T(8,128)(2,1)} %get-tuple-element.83.refs_3_.refs_5_), custom_call_target="tpu_custom_call" | custom-call | flops 12884901888 | bytes 29360128 | tf_op jit(solution)/shard_map/ff_forward/pallas_call | solution.py:373
  238.4 19.1 %ff_forward.11 = (bf16[4096,1280]{1,0:T(8,128)(2,1)}, bf16[4096,1280]{1,0:T(8,128)(2,1)}, bf16[4096,2048]{1,0:T(8,128)(2,1)}, bf16[4096,2048]{1,0:T(8,128)(2,1)}) custom-call(bf16[512,2048]{1,0:T(8,128)(2,1)} %collective-permute-done.2.refs_0_, ...), custom_call_target="tpu_custom_call", output_to_operand_aliasing={{0}: (6, {}), {1}: (7, {}), {2}: (8, {}), {3}: (9, {})} | custom-call | flops 10737418240 | bytes 27262976 | tf_op jit(solution)/shard_map/ff_forward/pallas_call | solution.py:373
  257.5 22.0 %ff_forward.12 = (bf16[4096,1536]{1,0:T(8,128)(2,1)}, bf16[4096,1536]{1,0:T(8,128)(2,1)}) custom-call(bf16[512,2048]{1,0:T(8,128)(2,1)} %collective-permute-done.2.refs_0_, bf16[1024,2048]{1,0:T(8,128)(2,1)} %collective-permute-done.refs_1_, bf16[512,2048]{1,0:T(8,128)(2,1)} %collective-permute-done.5.refs_2_, ...), custom_call_target="tpu_custom_call", output_to_operand_aliasing={{0}: (6, {}), {1}: (7, {})} | custom-call | flops 12884901888 | bytes 29360128 | tf_op jit(solution)/shard_map/ff_forward/pallas_call | solution.py:373
  279.5 11.4 grad_h.6
  291.4 9.6 collective-permute-done.7.refs_2_
  302.4 19.1 %ff_forward.13 = (bf16[4096,1280]{1,0:T(8,128)(2,1)}, bf16[4096,1280]{1,0:T(8,128)(2,1)}, bf16[4096,2048]{1,0:T(8,128)(2,1)}, bf16[4096,2048]{1,0:T(8,128)(2,1)}) custom-call(bf16[512,2048]{1,0:T(8,128)(2,1)} %copy-done.4, bf16[1024,2048]{1,0:T(8,128)(2,1)} %collective-permute-done.refs_1_, ...), custom_call_target="tpu_custom_call", output_to_operand_aliasing={{0}: (6, {}), {1}: (7, {}), {2}: (8, {}), {3}: (9, {})} | custom-call | flops 10737418240 | bytes 27262976 | tf_op jit(solution)/shard_map/ff_forward/pallas_call | solution.py:373
  321.6 14.4 %grad_h.7 = f32[512,2048]{1,0:T(8,128)} custom-call(bf16[4096,1280]{1,0:T(8,128)(2,1)} %get-tuple-element.104.refs_0_, bf16[2048,1280]{1,0:T(8,128)(2,1)} %get-tuple-element.70.refs_2_.refs_4_.refs_1_, bf16[4096,1536]{1,0:T(8,128)(2,1)} %get-tuple-element.103.refs_2_.refs_7_, bf16[2048,1536]{1,0:T(8,128)(2,1)} %get-tuple-element.82.refs_2_.refs_4_.refs_3_, ...), custom_call_target="tpu_custom_call" | custom-call | flops 5905580032 | bytes 18612224 | tf_op jit(solution)/shard_map/grad_h/pallas_call | solution.py:410
  336.0 26.5 %convolution_multiply_fusion.1 = f32[2048,1280]{1,0:T(8,128)} fusion(bf16[4096,2048]{1,0:T(8,128)(2,1)} %get-tuple-element.101, bf16[4096,1280]{1,0:T(8,128)(2,1)S(1)} %copy-done.2), kind=kOutput, calls=%fused_computation.6 | convolution fusion | flops 21477457920 | bytes 37748736 | tf_op jit(solution)/shard_map/dot_general | solution.py:33
  362.5 22.2 %ff_forward.14 = (bf16[4096,1536]{1,0:T(8,128)(2,1)}, bf16[4096,1536]{1,0:T(8,128)(2,1)}) custom-call(bf16[512,2048]{1,0:T(8,128)(2,1)} %copy-done.4, bf16[1024,2048]{1,0:T(8,128)(2,1)} %collective-permute-done.refs_1_, bf16[512,2048]{1,0:T(8,128)(2,1)} %copy-done.5, bf16[1024,2048]{1,0:T(8,128)(2,1)} %copy-done.3, ...), custom_call_target="tpu_custom_call", output_to_operand_aliasing={{0}: (6, {}), {1}: (7, {})} | custom-call | flops 12884901888 | bytes 29360128 | tf_op jit(solution)/shard_map/ff_forward/pallas_call | solution.py:373
  384.7 12.0 grad_h.8
  396.8 22.1 %ff_forward.15 = (bf16[4096,1536]{1,0:T(8,128)(2,1)}, bf16[4096,1536]{1,0:T(8,128)(2,1)}) custom-call(bf16[1024,2048]{1,0:T(8,128)(2,1)} %collective-permute-done.3.refs_0_, bf16[1024,2048]{1,0:T(8,128)(2,1)} %collective-permute-done.4.refs_1_, ...), custom_call_target="tpu_custom_call", output_to_operand_aliasing={{0}: (4, {}), {1}: (5, {})} | custom-call | flops 12884901888 | bytes 29360128 | tf_op jit(solution)/shard_map/ff_forward/pallas_call | solution.py:373
  418.8 14.2 %grad_h.9 = f32[512,2048]{1,0:T(8,128)} custom-call(bf16[4096,1280]{1,0:T(8,128)(2,1)} %get-tuple-element.104.refs_0_, bf16[2048,1280]{1,0:T(8,128)(2,1)} %get-tuple-element.70.refs_2_.refs_4_.refs_1_, bf16[4096,1536]{1,0:T(8,128)(2,1)} %get-tuple-element.118.refs_2_, bf16[2048,1536]{1,0:T(8,128)(2,1)} %get-tuple-element.82.refs_2_.refs_4_.refs_3_, ...), custom_call_target="tpu_custom_call" | custom-call | flops 5905580032 | bytes 18612224 | tf_op jit(solution)/shard_map/grad_h/pallas_call | solution.py:410
  433.0 34.8 %fusion.7 = f32[2048,1472]{1,0:T(8,128)} fusion(bf16[4096,2048]{1,0:T(8,128)(2,1)} %get-tuple-element.101, bf16[4096,1536]{1,0:T(8,128)(2,1)} %get-tuple-element.118.refs_2_), kind=kOutput, calls=%fused_computation.7 | convolution fusion | flops 24699076608 | bytes 41418752 | tf_op jit(solution)/shard_map/dot_general | solution.py:33
  467.9 30.5 %convolution_multiply_fusion = f32[1280,2048]{1,0:T(8,128)} fusion(bf16[4096,1280]{1,0:T(8,128)(2,1)} %get-tuple-element.114, bf16[4096,2048]{1,0:T(8,128)(2,1)} %get-tuple-element.115), kind=kOutput, calls=%fused_computation.5 | convolution fusion | flops 21477457920 | bytes 37748736 | tf_op jit(solution)/shard_map/dot_general | solution.py:33
  501.0 18.0 %grad_h.10 = f32[1024,2048]{1,0:T(8,128)} custom-call(bf16[4096,1280]{1,0:T(8,128)(2,1)} %get-tuple-element.104.refs_0_, bf16[2048,1280]{1,0:T(8,128)(2,1)S(1)} %copy-done, bf16[4096,1536]{1,0:T(8,128)(2,1)} %get-tuple-element.118.refs_2_, bf16[2048,1536]{1,0:T(8,128)(2,1)} %get-tuple-element.82.refs_2_.refs_4_.refs_3_), custom_call_target="tpu_custom_call" | custom-call | flops 11811160064 | bytes 25690112 | tf_op jit(solution)/shard_map/grad_h/pallas_call | solution.py:410
  521.0 33.9 %fusion.4 = f32[1472,2048]{1,0:T(8,128)} fusion(bf16[4096,2048]{1,0:T(8,128)(2,1)} %get-tuple-element.115, bf16[4096,1536]{1,0:T(8,128)(2,1)} %get-tuple-element.117), kind=kOutput, calls=%fused_computation.4 | convolution fusion | flops 24699076608 | bytes 41418752 | tf_op jit(solution)/shard_map/dot_general | solution.py:33
  555.1 57.7 %collective-permute-done.11.refs_6_ = f32[512,2048]{1,0:T(8,128)} collective-permute-done((f32[512,2048]{1,0:T(8,128)}, f32[512,2048]{1,0:T(8,128)}, u32[]{:S(2)}, u32[]{:S(2)}) %collective-permute-start.11) | collective-permute-done | bytes 4194336 | tf_op jit(solution)/shard_map/ppermute | solution.py:452
  612.7 89.4 %collective-permute-done.12.refs_7_ = f32[512,2048]{1,0:T(8,128)} collective-permute-done((f32[512,2048]{1,0:T(8,128)}, f32[512,2048]{1,0:T(8,128)}, u32[]{:S(2)}, u32[]{:S(2)}) %collective-permute-start.12) | collective-permute-done | bytes 4194336 | tf_op jit(solution)/shard_map/ppermute | solution.py:452
  702.2 20.9 %grad_h.11 = bf16[1024,2048]{1,0:T(8,128)(2,1)S(1)} custom-call(bf16[4096,1280]{1,0:T(8,128)(2,1)} %get-tuple-element.104.refs_0_, bf16[2048,1280]{1,0:T(8,128)(2,1)} %get-tuple-element.70.refs_2_.refs_4_.refs_1_, bf16[4096,1536]{1,0:T(8,128)(2,1)} %get-tuple-element.118.refs_2_, bf16[2048,1536]{1,0:T(8,128)(2,1)} %get-tuple-element.82.refs_2_.refs_4_.refs_3_, ...), custom_call_target="tpu_custom_call" | custom-call | flops 11811160064 | bytes 25690112 | tf_op jit(solution)/shard_map/grad_h/pallas_call | solution.py:410
  727.1 4.4 convolution_multiply_fusion.4
  733.9 4.4 convolution_multiply_fusion.3
  740.7 13.0 %convert_bitcast_fusion.do_ref = bf16[2048,1024]{1,0:T(8,128)(2,1)} fusion(bf16[1024,2048]{1,0:T(8,128)(2,1)S(1)} %grad_h.11, bf16[256,8,16,128]{3,2,1,0:T(8,128)(2,1)} %bitcast.206), kind=kOutput, calls=%fused_computation.31 | convolution fusion | flops 8592031744 | bytes 16777216 | tf_op jit(solution)/shard_map/dot_general | solution.py:37
  756.9 57.8 %attn_bwd.2 = (bf16[1024,1024]{1,0:T(8,128)(2,1)}, f32[8,2,128,512]{3,2,1,0:T(8,128)}) custom-call(s32[4,9]{1,0:T(4,128)} %pad_add_fusion.tab, bf16[2048,1024]{1,0:T(8,128)(2,1)} %fusion.26.q_ref, bf16[2048,1024]{1,0:T(8,128)(2,1)} %convert_bitcast_fusion.do_ref, f32[2048,1024]{1,0:T(8,128)} %get-tuple-element.123.of_ref, ...), custom_call_target="tpu_custom_call" | custom-call | flops 24159191040 | bytes 12582912 | tf_op jit(solution)/shard_map/attn_bwd/pallas_call | solution.py:191
  814.7 4.2 convolution_multiply_fusion.8
  829.4 4.2 multiply_add_fusion.2
  833.6 57.7 %attn_bwd.3 = (bf16[1024,1024]{1,0:T(8,128)(2,1)}, f32[8,2,128,512]{3,2,1,0:T(8,128)}) custom-call(s32[4,9]{1,0:T(4,128)} %pad_add_fusion.tab, bf16[2048,1024]{1,0:T(8,128)(2,1)} %fusion.26.q_ref, bf16[2048,1024]{1,0:T(8,128)(2,1)} %convert_bitcast_fusion.do_ref, f32[2048,1024]{1,0:T(8,128)} %get-tuple-element.123.of_ref, ...), custom_call_target="tpu_custom_call" | custom-call | flops 24159191040 | bytes 12582912 | tf_op jit(solution)/shard_map/attn_bwd/pallas_call | solution.py:191
  905.6 15.5 %collective-permute-done.19 = f32[2,2,128,512]{3,2,1,0:T(8,128)} collective-permute-done((f32[2,2,128,512]{3,2,1,0:T(8,128)}, f32[2,2,128,512]{3,2,1,0:T(8,128)}, u32[]{:S(2)}, u32[]{:S(2)}) %collective-permute-start.19) | collective-permute-done | bytes 1048608 | tf_op jit(solution)/shard_map/ppermute | solution.py:452
  923.3 19.7 %collective-permute-done.21 = f32[2,2,128,512]{3,2,1,0:T(8,128)} collective-permute-done((f32[2,2,128,512]{3,2,1,0:T(8,128)}, f32[2,2,128,512]{3,2,1,0:T(8,128)}, u32[]{:S(2)}, u32[]{:S(2)}) %collective-permute-start.21) | collective-permute-done | bytes 1048608 | tf_op jit(solution)/shard_map/ppermute | solution.py:452
  955.3 43.5 %collective-permute-done.27 = f32[512,1024]{1,0:T(8,128)S(1)} collective-permute-done((f32[512,1024]{1,0:T(8,128)S(1)}, f32[512,1024]{1,0:T(8,128)S(1)}, u32[]{:S(2)}, u32[]{:S(2)}) %collective-permute-start.27) | collective-permute-done | bytes 2097184 | tf_op jit(solution)/shard_map/ppermute | solution.py:452
  999.6 20.2 %collective-permute-done.30 = f32[512,512]{1,0:T(8,128)S(1)} collective-permute-done((f32[512,512]{1,0:T(8,128)S(1)}, f32[512,512]{1,0:T(8,128)S(1)}, u32[]{:S(2)}, u32[]{:S(2)}) %collective-permute-start.30) | collective-permute-done | bytes 1048608 | tf_op jit(solution)/shard_map/ppermute | solution.py:452
  1025.3 5.0 convolution_multiply_fusion.2
  1032.9 83.8 %collective-permute-done.23 = f32[512,2048]{1,0:T(8,128)S(1)} collective-permute-done((f32[512,2048]{1,0:T(8,128)}, f32[512,2048]{1,0:T(8,128)S(1)}, u32[]{:S(2)}, u32[]{:S(2)}) %collective-permute-start.23) | collective-permute-done | bytes 4194336 | tf_op jit(solution)/shard_map/ppermute | solution.py:452
  1118.4 42.8 %collective-permute-done.25 = f32[512,1024]{1,0:T(8,128)} collective-permute-done((f32[512,1024]{1,0:T(8,128)}, f32[512,1024]{1,0:T(8,128)}, u32[]{:S(2)}, u32[]{:S(2)}) %collective-permute-start.25) | collective-permute-done | bytes 2097184 | tf_op jit(solution)/shard_map/ppermute | solution.py:452
  1167.3 4.0 pad_maximum_fusion.2
  1177.3 5.7 fusion.85
  1190.6 17.8 %fusion.22 = bf16[1,1024,2048]{2,1,0:T(8,128)(2,1)} fusion(f32[1024,2048]{1,0:T(8,128)} %fusion.85, bf16[1024,2048]{1,0:T(8,128)(2,1)} %copy-done.1, bf16[2048,1024]{1,0:T(8,128)(2,1)} %pad_maximum_fusion.2, bf16[256,8,16,128]{3,2,1,0:T(8,128)(2,1)} %bitcast.208), kind=kOutput, calls=%fused_computation.24 | convolution fusion | flops 8598323200 | bytes 29360128 | tf_op jit(solution)/shard_map/dot_general | solution.py:37
  1211.8 6.9 pad_maximum_fusion.1
  1218.9 4.6 collective-permute-done.35
  1224.9 13.8 %collective-permute-done.36 = f32[128,1472]{0,1:T(8,128)} collective-permute-done((f32[128,1472]{0,1:T(8,128)}, f32[128,1472]{0,1:T(8,128)}, u32[]{:S(2)}, u32[]{:S(2)}) %collective-permute-start.36) | collective-permute-done | bytes 753696 | tf_op jit(solution)/shard_map/ppermute | solution.py:452
  1242.0 6.9 spread.1
  (275 shorter events, 121.7 us)
Async XLA Ops:
  7.2 52.4 %all-gather.2.cloned.1.call-start = ((), (), s32[]{:S(2)}) async-start(), calls=%async_computation.6 | async-start | bytes 5242880 | tf_op jit(solution)/shard_map/all_gather | solution.py:487
  14.8 1156.6 %reduce-scatter.11.cloned.1.call-start = ((), (), s32[]{:S(2)}) async-start(), calls=%async_computation.9 | async-start | bytes 13107200 | tf_op jit(solution)/shard_map/reduce_scatter | solution.py:455
  59.6 94.1 %collective-permute-start = (bf16[1024,2048]{1,0:T(8,128)(2,1)}, bf16[1024,2048]{1,0:T(8,128)(2,1)}, u32[]{:S(2)}, u32[]{:S(2)}) collective-permute-start(bf16[1024,2048]{1,0:T(8,128)(2,1)} %bitcast.185), channel_id=1, source_target_pairs={{0,2},{1,3},{2,0},{3,1},{4,6},{5,7},{6,4},{7,5},{8,10},{9,11},{10,... | collective-permute-start | bytes 12582920 | tf_op jit(solution)/shard_map/ppermute | solution.py:452
  62.8 130.2 %collective-permute-start.4 = (bf16[1024,2048]{1,0:T(8,128)(2,1)}, bf16[1024,2048]{1,0:T(8,128)(2,1)}, u32[]{:S(2)}, u32[]{:S(2)}) collective-permute-start(bf16[1024,2048]{1,0:T(8,128)(2,1)} %bitcast.186), channel_id=1, source_target_pairs={{0,1},{1,0},{2,3},{3,2},{4,5},{5,4},{6,7},{7,6},{8,9},{9,8},{10,11... | collective-permute-start | bytes 12582920 | tf_op jit(solution)/shard_map/ppermute | solution.py:452
  63.4 90.3 %copy-start.8 = (bf16[1,1024,2048]{2,1,0:T(8,128)(2,1)S(1)}, bf16[1,1024,2048]{2,1,0:T(8,128)(2,1)}, u32[]{:S(2)}) copy-start(bf16[1,1024,2048]{2,1,0:T(8,128)(2,1)} %param.8) | copy-start | bytes 12582916
  167.7 25.3 %collective-permute-start.3 = (bf16[1024,2048]{1,0:T(8,128)(2,1)}, bf16[1024,2048]{1,0:T(8,128)(2,1)}, u32[]{:S(2)}, u32[]{:S(2)}) collective-permute-start(bf16[1024,2048]{1,0:T(8,128)(2,1)} %add_convert_fusion.1.refs_0_), channel_id=1, source_target_pairs={{0,1},{1,0},{2,3},{3,2},{4,5},{5,4},{6,7},{7,6},{8,9},{9,8},{10,11... | collective-permute-start | bytes 12582920 | tf_op jit(solution)/shard_map/ppermute | solution.py:452
  171.8 62.0 %collective-permute-start.2 = (bf16[512,2048]{1,0:T(8,128)(2,1)S(1)}, bf16[512,2048]{1,0:T(8,128)(2,1)}, u32[]{:S(2)}, u32[]{:S(2)}) collective-permute-start(bf16[512,2048]{1,0:T(8,128)(2,1)S(1)} %get-tuple-element.169), channel_id=1, source_target_pairs={{0,2},{1,3},{2,0},{3,1},{4,6},{5,7},{6,4},{7,5},{8,10},{9,11},{10,... | collective-permute-start | bytes 6291464 | tf_op jit(solution)/shard_map/ppermute | solution.py:452
  173.6 60.9 %collective-permute-start.6 = (bf16[1024,2048]{1,0:T(8,128)(2,1)}, bf16[1024,2048]{1,0:T(8,128)(2,1)S(1)}, u32[]{:S(2)}, u32[]{:S(2)}) collective-permute-start(bf16[1024,2048]{1,0:T(8,128)(2,1)} %collective-permute-done.refs_1_), channel_id=1, source_target_pairs={{0,1},{1,0},{2,3},{3,2},{4,5},{5,4},{6,7},{7,6},{8,9},{9,8},{10,11... | collective-permute-start | bytes 12582920 | tf_op jit(solution)/shard_map/ppermute | solution.py:452
  233.8 4.5 collective-permute-start.5
  234.2 57.0 %collective-permute-start.1 = (bf16[512,2048]{1,0:T(8,128)(2,1)}, bf16[512,2048]{1,0:T(8,128)(2,1)S(1)}, u32[]{:S(2)}, u32[]{:S(2)}) collective-permute-start(bf16[512,2048]{1,0:T(8,128)(2,1)} %get-tuple-element.170), channel_id=1, source_target_pairs={{0,2},{1,3},{2,0},{3,1},{4,6},{5,7},{6,4},{7,5},{8,10},{9,11},{10,... | collective-permute-start | bytes 6291464 | tf_op jit(solution)/shard_map/ppermute | solution.py:452
  290.9 30.7 %collective-permute-start.8 = (f32[512,2048]{1,0:T(8,128)S(1)}, f32[512,2048]{1,0:T(8,128)}, u32[]{:S(2)}, u32[]{:S(2)}) collective-permute-start(f32[512,2048]{1,0:T(8,128)S(1)} %grad_h.6), channel_id=1, source_target_pairs={{0,1},{1,0},{2,3},{3,2},{4,5},{5,4},{6,7},{7,6},{8,9},{9,8},{10,11... | collective-permute-start | bytes 12582920 | tf_op jit(solution)/shard_map/ppermute | solution.py:452
  291.2 9.9 collective-permute-start.7
  362.4 820.5 %reduce-scatter.13.cloned.1.call-start = ((), (), s32[]{:S(2)}) async-start(), calls=%async_computation.10 | async-start | bytes 15728640 | tf_op jit(solution)/shard_map/reduce_scatter | solution.py:455
  396.7 22.1 %collective-permute-start.9 = (f32[512,2048]{1,0:T(8,128)S(1)}, f32[512,2048]{1,0:T(8,128)}, u32[]{:S(2)}, u32[]{:S(2)}) collective-permute-start(f32[512,2048]{1,0:T(8,128)S(1)} %grad_h.8), channel_id=1, source_target_pairs={{0,1},{1,0},{2,3},{3,2},{4,5},{5,4},{6,7},{7,6},{8,9},{9,8},{10,11... | collective-permute-start | bytes 12582920 | tf_op jit(solution)/shard_map/ppermute | solution.py:452
  467.9 743.9 %reduce-scatter.15.cloned.1.call-start = ((), (), s32[]{:S(2)}) async-start(), calls=%async_computation.11 | async-start | bytes 13107200 | tf_op jit(solution)/shard_map/reduce_scatter | solution.py:455
  498.4 713.3 %reduce-scatter.17.cloned.1.call-start = ((), (), s32[]{:S(2)}) async-start(), calls=%async_computation.12 | async-start | bytes 15073280 | tf_op jit(solution)/shard_map/reduce_scatter | solution.py:455
  519.0 183.2 %collective-permute-start.10 = (f32[1024,2048]{1,0:T(8,128)}, f32[1024,2048]{1,0:T(8,128)}, u32[]{:S(2)}, u32[]{:S(2)}) collective-permute-start(f32[1024,2048]{1,0:T(8,128)} %grad_h.10), channel_id=1, source_target_pairs={{0,1},{1,0},{2,3},{3,2},{4,5},{5,4},{6,7},{7,6},{8,9},{9,8},{10,11... | collective-permute-start | bytes 25165832 | tf_op jit(solution)/shard_map/ppermute | solution.py:452
  519.0 93.8 %collective-permute-start.11 = (f32[512,2048]{1,0:T(8,128)}, f32[512,2048]{1,0:T(8,128)}, u32[]{:S(2)}, u32[]{:S(2)}) collective-permute-start(f32[512,2048]{1,0:T(8,128)} %grad_h.7), channel_id=1, source_target_pairs={{0,2},{1,3},{2,0},{3,1},{4,6},{5,7},{6,4},{7,5},{8,10},{9,11},{10,... | collective-permute-start | bytes 12582920 | tf_op jit(solution)/shard_map/ppermute | solution.py:452
  519.0 183.2 %collective-permute-start.12 = (f32[512,2048]{1,0:T(8,128)}, f32[512,2048]{1,0:T(8,128)}, u32[]{:S(2)}, u32[]{:S(2)}) collective-permute-start(f32[512,2048]{1,0:T(8,128)} %grad_h.9), channel_id=1, source_target_pairs={{0,2},{1,3},{2,0},{3,1},{4,6},{5,7},{6,4},{7,5},{8,10},{9,11},{10,... | collective-permute-start | bytes 12582920 | tf_op jit(solution)/shard_map/ppermute | solution.py:452
  554.9 694.0 %reduce-scatter.9.cloned.1.call-start = ((), (), s32[]{:S(2)}) async-start(), calls=%async_computation.8 | async-start | bytes 3932160 | tf_op jit(solution)/shard_map/reduce_scatter | solution.py:455
  731.5 22.2 %collective-permute-start.13 = (f32[512,2048]{1,0:T(8,128)}, f32[512,2048]{1,0:T(8,128)S(1)}, u32[]{:S(2)}, u32[]{:S(2)}) collective-permute-start(f32[512,2048]{1,0:T(8,128)} %convolution_multiply_fusion.4), channel_id=1, source_target_pairs={{0,1},{1,0},{2,3},{3,2},{4,5},{5,4},{6,7},{7,6},{8,9},{9,8},{10,11... | collective-permute-start | bytes 12582920 | tf_op jit(solution)/shard_map/ppermute | solution.py:452
  819.0 10.4 collective-permute-start.15
  822.7 3.8 collective-permute-start.14
  894.2 4.7 collective-permute-start.17
  894.7 10.8 collective-permute-start.18
  894.7 26.3 %collective-permute-start.19 = (f32[2,2,128,512]{3,2,1,0:T(8,128)}, f32[2,2,128,512]{3,2,1,0:T(8,128)}, u32[]{:S(2)}, u32[]{:S(2)}) collective-permute-start(f32[2,2,128,512]{3,2,1,0:T(8,128)} %bitcast_add_fusion.3), channel_id=1, source_target_pairs={{0,2},{1,3},{2,0},{3,1},{4,6},{5,7},{6,4},{7,5},{8,10},{9,11},{10,... | collective-permute-start | bytes 3145736 | tf_op jit(solution)/shard_map/ppermute | solution.py:452
  898.4 47.8 %collective-permute-start.16 = (f32[512,1024]{1,0:T(8,128)}, f32[512,1024]{1,0:T(8,128)}, u32[]{:S(2)}, u32[]{:S(2)}) collective-permute-start(f32[512,1024]{1,0:T(8,128)} %convolution_multiply_fusion.6), channel_id=1, source_target_pairs={{0,1},{1,0},{2,3},{3,2},{4,5},{5,4},{6,7},{7,6},{8,9},{9,8},{10,11... | collective-permute-start | bytes 6291464 | tf_op jit(solution)/shard_map/ppermute | solution.py:452
  898.6 24.7 %collective-permute-start.20 = (f32[2,2,128,512]{3,2,1,0:T(8,128)}, f32[2,2,128,512]{3,2,1,0:T(8,128)}, u32[]{:S(2)}, u32[]{:S(2)}) collective-permute-start(f32[2,2,128,512]{3,2,1,0:T(8,128)} %get-tuple-element.167), channel_id=1, source_target_pairs={{0,1},{1,0},{2,3},{3,2},{4,5},{5,4},{6,7},{7,6},{8,9},{9,8},{10,11... | collective-permute-start | bytes 3145736 | tf_op jit(solution)/shard_map/ppermute | solution.py:452
  901.3 41.7 %collective-permute-start.21 = (f32[2,2,128,512]{3,2,1,0:T(8,128)}, f32[2,2,128,512]{3,2,1,0:T(8,128)}, u32[]{:S(2)}, u32[]{:S(2)}) collective-permute-start(f32[2,2,128,512]{3,2,1,0:T(8,128)} %bitcast_add_fusion.2), channel_id=1, source_target_pairs={{0,2},{1,3},{2,0},{3,1},{4,6},{5,7},{6,4},{7,5},{8,10},{9,11},{10,... | collective-permute-start | bytes 3145736 | tf_op jit(solution)/shard_map/ppermute | solution.py:452
  905.5 49.7 %collective-permute-start.26 = (f32[512,1024]{1,0:T(8,128)S(1)}, f32[512,1024]{1,0:T(8,128)S(1)}, u32[]{:S(2)}, u32[]{:S(2)}) collective-permute-start(f32[512,1024]{1,0:T(8,128)S(1)} %convolution_multiply_fusion.5), channel_id=1, source_target_pairs={{0,1},{1,0},{2,3},{3,2},{4,5},{5,4},{6,7},{7,6},{8,9},{9,8},{10,11... | collective-permute-start | bytes 6291464 | tf_op jit(solution)/shard_map/ppermute | solution.py:452
  923.2 96.6 %copy-start.51 = (bf16[128,512]{1,0:T(8,128)(2,1)}, bf16[128,512]{1,0:T(8,128)(2,1)S(1)}, u32[]{:S(2)}) copy-start(bf16[128,512]{1,0:T(8,128)(2,1)S(1)} %get-tuple-element.182) | copy-start | bytes 393220
  923.3 96.6 %copy-start.53 = (bf16[128,512]{1,0:T(8,128)(2,1)}, bf16[128,512]{1,0:T(8,128)(2,1)S(1)}, u32[]{:S(2)}) copy-start(bf16[128,512]{1,0:T(8,128)(2,1)S(1)} %get-tuple-element.183) | copy-start | bytes 393220
  923.3 96.6 %copy-start.55 = (bf16[128,512]{1,0:T(8,128)(2,1)}, bf16[128,512]{1,0:T(8,128)(2,1)S(1)}, u32[]{:S(2)}) copy-start(bf16[128,512]{1,0:T(8,128)(2,1)S(1)} %get-tuple-element.184) | copy-start | bytes 393220
  946.2 6.0 collective-permute-start.29
  950.2 48.5 %collective-permute-start.27 = (f32[512,1024]{1,0:T(8,128)S(1)}, f32[512,1024]{1,0:T(8,128)S(1)}, u32[]{:S(2)}, u32[]{:S(2)}) collective-permute-start(f32[512,1024]{1,0:T(8,128)S(1)} %multiply_add_fusion.1), channel_id=1, source_target_pairs={{0,2},{1,3},{2,0},{3,1},{4,6},{5,7},{6,4},{7,5},{8,10},{9,11},{10,... | collective-permute-start | bytes 6291464 | tf_op jit(solution)/shard_map/ppermute | solution.py:452
  952.1 47.5 %collective-permute-start.28 = (f32[512,512]{1,0:T(8,128)S(1)}, f32[512,512]{1,0:T(8,128)S(1)}, u32[]{:S(2)}, u32[]{:S(2)}) collective-permute-start(f32[512,512]{1,0:T(8,128)S(1)} %convolution_multiply_fusion.11), channel_id=1, source_target_pairs={{0,1},{1,0},{2,3},{3,2},{4,5},{5,4},{6,7},{7,6},{8,9},{9,8},{10,11... | collective-permute-start | bytes 3145736 | tf_op jit(solution)/shard_map/ppermute | solution.py:452
  952.9 66.9 %collective-permute-start.30 = (f32[512,512]{1,0:T(8,128)S(1)}, f32[512,512]{1,0:T(8,128)S(1)}, u32[]{:S(2)}, u32[]{:S(2)}) collective-permute-start(f32[512,512]{1,0:T(8,128)S(1)} %fusion.43), channel_id=1, source_target_pairs={{0,2},{1,3},{2,0},{3,1},{4,6},{5,7},{6,4},{7,5},{8,10},{9,11},{10,... | collective-permute-start | bytes 3145736 | tf_op jit(solution)/shard_map/ppermute | solution.py:452
  1022.7 228.7 %reduce-scatter.7.cloned.1.call-start = ((), (), s32[]{:S(2)}) async-start(), calls=%async_computation.7 | async-start | bytes 7864320 | tf_op jit(solution)/shard_map/reduce_scatter | solution.py:455
  1023.0 9.9 collective-permute-start.22
  1023.0 93.7 %collective-permute-start.23 = (f32[512,2048]{1,0:T(8,128)}, f32[512,2048]{1,0:T(8,128)S(1)}, u32[]{:S(2)}, u32[]{:S(2)}) collective-permute-start(f32[512,2048]{1,0:T(8,128)} %multiply_add_fusion), channel_id=1, source_target_pairs={{0,2},{1,3},{2,0},{3,1},{4,6},{5,7},{6,4},{7,5},{8,10},{9,11},{10,... | collective-permute-start | bytes 12582920 | tf_op jit(solution)/shard_map/ppermute | solution.py:452
  1024.1 94.3 %collective-permute-start.24 = (f32[512,1024]{1,0:T(8,128)}, f32[512,1024]{1,0:T(8,128)S(1)}, u32[]{:S(2)}, u32[]{:S(2)}) collective-permute-start(f32[512,1024]{1,0:T(8,128)} %convolution_multiply_fusion.7), channel_id=1, source_target_pairs={{0,1},{1,0},{2,3},{3,2},{4,5},{5,4},{6,7},{7,6},{8,9},{9,8},{10,11... | collective-permute-start | bytes 6291464 | tf_op jit(solution)/shard_map/ppermute | solution.py:452
  1024.3 136.9 %collective-permute-start.25 = (f32[512,1024]{1,0:T(8,128)}, f32[512,1024]{1,0:T(8,128)}, u32[]{:S(2)}, u32[]{:S(2)}) collective-permute-start(f32[512,1024]{1,0:T(8,128)} %multiply_add_fusion.2), channel_id=1, source_target_pairs={{0,2},{1,3},{2,0},{3,1},{4,6},{5,7},{6,4},{7,5},{8,10},{9,11},{10,... | collective-permute-start | bytes 6291464 | tf_op jit(solution)/shard_map/ppermute | solution.py:452
  1175.4 14.9 %collective-permute-start.31 = (f32[128,1280]{1,0:T(8,128)}, f32[128,1280]{1,0:T(8,128)}, u32[]{:S(2)}, u32[]{:S(2)}) collective-permute-start(f32[128,1280]{1,0:T(8,128)} %get-tuple-element.178), channel_id=1, source_target_pairs={{0,1},{1,0},{2,3},{3,2},{4,5},{5,4},{6,7},{7,6},{8,9},{9,8},{10,11... | collective-permute-start | bytes 1966088 | tf_op jit(solution)/shard_map/ppermute | solution.py:452
  1175.4 33.1 %collective-permute-start.32 = (f32[128,1280]{1,0:T(8,128)}, f32[128,1280]{1,0:T(8,128)}, u32[]{:S(2)}, u32[]{:S(2)}) collective-permute-start(f32[128,1280]{1,0:T(8,128)} %get-tuple-element.177), channel_id=1, source_target_pairs={{0,2},{1,3},{2,0},{3,1},{4,6},{5,7},{6,4},{7,5},{8,10},{9,11},{10,... | collective-permute-start | bytes 1966088 | tf_op jit(solution)/shard_map/ppermute | solution.py:452
  1176.7 31.8 %collective-permute-start.33 = (f32[128,1280]{1,0:T(8,128)}, f32[128,1280]{1,0:T(8,128)}, u32[]{:S(2)}, u32[]{:S(2)}) collective-permute-start(f32[128,1280]{1,0:T(8,128)} %get-tuple-element.176), channel_id=1, source_target_pairs={{0,3},{1,2},{2,1},{3,0},{4,7},{5,6},{6,5},{7,4},{8,11},{9,10},{10,... | collective-permute-start | bytes 1966088 | tf_op jit(solution)/shard_map/ppermute | solution.py:452
  1186.5 32.2 %collective-permute-start.34 = (f32[128,1472]{0,1:T(8,128)}, f32[128,1472]{0,1:T(8,128)S(1)}, u32[]{:S(2)}, u32[]{:S(2)}) collective-permute-start(f32[128,1472]{0,1:T(8,128)} %copy.39), channel_id=1, source_target_pairs={{0,1},{1,0},{2,3},{3,2},{4,5},{5,4},{6,7},{7,6},{8,9},{9,8},{10,11... | collective-permute-start | bytes 2261000 | tf_op jit(solution)/shard_map/ppermute | solution.py:452
  1187.8 35.7 %collective-permute-start.35 = (f32[128,1472]{0,1:T(8,128)}, f32[128,1472]{0,1:T(8,128)}, u32[]{:S(2)}, u32[]{:S(2)}) collective-permute-start(f32[128,1472]{0,1:T(8,128)} %copy.41), channel_id=1, source_target_pairs={{0,2},{1,3},{2,0},{3,1},{4,6},{5,7},{6,4},{7,5},{8,10},{9,11},{10,... | collective-permute-start | bytes 2261000 | tf_op jit(solution)/shard_map/ppermute | solution.py:452
  1190.3 48.5 %collective-permute-start.36 = (f32[128,1472]{0,1:T(8,128)}, f32[128,1472]{0,1:T(8,128)}, u32[]{:S(2)}, u32[]{:S(2)}) collective-permute-start(f32[128,1472]{0,1:T(8,128)} %copy.43), channel_id=1, source_target_pairs={{0,3},{1,2},{2,1},{3,0},{4,7},{5,6},{6,5},{7,4},{8,11},{9,10},{10,... | collective-permute-start | bytes 2261000 | tf_op jit(solution)/shard_map/ppermute | solution.py:452
  (63 other events, 963.2 us)
Sparse Core Ops, SparseCore 0:
  14.9 35.3 all-gather.1
  362.6 99.9 reduce-scatter.10
  468.0 116.6 reduce-scatter.12
  587.6 99.7 reduce-scatter.14
  690.4 112.5 reduce-scatter.16
  1022.8 39.9 reduce-scatter.8
  1167.4 66.0 reduce-scatter.6

commit v4 on v3

--- a/solution.py
+++ b/solution.py
@@ -126,7 +126,6 @@
         compiler_params=pltpu.CompilerParams(vmem_limit_bytes=56 * 2 ** 20),
         cost_estimate=pl.CostEstimate(flops=4 * width * half * half * n_pairs,
                                       bytes_accessed=12 * width * seq, transcendentals=width // head_dim * half * half * n_pairs),
-        name='attn_fwd',
     )(tab, q_t, kv_all, kv_all)
 
 
@@ -205,7 +204,6 @@
         compiler_params=pltpu.CompilerParams(vmem_limit_bytes=56 * 2 ** 20),
         cost_estimate=pl.CostEstimate(flops=10 * rows * half * half * n_pairs,
                                       bytes_accessed=12 * rows * seq, transcendentals=group * half * half * n_pairs),
-        name='attn_bwd',
     )(tab, q_t, do_t, o_f32, lse, kv_all, kv_all)
 
 
@@ -219,7 +217,7 @@
 
 
 def prep_kernel(segs, parts, idx_ref, *refs):
-    n_blocks = sum(seg['tiles'] + 1 for seg in segs)
+    n_blocks = sum(seg[3] + 1 for seg in segs)
     blocks, down_ref = refs[:n_blocks], refs[n_blocks]
     n_parts = len(parts)
     up_refs, down_refs = refs[n_blocks + 1:n_blocks + 1 + n_parts], refs[n_blocks + 1 + n_parts:n_blocks + 1 + 2 * n_parts]
@@ -231,11 +229,11 @@
     outs = []
     for part, down_out in zip(parts, down_refs):
         for own in range(n_own):
-            outs.append(pltpu.make_async_copy(buf_ref.at[own, pl.ds(part['first'], part['rows'])],
-                                              down_out.at[pl.ds(own * part['rows'], part['rows'])], out_sem.at[len(outs)]))
-        if part['pad']:
-            outs.append(pltpu.make_async_copy(zero_ref.at[pl.ds(0, part['pad'])],
-                                              down_out.at[pl.ds(n_own * part['rows'], part['pad'])], out_sem.at[len(outs)]))
+            outs.append(pltpu.make_async_copy(buf_ref.at[own, pl.ds(part[0], part[1])],
+                                              down_out.at[pl.ds(own * part[1], part[1])], out_sem.at[len(outs)]))
+        if part[2]:
+            outs.append(pltpu.make_async_copy(zero_ref.at[pl.ds(0, part[2])],
+                                              down_out.at[pl.ds(n_own * part[1], part[2])], out_sem.at[len(outs)]))
 
     @pl.when(step == 0)
     def _():
@@ -256,13 +254,13 @@
     pos = 0
     for number, seg in enumerate(segs):
         shift = idx_ref[1, number]
-        turned = [pltpu.roll(blocks[pos + tile][...].astype(F32), (128 - shift) % 128, 1) for tile in range(seg['tiles'] + 1)]
-        pos += seg['tiles'] + 1
-        for tile in range(seg['tiles']):
-            cover[seg['part']].setdefault(seg['tile'] + tile, []).append(
-                (seg['start'], jnp.where(lanes < 128 - shift, turned[tile], turned[tile + 1])))
+        turned = [pltpu.roll(blocks[pos + tile][...].astype(F32), (128 - shift) % 128, 1) for tile in range(seg[3] + 1)]
+        pos += seg[3] + 1
+        for tile in range(seg[3]):
+            cover[seg[0]].setdefault(seg[2] + tile, []).append(
+                (seg[1], jnp.where(lanes < 128 - shift, turned[tile], turned[tile + 1])))
     for part, tiles, up_ref in zip(parts, cover, up_refs):
-        used = n_own * part['rows']
+        used = n_own * part[1]
         for tile in range(up_ref.shape[1] // 128):
             value = jnp.zeros((rows, 128), F32)
             for start, piece in tiles.get(tile, []):
@@ -280,13 +278,13 @@
 def prepare(starts, splits, w_up, w_down):
     d_model, own_rows = w_up.shape[0], splits[-1][0] + splits[-1][1]
     n_own = starts.shape[0]
-    parts = [{'first': first, 'rows': count, 'pad': -(n_own * count) % FF_TILE} for first, count in splits]
+    parts = [(first, count, -(n_own * count) % FF_TILE) for first, count in splits]
     segs, shifts, bases = [], [], []
     for number, part in enumerate(parts):
         for own in range(n_own):
-            dest = own * part['rows']
-            segs.append({'part': number, 'start': dest, 'tile': dest // 128, 'tiles': -(-(dest % 128 + part['rows']) // 128)})
-            source = starts[own] + part['first'] - dest % 128
+            dest = own * part[1]
+            segs.append((number, dest, dest // 128, -(-(dest % 128 + part[1]) // 128)))
+            source = starts[own] + part[0] - dest % 128
             shifts.append(source % 128)
             bases.append(source // 128)
     table = jnp.stack([jnp.pad(starts, (0, len(segs) - n_own)), jnp.stack(shifts), jnp.stack(bases)]).astype(jnp.int32)
@@ -294,10 +292,10 @@
     last = w_up.shape[1] // 128 - 1
     in_specs = []
     for number, seg in enumerate(segs):
-        for tile in range(seg['tiles'] + 1):
+        for tile in range(seg[3] + 1):
             in_specs.append(pl.BlockSpec((rows, 128), lambda i, t, number=number, tile=tile:
                                          (i, jnp.clip(t[2, number] + tile, 0, last))))
-    widths = [n_own * part['rows'] + part['pad'] for part in parts]
+    widths = [n_own * part[1] + part[2] for part in parts]
     outs = pl.pallas_call(
         functools.partial(prep_kernel, segs, parts),
         grid_spec=pltpu.PrefetchScalarGridSpec(
@@ -312,78 +310,112 @@
         + [jax.ShapeDtypeStruct((width, d_model), BF16) for width in widths],
         compiler_params=pltpu.CompilerParams(vmem_limit_bytes=56 * 2 ** 20),
         cost_estimate=pl.CostEstimate(flops=8 * d_model * sum(widths), bytes_accessed=9 * d_model * sum(widths), transcendentals=0),
-        name='prepare',
     )(table, *([w_up] * len(in_specs)), w_down)
     return outs[:len(parts)], outs[len(parts):]
 
 
-def ff_kernel(step_rows, copies, first_row, n_pieces, *refs):
-    pieces = [(refs[2 * piece], refs[2 * piece + 1]) for piece in range(n_pieces)]
-    up_ref, down_ref = refs[2 * n_pieces:2 * n_pieces + 2]
+def ff_kernel(chunk, copies, first_row, cot_rows, tiles, *refs):
+    n_pieces = len(cot_rows)
+    weights = refs[2 * n_pieces:2 * n_pieces + 2 * len(tiles)]
+    h_buf, cot_buf, in_sem, out_sem = refs[-4:]
+    n_copied = 2 if copies else 0
+    outs = refs[-4 - n_copied - 2 * len(tiles):-4]
+    step = pl.program_id(0)
+    loads = []
+    for piece, cot_row in enumerate(cot_rows):
+        for first in range(0, refs[2 * piece].shape[0], chunk):
+            number = len(loads)
+            rows = pl.ds(number * chunk, chunk)
+            loads.append((pltpu.make_async_copy(refs[2 * piece].at[pl.ds(first, chunk)], h_buf.at[rows], in_sem.at[2 * number]),
+                          pltpu.make_async_copy(refs[2 * piece + 1].at[pl.ds(cot_row + first, chunk)], cot_buf.at[rows],
+                                                in_sem.at[2 * number + 1])))
+    moves = []
     if copies:
-        act_ref, du_ref, h_out, cot_out, sem = refs[-5:]
-        moves, row = [], first_row
-        for h_ref, cot_ref in pieces:
-            rows = pl.ds(row, h_ref.shape[0])
-            moves.append(pltpu.make_async_copy(h_ref, h_out.at[rows], sem.at[len(moves)]))
-            moves.append(pltpu.make_async_copy(cot_ref, cot_out.at[rows], sem.at[len(moves)]))
-            row += h_ref.shape[0]
-
-        @pl.when(pl.program_id(0) == 0)
+        rows = pl.ds(first_row, h_buf.shape[0])
+        moves = [pltpu.make_async_copy(h_buf, outs[-2].at[rows], out_sem.at[0]),
+                 pltpu.make_async_copy(cot_buf, outs[-1].at[rows], out_sem.at[1])]
+
+    @pl.when(step == 0)
+    def _():
+        for pair in loads:
+            for load in pair:
+                load.start()
+
+    first_tile = 0
+    for part, count in enumerate(tiles):
+        up_ref, down_ref = weights[2 * part:2 * part + 2]
+        act_ref, du_ref = outs[2 * part:2 * part + 2]
+
+        @pl.when((step >= first_tile) & (step < first_tile + count))
+        def _(up_ref=up_ref, down_ref=down_ref, act_ref=act_ref, du_ref=du_ref, part=part):
+            for number, pair in enumerate(loads):
+                if part == 0:
+                    @pl.when(step == 0)
+                    def _(pair=pair):
+                        for load in pair:
+                            load.wait()
+
+                rows = slice(number * chunk, (number + 1) * chunk)
+                hidden = dot_nn(h_buf[rows, :], up_ref[...])
+                grad_act = dot_nt(cot_buf[rows, :], down_ref[...]).astype(BF16).astype(F32)
+                act, slope = gelu_parts(hidden)
+                act_ref[rows, :] = act.astype(BF16)
+                du_ref[rows, :] = (grad_act * slope).astype(BF16)
+
+        first_tile += count
+
+    if copies:
+        @pl.when(step == 1)
         def _():
             for move in moves:
                 move.start()
-    else:
-        act_ref, du_ref = refs[-2:]
-
-    base = 0
-    for h_ref, cot_ref in pieces:
-        for first in range(0, h_ref.shape[0], step_rows):
-            rows = slice(first, first + step_rows)
-            out_rows = slice(base + first, base + first + step_rows)
-            hidden = dot_nn(h_ref[rows, :], up_ref[...])
-            grad_act = dot_nt(cot_ref[rows, :], down_ref[...]).astype(BF16).astype(F32)
-            act, slope = gelu_parts(hidden)
-            act_ref[out_rows, :] = act.astype(BF16)
-            du_ref[out_rows, :] = (grad_act * slope).astype(BF16)
-        base += h_ref.shape[0]
-
-    if copies:
-        @pl.when(pl.program_id(0) == pl.num_programs(0) - 1)
+
+        @pl.when(step == pl.num_programs(0) - 1)
         def _():
             for move in moves:
                 move.wait()
 
 
-def ff_forward(index, count, pieces, up, down, copies, carry):
+def ff_forward(index, count, pieces, ups, downs, copies, carry):
     tokens = sum(piece[0].shape[0] for piece in pieces)
-    d_model, width = up.shape
+    d_model = ups[0].shape[0]
     tile = FF_TILE
-    shapes = [jax.ShapeDtypeStruct((count * tokens, width), BF16)] * 2
-    specs = [pl.BlockSpec((tokens, tile), lambda n: (index, n))] * 2
+    tiles = [up.shape[1] // tile for up in ups]
+    width = sum(up.shape[1] for up in ups)
+    chunk = 512
+    hbm = pl.BlockSpec(memory_space=pl.ANY)
+    shapes, specs, args, in_specs = [], [], [], []
+    for h_blk, cot_blk, _ in pieces:
+        args += [h_blk, cot_blk]
+        in_specs += [hbm, hbm]
+    first_tile = 0
+    for up, down, n_tiles in zip(ups, downs, tiles):
+        def place(n, first_tile=first_tile, n_tiles=n_tiles):
+            return jnp.clip(n - first_tile, 0, n_tiles - 1)
+
+        shapes += [jax.ShapeDtypeStruct((count * tokens, up.shape[1]), BF16)] * 2
+        specs += [pl.BlockSpec((tokens, tile), lambda n, place=place: (index, place(n)))] * 2
+        args += [up, down]
+        in_specs += [pl.BlockSpec((d_model, tile), lambda n, place=place: (0, place(n))),
+                     pl.BlockSpec((tile, d_model), lambda n, place=place: (place(n), 0))]
+        first_tile += n_tiles
     if copies:
-        shapes = shapes + [jax.ShapeDtypeStruct((count * tokens, d_model), BF16)] * 2
-        specs = specs + [pl.BlockSpec(memory_space=pl.ANY)] * 2
-    in_specs, args = [], []
-    for h_blk, cot_blk, row_blk in pieces:
-        in_specs += [pl.BlockSpec(h_blk.shape, lambda n: (0, 0)),
-                     pl.BlockSpec(h_blk.shape, lambda n, row_blk=row_blk: (row_blk, 0))]
-        args += [h_blk, cot_blk]
+        shapes += [jax.ShapeDtypeStruct((count * tokens, d_model), BF16)] * 2
+        specs += [hbm, hbm]
     carry = list(carry)
     return pl.pallas_call(
-        functools.partial(ff_kernel, 512, copies, index * tokens, len(pieces)),
-        grid=(width // tile,),
-        in_specs=in_specs + [pl.BlockSpec((d_model, tile), lambda n: (0, n)), pl.BlockSpec((tile, d_model), lambda n: (n, 0))]
-        + [pl.BlockSpec(memory_space=pl.ANY)] * len(carry),
+        functools.partial(ff_kernel, chunk, copies, index * tokens, [piece[2] for piece in pieces], tiles),
+        grid=(sum(tiles),),
+        in_specs=in_specs + [hbm] * len(carry),
         out_specs=specs,
         out_shape=shapes,
-        input_output_aliases={len(args) + 2 + pos: pos for pos in range(len(carry))},
-        scratch_shapes=[pltpu.SemaphoreType.DMA((2 * len(pieces),))] if copies else [],
+        input_output_aliases={len(args) + pos: pos for pos in range(len(carry))},
+        scratch_shapes=[pltpu.VMEM((tokens, d_model), BF16)] * 2
+        + [pltpu.SemaphoreType.DMA((2 * tokens // chunk,)), pltpu.SemaphoreType.DMA((2,))],
         compiler_params=pltpu.CompilerParams(vmem_limit_bytes=56 * 2 ** 20),
         cost_estimate=pl.CostEstimate(flops=4 * tokens * d_model * width, bytes_accessed=4 * d_model * (width + 2 * tokens),
                                       transcendentals=tokens * width),
-        name='ff_forward',
-    )(*args, up, down, *carry)
+    )(*args, *carry)
 
 
 def grad_h_kernel(n_parts, *refs):
@@ -416,7 +448,6 @@
         compiler_params=pltpu.CompilerParams(vmem_limit_bytes=48 * 2 ** 20),
         cost_estimate=pl.CostEstimate(flops=2 * tokens * d_model * width, bytes_accessed=2 * width * (d_model + tokens) + 4 * tokens * d_model,
                                       transcendentals=0),
-        name='grad_h',
     )(*args, *extras)
 
 
@@ -439,7 +470,6 @@
         out_specs=pl.BlockSpec(memory_space=pltpu.VMEM),
         out_shape=jax.ShapeDtypeStruct((rows, width), F32),
         cost_estimate=pl.CostEstimate(flops=rows * width, bytes_accessed=8 * rows * width, transcendentals=0),
-        name='spread',
     )(my_idx.reshape(1), *got)
 
 
@@ -497,57 +527,53 @@
         kv_all = after(kv_all, q_t, w_up_own[0])
         cot_far = swap(after(cot, kv_all), 2)
         o_f32, o_t, lse = attn_forward(tab, q_t, kv_all, kv_heads, head_dim)
-        o_t = after(o_t, cot_far)
 
         h_act = (x + dot_tt(o_t, w_o)).astype(BF16)
         h_far = [swap(h_act[:half], 2), swap(h_act[half:], 2)]
         h_near = swap(h_act, 1)
         cot_last = swap(cot_far, 1)
 
-        def ff_call(index, part, pieces, carry, *earlier):
+        def ff_call(index, parts, pieces, carry, *earlier):
             first = after(pieces[0][0], *earlier) if earlier else pieces[0][0]
             pieces = [(first,) + pieces[0][1:]] + pieces[1:]
-            return ff_forward(index, cp_size, pieces, w_up_own[part], w_down_own[part], part == 0, carry)
-
-        own, near = [(h_act, cot, 0)], [(h_near, cot_near, 0)]
-        state = ff_call(0, 0, own, ())
-        state = ff_call(1, 0, near, state)
-        more = ff_call(0, 1, own, (), state[0])
+            return ff_forward(index, cp_size, pieces, [w_up_own[part] for part in parts], [w_down_own[part] for part in parts],
+                              0 in parts, carry)
 
         def remote(piece, *earlier):
             far_piece = after(h_far[piece], *earlier)
-            return [(far_piece, cot_far, piece), (swap(far_piece, 1), cot_last, piece)]
-
-        remote0 = remote(0, more[0])
-        state = ff_call(2, 0, remote0, state)
-        more = ff_call(2, 1, remote0, more, state[0])
-        remote1 = remote(1, more[0])
-
-        def grad_h(index, tokens, grads, earlier, extras, dtype):
-            later = after(grads[1], earlier)
-            return grad_h_block(index, tokens, (grads[0], later), w_up_own, extras, dtype)
-
-        gh_last0 = grad_h(5, half, (state[1], more[1]), more[0], [], F32)
-        near0 = swap(gh_last0, 1)
-        act0, grad_u0, h_all, cot_all = ff_call(3, 0, remote1, state, gh_last0)
-        part = grad_h(4, half, (grad_u0, more[1]), act0, [near0], F32)
+            return [(far_piece, cot_far, piece * half), (swap(far_piece, 1), cot_last, piece * half)]
+
+        act0, grad_u0, act1, grad_u1, h_all, cot_all = ff_call(0, (0, 1), [(h_act, cot, 0)], ())
+        near = [(h_near, cot_near, 0)]
+        act0, grad_u0, h_all, cot_all = ff_call(1, (0,), near, (act0, grad_u0, h_all, cot_all), act1)
+        block = remote(0, act0)
+        act0, grad_u0, act1, grad_u1, h_all, cot_all = ff_call(2, (0, 1), block, (act0, grad_u0, act1, grad_u1, h_all, cot_all))
+        block = remote(1, act1)
+        act0, grad_u0, h_all, cot_all = ff_call(3, (0,), block, (act0, grad_u0, h_all, cot_all))
+        part = row_major(inv_count * dot_tn(h_all, grad_u0))
+        up_rows = [dp_reduce(part)]
+
+        def grad_h(index, tokens, earlier, extras, dtype):
+            later = after(grad_u1, earlier)
+            return grad_h_block(index, tokens, (grad_u0, later), w_up_own, extras, dtype)
+
+        part = grad_h(5, half, part, [], F32)
+        near0 = swap(part, 1)
+        act1, grad_u1 = ff_call(3, (1,), block, (act1, grad_u1), part)
+        part = grad_h(4, half, act1, [near0], F32)
         far0 = swap(part, 2)
-        later = after(grad_u0, part)
-        part = row_major(inv_count * dot_tn(h_all, later))
-        up_rows = [dp_reduce(part)]
-        more = ff_call(3, 1, remote1, more, part)
-        gh_last1 = grad_h(7, half, (grad_u0, more[1]), more[0], [], F32)
-        near1 = swap(gh_last1, 1)
-        act1, grad_u1 = ff_call(1, 1, near, more, gh_last1)
-        part = grad_h(6, half, (grad_u0, grad_u1), act1, [near1], F32)
-        far1 = swap(part, 2)
-        later = after(grad_u1, part)
+        part = grad_h(7, half, part, [], F32)
+        near1 = swap(part, 1)
+        act1, grad_u1 = ff_call(1, (1,), near, (act1, grad_u1), part)
+        later = after(grad_u1, act1)
         part = row_major(inv_count * dot_tn(h_all, later[:, :used[1]]))
         up_rows.append(dp_reduce(part))
+        part = grad_h(6, half, part, [near1], F32)
+        far1 = swap(part, 2)
         later = after(act0, part)
         part = row_major(inv_count * dot_tn(later, cot_all))
         down_rows = [dp_reduce(part)]
-        part = grad_h(1, seq_len, (grad_u0, grad_u1), part, [], F32)
+        part = grad_h(1, seq_len, part, [], F32)
         side = swap(part, 1)
         later = after(act1, part)
         part = row_major(inv_count * dot_tn(later[:, :used[1]], cot_all))
@@ -560,7 +586,7 @@
             blocks = [lax.dynamic_slice_in_dim(rows_of, (my_idx ^ bits) * own_rows, own_rows, axis=0) for bits in range(cp_size)]
             up_got.append(jnp.stack([blocks[0]] + [row_major(swap(row_major(blocks[bits]), bits))
                                                    for bits in range(1, cp_size)]))
-        grad_h_bf = grad_h(0, seq_len, (grad_u0, grad_u1), part, [cot, side, far0, far1], BF16)
+        grad_h_bf = grad_h(0, seq_len, part, [cot, side, far0, far1], BF16)
         grad_w_up = spread_columns(my_idx, up_got, splits)
 
         def block_sum(left, right_t):
@@ -591,30 +617,32 @@
 
         dq0_t, dkv0 = attn_backward(tab, q_t, do_t, o_f32, lse, kv_all, kv_heads, head_dim, 0)
         kv0_block, q0_block = kv_block(dkv0), block_sum(x, dq0_t)
-        kv0_sent, _ = first_sends(kv0_block)
+        kv0_sent, parts_kv = first_sends(kv0_block)
         q0_sent, parts_q = first_sends(q0_block)
         kv0_far, part_kv = second_send(kv0_block, (after(kv0_sent[0], *parts_q), kv0_sent[1]))
         q0_far, part_q = second_send(q0_block, q0_sent)
         do_t = after(do_t, part_kv, part_q)
         dq1_t, dkv1 = attn_backward(tab, q_t, do_t, o_f32, lse, kv_all, kv_heads, head_dim, 1)
         kv1_block, q1_block = kv_block(dkv1), block_sum(x, dq1_t)
-        kv1_sent, _ = first_sends(kv1_block)
+        kv1_sent, parts_kv = first_sends(kv1_block)
         q1_sent, parts_q = first_sends(q1_block)
-        sum_o = after(o_block(0), *parts_q) + o_sent[1] + o_far
-        kv1_far, part_kv = second_send(kv1_block, kv1_sent)
-        q1_far, part_q = second_send(q1_block, q1_sent)
-        grad_oq = dp_reduce(jnp.concatenate([sum_o, q0_block(0) + q0_sent[1] + q0_far], axis=1))
-        later = after(jnp.concatenate([dq0_t, dq1_t], axis=0), part_q, part_kv)
+        kv1_far, part_kv = second_send(kv1_block, (after(kv1_sent[0], *parts_q), kv1_sent[1]))
+        q1_far, part_q = second_send(q1_block, (after(q1_sent[0], part_kv), q1_sent[1]))
+        o_far = after(o_far, part_q)
+        base_o, base_q = o_block(0), q0_block(0)
+        sum_o = base_o + o_sent[1] + o_far
+        grad_oq = dp_reduce(jnp.concatenate([sum_o, base_q + q0_sent[1] + q0_far], axis=1))
+        kv0_own = (kv0_block(0) + kv0_sent[1] + after(kv0_far, part_q)).astype(BF16)
+        kv1_own = (kv1_block(0) + kv1_sent[1] + after(kv1_far, kv0_own)).astype(BF16)
+        dkv_t = jnp.concatenate([jnp.concatenate([part[0, which], part[1, which]], axis=1)
+                                 for which in range(2) for part in (kv0_own, kv1_own)], axis=0)
+        w_block = block_sum(x, dkv_t)
+        w_sent, parts = first_sends(w_block)
+        w_far, part_w = second_send(w_block, w_sent)
+        later = after(jnp.concatenate([dq0_t, dq1_t], axis=0), part_w)
         grad_x = dot_tt(later, w_q)
-        grad_x = grad_h_bf + grad_x
-        dkv_parts = [(kv0_block(0) + kv0_sent[1] + kv0_far).astype(BF16), (kv1_block(0) + kv1_sent[1] + kv1_far).astype(BF16)]
-        dkv_t = jnp.concatenate([jnp.concatenate([part[0, which], part[1, which]], axis=1)
-                                 for which in range(2) for part in dkv_parts], axis=0)
-        w_block = block_sum(x, dkv_t)
-        w_sent, _ = first_sends(w_block)
-        w_far, _ = second_send(w_block, w_sent)
+        grad_x = grad_h_bf + grad_x + dot_tt(after(dkv_t, part_w), w_kv)
         sum_q1 = q1_block(0) + q1_sent[1] + q1_far
-        grad_x = grad_x + dot_tt(dkv_t, w_kv)
         grad_qk = dp_reduce(jnp.concatenate([sum_q1, w_block(0) + w_sent[1] + w_far], axis=1))
         o_width = n_heads * head_dim
         grad_w_down = jnp.concatenate(down_rows, axis=0)

time: 1270 us -> 1370 us (1.079)
  waiting for transfers between devices: 413 us -> 507 us
    ppermute x37, waiting for transfers between devices: 413 us -> 507 us  [swap(): lax.ppermute(values, 'cp', [(src, src ^ bits) for src in range(cp_size)])]
    pallas_call x8 -> x6, Pallas kernels: 165 us -> 166 us  [ff_forward(): pl.pallas_call(functools.partial(ff_kernel, chunk, copies, index * tokens...]
  transfers between devices with their start and end apart: 44 -> 44, of which waited for: 13 -> 16; matrix products, arithmetic and copies ran while one was open for 22% -> 20% of each run, Pallas kernels for 37% -> 28%
where the time goes in v4:
time: 1370 us; the launch traced here: 1360 us
  waiting for transfers between devices  507 us (37%)
  Pallas kernels  481 us (35%)
  matrix products  240 us (18%)
  local copies, waits for them, and re-layouts  47 us (3%)
  other arithmetic  33.4 us (2%)
  between operations  25 us (2%)
  starting transfers between devices  24 us (2%)
    ppermute x37, waiting for transfers between devices, swap(): lax.ppermute(values, 'cp', [(src, src ^ bits) for src in range(cp_size)])  507 us
    pallas_call x6, Pallas kernels, ff_forward(): pl.pallas_call(functools.partial(ff_kernel, chunk, copies, index * tokens...  166 us
    dot_general x4, matrix products, dot_tn(): lax.dot_general(lhs, rhs, (((0,), (0,)), ((), ())), preferred_element_typ...  129 us
    pallas_call x2, Pallas kernels, attn_backward(): pl.pallas_call(functools.partial(attn_bwd_kernel, group, head_dim ** (-0....  116 us
    dot_general x21, matrix products, dot_tt(): lax.dot_general(lhs, rhs, (((0,), (1,)), ((), ())), preferred_element_typ...  108 us
    pallas_call x6, Pallas kernels, grad_h_block(): pl.pallas_call(functools.partial(grad_h_kernel, len(up)), grid=(d_model /...  90.3 us
    pallas_call x1, Pallas kernels, attn_forward(): pl.pallas_call(functools.partial(attn_fwd_kernel, group, head_dim ** (-0....  81.5 us
  transfers between devices with their start and end apart: 44, of which 16 were waited for; matrix products, arithmetic and copies ran while one was open for 20% of the time, Pallas kernels for 28%

profile of v4, /device:TPU:0, one launch (start us, length us, event | category | flops | bytes accessed | tf_op | source)
XLA Modules:
  0.0 1357.6 jit_solution(15449817063463131991)
XLA Ops:
  25.6 21.3 %shard_map.135 = (bf16[2048,1280]{1,0:T(8,128)(2,1)}, bf16[2048,1536]{1,0:T(8,128)(2,1)}, bf16[1280,2048]{1,0:T(8,128)(2,1)}, bf16[1536,2048]{1,0:T(8,128)(2,1)}) custom-call(s32[3,8]{1,0:T(4,128)} %pad_add_fusion.1.idx_ref, bf16[2048,11008]{1,0:T(8,128)(2,1)} %refs_34_.1, bf16[2048,11008]{1,0:T(8,128)(2,1)} %refs_34_.1, bf16[2048,11008]{1,0:T(8,128)(2,1)} %refs_34_.1, ...), custom_call_target="tpu_custom_call" | custom-call | flops 46137344 | bytes 51904512 | tf_op jit(solution)/shard_map/pallas_call | solution.py:299
  47.6 12.6 fusion.26.q_ref
  60.2 81.5 %shard_map.136 = (f32[2048,1024]{1,0:T(8,128)}, bf16[2048,1024]{1,0:T(8,128)(2,1)}, f32[2,8,1024]{2,1,0:T(8,128)}) custom-call(s32[4,9]{1,0:T(4,128)} %pad_add_fusion.tab, bf16[2048,1024]{1,0:T(8,128)(2,1)} %fusion.26.q_ref, bf16[4096,512]{1,0:T(8,128)(2,1)} %all-gather.2.cloned.1.call-done.k_ref.v_ref, ...), custom_call_target="tpu_custom_call" | custom-call | flops 19327352832 | bytes 25165824 | tf_op jit(solution)/shard_map/pallas_call | solution.py:113
  144.9 14.7 %add_convert_fusion.1.refs_0_ = bf16[1024,2048]{1,0:T(8,128)(2,1)} fusion(bf16[1,1024,2048]{2,1,0:T(8,128)(2,1)} %param.8, bf16[2048,1024]{1,0:T(8,128)(2,1)} %get-tuple-element.73, bf16[256,8,16,128]{3,2,1,0:T(8,128)(2,1)} %bitcast.208), kind=kOutput, calls=%fused_computation.17 | convolution fusion | flops 8596226048 | bytes 20971520 | tf_op jit(solution)/shard_map/dot_general | solution.py:37
  160.0 4.2 fusion.85
  164.3 72.2 %collective-permute-done.4.refs_1_ = bf16[1024,2048]{1,0:T(8,128)(2,1)S(1)} collective-permute-done((bf16[1024,2048]{1,0:T(8,128)(2,1)}, bf16[1024,2048]{1,0:T(8,128)(2,1)S(1)}, u32[]{:S(2)}, u32[]{:S(2)}) %collective-permute-start.4) | collective-permute-done | bytes 4194336 | tf_op jit(solution)/shard_map/ppermute | solution.py:482
  236.5 40.1 %shard_map.137 = (bf16[4096,1280]{1,0:T(8,128)(2,1)}, bf16[4096,1280]{1,0:T(8,128)(2,1)}, bf16[4096,1536]{1,0:T(8,128)(2,1)}, bf16[4096,1536]{1,0:T(8,128)(2,1)}...) custom-call(bf16[1024,2048]{1,0:T(8,128)(2,1)} %add_convert_fusion.1.refs_0_, ...), custom_call_target="tpu_custom_call" | custom-call | flops 23622320128 | bytes 39845888 | tf_op jit(solution)/shard_map/pallas_call | solution.py:406
  276.6 20.7 %shard_map.138 = (bf16[4096,1280]{1,0:T(8,128)(2,1)}, bf16[4096,1280]{1,0:T(8,128)(2,1)}, bf16[4096,2048]{1,0:T(8,128)(2,1)}, bf16[4096,2048]{1,0:T(8,128)(2,1)}) custom-call(bf16[1024,2048]{1,0:T(8,128)(2,1)} %collective-permute-done.2.refs_0_, ...), custom_call_target="tpu_custom_call", output_to_operand_aliasing={{0}: (4, {}), {1}: (5, {}), {2}: (6, {}), {3}: (7, {})} | custom-call | flops 10737418240 | bytes 27262976 | tf_op jit(solution)/shard_map/pallas_call | solution.py:406
  303.0 39.0 %shard_map.139 = (bf16[4096,1280]{1,0:T(8,128)(2,1)}, bf16[4096,1280]{1,0:T(8,128)(2,1)}, bf16[4096,1536]{1,0:T(8,128)(2,1)}, bf16[4096,1536]{1,0:T(8,128)(2,1)}...) custom-call(bf16[512,2048]{1,0:T(8,128)(2,1)} %collective-permute-do, ...), custom_call_target="tpu_custom_call", output_to_operand_aliasing={{0}: (8, {}), {1}: (9, {}), {2}: (10, {}), {3}: (11, {}), {... | custom-call | flops 23622320128 | bytes 39845888 | tf_op jit(solution)/shard_map/pallas_call | solution.py:406
  342.0 3.9 collective-permute-done.refs_0_
  345.9 4.2 collective-permute-done.7.refs_2_
  351.4 20.5 %shard_map.140 = (bf16[4096,1280]{1,0:T(8,128)(2,1)}, bf16[4096,1280]{1,0:T(8,128)(2,1)}, bf16[4096,2048]{1,0:T(8,128)(2,1)}, bf16[4096,2048]{1,0:T(8,128)(2,1)}) custom-call(bf16[512,2048]{1,0:T(8,128)(2,1)} %copy-done.4, bf16[1024,2048]{1,0:T(8,128)(2,1)} %copy-done.3, ...), custom_call_target="tpu_custom_call", output_to_operand_aliasing={{0}: (6, {}), {1}: (7, {}), {2}: (8, {}), {3}: (9, {})} | custom-call | flops 10737418240 | bytes 27262976 | tf_op jit(solution)/shard_map/pallas_call | solution.py:406
  371.9 29.5 %convolution_multiply_fusion.1 = f32[2048,1280]{1,0:T(8,128)} fusion(bf16[4096,2048]{1,0:T(8,128)(2,1)} %get-tuple-element.98, bf16[4096,1280]{1,0:T(8,128)(2,1)} %get-tuple-element.96.refs_0_), kind=kOutput, calls=%fused_computation.6 | convolution fusion | flops 21477457920 | bytes 37748736 | tf_op jit(solution)/shard_map/dot_general | solution.py:33
  401.4 11.9 shard_map.141
  413.5 22.7 %shard_map.142 = (bf16[4096,1536]{1,0:T(8,128)(2,1)}, bf16[4096,1536]{1,0:T(8,128)(2,1)}) custom-call(bf16[512,2048]{1,0:T(8,128)(2,1)} %copy-done.4, bf16[1024,2048]{1,0:T(8,128)(2,1)} %copy-done.3, bf16[512,2048]{1,0:T(8,128)(2,1)} %copy-done.5, bf16[1024,2048]{1,0:T(8,128)(2,1)} %collective-permute-done.6.refs_3_, ...), custom_call_target="tpu_custom_call", output_to_operand_aliasing={{0}: (6, {}), {1}: (7, {})} | custom-call | flops 12884901888 | bytes 29360128 | tf_op jit(solution)/shard_map/pallas_call | solution.py:406
  436.2 13.8 %shard_map.143 = f32[512,2048]{1,0:T(8,128)} custom-call(bf16[4096,1280]{1,0:T(8,128)(2,1)} %get-tuple-element.96.refs_0_, bf16[2048,1280]{1,0:T(8,128)(2,1)} %get-tuple-element.71.refs_2_.refs_4_.refs_1_, bf16[4096,1536]{1,0:T(8,128)(2,1)} %get-tuple-element.104.refs_2_.refs_5_, bf16[2048,1536]{1,0:T(8,128)(2,1)} %get-tuple-element.75.refs_4_.refs_6_.refs_3_.refs_2_, ...), custom_call_target="tpu_custom_call" | custom-call | flops 5905580032 | bytes 18612224 | tf_op jit(solution)/shard_map/pallas_call | solution.py:442
  450.0 11.5 shard_map.144
  463.5 22.6 %shard_map.145 = (bf16[4096,1536]{1,0:T(8,128)(2,1)}, bf16[4096,1536]{1,0:T(8,128)(2,1)}) custom-call(bf16[1024,2048]{1,0:T(8,128)(2,1)} %collective-permute-done.2.refs_0_, bf16[1024,2048]{1,0:T(8,128)(2,1)} %collective-permute-done.3.refs_1_, ...), custom_call_target="tpu_custom_call", output_to_operand_aliasing={{0}: (4, {}), {1}: (5, {})} | custom-call | flops 12884901888 | bytes 29360128 | tf_op jit(solution)/shard_map/pallas_call | solution.py:406
  486.1 34.9 %fusion.7 = f32[2048,1472]{1,0:T(8,128)} fusion(bf16[4096,2048]{1,0:T(8,128)(2,1)} %get-tuple-element.98, bf16[4096,1536]{1,0:T(8,128)(2,1)} %get-tuple-element.115.refs_2_), kind=kOutput, calls=%fused_computation.7 | convolution fusion | flops 24699076608 | bytes 41418752 | tf_op jit(solution)/shard_map/dot_general | solution.py:33
  522.6 7.0 collective-permute-done.9.refs_4_
  531.5 14.3 %shard_map.146 = f32[512,2048]{1,0:T(8,128)} custom-call(bf16[4096,1280]{1,0:T(8,128)(2,1)} %get-tuple-element.96.refs_0_, bf16[2048,1280]{1,0:T(8,128)(2,1)} %get-tuple-element.71.refs_2_.refs_4_.refs_1_, bf16[4096,1536]{1,0:T(8,128)(2,1)} %get-tuple-element.115.refs_2_, bf16[2048,1536]{1,0:T(8,128)(2,1)} %get-tuple-element.75.refs_4_.refs_6_.refs_3_.refs_2_, ...), custom_call_target="tpu_custom_call" | custom-call | flops 5905580032 | bytes 18612224 | tf_op jit(solution)/shard_map/pallas_call | solution.py:442
  545.9 29.8 %convolution_multiply_fusion = f32[1280,2048]{1,0:T(8,128)} fusion(bf16[4096,1280]{1,0:T(8,128)(2,1)} %get-tuple-element.111, bf16[4096,2048]{1,0:T(8,128)(2,1)} %get-tuple-element.112), kind=kOutput, calls=%fused_computation.5 | convolution fusion | flops 21477457920 | bytes 37748736 | tf_op jit(solution)/shard_map/dot_general | solution.py:33
  578.3 17.7 %shard_map.147 = f32[1024,2048]{1,0:T(8,128)} custom-call(bf16[4096,1280]{1,0:T(8,128)(2,1)} %get-tuple-element.96.refs_0_, bf16[2048,1280]{1,0:T(8,128)(2,1)S(1)} %copy-done, bf16[4096,1536]{1,0:T(8,128)(2,1)} %get-tuple-element.115.refs_2_, bf16[2048,1536]{1,0:T(8,128)(2,1)} %get-tuple-element.75.refs_4_.refs_6_.refs_3_.refs_2_), custom_call_target="tpu_custom_call" | custom-call | flops 11811160064 | bytes 25690112 | tf_op jit(solution)/shard_map/pallas_call | solution.py:442
  598.2 34.5 %fusion.4 = f32[1472,2048]{1,0:T(8,128)} fusion(bf16[4096,2048]{1,0:T(8,128)(2,1)} %get-tuple-element.112, bf16[4096,1536]{1,0:T(8,128)(2,1)} %get-tuple-element.114), kind=kOutput, calls=%fused_computation.4 | convolution fusion | flops 24699076608 | bytes 41418752 | tf_op jit(solution)/shard_map/dot_general | solution.py:33
  633.4 56.5 %collective-permute-done.11.refs_6_ = f32[512,2048]{1,0:T(8,128)} collective-permute-done((f32[512,2048]{1,0:T(8,128)}, f32[512,2048]{1,0:T(8,128)}, u32[]{:S(2)}, u32[]{:S(2)}) %collective-permute-start.11) | collective-permute-done | bytes 4194336 | tf_op jit(solution)/shard_map/ppermute | solution.py:482
  690.0 89.3 %collective-permute-done.12.refs_7_ = f32[512,2048]{1,0:T(8,128)} collective-permute-done((f32[512,2048]{1,0:T(8,128)}, f32[512,2048]{1,0:T(8,128)}, u32[]{:S(2)}, u32[]{:S(2)}) %collective-permute-start.12) | collective-permute-done | bytes 4194336 | tf_op jit(solution)/shard_map/ppermute | solution.py:482
  779.2 21.1 %shard_map.148 = bf16[1024,2048]{1,0:T(8,128)(2,1)S(1)} custom-call(bf16[4096,1280]{1,0:T(8,128)(2,1)} %get-tuple-element.96.refs_0_, bf16[2048,1280]{1,0:T(8,128)(2,1)} %get-tuple-element.71.refs_2_.refs_4_.refs_1_, bf16[4096,1536]{1,0:T(8,128)(2,1)} %get-tuple-element.115.refs_2_, bf16[2048,1536]{1,0:T(8,128)(2,1)} %get-tuple-element.75.refs_4_.refs_6_.refs_3_.refs_2_, ...), custom_call_target="tpu_custom_call" | custom-call | flops 11811160064 | bytes 25690112 | tf_op jit(solution)/shard_map/pallas_call | solution.py:442
  804.4 4.4 convolution_multiply_fusion.3
  811.2 4.4 convolution_multiply_fusion.2
  817.9 13.1 convert_bitcast_fusion.do_ref
  834.2 58.0 %shard_map.149 = (bf16[1024,1024]{1,0:T(8,128)(2,1)}, f32[8,2,128,512]{3,2,1,0:T(8,128)}) custom-call(s32[4,9]{1,0:T(4,128)} %pad_add_fusion.tab, bf16[2048,1024]{1,0:T(8,128)(2,1)} %fusion.26.q_ref, bf16[2048,1024]{1,0:T(8,128)(2,1)} %convert_bitcast_fusion.do_ref, f32[2048,1024]{1,0:T(8,128)} %get-tuple-element.120.of_ref, ...), custom_call_target="tpu_custom_call" | custom-call | flops 24159191040 | bytes 12582912 | tf_op jit(solution)/shard_map/pallas_call | solution.py:190
  892.2 4.2 convolution_multiply_fusion.7
  906.5 4.2 multiply_add_fusion.2
  910.7 57.8 %shard_map.150 = (bf16[1024,1024]{1,0:T(8,128)(2,1)}, f32[8,2,128,512]{3,2,1,0:T(8,128)}) custom-call(s32[4,9]{1,0:T(4,128)} %pad_add_fusion.tab, bf16[2048,1024]{1,0:T(8,128)(2,1)} %fusion.26.q_ref, bf16[2048,1024]{1,0:T(8,128)(2,1)} %convert_bitcast_fusion.do_ref, f32[2048,1024]{1,0:T(8,128)} %get-tuple-element.120.of_ref, ...), custom_call_target="tpu_custom_call" | custom-call | flops 24159191040 | bytes 12582912 | tf_op jit(solution)/shard_map/pallas_call | solution.py:190
  968.6 4.4 convolution_multiply_fusion.5
  985.4 16.1 %collective-permute-done.17 = f32[2,2,128,512]{3,2,1,0:T(8,128)} collective-permute-done((f32[2,2,128,512]{3,2,1,0:T(8,128)}, f32[2,2,128,512]{3,2,1,0:T(8,128)}, u32[]{:S(2)}, u32[]{:S(2)}) %collective-permute-start.17) | collective-permute-done | bytes 1048608 | tf_op jit(solution)/shard_map/ppermute | solution.py:482
  1003.6 19.4 %collective-permute-done.21 = f32[2,2,128,512]{3,2,1,0:T(8,128)} collective-permute-done((f32[2,2,128,512]{3,2,1,0:T(8,128)}, f32[2,2,128,512]{3,2,1,0:T(8,128)}, u32[]{:S(2)}, u32[]{:S(2)}) %collective-permute-start.21) | collective-permute-done | bytes 1048608 | tf_op jit(solution)/shard_map/ppermute | solution.py:482
  1033.3 64.0 %collective-permute-done.30 = f32[512,512]{1,0:T(8,128)S(1)} collective-permute-done((f32[512,512]{1,0:T(8,128)S(1)}, f32[512,512]{1,0:T(8,128)S(1)}, u32[]{:S(2)}, u32[]{:S(2)}) %collective-permute-start.30) | collective-permute-done | bytes 1048608 | tf_op jit(solution)/shard_map/ppermute | solution.py:482
  1103.9 5.0 fusion.66
  1110.2 84.8 %collective-permute-done.24 = f32[512,2048]{1,0:T(8,128)S(1)} collective-permute-done((f32[512,2048]{1,0:T(8,128)}, f32[512,2048]{1,0:T(8,128)S(1)}, u32[]{:S(2)}, u32[]{:S(2)}) %collective-permute-start.24) | collective-permute-done | bytes 4194336 | tf_op jit(solution)/shard_map/ppermute | solution.py:482
  1195.0 43.6 %collective-permute-done.26 = f32[512,1024]{1,0:T(8,128)S(1)} collective-permute-done((f32[512,1024]{1,0:T(8,128)}, f32[512,1024]{1,0:T(8,128)S(1)}, u32[]{:S(2)}, u32[]{:S(2)}) %collective-permute-start.26) | collective-permute-done | bytes 2097184 | tf_op jit(solution)/shard_map/ppermute | solution.py:482
  1248.1 15.1 %collective-permute-done.33 = f32[128,1280]{1,0:T(8,128)S(1)} collective-permute-done((f32[128,1280]{1,0:T(8,128)S(1)}, f32[128,1280]{1,0:T(8,128)S(1)}, u32[]{:S(2)}, u32[]{:S(2)}) %collective-permute-start.33) | collective-permute-done | bytes 655392 | tf_op jit(solution)/shard_map/ppermute | solution.py:482
  1263.2 14.1 %collective-permute-done.32 = f32[128,1280]{1,0:T(8,128)S(1)} collective-permute-done((f32[128,1280]{1,0:T(8,128)S(1)}, f32[128,1280]{1,0:T(8,128)S(1)}, u32[]{:S(2)}, u32[]{:S(2)}) %collective-permute-start.32) | collective-permute-done | bytes 655392 | tf_op jit(solution)/shard_map/ppermute | solution.py:482
  1282.3 5.7 fusion.90
  1295.3 17.4 %fusion.22 = bf16[1,1024,2048]{2,1,0:T(8,128)(2,1)} fusion(f32[1024,2048]{1,0:T(8,128)} %fusion.90, bf16[1024,2048]{1,0:T(8,128)(2,1)} %copy-done.1, bf16[2048,1024]{1,0:T(8,128)(2,1)} %pad_maximum_fusion.2, bf16[256,8,16,128]{3,2,1,0:T(8,128)(2,1)} %bitcast.211), kind=kOutput, calls=%fused_computation.24 | convolution fusion | flops 8598323200 | bytes 29360128 | tf_op jit(solution)/shard_map/dot_general | solution.py:37
  1313.0 13.8 %collective-permute-done.35 = f32[128,1472]{0,1:T(8,128)} collective-permute-done((f32[128,1472]{0,1:T(8,128)}, f32[128,1472]{0,1:T(8,128)}, u32[]{:S(2)}, u32[]{:S(2)}) %collective-permute-start.35) | collective-permute-done | bytes 753696 | tf_op jit(solution)/shard_map/ppermute | solution.py:482
  1331.4 6.9 shard_map.151
  1338.3 5.8 pad_maximum_fusion.1
  (259 shorter events, 118.7 us)
Async XLA Ops:
  7.2 53.0 %all-gather.2.cloned.1.call-start = ((), (), s32[]{:S(2)}) async-start(), calls=%async_computation.6 | async-start | bytes 5242880 | tf_op jit(solution)/shard_map/all_gather | solution.py:517
  14.8 1229.4 %reduce-scatter.11.cloned.1.call-start = ((), (), s32[]{:S(2)}) async-start(), calls=%async_computation.9 | async-start | bytes 13107200 | tf_op jit(solution)/shard_map/reduce_scatter | solution.py:485
  141.7 94.8 %collective-permute-start.4 = (bf16[1024,2048]{1,0:T(8,128)(2,1)}, bf16[1024,2048]{1,0:T(8,128)(2,1)S(1)}, u32[]{:S(2)}, u32[]{:S(2)}) collective-permute-start(bf16[1024,2048]{1,0:T(8,128)(2,1)} %bitcast.27.refs_1_.refs_4_), channel_id=1, source_target_pairs={{0,2},{1,3},{2,0},{3,1},{4,6},{5,7},{6,4},{7,5},{8,10},{9,11},{10,... | collective-permute-start | bytes 12582920 | tf_op jit(solution)/shard_map/ppermute | solution.py:482
  159.5 117.1 %collective-permute-start.2 = (bf16[1024,2048]{1,0:T(8,128)(2,1)}, bf16[1024,2048]{1,0:T(8,128)(2,1)}, u32[]{:S(2)}, u32[]{:S(2)}) collective-permute-start(bf16[1024,2048]{1,0:T(8,128)(2,1)} %add_convert_fusion.1.refs_0_), channel_id=1, source_target_pairs={{0,1},{1,0},{2,3},{3,2},{4,5},{5,4},{6,7},{7,6},{8,9},{9,8},{10,11... | collective-permute-start | bytes 12582920 | tf_op jit(solution)/shard_map/ppermute | solution.py:482
  159.5 117.1 %collective-permute-start.3 = (bf16[1024,2048]{1,0:T(8,128)(2,1)}, bf16[1024,2048]{1,0:T(8,128)(2,1)}, u32[]{:S(2)}, u32[]{:S(2)}) collective-permute-start(bf16[1024,2048]{1,0:T(8,128)(2,1)} %bitcast.27.refs_1_.refs_4_), channel_id=1, source_target_pairs={{0,1},{1,0},{2,3},{3,2},{4,5},{5,4},{6,7},{7,6},{8,9},{9,8},{10,11... | collective-permute-start | bytes 12582920 | tf_op jit(solution)/shard_map/ppermute | solution.py:482
  164.2 133.1 %collective-permute-start.1 = (bf16[512,2048]{1,0:T(8,128)(2,1)S(1)}, bf16[512,2048]{1,0:T(8,128)(2,1)}, u32[]{:S(2)}, u32[]{:S(2)}) collective-permute-start(bf16[512,2048]{1,0:T(8,128)(2,1)S(1)} %get-tuple-element.171), channel_id=1, source_target_pairs={{0,2},{1,3},{2,0},{3,1},{4,6},{5,7},{6,4},{7,5},{8,10},{9,11},{10,... | collective-permute-start | bytes 6291464 | tf_op jit(solution)/shard_map/ppermute | solution.py:482
  236.5 65.2 %collective-permute-start.6 = (bf16[1024,2048]{1,0:T(8,128)(2,1)S(1)}, bf16[1024,2048]{1,0:T(8,128)(2,1)}, u32[]{:S(2)}, u32[]{:S(2)}) collective-permute-start(bf16[1024,2048]{1,0:T(8,128)(2,1)S(1)} %collective-permute-done.4.refs_1_), channel_id=1, source_target_pairs={{0,1},{1,0},{2,3},{3,2},{4,5},{5,4},{6,7},{7,6},{8,9},{9,8},{10,11... | collective-permute-start | bytes 12582920 | tf_op jit(solution)/shard_map/ppermute | solution.py:482
  297.3 4.4 collective-permute-start.5
  297.4 48.5 %collective-permute-start = (bf16[512,2048]{1,0:T(8,128)(2,1)}, bf16[512,2048]{1,0:T(8,128)(2,1)S(1)}, u32[]{:S(2)}, u32[]{:S(2)}) collective-permute-start(bf16[512,2048]{1,0:T(8,128)(2,1)} %get-tuple-element.172), channel_id=1, source_target_pairs={{0,2},{1,3},{2,0},{3,1},{4,6},{5,7},{6,4},{7,5},{8,10},{9,11},{10,... | collective-permute-start | bytes 6291464 | tf_op jit(solution)/shard_map/ppermute | solution.py:482
  345.9 4.2 collective-permute-start.7
  401.4 886.6 %reduce-scatter.13.cloned.1.call-start = ((), (), s32[]{:S(2)}) async-start(), calls=%async_computation.10 | async-start | bytes 15728640 | tf_op jit(solution)/shard_map/reduce_scatter | solution.py:485
  413.3 22.9 %collective-permute-start.8 = (f32[512,2048]{1,0:T(8,128)S(1)}, f32[512,2048]{1,0:T(8,128)}, u32[]{:S(2)}, u32[]{:S(2)}) collective-permute-start(f32[512,2048]{1,0:T(8,128)S(1)} %shard_map.141), channel_id=1, source_target_pairs={{0,1},{1,0},{2,3},{3,2},{4,5},{5,4},{6,7},{7,6},{8,9},{9,8},{10,11... | collective-permute-start | bytes 12582920 | tf_op jit(solution)/shard_map/ppermute | solution.py:482
  521.0 817.3 %reduce-scatter.15.cloned.1.call-start = ((), (), s32[]{:S(2)}) async-start(), calls=%async_computation.11 | async-start | bytes 13107200 | tf_op jit(solution)/shard_map/reduce_scatter | solution.py:485
  521.3 8.3 collective-permute-start.9
  575.7 762.5 %reduce-scatter.17.cloned.1.call-start = ((), (), s32[]{:S(2)}) async-start(), calls=%async_computation.12 | async-start | bytes 15073280 | tf_op jit(solution)/shard_map/reduce_scatter | solution.py:485
  596.0 183.2 %collective-permute-start.10 = (f32[1024,2048]{1,0:T(8,128)}, f32[1024,2048]{1,0:T(8,128)}, u32[]{:S(2)}, u32[]{:S(2)}) collective-permute-start(f32[1024,2048]{1,0:T(8,128)} %shard_map.147), channel_id=1, source_target_pairs={{0,1},{1,0},{2,3},{3,2},{4,5},{5,4},{6,7},{7,6},{8,9},{9,8},{10,11... | collective-permute-start | bytes 25165832 | tf_op jit(solution)/shard_map/ppermute | solution.py:482
  596.2 93.8 %collective-permute-start.11 = (f32[512,2048]{1,0:T(8,128)}, f32[512,2048]{1,0:T(8,128)}, u32[]{:S(2)}, u32[]{:S(2)}) collective-permute-start(f32[512,2048]{1,0:T(8,128)} %shard_map.143), channel_id=1, source_target_pairs={{0,2},{1,3},{2,0},{3,1},{4,6},{5,7},{6,4},{7,5},{8,10},{9,11},{10,... | collective-permute-start | bytes 12582920 | tf_op jit(solution)/shard_map/ppermute | solution.py:482
  598.0 181.2 %collective-permute-start.12 = (f32[512,2048]{1,0:T(8,128)}, f32[512,2048]{1,0:T(8,128)}, u32[]{:S(2)}, u32[]{:S(2)}) collective-permute-start(f32[512,2048]{1,0:T(8,128)} %shard_map.146), channel_id=1, source_target_pairs={{0,2},{1,3},{2,0},{3,1},{4,6},{5,7},{6,4},{7,5},{8,10},{9,11},{10,... | collective-permute-start | bytes 12582920 | tf_op jit(solution)/shard_map/ppermute | solution.py:482
  632.8 711.3 %reduce-scatter.9.cloned.1.call-start = ((), (), s32[]{:S(2)}) async-start(), calls=%async_computation.8 | async-start | bytes 3932160 | tf_op jit(solution)/shard_map/reduce_scatter | solution.py:485
  808.8 22.2 %collective-permute-start.13 = (f32[512,2048]{1,0:T(8,128)}, f32[512,2048]{1,0:T(8,128)S(1)}, u32[]{:S(2)}, u32[]{:S(2)}) collective-permute-start(f32[512,2048]{1,0:T(8,128)} %convolution_multiply_fusion.3), channel_id=1, source_target_pairs={{0,1},{1,0},{2,3},{3,2},{4,5},{5,4},{6,7},{7,6},{8,9},{9,8},{10,11... | collective-permute-start | bytes 12582920 | tf_op jit(solution)/shard_map/ppermute | solution.py:482
  811.2 81.0 %copy-start.44 = (bf16[1024,128]{1,0:T(8,128)(2,1)}, bf16[1024,128]{1,0:T(8,128)(2,1)S(1)}, u32[]{:S(2)}) copy-start(bf16[1024,128]{1,0:T(8,128)(2,1)S(1)} %get-tuple-element.161) | copy-start | bytes 786436
  811.2 81.0 %copy-start.47 = (bf16[1024,128]{1,0:T(8,128)(2,1)}, bf16[1024,128]{1,0:T(8,128)(2,1)S(1)}, u32[]{:S(2)}) copy-start(bf16[1024,128]{1,0:T(8,128)(2,1)S(1)} %get-tuple-element.162) | copy-start | bytes 786436
  811.2 81.0 %copy-start.50 = (bf16[1024,128]{1,0:T(8,128)(2,1)}, bf16[1024,128]{1,0:T(8,128)(2,1)S(1)}, u32[]{:S(2)}) copy-start(bf16[1024,128]{1,0:T(8,128)(2,1)S(1)} %get-tuple-element.163) | copy-start | bytes 786436
  811.2 81.0 %copy-start.53 = (bf16[1024,128]{1,0:T(8,128)(2,1)}, bf16[1024,128]{1,0:T(8,128)(2,1)S(1)}, u32[]{:S(2)}) copy-start(bf16[1024,128]{1,0:T(8,128)(2,1)S(1)} %get-tuple-element.164) | copy-start | bytes 786436
  896.4 10.0 collective-permute-start.15
  899.8 3.8 collective-permute-start.14
  973.0 12.0 collective-permute-start.18
  974.6 4.6 collective-permute-start.19
  974.7 26.8 %collective-permute-start.16 = (f32[2,2,128,512]{3,2,1,0:T(8,128)S(1)}, f32[2,2,128,512]{3,2,1,0:T(8,128)}, u32[]{:S(2)}, u32[]{:S(2)}) collective-permute-start(f32[2,2,128,512]{3,2,1,0:T(8,128)S(1)} %get-tuple-element.169), channel_id=1, source_target_pairs={{0,1},{1,0},{2,3},{3,2},{4,5},{5,4},{6,7},{7,6},{8,9},{9,8},{10,11... | collective-permute-start | bytes 3145736 | tf_op jit(solution)/shard_map/ppermute | solution.py:482
  975.2 26.3 %collective-permute-start.17 = (f32[2,2,128,512]{3,2,1,0:T(8,128)}, f32[2,2,128,512]{3,2,1,0:T(8,128)}, u32[]{:S(2)}, u32[]{:S(2)}) collective-permute-start(f32[2,2,128,512]{3,2,1,0:T(8,128)} %bitcast_add_fusion.3), channel_id=1, source_target_pairs={{0,2},{1,3},{2,0},{3,1},{4,6},{5,7},{6,4},{7,5},{8,10},{9,11},{10,... | collective-permute-start | bytes 3145736 | tf_op jit(solution)/shard_map/ppermute | solution.py:482
  980.5 42.6 %collective-permute-start.21 = (f32[2,2,128,512]{3,2,1,0:T(8,128)}, f32[2,2,128,512]{3,2,1,0:T(8,128)}, u32[]{:S(2)}, u32[]{:S(2)}) collective-permute-start(f32[2,2,128,512]{3,2,1,0:T(8,128)} %bitcast_add_fusion.1), channel_id=1, source_target_pairs={{0,2},{1,3},{2,0},{3,1},{4,6},{5,7},{6,4},{7,5},{8,10},{9,11},{10,... | collective-permute-start | bytes 3145736 | tf_op jit(solution)/shard_map/ppermute | solution.py:482
  981.7 41.5 %collective-permute-start.20 = (f32[2,2,128,512]{3,2,1,0:T(8,128)}, f32[2,2,128,512]{3,2,1,0:T(8,128)S(1)}, u32[]{:S(2)}, u32[]{:S(2)}) collective-permute-start(f32[2,2,128,512]{3,2,1,0:T(8,128)} %get-tuple-element.167), channel_id=1, source_target_pairs={{0,1},{1,0},{2,3},{3,2},{4,5},{5,4},{6,7},{7,6},{8,9},{9,8},{10,11... | collective-permute-start | bytes 3145736 | tf_op jit(solution)/shard_map/ppermute | solution.py:482
  1026.1 3.3 collective-permute-start.22
  1026.9 71.3 %collective-permute-start.27 = (f32[512,1024]{1,0:T(8,128)S(1)}, f32[512,1024]{1,0:T(8,128)S(1)}, u32[]{:S(2)}, u32[]{:S(2)}) collective-permute-start(f32[512,1024]{1,0:T(8,128)S(1)} %copy-done.56), channel_id=1, source_target_pairs={{0,1},{1,0},{2,3},{3,2},{4,5},{5,4},{6,7},{7,6},{8,9},{9,8},{10,11... | collective-permute-start | bytes 6291464 | tf_op jit(solution)/shard_map/ppermute | solution.py:482
  1026.9 71.3 %collective-permute-start.28 = (f32[512,1024]{1,0:T(8,128)S(1)}, f32[512,1024]{1,0:T(8,128)S(1)}, u32[]{:S(2)}, u32[]{:S(2)}) collective-permute-start(f32[512,1024]{1,0:T(8,128)S(1)} %multiply_add_fusion.1), channel_id=1, source_target_pairs={{0,2},{1,3},{2,0},{3,1},{4,6},{5,7},{6,4},{7,5},{8,10},{9,11},{10,... | collective-permute-start | bytes 6291464 | tf_op jit(solution)/shard_map/ppermute | solution.py:482
  1029.2 4.1 collective-permute-start.29
  1030.3 67.1 %collective-permute-start.30 = (f32[512,512]{1,0:T(8,128)S(1)}, f32[512,512]{1,0:T(8,128)S(1)}, u32[]{:S(2)}, u32[]{:S(2)}) collective-permute-start(f32[512,512]{1,0:T(8,128)S(1)} %fusion.42), channel_id=1, source_target_pairs={{0,2},{1,3},{2,0},{3,1},{4,6},{5,7},{6,4},{7,5},{8,10},{9,11},{10,... | collective-permute-start | bytes 3145736 | tf_op jit(solution)/shard_map/ppermute | solution.py:482
  1101.0 245.6 %reduce-scatter.7.cloned.1.call-start = ((), (), s32[]{:S(2)}) async-start(), calls=%async_computation.7 | async-start | bytes 7864320 | tf_op jit(solution)/shard_map/reduce_scatter | solution.py:485
  1101.3 93.7 %collective-permute-start.24 = (f32[512,2048]{1,0:T(8,128)}, f32[512,2048]{1,0:T(8,128)S(1)}, u32[]{:S(2)}, u32[]{:S(2)}) collective-permute-start(f32[512,2048]{1,0:T(8,128)} %multiply_add_fusion), channel_id=1, source_target_pairs={{0,2},{1,3},{2,0},{3,1},{4,6},{5,7},{6,4},{7,5},{8,10},{9,11},{10,... | collective-permute-start | bytes 12582920 | tf_op jit(solution)/shard_map/ppermute | solution.py:482
  1102.8 136.5 %collective-permute-start.23 = (f32[512,2048]{1,0:T(8,128)}, f32[512,2048]{1,0:T(8,128)S(1)}, u32[]{:S(2)}, u32[]{:S(2)}) collective-permute-start(f32[512,2048]{1,0:T(8,128)} %convolution_multiply_fusion.2), channel_id=1, source_target_pairs={{0,1},{1,0},{2,3},{3,2},{4,5},{5,4},{6,7},{7,6},{8,9},{9,8},{10,11... | collective-permute-start | bytes 12582920 | tf_op jit(solution)/shard_map/ppermute | solution.py:482
  1102.8 92.2 %collective-permute-start.25 = (f32[512,1024]{1,0:T(8,128)}, f32[512,1024]{1,0:T(8,128)S(1)}, u32[]{:S(2)}, u32[]{:S(2)}) collective-permute-start(f32[512,1024]{1,0:T(8,128)} %convolution_multiply_fusion.6), channel_id=1, source_target_pairs={{0,1},{1,0},{2,3},{3,2},{4,5},{5,4},{6,7},{7,6},{8,9},{9,8},{10,11... | collective-permute-start | bytes 6291464 | tf_op jit(solution)/shard_map/ppermute | solution.py:482
  1103.3 135.3 %collective-permute-start.26 = (f32[512,1024]{1,0:T(8,128)}, f32[512,1024]{1,0:T(8,128)S(1)}, u32[]{:S(2)}, u32[]{:S(2)}) collective-permute-start(f32[512,1024]{1,0:T(8,128)} %multiply_add_fusion.2), channel_id=1, source_target_pairs={{0,2},{1,3},{2,0},{3,1},{4,6},{5,7},{6,4},{7,5},{8,10},{9,11},{10,... | collective-permute-start | bytes 6291464 | tf_op jit(solution)/shard_map/ppermute | solution.py:482
  1246.2 17.0 %collective-permute-start.33 = (f32[128,1280]{1,0:T(8,128)S(1)}, f32[128,1280]{1,0:T(8,128)S(1)}, u32[]{:S(2)}, u32[]{:S(2)}) collective-permute-start(f32[128,1280]{1,0:T(8,128)S(1)} %get-tuple-element.178), channel_id=1, source_target_pairs={{0,3},{1,2},{2,1},{3,0},{4,7},{5,6},{6,5},{7,4},{8,11},{9,10},{10,... | collective-permute-start | bytes 1966088 | tf_op jit(solution)/shard_map/ppermute | solution.py:482
  1246.2 31.1 %collective-permute-start.32 = (f32[128,1280]{1,0:T(8,128)S(1)}, f32[128,1280]{1,0:T(8,128)S(1)}, u32[]{:S(2)}, u32[]{:S(2)}) collective-permute-start(f32[128,1280]{1,0:T(8,128)S(1)} %get-tuple-element.179), channel_id=1, source_target_pairs={{0,2},{1,3},{2,0},{3,1},{4,6},{5,7},{6,4},{7,5},{8,10},{9,11},{10,... | collective-permute-start | bytes 1966088 | tf_op jit(solution)/shard_map/ppermute | solution.py:482
  1247.7 29.5 %collective-permute-start.31 = (f32[128,1280]{1,0:T(8,128)S(1)}, f32[128,1280]{1,0:T(8,128)S(1)}, u32[]{:S(2)}, u32[]{:S(2)}) collective-permute-start(f32[128,1280]{1,0:T(8,128)S(1)} %get-tuple-element.180), channel_id=1, source_target_pairs={{0,1},{1,0},{2,3},{3,2},{4,5},{5,4},{6,7},{7,6},{8,9},{9,8},{10,11... | collective-permute-start | bytes 1966088 | tf_op jit(solution)/shard_map/ppermute | solution.py:482
  1291.1 21.6 %collective-permute-start.36 = (f32[128,1472]{0,1:T(8,128)}, f32[128,1472]{0,1:T(8,128)S(1)}, u32[]{:S(2)}, u32[]{:S(2)}) collective-permute-start(f32[128,1472]{0,1:T(8,128)} %copy.43), channel_id=1, source_target_pairs={{0,3},{1,2},{2,1},{3,0},{4,7},{5,6},{6,5},{7,4},{8,11},{9,10},{10,... | collective-permute-start | bytes 2261000 | tf_op jit(solution)/shard_map/ppermute | solution.py:482
  1292.7 34.0 %collective-permute-start.35 = (f32[128,1472]{0,1:T(8,128)}, f32[128,1472]{0,1:T(8,128)}, u32[]{:S(2)}, u32[]{:S(2)}) collective-permute-start(f32[128,1472]{0,1:T(8,128)} %copy.41), channel_id=1, source_target_pairs={{0,2},{1,3},{2,0},{3,1},{4,6},{5,7},{6,4},{7,5},{8,10},{9,11},{10,... | collective-permute-start | bytes 2261000 | tf_op jit(solution)/shard_map/ppermute | solution.py:482
  1295.3 32.9 %collective-permute-start.34 = (f32[128,1472]{0,1:T(8,128)}, f32[128,1472]{0,1:T(8,128)}, u32[]{:S(2)}, u32[]{:S(2)}) collective-permute-start(f32[128,1472]{0,1:T(8,128)} %copy.39), channel_id=1, source_target_pairs={{0,1},{1,0},{2,3},{3,2},{4,5},{5,4},{6,7},{7,6},{8,9},{9,8},{10,11... | collective-permute-start | bytes 2261000 | tf_op jit(solution)/shard_map/ppermute | solution.py:482
  (55 other events, 458.7 us)
Sparse Core Ops, SparseCore 0:
  15.0 35.3 all-gather.1
  401.5 101.1 reduce-scatter.10
  521.1 119.0 reduce-scatter.12
  643.1 99.7 reduce-scatter.14
  745.8 112.5 reduce-scatter.16
  1101.2 41.6 reduce-scatter.8
  1244.3 67.8 reduce-scatter.6

commit v5 on v3

--- a/solution.py
+++ b/solution.py
@@ -14,6 +14,7 @@
 LOG2E = math.log2(math.e)
 F32 = jnp.float32
 FF_TILE = 256
+FF_ROWS = 512
 BF16 = jnp.bfloat16
 
 
@@ -53,7 +54,7 @@
     return keys <= queries
 
 
-def attn_fwd_kernel(group, scale, tab, q_ref, k_ref, v_ref, of_ref, ob_ref, lse_ref, m_ref, l_ref):
+def attn_fwd_kernel(group, scale, tab, q_ref, k_ref, v_ref, of_ref, ob_ref, lse_ref, m_ref, l_ref, acc_ref):
     dim = k_ref.shape[1]
     half = q_ref.shape[1] // 2
     factor = scale * LOG2E
@@ -66,23 +67,29 @@
         def _():
             m_ref[...] = jnp.full(m_ref.shape, NEG_BIG, F32)
             l_ref[...] = jnp.zeros(l_ref.shape, F32)
-            of_ref[:, cols] = jnp.zeros((of_ref.shape[0], half), F32)
+            acc_ref[...] = jnp.zeros(acc_ref.shape, F32)
 
         def run(masked):
             keys = k_ref[slot, :]
             vals_t = v_ref[slot, :].T
+
+            def scores_of(head):
+                scores = dot_nn(keys, q_ref[head * dim:(head + 1) * dim, cols])
+                return jnp.where(causal_keep(half), scores, NEG_BIG) if masked else scores
+
+            following = scores_of(0)
             for head in range(group):
+                scores = following
+                if head + 1 < group:
+                    following = scores_of(head + 1)
                 rows = slice(head * dim, (head + 1) * dim)
-                scores = dot_nn(keys, q_ref[rows, cols])
-                if masked:
-                    scores = jnp.where(causal_keep(half), scores, NEG_BIG)
                 old_max = m_ref[head:head + 1, :]
                 new_max = jnp.maximum(old_max, jnp.max(scores, axis=0, keepdims=True))
-                probs = jnp.exp2((scores - new_max) * factor)
+                probs = jnp.exp2(scores * factor - new_max * factor)
                 alpha = jnp.exp2((old_max - new_max) * factor)
                 m_ref[head:head + 1, :] = new_max
                 l_ref[head:head + 1, :] = alpha * l_ref[head:head + 1, :] + jnp.sum(probs, axis=0, keepdims=True)
-                of_ref[rows, cols] = alpha * of_ref[rows, cols] + dot_nn(vals_t, probs.astype(BF16))
+                acc_ref[rows, :] = alpha * acc_ref[rows, :] + dot_nn(vals_t, probs.astype(BF16))
 
         @pl.when(tab[2, pair] == 0)
         def _():
@@ -94,7 +101,7 @@
             lse_ref[0, :, cols] = m_ref[...] * factor + jnp.log2(l_ref[...])
             for head in range(group):
                 rows = slice(head * dim, (head + 1) * dim)
-                out = of_ref[rows, cols] / l_ref[head:head + 1, :]
+                out = acc_ref[rows, :] / l_ref[head:head + 1, :]
                 of_ref[rows, cols] = out
                 ob_ref[rows, cols] = out.astype(BF16)
 
@@ -120,13 +127,12 @@
                       pl.BlockSpec((kv_all.shape[0], head_dim), lambda k, t: (0, kv_heads + k))],
             out_specs=[q_spec, q_spec,
                        pl.BlockSpec((1, group, seq), lambda k, t: (k, 0, 0))],
-            scratch_shapes=[pltpu.VMEM((group, half), F32), pltpu.VMEM((group, half), F32)]),
+            scratch_shapes=[pltpu.VMEM((group, half), F32), pltpu.VMEM((group, half), F32), pltpu.VMEM((rows, half), F32)]),
         out_shape=[jax.ShapeDtypeStruct((width, seq), F32), jax.ShapeDtypeStruct((width, seq), BF16),
                    jax.ShapeDtypeStruct((kv_heads, group, seq), F32)],
         compiler_params=pltpu.CompilerParams(vmem_limit_bytes=56 * 2 ** 20),
         cost_estimate=pl.CostEstimate(flops=4 * width * half * half * n_pairs,
                                       bytes_accessed=12 * width * seq, transcendentals=width // head_dim * half * half * n_pairs),
-        name='attn_fwd',
     )(tab, q_t, kv_all, kv_all)
 
 
@@ -152,19 +158,28 @@
             keys = k_ref[slot_rows, :]
             vals = v_ref[slot_rows, :]
             keys_t = keys.T
-            for head in range(group):
+
+            def products(head):
                 rows = slice(head * dim, (head + 1) * dim)
-                q_head = q_ref[rows, cols]
-                do_head = do_ref[rows, cols]
-                scores = dot_nn(keys, q_head)
+                scores = dot_nn(keys, q_ref[rows, cols])
                 if masked:
                     scores = jnp.where(causal_keep(half), scores, NEG_BIG)
+                return scores, dot_nn(vals, do_ref[rows, cols])
+
+            following = products(0)
+            grad_v = grad_k = jnp.zeros((dim, half), F32)
+            for head in range(group):
+                scores, grad_p = following
+                if head + 1 < group:
+                    following = products(head + 1)
+                rows = slice(head * dim, (head + 1) * dim)
                 probs = jnp.exp2(scores * factor - lse_ref[0, head:head + 1, cols])
-                grad_p = dot_nn(vals, do_head)
                 grad_s = (probs * (grad_p - delta_ref[head:head + 1, :])).astype(BF16)
-                dkv_ref[slot, 1] += dot_nt(do_head, probs.astype(BF16))
-                dkv_ref[slot, 0] += scale * dot_nt(q_head, grad_s)
+                grad_v = grad_v + dot_nt(do_ref[rows, cols], probs.astype(BF16))
+                grad_k = grad_k + dot_nt(q_ref[rows, cols], grad_s)
                 acc_ref[rows, :] += dot_nn(keys_t, grad_s)
+            dkv_ref[slot, 1] += grad_v
+            dkv_ref[slot, 0] += scale * grad_k
 
         @pl.when(tab[2, pair] == 0)
         def _():
@@ -205,7 +220,6 @@
         compiler_params=pltpu.CompilerParams(vmem_limit_bytes=56 * 2 ** 20),
         cost_estimate=pl.CostEstimate(flops=10 * rows * half * half * n_pairs,
                                       bytes_accessed=12 * rows * seq, transcendentals=group * half * half * n_pairs),
-        name='attn_bwd',
     )(tab, q_t, do_t, o_f32, lse, kv_all, kv_all)
 
 
@@ -219,7 +233,7 @@
 
 
 def prep_kernel(segs, parts, idx_ref, *refs):
-    n_blocks = sum(seg['tiles'] + 1 for seg in segs)
+    n_blocks = sum(seg[3] + 1 for seg in segs)
     blocks, down_ref = refs[:n_blocks], refs[n_blocks]
     n_parts = len(parts)
     up_refs, down_refs = refs[n_blocks + 1:n_blocks + 1 + n_parts], refs[n_blocks + 1 + n_parts:n_blocks + 1 + 2 * n_parts]
@@ -231,11 +245,11 @@
     outs = []
     for part, down_out in zip(parts, down_refs):
         for own in range(n_own):
-            outs.append(pltpu.make_async_copy(buf_ref.at[own, pl.ds(part['first'], part['rows'])],
-                                              down_out.at[pl.ds(own * part['rows'], part['rows'])], out_sem.at[len(outs)]))
-        if part['pad']:
-            outs.append(pltpu.make_async_copy(zero_ref.at[pl.ds(0, part['pad'])],
-                                              down_out.at[pl.ds(n_own * part['rows'], part['pad'])], out_sem.at[len(outs)]))
+            outs.append(pltpu.make_async_copy(buf_ref.at[own, pl.ds(part[0], part[1])],
+                                              down_out.at[pl.ds(own * part[1], part[1])], out_sem.at[len(outs)]))
+        if part[2]:
+            outs.append(pltpu.make_async_copy(zero_ref.at[pl.ds(0, part[2])],
+                                              down_out.at[pl.ds(n_own * part[1], part[2])], out_sem.at[len(outs)]))
 
     @pl.when(step == 0)
     def _():
@@ -256,13 +270,13 @@
     pos = 0
     for number, seg in enumerate(segs):
         shift = idx_ref[1, number]
-        turned = [pltpu.roll(blocks[pos + tile][...].astype(F32), (128 - shift) % 128, 1) for tile in range(seg['tiles'] + 1)]
-        pos += seg['tiles'] + 1
-        for tile in range(seg['tiles']):
-            cover[seg['part']].setdefault(seg['tile'] + tile, []).append(
-                (seg['start'], jnp.where(lanes < 128 - shift, turned[tile], turned[tile + 1])))
+        turned = [pltpu.roll(blocks[pos + tile][...].astype(F32), (128 - shift) % 128, 1) for tile in range(seg[3] + 1)]
+        pos += seg[3] + 1
+        for tile in range(seg[3]):
+            cover[seg[0]].setdefault(seg[2] + tile, []).append(
+                (seg[1], jnp.where(lanes < 128 - shift, turned[tile], turned[tile + 1])))
     for part, tiles, up_ref in zip(parts, cover, up_refs):
-        used = n_own * part['rows']
+        used = n_own * part[1]
         for tile in range(up_ref.shape[1] // 128):
             value = jnp.zeros((rows, 128), F32)
             for start, piece in tiles.get(tile, []):
@@ -280,13 +294,13 @@
 def prepare(starts, splits, w_up, w_down):
     d_model, own_rows = w_up.shape[0], splits[-1][0] + splits[-1][1]
     n_own = starts.shape[0]
-    parts = [{'first': first, 'rows': count, 'pad': -(n_own * count) % FF_TILE} for first, count in splits]
+    parts = [(first, count, -(n_own * count) % FF_TILE) for first, count in splits]
     segs, shifts, bases = [], [], []
     for number, part in enumerate(parts):
         for own in range(n_own):
-            dest = own * part['rows']
-            segs.append({'part': number, 'start': dest, 'tile': dest // 128, 'tiles': -(-(dest % 128 + part['rows']) // 128)})
-            source = starts[own] + part['first'] - dest % 128
+            dest = own * part[1]
+            segs.append((number, dest, dest // 128, -(-(dest % 128 + part[1]) // 128)))
+            source = starts[own] + part[0] - dest % 128
             shifts.append(source % 128)
             bases.append(source // 128)
     table = jnp.stack([jnp.pad(starts, (0, len(segs) - n_own)), jnp.stack(shifts), jnp.stack(bases)]).astype(jnp.int32)
@@ -294,10 +308,10 @@
     last = w_up.shape[1] // 128 - 1
     in_specs = []
     for number, seg in enumerate(segs):
-        for tile in range(seg['tiles'] + 1):
+        for tile in range(seg[3] + 1):
             in_specs.append(pl.BlockSpec((rows, 128), lambda i, t, number=number, tile=tile:
                                          (i, jnp.clip(t[2, number] + tile, 0, last))))
-    widths = [n_own * part['rows'] + part['pad'] for part in parts]
+    widths = [n_own * part[1] + part[2] for part in parts]
     outs = pl.pallas_call(
         functools.partial(prep_kernel, segs, parts),
         grid_spec=pltpu.PrefetchScalarGridSpec(
@@ -312,7 +326,6 @@
         + [jax.ShapeDtypeStruct((width, d_model), BF16) for width in widths],
         compiler_params=pltpu.CompilerParams(vmem_limit_bytes=56 * 2 ** 20),
         cost_estimate=pl.CostEstimate(flops=8 * d_model * sum(widths), bytes_accessed=9 * d_model * sum(widths), transcendentals=0),
-        name='prepare',
     )(table, *([w_up] * len(in_specs)), w_down)
     return outs[:len(parts)], outs[len(parts):]
 
@@ -336,17 +349,24 @@
     else:
         act_ref, du_ref = refs[-2:]
 
-    base = 0
+    places, base = [], 0
     for h_ref, cot_ref in pieces:
-        for first in range(0, h_ref.shape[0], step_rows):
-            rows = slice(first, first + step_rows)
-            out_rows = slice(base + first, base + first + step_rows)
-            hidden = dot_nn(h_ref[rows, :], up_ref[...])
-            grad_act = dot_nt(cot_ref[rows, :], down_ref[...]).astype(BF16).astype(F32)
-            act, slope = gelu_parts(hidden)
-            act_ref[out_rows, :] = act.astype(BF16)
-            du_ref[out_rows, :] = (grad_act * slope).astype(BF16)
+        places += [(h_ref, cot_ref, first, base + first) for first in range(0, h_ref.shape[0], step_rows)]
         base += h_ref.shape[0]
+
+    def products(h_ref, cot_ref, first, _):
+        rows = slice(first, first + step_rows)
+        return dot_nn(h_ref[rows, :], up_ref[...]), dot_nt(cot_ref[rows, :], down_ref[...])
+
+    following = products(*places[0])
+    for number, place in enumerate(places):
+        hidden, grad_act = following
+        if number + 1 < len(places):
+            following = products(*places[number + 1])
+        out_rows = slice(place[3], place[3] + step_rows)
+        act, slope = gelu_parts(hidden)
+        act_ref[out_rows, :] = act.astype(BF16)
+        du_ref[out_rows, :] = (grad_act.astype(BF16).astype(F32) * slope).astype(BF16)
 
     if copies:
         @pl.when(pl.program_id(0) == pl.num_programs(0) - 1)
@@ -371,7 +391,7 @@
         args += [h_blk, cot_blk]
     carry = list(carry)
     return pl.pallas_call(
-        functools.partial(ff_kernel, 512, copies, index * tokens, len(pieces)),
+        functools.partial(ff_kernel, FF_ROWS, copies, index * tokens, len(pieces)),
         grid=(width // tile,),
         in_specs=in_specs + [pl.BlockSpec((d_model, tile), lambda n: (0, n)), pl.BlockSpec((tile, d_model), lambda n: (n, 0))]
         + [pl.BlockSpec(memory_space=pl.ANY)] * len(carry),
@@ -382,7 +402,6 @@
         compiler_params=pltpu.CompilerParams(vmem_limit_bytes=56 * 2 ** 20),
         cost_estimate=pl.CostEstimate(flops=4 * tokens * d_model * width, bytes_accessed=4 * d_model * (width + 2 * tokens),
                                       transcendentals=tokens * width),
-        name='ff_forward',
     )(*args, up, down, *carry)
 
 
@@ -416,7 +435,6 @@
         compiler_params=pltpu.CompilerParams(vmem_limit_bytes=48 * 2 ** 20),
         cost_estimate=pl.CostEstimate(flops=2 * tokens * d_model * width, bytes_accessed=2 * width * (d_model + tokens) + 4 * tokens * d_model,
                                       transcendentals=0),
-        name='grad_h',
     )(*args, *extras)
 
 
@@ -439,7 +457,6 @@
         out_specs=pl.BlockSpec(memory_space=pltpu.VMEM),
         out_shape=jax.ShapeDtypeStruct((rows, width), F32),
         cost_estimate=pl.CostEstimate(flops=rows * width, bytes_accessed=8 * rows * width, transcendentals=0),
-        name='spread',
     )(my_idx.reshape(1), *got)
 
 
@@ -492,54 +509,53 @@
         splits = ((0, first_part), (first_part, ff_part - first_part))
         used = [dp_size * count for _, count in splits]
         starts = (jnp.arange(dp_size) * cp_size + my_idx) * ff_part
+        cot_far = swap(after(cot, tab), 2)
         w_up_own, w_down_own = prepare(starts, splits, w_up, w_down)
 
         kv_all = after(kv_all, q_t, w_up_own[0])
-        cot_far = swap(after(cot, kv_all), 2)
         o_f32, o_t, lse = attn_forward(tab, q_t, kv_all, kv_heads, head_dim)
-        o_t = after(o_t, cot_far)
 
         h_act = (x + dot_tt(o_t, w_o)).astype(BF16)
-        h_far = [swap(h_act[:half], 2), swap(h_act[half:], 2)]
+        h_far0 = swap(h_act[:half], 2)
         h_near = swap(h_act, 1)
-        cot_last = swap(cot_far, 1)
 
         def ff_call(index, part, pieces, carry, *earlier):
             first = after(pieces[0][0], *earlier) if earlier else pieces[0][0]
             pieces = [(first,) + pieces[0][1:]] + pieces[1:]
             return ff_forward(index, cp_size, pieces, w_up_own[part], w_down_own[part], part == 0, carry)
 
+        def remote(piece, far_piece):
+            return [(far_piece, cot_far, piece), (swap(far_piece, 1), cot_last, piece)]
+
         own, near = [(h_act, cot, 0)], [(h_near, cot_near, 0)]
         state = ff_call(0, 0, own, ())
+        h_far1 = swap(after(h_act, state[0])[half:], 2)
+        cot_last = swap(after(cot_far, state[0]), 1)
         state = ff_call(1, 0, near, state)
         more = ff_call(0, 1, own, (), state[0])
-
-        def remote(piece, *earlier):
-            far_piece = after(h_far[piece], *earlier)
-            return [(far_piece, cot_far, piece), (swap(far_piece, 1), cot_last, piece)]
-
-        remote0 = remote(0, more[0])
-        state = ff_call(2, 0, remote0, state)
-        more = ff_call(2, 1, remote0, more, state[0])
-        remote1 = remote(1, more[0])
-
-        def grad_h(index, tokens, grads, earlier, extras, dtype):
-            later = after(grads[1], earlier)
-            return grad_h_block(index, tokens, (grads[0], later), w_up_own, extras, dtype)
-
-        gh_last0 = grad_h(5, half, (state[1], more[1]), more[0], [], F32)
-        near0 = swap(gh_last0, 1)
-        act0, grad_u0, h_all, cot_all = ff_call(3, 0, remote1, state, gh_last0)
-        part = grad_h(4, half, (grad_u0, more[1]), act0, [near0], F32)
+        block = remote(0, after(h_far0, more[0]))
+        state = ff_call(2, 0, block, state)
+        act1, grad_u1 = ff_call(2, 1, block, more, state[0])
+
+        def grad_h(index, tokens, earlier, extras, dtype):
+            later = after(grad_u1, earlier)
+            return grad_h_block(index, tokens, (state[1], later), w_up_own, extras, dtype)
+
+        part = grad_h(5, half, act1, [], F32)
+        near0 = swap(part, 1)
+        block = remote(1, after(h_far1, act1))
+        state = ff_call(3, 0, block, state, part)
+        part = grad_h(4, half, state[0], [near0], F32)
         far0 = swap(part, 2)
+        act0, grad_u0, h_all, cot_all = state
         later = after(grad_u0, part)
         part = row_major(inv_count * dot_tn(h_all, later))
         up_rows = [dp_reduce(part)]
-        more = ff_call(3, 1, remote1, more, part)
-        gh_last1 = grad_h(7, half, (grad_u0, more[1]), more[0], [], F32)
-        near1 = swap(gh_last1, 1)
-        act1, grad_u1 = ff_call(1, 1, near, more, gh_last1)
-        part = grad_h(6, half, (grad_u0, grad_u1), act1, [near1], F32)
+        act1, grad_u1 = ff_call(3, 1, block, (act1, grad_u1), part)
+        part = grad_h(7, half, act1, [], F32)
+        near1 = swap(part, 1)
+        act1, grad_u1 = ff_call(1, 1, near, (act1, grad_u1), part)
+        part = grad_h(6, half, act1, [near1], F32)
         far1 = swap(part, 2)
         later = after(grad_u1, part)
         part = row_major(inv_count * dot_tn(h_all, later[:, :used[1]]))
@@ -547,7 +563,7 @@
         later = after(act0, part)
         part = row_major(inv_count * dot_tn(later, cot_all))
         down_rows = [dp_reduce(part)]
-        part = grad_h(1, seq_len, (grad_u0, grad_u1), part, [], F32)
+        part = grad_h(1, seq_len, part, [], F32)
         side = swap(part, 1)
         later = after(act1, part)
         part = row_major(inv_count * dot_tn(later[:, :used[1]], cot_all))
@@ -560,7 +576,7 @@
             blocks = [lax.dynamic_slice_in_dim(rows_of, (my_idx ^ bits) * own_rows, own_rows, axis=0) for bits in range(cp_size)]
             up_got.append(jnp.stack([blocks[0]] + [row_major(swap(row_major(blocks[bits]), bits))
                                                    for bits in range(1, cp_size)]))
-        grad_h_bf = grad_h(0, seq_len, (grad_u0, grad_u1), part, [cot, side, far0, far1], BF16)
+        grad_h_bf = grad_h(0, seq_len, part, [cot, side, far0, far1], BF16)
         grad_w_up = spread_columns(my_idx, up_got, splits)
 
         def block_sum(left, right_t):
@@ -591,30 +607,32 @@
 
         dq0_t, dkv0 = attn_backward(tab, q_t, do_t, o_f32, lse, kv_all, kv_heads, head_dim, 0)
         kv0_block, q0_block = kv_block(dkv0), block_sum(x, dq0_t)
-        kv0_sent, _ = first_sends(kv0_block)
+        kv0_sent, parts_kv = first_sends(kv0_block)
         q0_sent, parts_q = first_sends(q0_block)
         kv0_far, part_kv = second_send(kv0_block, (after(kv0_sent[0], *parts_q), kv0_sent[1]))
         q0_far, part_q = second_send(q0_block, q0_sent)
         do_t = after(do_t, part_kv, part_q)
         dq1_t, dkv1 = attn_backward(tab, q_t, do_t, o_f32, lse, kv_all, kv_heads, head_dim, 1)
         kv1_block, q1_block = kv_block(dkv1), block_sum(x, dq1_t)
-        kv1_sent, _ = first_sends(kv1_block)
+        kv1_sent, parts_kv = first_sends(kv1_block)
         q1_sent, parts_q = first_sends(q1_block)
-        sum_o = after(o_block(0), *parts_q) + o_sent[1] + o_far
-        kv1_far, part_kv = second_send(kv1_block, kv1_sent)
-        q1_far, part_q = second_send(q1_block, q1_sent)
-        grad_oq = dp_reduce(jnp.concatenate([sum_o, q0_block(0) + q0_sent[1] + q0_far], axis=1))
-        later = after(jnp.concatenate([dq0_t, dq1_t], axis=0), part_q, part_kv)
+        kv1_far, part_kv = second_send(kv1_block, (after(kv1_sent[0], *parts_q), kv1_sent[1]))
+        q1_far, part_q = second_send(q1_block, (after(q1_sent[0], part_kv), q1_sent[1]))
+        o_far = after(o_far, part_q)
+        base_o, base_q = o_block(0), q0_block(0)
+        sum_o = base_o + o_sent[1] + o_far
+        grad_oq = dp_reduce(jnp.concatenate([sum_o, base_q + q0_sent[1] + q0_far], axis=1))
+        kv0_own = (kv0_block(0) + kv0_sent[1] + after(kv0_far, part_q)).astype(BF16)
+        kv1_own = (kv1_block(0) + kv1_sent[1] + after(kv1_far, kv0_own)).astype(BF16)
+        dkv_t = jnp.concatenate([jnp.concatenate([part[0, which], part[1, which]], axis=1)
+                                 for which in range(2) for part in (kv0_own, kv1_own)], axis=0)
+        w_block = block_sum(x, dkv_t)
+        w_sent, parts = first_sends(w_block)
+        w_far, part_w = second_send(w_block, w_sent)
+        later = after(jnp.concatenate([dq0_t, dq1_t], axis=0), part_w)
         grad_x = dot_tt(later, w_q)
-        grad_x = grad_h_bf + grad_x
-        dkv_parts = [(kv0_block(0) + kv0_sent[1] + kv0_far).astype(BF16), (kv1_block(0) + kv1_sent[1] + kv1_far).astype(BF16)]
-        dkv_t = jnp.concatenate([jnp.concatenate([part[0, which], part[1, which]], axis=1)
-                                 for which in range(2) for part in dkv_parts], axis=0)
-        w_block = block_sum(x, dkv_t)
-        w_sent, _ = first_sends(w_block)
-        w_far, _ = second_send(w_block, w_sent)
+        grad_x = grad_h_bf + grad_x + dot_tt(after(dkv_t, part_w), w_kv)
         sum_q1 = q1_block(0) + q1_sent[1] + q1_far
-        grad_x = grad_x + dot_tt(dkv_t, w_kv)
         grad_qk = dp_reduce(jnp.concatenate([sum_q1, w_block(0) + w_sent[1] + w_far], axis=1))
         o_width = n_heads * head_dim
         grad_w_down = jnp.concatenate(down_rows, axis=0)

time: 1270 us -> 1270 us (level)
  waiting for transfers between devices: 413 us -> 437 us
    ppermute x37, waiting for transfers between devices: 413 us -> 428 us  [swap(): lax.ppermute(values, 'cp', [(src, src ^ bits) for src in range(cp_size)])]
    pallas_call x1, Pallas kernels: 81.9 us -> 67.3 us  [attn_forward(): pl.pallas_call(functools.partial(attn_fwd_kernel, group, head_dim ** (-0....]
  transfers between devices with their start and end apart: 44 -> 44, of which waited for: 13 -> 15; matrix products, arithmetic and copies ran while one was open for 22% -> 21% of each run, Pallas kernels for 37% -> 36%
where the time goes in v5:
time: 1270 us
  Pallas kernels  469 us (37%)
  waiting for transfers between devices  437 us (34%)
  matrix products  235 us (19%)
  local copies, waits for them, and re-layouts  44 us (3%)
  other arithmetic  33.6 us (3%)
  between operations  24.9 us (2%)
  starting transfers between devices  21.5 us (2%)
    ppermute x37, waiting for transfers between devices, swap(): lax.ppermute(values, 'cp', [(src, src ^ bits) for src in range(cp_size)])  428 us
    pallas_call x8, Pallas kernels, ff_forward(): pl.pallas_call(functools.partial(ff_kernel, FF_ROWS, copies, index * toke...  165 us
    dot_general x4, matrix products, dot_tn(): lax.dot_general(lhs, rhs, (((0,), (0,)), ((), ())), preferred_element_typ...  124 us
    pallas_call x2, Pallas kernels, attn_backward(): pl.pallas_call(functools.partial(attn_bwd_kernel, group, head_dim ** (-0....  119 us
    dot_general x21, matrix products, dot_tt(): lax.dot_general(lhs, rhs, (((0,), (1,)), ((), ())), preferred_element_typ...  107 us
    pallas_call x6, Pallas kernels, grad_h_block(): pl.pallas_call(functools.partial(grad_h_kernel, len(up)), grid=(d_model /...  90.3 us
    pallas_call x1, Pallas kernels, attn_forward(): pl.pallas_call(functools.partial(attn_fwd_kernel, group, head_dim ** (-0....  67.3 us
  transfers between devices with their start and end apart: 44, of which 15 were waited for; matrix products, arithmetic and copies ran while one was open for 21% of the time, Pallas kernels for 36%

profile of v5, /device:TPU:0, one launch (start us, length us, event | category | flops | bytes accessed | tf_op | source)
XLA Modules:
  0.0 1265.6 jit_solution(12691879993740923837)
XLA Ops:
  29.5 21.2 %shard_map.135 = (bf16[2048,1280]{1,0:T(8,128)(2,1)}, bf16[2048,1536]{1,0:T(8,128)(2,1)}, bf16[1280,2048]{1,0:T(8,128)(2,1)}, bf16[1536,2048]{1,0:T(8,128)(2,1)}) custom-call(s32[3,8]{1,0:T(4,128)} %pad_add_fusion.1.idx_ref, bf16[2048,11008]{1,0:T(8,128)(2,1)} %refs_34_.1, bf16[2048,11008]{1,0:T(8,128)(2,1)} %refs_34_.1, bf16[2048,11008]{1,0:T(8,128)(2,1)} %refs_34_.1, ...), custom_call_target="tpu_custom_call" | custom-call | flops 46137344 | bytes 51904512 | tf_op jit(solution)/shard_map/pallas_call | solution.py:315
  50.8 12.6 fusion.26.q_ref
  63.4 9.5 all-gather.2.cloned.1.call-done.k_ref.v_ref
  73.0 67.3 %shard_map.136 = (f32[2048,1024]{1,0:T(8,128)}, bf16[2048,1024]{1,0:T(8,128)(2,1)}, f32[2,8,1024]{2,1,0:T(8,128)}) custom-call(s32[4,9]{1,0:T(4,128)} %pad_add_fusion.tab, bf16[2048,1024]{1,0:T(8,128)(2,1)} %fusion.26.q_ref, bf16[4096,512]{1,0:T(8,128)(2,1)} %all-gather.2.cloned.1.call-done.k_ref.v_ref, ...), custom_call_target="tpu_custom_call" | custom-call | flops 19327352832 | bytes 25165824 | tf_op jit(solution)/shard_map/pallas_call | solution.py:120
  140.3 14.0 %add_convert_fusion.1.refs_0_ = bf16[1024,2048]{1,0:T(8,128)(2,1)} fusion(bf16[1,1024,2048]{2,1,0:T(8,128)(2,1)S(1)} %copy-done.8, bf16[2048,1024]{1,0:T(8,128)(2,1)} %get-tuple-element.78, bf16[256,8,16,128]{3,2,1,0:T(8,128)(2,1)} %bitcast.213), kind=kOutput, calls=%fused_computation.17 | convolution fusion | flops 8596226048 | bytes 20971520 | tf_op jit(solution)/shard_map/dot_general | solution.py:38
  156.3 19.3 %shard_map.137 = (bf16[4096,1280]{1,0:T(8,128)(2,1)}, bf16[4096,1280]{1,0:T(8,128)(2,1)}, bf16[4096,2048]{1,0:T(8,128)(2,1)}, bf16[4096,2048]{1,0:T(8,128)(2,1)}) custom-call(bf16[1024,2048]{1,0:T(8,128)(2,1)} %add_convert_fusion.1.refs_0_, bf16[1024,2048]{1,0:T(8,128)(2,1)} %bitcast.192, bf16[2048,1280]{1,0:T(8,128)(2,1)} %get-tuple-element.76.refs_2_.refs_4_.refs_1_, ...), custom_call_target="tpu_custom_call" | custom-call | flops 10737418240 | bytes 27262976 | tf_op jit(solution)/shard_map/pallas_call | solution.py:393
  176.0 19.2 %shard_map.138 = (bf16[4096,1280]{1,0:T(8,128)(2,1)}, bf16[4096,1280]{1,0:T(8,128)(2,1)}, bf16[4096,2048]{1,0:T(8,128)(2,1)}, bf16[4096,2048]{1,0:T(8,128)(2,1)}) custom-call(bf16[1024,2048]{1,0:T(8,128)(2,1)} %collective-permute-done.2.refs_0_, ...), custom_call_target="tpu_custom_call", output_to_operand_aliasing={{0}: (4, {}), {1}: (5, {}), {2}: (6, {}), {3}: (7, {})} | custom-call | flops 10737418240 | bytes 27262976 | tf_op jit(solution)/shard_map/pallas_call | solution.py:393
  195.2 21.8 %shard_map.139 = (bf16[4096,1536]{1,0:T(8,128)(2,1)}, bf16[4096,1536]{1,0:T(8,128)(2,1)}) custom-call(bf16[1024,2048]{1,0:T(8,128)(2,1)} %add_convert_fusion.1.refs_0_, bf16[1024,2048]{1,0:T(8,128)(2,1)} %bitcast.193, bf16[2048,1536]{1,0:T(8,128)(2,1)} %get-tuple-element.87.refs_2_.refs_4_.refs_3_, bf16[1536,2048]{1,0:T(8,128)(2,1)} %get-tuple-element.88.refs_3_.refs_5_), custom_call_target="tpu_custom_call" | custom-call | flops 12884901888 | bytes 29360128 | tf_op jit(solution)/shard_map/pallas_call | solution.py:393
  217.0 6.6 collective-permute-done.1.refs_0_
  229.0 19.2 %shard_map.140 = (bf16[4096,1280]{1,0:T(8,128)(2,1)}, bf16[4096,1280]{1,0:T(8,128)(2,1)}, bf16[4096,2048]{1,0:T(8,128)(2,1)}, bf16[4096,2048]{1,0:T(8,128)(2,1)}) custom-call(bf16[512,2048]{1,0:T(8,128)(2,1)} %collective-permute-done.1.refs_0_, ...), custom_call_target="tpu_custom_call", output_to_operand_aliasing={{0}: (6, {}), {1}: (7, {}), {2}: (8, {}), {3}: (9, {})} | custom-call | flops 10737418240 | bytes 27262976 | tf_op jit(solution)/shard_map/pallas_call | solution.py:393
  248.2 21.9 %shard_map.141 = (bf16[4096,1536]{1,0:T(8,128)(2,1)}, bf16[4096,1536]{1,0:T(8,128)(2,1)}) custom-call(bf16[512,2048]{1,0:T(8,128)(2,1)} %collective-permute-done.1.refs_0_, bf16[1024,2048]{1,0:T(8,128)(2,1)} %collective-permute-done.4.refs_1_, bf16[512,2048]{1,0:T(8,128)(2,1)} %collective-permute-done.5.refs_2_, ...), custom_call_target="tpu_custom_call", output_to_operand_aliasing={{0}: (6, {}), {1}: (7, {})} | custom-call | flops 12884901888 | bytes 29360128 | tf_op jit(solution)/shard_map/pallas_call | solution.py:393
  270.1 11.8 shard_map.142
  282.5 9.6 collective-permute-done.7.refs_2_
  293.5 19.2 %shard_map.143 = (bf16[4096,1280]{1,0:T(8,128)(2,1)}, bf16[4096,1280]{1,0:T(8,128)(2,1)}, bf16[4096,2048]{1,0:T(8,128)(2,1)}, bf16[4096,2048]{1,0:T(8,128)(2,1)}) custom-call(bf16[512,2048]{1,0:T(8,128)(2,1)} %copy-done.4, ...), custom_call_target="tpu_custom_call", output_to_operand_aliasing={{0}: (6, {}), {1}: (7, {}), {2}: (8, {}), {3}: (9, {})} | custom-call | flops 10737418240 | bytes 27262976 | tf_op jit(solution)/shard_map/pallas_call | solution.py:393
  312.7 14.4 %shard_map.144 = f32[512,2048]{1,0:T(8,128)} custom-call(bf16[4096,1280]{1,0:T(8,128)(2,1)} %get-tuple-element.111.refs_0_, bf16[2048,1280]{1,0:T(8,128)(2,1)} %get-tuple-element.76.refs_2_.refs_4_.refs_1_, bf16[4096,1536]{1,0:T(8,128)(2,1)} %get-tuple-element.110.refs_2_.refs_7_, bf16[2048,1536]{1,0:T(8,128)(2,1)} %get-tuple-element.87.refs_2_.refs_4_.refs_3_, ...), custom_call_target="tpu_custom_call" | custom-call | flops 5905580032 | bytes 18612224 | tf_op jit(solution)/shard_map/pallas_call | solution.py:429
  327.1 26.4 %convolution_multiply_fusion.1 = f32[2048,1280]{1,0:T(8,128)} fusion(bf16[4096,2048]{1,0:T(8,128)(2,1)} %get-tuple-element.108, bf16[4096,1280]{1,0:T(8,128)(2,1)S(1)} %copy-done.2), kind=kOutput, calls=%fused_computation.6 | convolution fusion | flops 21477457920 | bytes 37748736 | tf_op jit(solution)/shard_map/dot_general | solution.py:34
  353.5 22.1 %shard_map.145 = (bf16[4096,1536]{1,0:T(8,128)(2,1)}, bf16[4096,1536]{1,0:T(8,128)(2,1)}) custom-call(bf16[512,2048]{1,0:T(8,128)(2,1)} %copy-done.4, bf16[1024,2048]{1,0:T(8,128)(2,1)} %collective-permute-done.4.refs_1_, bf16[512,2048]{1,0:T(8,128)(2,1)} %copy-done.5, bf16[1024,2048]{1,0:T(8,128)(2,1)} %copy-done.3, ...), custom_call_target="tpu_custom_call", output_to_operand_aliasing={{0}: (6, {}), {1}: (7, {})} | custom-call | flops 12884901888 | bytes 29360128 | tf_op jit(solution)/shard_map/pallas_call | solution.py:393
  375.7 11.8 shard_map.146
  388.0 22.1 %shard_map.147 = (bf16[4096,1536]{1,0:T(8,128)(2,1)}, bf16[4096,1536]{1,0:T(8,128)(2,1)}) custom-call(bf16[1024,2048]{1,0:T(8,128)(2,1)} %collective-permute-done.2.refs_0_, bf16[1024,2048]{1,0:T(8,128)(2,1)} %collective-permute-done.3.refs_1_, ...), custom_call_target="tpu_custom_call", output_to_operand_aliasing={{0}: (4, {}), {1}: (5, {})} | custom-call | flops 12884901888 | bytes 29360128 | tf_op jit(solution)/shard_map/pallas_call | solution.py:393
  410.0 13.8 %shard_map.148 = f32[512,2048]{1,0:T(8,128)} custom-call(bf16[4096,1280]{1,0:T(8,128)(2,1)} %get-tuple-element.111.refs_0_, bf16[2048,1280]{1,0:T(8,128)(2,1)} %get-tuple-element.76.refs_2_.refs_4_.refs_1_, bf16[4096,1536]{1,0:T(8,128)(2,1)} %get-tuple-element.125.refs_2_, bf16[2048,1536]{1,0:T(8,128)(2,1)} %get-tuple-element.87.refs_2_.refs_4_.refs_3_, ...), custom_call_target="tpu_custom_call" | custom-call | flops 5905580032 | bytes 18612224 | tf_op jit(solution)/shard_map/pallas_call | solution.py:429
  423.9 34.5 %fusion.7 = f32[2048,1472]{1,0:T(8,128)} fusion(bf16[4096,2048]{1,0:T(8,128)(2,1)} %get-tuple-element.108, bf16[4096,1536]{1,0:T(8,128)(2,1)} %get-tuple-element.125.refs_2_), kind=kOutput, calls=%fused_computation.7 | convolution fusion | flops 24699076608 | bytes 41418752 | tf_op jit(solution)/shard_map/dot_general | solution.py:34
  458.5 29.7 %convolution_multiply_fusion = f32[1280,2048]{1,0:T(8,128)} fusion(bf16[4096,1280]{1,0:T(8,128)(2,1)} %get-tuple-element.121, bf16[4096,2048]{1,0:T(8,128)(2,1)} %get-tuple-element.122), kind=kOutput, calls=%fused_computation.5 | convolution fusion | flops 21477457920 | bytes 37748736 | tf_op jit(solution)/shard_map/dot_general | solution.py:34
  491.1 17.7 %shard_map.149 = f32[1024,2048]{1,0:T(8,128)} custom-call(bf16[4096,1280]{1,0:T(8,128)(2,1)} %get-tuple-element.111.refs_0_, bf16[2048,1280]{1,0:T(8,128)(2,1)S(1)} %copy-done, bf16[4096,1536]{1,0:T(8,128)(2,1)} %get-tuple-element.125.refs_2_, bf16[2048,1536]{1,0:T(8,128)(2,1)} %get-tuple-element.87.refs_2_.refs_4_.refs_3_), custom_call_target="tpu_custom_call" | custom-call | flops 11811160064 | bytes 25690112 | tf_op jit(solution)/shard_map/pallas_call | solution.py:429
  511.4 33.8 %fusion.4 = f32[1472,2048]{1,0:T(8,128)} fusion(bf16[4096,2048]{1,0:T(8,128)(2,1)} %get-tuple-element.122, bf16[4096,1536]{1,0:T(8,128)(2,1)} %get-tuple-element.124), kind=kOutput, calls=%fused_computation.4 | convolution fusion | flops 24699076608 | bytes 41418752 | tf_op jit(solution)/shard_map/dot_general | solution.py:34
  545.4 57.7 %collective-permute-done.11.refs_6_ = f32[512,2048]{1,0:T(8,128)} collective-permute-done((f32[512,2048]{1,0:T(8,128)}, f32[512,2048]{1,0:T(8,128)}, u32[]{:S(2)}, u32[]{:S(2)}) %collective-permute-start.11) | collective-permute-done | bytes 4194336 | tf_op jit(solution)/shard_map/ppermute | solution.py:469
  603.2 89.0 %collective-permute-done.12.refs_7_ = f32[512,2048]{1,0:T(8,128)} collective-permute-done((f32[512,2048]{1,0:T(8,128)}, f32[512,2048]{1,0:T(8,128)}, u32[]{:S(2)}, u32[]{:S(2)}) %collective-permute-start.12) | collective-permute-done | bytes 4194336 | tf_op jit(solution)/shard_map/ppermute | solution.py:469
  692.2 20.8 %shard_map.150 = bf16[1024,2048]{1,0:T(8,128)(2,1)S(1)} custom-call(bf16[4096,1280]{1,0:T(8,128)(2,1)} %get-tuple-element.111.refs_0_, bf16[2048,1280]{1,0:T(8,128)(2,1)} %get-tuple-element.76.refs_2_.refs_4_.refs_1_, bf16[4096,1536]{1,0:T(8,128)(2,1)} %get-tuple-element.125.refs_2_, bf16[2048,1536]{1,0:T(8,128)(2,1)} %get-tuple-element.87.refs_2_.refs_4_.refs_3_, ...), custom_call_target="tpu_custom_call" | custom-call | flops 11811160064 | bytes 25690112 | tf_op jit(solution)/shard_map/pallas_call | solution.py:429
  717.1 4.4 convolution_multiply_fusion.3
  723.9 4.4 convolution_multiply_fusion.2
  730.6 13.3 %convert_bitcast_fusion.do_ref = bf16[2048,1024]{1,0:T(8,128)(2,1)} fusion(bf16[1024,2048]{1,0:T(8,128)(2,1)S(1)} %shard_map.150, bf16[256,8,16,128]{3,2,1,0:T(8,128)(2,1)} %bitcast.214), kind=kOutput, calls=%fused_computation.31 | convolution fusion | flops 8592031744 | bytes 16777216 | tf_op jit(solution)/shard_map/dot_general | solution.py:38
  747.2 59.4 %shard_map.151 = (bf16[1024,1024]{1,0:T(8,128)(2,1)}, f32[8,2,128,512]{3,2,1,0:T(8,128)}) custom-call(s32[4,9]{1,0:T(4,128)} %pad_add_fusion.tab, bf16[2048,1024]{1,0:T(8,128)(2,1)} %fusion.26.q_ref, bf16[2048,1024]{1,0:T(8,128)(2,1)} %convert_bitcast_fusion.do_ref, f32[2048,1024]{1,0:T(8,128)} %get-tuple-element.130.of_ref, ...), custom_call_target="tpu_custom_call" | custom-call | flops 24159191040 | bytes 12582912 | tf_op jit(solution)/shard_map/pallas_call | solution.py:206
  806.6 4.2 convolution_multiply_fusion.7
  821.0 4.2 multiply_add_fusion.2
  825.2 59.5 %shard_map.152 = (bf16[1024,1024]{1,0:T(8,128)(2,1)}, f32[8,2,128,512]{3,2,1,0:T(8,128)}) custom-call(s32[4,9]{1,0:T(4,128)} %pad_add_fusion.tab, bf16[2048,1024]{1,0:T(8,128)(2,1)} %fusion.26.q_ref, bf16[2048,1024]{1,0:T(8,128)(2,1)} %convert_bitcast_fusion.do_ref, f32[2048,1024]{1,0:T(8,128)} %get-tuple-element.130.of_ref, ...), custom_call_target="tpu_custom_call" | custom-call | flops 24159191040 | bytes 12582912 | tf_op jit(solution)/shard_map/pallas_call | solution.py:206
  884.8 4.4 convolution_multiply_fusion.5
  901.3 15.9 %collective-permute-done.17 = f32[2,2,128,512]{3,2,1,0:T(8,128)} collective-permute-done((f32[2,2,128,512]{3,2,1,0:T(8,128)}, f32[2,2,128,512]{3,2,1,0:T(8,128)}, u32[]{:S(2)}, u32[]{:S(2)}) %collective-permute-start.17) | collective-permute-done | bytes 1048608 | tf_op jit(solution)/shard_map/ppermute | solution.py:469
  919.4 19.8 %collective-permute-done.21 = f32[2,2,128,512]{3,2,1,0:T(8,128)} collective-permute-done((f32[2,2,128,512]{3,2,1,0:T(8,128)}, f32[2,2,128,512]{3,2,1,0:T(8,128)}, u32[]{:S(2)}, u32[]{:S(2)}) %collective-permute-start.21) | collective-permute-done | bytes 1048608 | tf_op jit(solution)/shard_map/ppermute | solution.py:469
  949.5 64.0 %collective-permute-done.30 = f32[512,512]{1,0:T(8,128)S(1)} collective-permute-done((f32[512,512]{1,0:T(8,128)S(1)}, f32[512,512]{1,0:T(8,128)S(1)}, u32[]{:S(2)}, u32[]{:S(2)}) %collective-permute-start.30) | collective-permute-done | bytes 1048608 | tf_op jit(solution)/shard_map/ppermute | solution.py:469
  1020.1 5.0 fusion.66
  1026.4 84.8 %collective-permute-done.24 = f32[512,2048]{1,0:T(8,128)S(1)} collective-permute-done((f32[512,2048]{1,0:T(8,128)}, f32[512,2048]{1,0:T(8,128)S(1)}, u32[]{:S(2)}, u32[]{:S(2)}) %collective-permute-start.24) | collective-permute-done | bytes 4194336 | tf_op jit(solution)/shard_map/ppermute | solution.py:469
  1111.2 43.6 %collective-permute-done.26 = f32[512,1024]{1,0:T(8,128)S(1)} collective-permute-done((f32[512,1024]{1,0:T(8,128)}, f32[512,1024]{1,0:T(8,128)S(1)}, u32[]{:S(2)}, u32[]{:S(2)}) %collective-permute-start.26) | collective-permute-done | bytes 2097184 | tf_op jit(solution)/shard_map/ppermute | solution.py:469
  1166.9 12.7 %collective-permute-done.33 = f32[128,1280]{1,0:T(8,128)S(1)} collective-permute-done((f32[128,1280]{1,0:T(8,128)S(1)}, f32[128,1280]{1,0:T(8,128)S(1)}, u32[]{:S(2)}, u32[]{:S(2)}) %collective-permute-start.33) | collective-permute-done | bytes 655392 | tf_op jit(solution)/shard_map/ppermute | solution.py:469
  1179.6 14.0 %collective-permute-done.32 = f32[128,1280]{1,0:T(8,128)S(1)} collective-permute-done((f32[128,1280]{1,0:T(8,128)S(1)}, f32[128,1280]{1,0:T(8,128)S(1)}, u32[]{:S(2)}, u32[]{:S(2)}) %collective-permute-start.32) | collective-permute-done | bytes 655392 | tf_op jit(solution)/shard_map/ppermute | solution.py:469
  1196.1 5.7 fusion.89
  1209.2 17.3 %fusion.22 = bf16[1,1024,2048]{2,1,0:T(8,128)(2,1)} fusion(f32[1024,2048]{1,0:T(8,128)} %fusion.89, bf16[1024,2048]{1,0:T(8,128)(2,1)} %copy-done.1, bf16[2048,1024]{1,0:T(8,128)(2,1)} %pad_maximum_fusion.2, bf16[256,8,16,128]{3,2,1,0:T(8,128)(2,1)} %bitcast.216), kind=kOutput, calls=%fused_computation.24 | convolution fusion | flops 8598323200 | bytes 29360128 | tf_op jit(solution)/shard_map/dot_general | solution.py:38
  1226.5 6.0 pad_maximum_fusion.1
  1232.7 7.9 collective-permute-done.35
  1245.2 6.9 shard_map.153
  (260 shorter events, 116.2 us)
Async XLA Ops:
  7.2 65.8 %all-gather.2.cloned.1.call-start = ((), (), s32[]{:S(2)}) async-start(), calls=%async_computation.6 | async-start | bytes 5242880 | tf_op jit(solution)/shard_map/all_gather | solution.py:504
  14.8 1145.6 %reduce-scatter.11.cloned.1.call-start = ((), (), s32[]{:S(2)}) async-start(), calls=%async_computation.9 | async-start | bytes 13107200 | tf_op jit(solution)/shard_map/reduce_scatter | solution.py:472
  14.9 161.1 %collective-permute-start.3 = (bf16[1024,2048]{1,0:T(8,128)(2,1)}, bf16[1024,2048]{1,0:T(8,128)(2,1)}, u32[]{:S(2)}, u32[]{:S(2)}) collective-permute-start(bf16[1024,2048]{1,0:T(8,128)(2,1)} %bitcast.190), channel_id=1, source_target_pairs={{0,1},{1,0},{2,3},{3,2},{4,5},{5,4},{6,7},{7,6},{8,9},{9,8},{10,11... | collective-permute-start | bytes 12582920 | tf_op jit(solution)/shard_map/ppermute | solution.py:469
  16.3 159.5 %collective-permute-start.4 = (bf16[1024,2048]{1,0:T(8,128)(2,1)}, bf16[1024,2048]{1,0:T(8,128)(2,1)}, u32[]{:S(2)}, u32[]{:S(2)}) collective-permute-start(bf16[1024,2048]{1,0:T(8,128)(2,1)} %bitcast.191), channel_id=1, source_target_pairs={{0,2},{1,3},{2,0},{3,1},{4,6},{5,7},{6,4},{7,5},{8,10},{9,11},{10,... | collective-permute-start | bytes 12582920 | tf_op jit(solution)/shard_map/ppermute | solution.py:469
  154.3 21.7 %collective-permute-start.2 = (bf16[1024,2048]{1,0:T(8,128)(2,1)}, bf16[1024,2048]{1,0:T(8,128)(2,1)}, u32[]{:S(2)}, u32[]{:S(2)}) collective-permute-start(bf16[1024,2048]{1,0:T(8,128)(2,1)} %add_convert_fusion.1.refs_0_), channel_id=1, source_target_pairs={{0,1},{1,0},{2,3},{3,2},{4,5},{5,4},{6,7},{7,6},{8,9},{9,8},{10,11... | collective-permute-start | bytes 12582920 | tf_op jit(solution)/shard_map/ppermute | solution.py:469
  175.6 48.0 %collective-permute-start.1 = (bf16[512,2048]{1,0:T(8,128)(2,1)S(1)}, bf16[512,2048]{1,0:T(8,128)(2,1)}, u32[]{:S(2)}, u32[]{:S(2)}) collective-permute-start(bf16[512,2048]{1,0:T(8,128)(2,1)S(1)} %slice.88), channel_id=1, source_target_pairs={{0,2},{1,3},{2,0},{3,1},{4,6},{5,7},{6,4},{7,5},{8,10},{9,11},{10,... | collective-permute-start | bytes 6291464 | tf_op jit(solution)/shard_map/ppermute | solution.py:469
  175.8 51.3 %collective-permute-start.6 = (bf16[1024,2048]{1,0:T(8,128)(2,1)}, bf16[1024,2048]{1,0:T(8,128)(2,1)S(1)}, u32[]{:S(2)}, u32[]{:S(2)}) collective-permute-start(bf16[1024,2048]{1,0:T(8,128)(2,1)} %collective-permute-done.4.refs_1_), channel_id=1, source_target_pairs={{0,1},{1,0},{2,3},{3,2},{4,5},{5,4},{6,7},{7,6},{8,9},{9,8},{10,11... | collective-permute-start | bytes 12582920 | tf_op jit(solution)/shard_map/ppermute | solution.py:469
  223.6 4.5 collective-permute-start.5
  226.8 55.4 %collective-permute-start = (bf16[512,2048]{1,0:T(8,128)(2,1)}, bf16[512,2048]{1,0:T(8,128)(2,1)S(1)}, u32[]{:S(2)}, u32[]{:S(2)}) collective-permute-start(bf16[512,2048]{1,0:T(8,128)(2,1)} %slice.71), channel_id=1, source_target_pairs={{0,2},{1,3},{2,0},{3,1},{4,6},{5,7},{6,4},{7,5},{8,10},{9,11},{10,... | collective-permute-start | bytes 6291464 | tf_op jit(solution)/shard_map/ppermute | solution.py:469
  281.9 30.7 %collective-permute-start.8 = (f32[512,2048]{1,0:T(8,128)S(1)}, f32[512,2048]{1,0:T(8,128)}, u32[]{:S(2)}, u32[]{:S(2)}) collective-permute-start(f32[512,2048]{1,0:T(8,128)S(1)} %shard_map.142), channel_id=1, source_target_pairs={{0,1},{1,0},{2,3},{3,2},{4,5},{5,4},{6,7},{7,6},{8,9},{9,8},{10,11... | collective-permute-start | bytes 12582920 | tf_op jit(solution)/shard_map/ppermute | solution.py:469
  282.2 9.9 collective-permute-start.7
  353.5 848.3 %reduce-scatter.13.cloned.1.call-start = ((), (), s32[]{:S(2)}) async-start(), calls=%async_computation.10 | async-start | bytes 15728640 | tf_op jit(solution)/shard_map/reduce_scatter | solution.py:472
  387.5 22.6 %collective-permute-start.9 = (f32[512,2048]{1,0:T(8,128)S(1)}, f32[512,2048]{1,0:T(8,128)}, u32[]{:S(2)}, u32[]{:S(2)}) collective-permute-start(f32[512,2048]{1,0:T(8,128)S(1)} %shard_map.146), channel_id=1, source_target_pairs={{0,1},{1,0},{2,3},{3,2},{4,5},{5,4},{6,7},{7,6},{8,9},{9,8},{10,11... | collective-permute-start | bytes 12582920 | tf_op jit(solution)/shard_map/ppermute | solution.py:469
  458.4 768.0 %reduce-scatter.15.cloned.1.call-start = ((), (), s32[]{:S(2)}) async-start(), calls=%async_computation.11 | async-start | bytes 13107200 | tf_op jit(solution)/shard_map/reduce_scatter | solution.py:472
  488.2 738.3 %reduce-scatter.17.cloned.1.call-start = ((), (), s32[]{:S(2)}) async-start(), calls=%async_computation.12 | async-start | bytes 15073280 | tf_op jit(solution)/shard_map/reduce_scatter | solution.py:472
  508.8 183.4 %collective-permute-start.10 = (f32[1024,2048]{1,0:T(8,128)}, f32[1024,2048]{1,0:T(8,128)}, u32[]{:S(2)}, u32[]{:S(2)}) collective-permute-start(f32[1024,2048]{1,0:T(8,128)} %shard_map.149), channel_id=1, source_target_pairs={{0,1},{1,0},{2,3},{3,2},{4,5},{5,4},{6,7},{7,6},{8,9},{9,8},{10,11... | collective-permute-start | bytes 25165832 | tf_op jit(solution)/shard_map/ppermute | solution.py:469
  509.4 93.8 %collective-permute-start.11 = (f32[512,2048]{1,0:T(8,128)}, f32[512,2048]{1,0:T(8,128)}, u32[]{:S(2)}, u32[]{:S(2)}) collective-permute-start(f32[512,2048]{1,0:T(8,128)} %shard_map.144), channel_id=1, source_target_pairs={{0,2},{1,3},{2,0},{3,1},{4,6},{5,7},{6,4},{7,5},{8,10},{9,11},{10,... | collective-permute-start | bytes 12582920 | tf_op jit(solution)/shard_map/ppermute | solution.py:469
  511.2 181.0 %collective-permute-start.12 = (f32[512,2048]{1,0:T(8,128)}, f32[512,2048]{1,0:T(8,128)}, u32[]{:S(2)}, u32[]{:S(2)}) collective-permute-start(f32[512,2048]{1,0:T(8,128)} %shard_map.148), channel_id=1, source_target_pairs={{0,2},{1,3},{2,0},{3,1},{4,6},{5,7},{6,4},{7,5},{8,10},{9,11},{10,... | collective-permute-start | bytes 12582920 | tf_op jit(solution)/shard_map/ppermute | solution.py:469
  545.3 706.8 %reduce-scatter.9.cloned.1.call-start = ((), (), s32[]{:S(2)}) async-start(), calls=%async_computation.8 | async-start | bytes 3932160 | tf_op jit(solution)/shard_map/reduce_scatter | solution.py:472
  721.5 22.4 %collective-permute-start.13 = (f32[512,2048]{1,0:T(8,128)}, f32[512,2048]{1,0:T(8,128)S(1)}, u32[]{:S(2)}, u32[]{:S(2)}) collective-permute-start(f32[512,2048]{1,0:T(8,128)} %convolution_multiply_fusion.3), channel_id=1, source_target_pairs={{0,1},{1,0},{2,3},{3,2},{4,5},{5,4},{6,7},{7,6},{8,9},{9,8},{10,11... | collective-permute-start | bytes 12582920 | tf_op jit(solution)/shard_map/ppermute | solution.py:469
  723.9 82.8 %copy-start.43 = (bf16[1024,128]{1,0:T(8,128)(2,1)}, bf16[1024,128]{1,0:T(8,128)(2,1)S(1)}, u32[]{:S(2)}) copy-start(bf16[1024,128]{1,0:T(8,128)(2,1)S(1)} %get-tuple-element.171) | copy-start | bytes 786436
  723.9 82.8 %copy-start.46 = (bf16[1024,128]{1,0:T(8,128)(2,1)}, bf16[1024,128]{1,0:T(8,128)(2,1)S(1)}, u32[]{:S(2)}) copy-start(bf16[1024,128]{1,0:T(8,128)(2,1)S(1)} %get-tuple-element.172) | copy-start | bytes 786436
  723.9 82.8 %copy-start.49 = (bf16[1024,128]{1,0:T(8,128)(2,1)}, bf16[1024,128]{1,0:T(8,128)(2,1)S(1)}, u32[]{:S(2)}) copy-start(bf16[1024,128]{1,0:T(8,128)(2,1)S(1)} %get-tuple-element.173) | copy-start | bytes 786436
  723.9 82.7 %copy-start.52 = (bf16[1024,128]{1,0:T(8,128)(2,1)}, bf16[1024,128]{1,0:T(8,128)(2,1)S(1)}, u32[]{:S(2)}) copy-start(bf16[1024,128]{1,0:T(8,128)(2,1)S(1)} %get-tuple-element.174) | copy-start | bytes 786436
  810.8 10.1 collective-permute-start.15
  813.9 4.2 collective-permute-start.14
  889.1 11.8 collective-permute-start.18
  890.4 4.8 collective-permute-start.19
  890.8 26.4 %collective-permute-start.16 = (f32[2,2,128,512]{3,2,1,0:T(8,128)S(1)}, f32[2,2,128,512]{3,2,1,0:T(8,128)}, u32[]{:S(2)}, u32[]{:S(2)}) collective-permute-start(f32[2,2,128,512]{3,2,1,0:T(8,128)S(1)} %get-tuple-element.179), channel_id=1, source_target_pairs={{0,1},{1,0},{2,3},{3,2},{4,5},{5,4},{6,7},{7,6},{8,9},{9,8},{10,11... | collective-permute-start | bytes 3145736 | tf_op jit(solution)/shard_map/ppermute | solution.py:469
  890.9 26.3 %collective-permute-start.17 = (f32[2,2,128,512]{3,2,1,0:T(8,128)}, f32[2,2,128,512]{3,2,1,0:T(8,128)}, u32[]{:S(2)}, u32[]{:S(2)}) collective-permute-start(f32[2,2,128,512]{3,2,1,0:T(8,128)} %bitcast_add_fusion.3), channel_id=1, source_target_pairs={{0,2},{1,3},{2,0},{3,1},{4,6},{5,7},{6,4},{7,5},{8,10},{9,11},{10,... | collective-permute-start | bytes 3145736 | tf_op jit(solution)/shard_map/ppermute | solution.py:469
  896.4 42.8 %collective-permute-start.21 = (f32[2,2,128,512]{3,2,1,0:T(8,128)}, f32[2,2,128,512]{3,2,1,0:T(8,128)}, u32[]{:S(2)}, u32[]{:S(2)}) collective-permute-start(f32[2,2,128,512]{3,2,1,0:T(8,128)} %bitcast_add_fusion.1), channel_id=1, source_target_pairs={{0,2},{1,3},{2,0},{3,1},{4,6},{5,7},{6,4},{7,5},{8,10},{9,11},{10,... | collective-permute-start | bytes 3145736 | tf_op jit(solution)/shard_map/ppermute | solution.py:469
  897.7 41.6 %collective-permute-start.20 = (f32[2,2,128,512]{3,2,1,0:T(8,128)}, f32[2,2,128,512]{3,2,1,0:T(8,128)S(1)}, u32[]{:S(2)}, u32[]{:S(2)}) collective-permute-start(f32[2,2,128,512]{3,2,1,0:T(8,128)} %get-tuple-element.177), channel_id=1, source_target_pairs={{0,1},{1,0},{2,3},{3,2},{4,5},{5,4},{6,7},{7,6},{8,9},{9,8},{10,11... | collective-permute-start | bytes 3145736 | tf_op jit(solution)/shard_map/ppermute | solution.py:469
  942.3 3.3 collective-permute-start.22
  943.0 71.3 %collective-permute-start.27 = (f32[512,1024]{1,0:T(8,128)S(1)}, f32[512,1024]{1,0:T(8,128)S(1)}, u32[]{:S(2)}, u32[]{:S(2)}) collective-permute-start(f32[512,1024]{1,0:T(8,128)S(1)} %copy-done.55), channel_id=1, source_target_pairs={{0,1},{1,0},{2,3},{3,2},{4,5},{5,4},{6,7},{7,6},{8,9},{9,8},{10,11... | collective-permute-start | bytes 6291464 | tf_op jit(solution)/shard_map/ppermute | solution.py:469
  943.0 71.3 %collective-permute-start.28 = (f32[512,1024]{1,0:T(8,128)S(1)}, f32[512,1024]{1,0:T(8,128)S(1)}, u32[]{:S(2)}, u32[]{:S(2)}) collective-permute-start(f32[512,1024]{1,0:T(8,128)S(1)} %multiply_add_fusion.1), channel_id=1, source_target_pairs={{0,2},{1,3},{2,0},{3,1},{4,6},{5,7},{6,4},{7,5},{8,10},{9,11},{10,... | collective-permute-start | bytes 6291464 | tf_op jit(solution)/shard_map/ppermute | solution.py:469
  945.3 4.2 collective-permute-start.29
  946.4 67.2 %collective-permute-start.30 = (f32[512,512]{1,0:T(8,128)S(1)}, f32[512,512]{1,0:T(8,128)S(1)}, u32[]{:S(2)}, u32[]{:S(2)}) collective-permute-start(f32[512,512]{1,0:T(8,128)S(1)} %fusion.42), channel_id=1, source_target_pairs={{0,2},{1,3},{2,0},{3,1},{4,6},{5,7},{6,4},{7,5},{8,10},{9,11},{10,... | collective-permute-start | bytes 3145736 | tf_op jit(solution)/shard_map/ppermute | solution.py:469
  1017.2 237.4 %reduce-scatter.7.cloned.1.call-start = ((), (), s32[]{:S(2)}) async-start(), calls=%async_computation.7 | async-start | bytes 7864320 | tf_op jit(solution)/shard_map/reduce_scatter | solution.py:472
  1017.5 93.7 %collective-permute-start.24 = (f32[512,2048]{1,0:T(8,128)}, f32[512,2048]{1,0:T(8,128)S(1)}, u32[]{:S(2)}, u32[]{:S(2)}) collective-permute-start(f32[512,2048]{1,0:T(8,128)} %multiply_add_fusion), channel_id=1, source_target_pairs={{0,2},{1,3},{2,0},{3,1},{4,6},{5,7},{6,4},{7,5},{8,10},{9,11},{10,... | collective-permute-start | bytes 12582920 | tf_op jit(solution)/shard_map/ppermute | solution.py:469
  1018.9 136.5 %collective-permute-start.23 = (f32[512,2048]{1,0:T(8,128)}, f32[512,2048]{1,0:T(8,128)S(1)}, u32[]{:S(2)}, u32[]{:S(2)}) collective-permute-start(f32[512,2048]{1,0:T(8,128)} %convolution_multiply_fusion.2), channel_id=1, source_target_pairs={{0,1},{1,0},{2,3},{3,2},{4,5},{5,4},{6,7},{7,6},{8,9},{9,8},{10,11... | collective-permute-start | bytes 12582920 | tf_op jit(solution)/shard_map/ppermute | solution.py:469
  1018.9 92.2 %collective-permute-start.25 = (f32[512,1024]{1,0:T(8,128)}, f32[512,1024]{1,0:T(8,128)S(1)}, u32[]{:S(2)}, u32[]{:S(2)}) collective-permute-start(f32[512,1024]{1,0:T(8,128)} %convolution_multiply_fusion.6), channel_id=1, source_target_pairs={{0,1},{1,0},{2,3},{3,2},{4,5},{5,4},{6,7},{7,6},{8,9},{9,8},{10,11... | collective-permute-start | bytes 6291464 | tf_op jit(solution)/shard_map/ppermute | solution.py:469
  1019.5 135.3 %collective-permute-start.26 = (f32[512,1024]{1,0:T(8,128)}, f32[512,1024]{1,0:T(8,128)S(1)}, u32[]{:S(2)}, u32[]{:S(2)}) collective-permute-start(f32[512,1024]{1,0:T(8,128)} %multiply_add_fusion.2), channel_id=1, source_target_pairs={{0,2},{1,3},{2,0},{3,1},{4,6},{5,7},{6,4},{7,5},{8,10},{9,11},{10,... | collective-permute-start | bytes 6291464 | tf_op jit(solution)/shard_map/ppermute | solution.py:469
  1162.5 17.1 %collective-permute-start.33 = (f32[128,1280]{1,0:T(8,128)S(1)}, f32[128,1280]{1,0:T(8,128)S(1)}, u32[]{:S(2)}, u32[]{:S(2)}) collective-permute-start(f32[128,1280]{1,0:T(8,128)S(1)} %get-tuple-element.186), channel_id=1, source_target_pairs={{0,3},{1,2},{2,1},{3,0},{4,7},{5,6},{6,5},{7,4},{8,11},{9,10},{10,... | collective-permute-start | bytes 1966088 | tf_op jit(solution)/shard_map/ppermute | solution.py:469
  1162.6 31.0 %collective-permute-start.32 = (f32[128,1280]{1,0:T(8,128)S(1)}, f32[128,1280]{1,0:T(8,128)S(1)}, u32[]{:S(2)}, u32[]{:S(2)}) collective-permute-start(f32[128,1280]{1,0:T(8,128)S(1)} %get-tuple-element.187), channel_id=1, source_target_pairs={{0,2},{1,3},{2,0},{3,1},{4,6},{5,7},{6,4},{7,5},{8,10},{9,11},{10,... | collective-permute-start | bytes 1966088 | tf_op jit(solution)/shard_map/ppermute | solution.py:469
  1164.0 29.6 %collective-permute-start.31 = (f32[128,1280]{1,0:T(8,128)S(1)}, f32[128,1280]{1,0:T(8,128)S(1)}, u32[]{:S(2)}, u32[]{:S(2)}) collective-permute-start(f32[128,1280]{1,0:T(8,128)S(1)} %get-tuple-element.188), channel_id=1, source_target_pairs={{0,1},{1,0},{2,3},{3,2},{4,5},{5,4},{6,7},{7,6},{8,9},{9,8},{10,11... | collective-permute-start | bytes 1966088 | tf_op jit(solution)/shard_map/ppermute | solution.py:469
  1205.0 27.5 %collective-permute-start.36 = (f32[128,1472]{0,1:T(8,128)}, f32[128,1472]{0,1:T(8,128)S(1)}, u32[]{:S(2)}, u32[]{:S(2)}) collective-permute-start(f32[128,1472]{0,1:T(8,128)} %copy.43), channel_id=1, source_target_pairs={{0,3},{1,2},{2,1},{3,0},{4,7},{5,6},{6,5},{7,4},{8,11},{9,10},{10,... | collective-permute-start | bytes 2261000 | tf_op jit(solution)/shard_map/ppermute | solution.py:469
  1206.5 34.0 %collective-permute-start.35 = (f32[128,1472]{0,1:T(8,128)}, f32[128,1472]{0,1:T(8,128)}, u32[]{:S(2)}, u32[]{:S(2)}) collective-permute-start(f32[128,1472]{0,1:T(8,128)} %copy.41), channel_id=1, source_target_pairs={{0,2},{1,3},{2,0},{3,1},{4,6},{5,7},{6,4},{7,5},{8,10},{9,11},{10,... | collective-permute-start | bytes 2261000 | tf_op jit(solution)/shard_map/ppermute | solution.py:469
  1209.1 32.8 %collective-permute-start.34 = (f32[128,1472]{0,1:T(8,128)}, f32[128,1472]{0,1:T(8,128)}, u32[]{:S(2)}, u32[]{:S(2)}) collective-permute-start(f32[128,1472]{0,1:T(8,128)} %copy.39), channel_id=1, source_target_pairs={{0,1},{1,0},{2,3},{3,2},{4,5},{5,4},{6,7},{7,6},{8,9},{9,8},{10,11... | collective-permute-start | bytes 2261000 | tf_op jit(solution)/shard_map/ppermute | solution.py:469
  (54 other events, 510.2 us)
Sparse Core Ops, SparseCore 0:
  15.0 57.9 all-gather.1
  353.6 100.9 reduce-scatter.10
  458.5 118.2 reduce-scatter.12
  579.8 99.7 reduce-scatter.14
  682.5 112.5 reduce-scatter.16
  1017.3 41.6 reduce-scatter.8
  1160.5 67.7 reduce-scatter.6

commit v6 on v5

--- a/solution.py
+++ b/solution.py
@@ -136,11 +136,12 @@
     )(tab, q_t, kv_all, kv_all)
 
 
-def attn_bwd_kernel(group, scale, tab, q_ref, do_ref, of_ref, lse_ref, k_ref, v_ref, dq_ref, dkv_ref, delta_ref, acc_ref):
+def attn_bwd_kernel(group, first_head, scale, tab, q_ref, do_ref, of_ref, lse_ref, k_ref, v_ref, *refs):
     dim = k_ref.shape[1]
     half = q_ref.shape[1] // 2
     factor = scale * LOG2E
-    dkv_ref[...] = jnp.zeros(dkv_ref.shape, F32)
+    dq_ref, dkv_ref, delta_ref, acc_ref = refs[-4:]
+    dkv_ref[...] = refs[0][...] if len(refs) > 4 else jnp.zeros(dkv_ref.shape, F32)
 
     def pair_step(pair, carry):
         cols = pl.ds(pl.multiple_of(tab[0, pair] * half, half), half)
@@ -173,7 +174,7 @@
                 if head + 1 < group:
                     following = products(head + 1)
                 rows = slice(head * dim, (head + 1) * dim)
-                probs = jnp.exp2(scores * factor - lse_ref[0, head:head + 1, cols])
+                probs = jnp.exp2(scores * factor - lse_ref[0, first_head + head:first_head + head + 1, cols])
                 grad_s = (probs * (grad_p - delta_ref[head:head + 1, :])).astype(BF16)
                 grad_v = grad_v + dot_nt(do_ref[rows, cols], probs.astype(BF16))
                 grad_k = grad_k + dot_nt(q_ref[rows, cols], grad_s)
@@ -195,32 +196,35 @@
     lax.fori_loop(0, tab.shape[1], pair_step, 0)
 
 
-def attn_backward(tab, q_t, do_t, o_f32, lse, kv_all, kv_heads, head_dim, kv_head):
+def attn_backward(tab, q_t, do_t, o_f32, lse, kv_all, kv_heads, head_dim, kv_head, piece=0, n_pieces=1, carry=()):
     width, seq = q_t.shape
     half = seq // 2
     group = width // (kv_heads * head_dim)
-    rows = group * head_dim
+    heads = group // n_pieces
+    rows = heads * head_dim
     n_slots = kv_all.shape[0] // half
     n_pairs = tab.shape[1]
-    q_spec = pl.BlockSpec((rows, seq), lambda p, t: (kv_head, 0))
+    q_spec = pl.BlockSpec((rows, seq), lambda p, t: (kv_head * n_pieces + piece, 0))
+    dkv_spec = pl.BlockSpec((n_slots, 2, head_dim, half), lambda p, t: (0, 0, 0, 0))
     return pl.pallas_call(
-        functools.partial(attn_bwd_kernel, group, head_dim ** -0.5),
+        functools.partial(attn_bwd_kernel, heads, piece * heads, head_dim ** -0.5),
         grid_spec=pltpu.PrefetchScalarGridSpec(
             num_scalar_prefetch=1,
             grid=(1,),
             in_specs=[q_spec, q_spec, q_spec,
                       pl.BlockSpec((1, group, seq), lambda p, t: (kv_head, 0, 0)),
                       pl.BlockSpec((kv_all.shape[0], head_dim), lambda p, t: (0, kv_head)),
-                      pl.BlockSpec((kv_all.shape[0], head_dim), lambda p, t: (0, kv_heads + kv_head))],
+                      pl.BlockSpec((kv_all.shape[0], head_dim), lambda p, t: (0, kv_heads + kv_head))]
+            + [dkv_spec] * len(carry),
             out_specs=[pl.BlockSpec((rows, seq), lambda p, t: (0, 0)),
-                       pl.BlockSpec((n_slots, 2, head_dim, half), lambda p, t: (0, 0, 0, 0))],
-            scratch_shapes=[pltpu.VMEM((group, half), F32), pltpu.VMEM((rows, half), F32)]),
+                       dkv_spec],
+            scratch_shapes=[pltpu.VMEM((heads, half), F32), pltpu.VMEM((rows, half), F32)]),
         out_shape=[jax.ShapeDtypeStruct((rows, seq), BF16),
                    jax.ShapeDtypeStruct((n_slots, 2, head_dim, half), F32)],
         compiler_params=pltpu.CompilerParams(vmem_limit_bytes=56 * 2 ** 20),
         cost_estimate=pl.CostEstimate(flops=10 * rows * half * half * n_pairs,
-                                      bytes_accessed=12 * rows * seq, transcendentals=group * half * half * n_pairs),
-    )(tab, q_t, do_t, o_f32, lse, kv_all, kv_all)
+                                      bytes_accessed=12 * rows * seq, transcendentals=heads * half * half * n_pairs),
+    )(tab, q_t, do_t, o_f32, lse, kv_all, kv_all, *carry)
 
 
 def gelu_parts(values):
@@ -503,14 +507,15 @@
         kv_own = dot_nn(x, w_kv).astype(BF16)
         kv_all = lax.all_gather(kv_own, 'cp', axis=0, tiled=True)
         cot_near = swap(cot, 1)
-        q_t = dot_tt(w_q, x).astype(BF16)
 
         first_part = FF_TILE * (dp_size * ff_part // (2 * FF_TILE)) // dp_size
         splits = ((0, first_part), (first_part, ff_part - first_part))
         used = [dp_size * count for _, count in splits]
         starts = (jnp.arange(dp_size) * cp_size + my_idx) * ff_part
-        cot_far = swap(after(cot, tab), 2)
         w_up_own, w_down_own = prepare(starts, splits, w_up, w_down)
+        cot_far = swap(after(cot, w_up_own[0]), 2)
+        later = after(x, w_up_own[0])
+        q_t = dot_tt(w_q, later).astype(BF16)
 
         kv_all = after(kv_all, q_t, w_up_own[0])
         o_f32, o_t, lse = attn_forward(tab, q_t, kv_all, kv_heads, head_dim)
@@ -518,6 +523,7 @@
         h_act = (x + dot_tt(o_t, w_o)).astype(BF16)
         h_far0 = swap(h_act[:half], 2)
         h_near = swap(h_act, 1)
+        o_near = swap(o_t, 1)
 
         def ff_call(index, part, pieces, carry, *earlier):
             first = after(pieces[0][0], *earlier) if earlier else pieces[0][0]
@@ -541,25 +547,27 @@
             later = after(grad_u1, earlier)
             return grad_h_block(index, tokens, (state[1], later), w_up_own, extras, dtype)
 
-        part = grad_h(5, half, act1, [], F32)
+        h_far1 = after(h_far1, act1)
+        block = remote(1, h_far1)
+        o_far = swap(after(o_t, h_far1), 2)
+        state = ff_call(3, 0, block, state, act1)
+        o_last = swap(o_far, 1)
+        act0, grad_u0, h_all, cot_all = state
+        part = row_major(inv_count * dot_tn(h_all, grad_u0))
+        up_rows = [dp_reduce(part)]
+        part = grad_h(5, half, part, [], F32)
         near0 = swap(part, 1)
-        block = remote(1, after(h_far1, act1))
-        state = ff_call(3, 0, block, state, part)
-        part = grad_h(4, half, state[0], [near0], F32)
+        act1, grad_u1 = ff_call(3, 1, block, (act1, grad_u1), part)
+        part = grad_h(4, half, act1, [near0], F32)
         far0 = swap(part, 2)
-        act0, grad_u0, h_all, cot_all = state
-        later = after(grad_u0, part)
-        part = row_major(inv_count * dot_tn(h_all, later))
-        up_rows = [dp_reduce(part)]
-        act1, grad_u1 = ff_call(3, 1, block, (act1, grad_u1), part)
+        act1, grad_u1 = ff_call(1, 1, near, (act1, grad_u1), part)
         part = grad_h(7, half, act1, [], F32)
         near1 = swap(part, 1)
-        act1, grad_u1 = ff_call(1, 1, near, (act1, grad_u1), part)
-        part = grad_h(6, half, act1, [near1], F32)
-        far1 = swap(part, 2)
         later = after(grad_u1, part)
         part = row_major(inv_count * dot_tn(h_all, later[:, :used[1]]))
         up_rows.append(dp_reduce(part))
+        part = grad_h(6, half, part, [near1], F32)
+        far1 = swap(part, 2)
         later = after(act0, part)
         part = row_major(inv_count * dot_tn(later, cot_all))
         down_rows = [dp_reduce(part)]
@@ -593,13 +601,9 @@
             part = block(2) + sent[0]
             return swap(part, 2), part
 
-        o_block = block_sum(grad_h_bf, o_t)
-        o_sent, parts = first_sends(o_block)
-        later = after(grad_h_bf, *parts)
-        do_t = dot_tt(w_o, later).astype(BF16)
-        o_sent = (after(o_sent[0], do_t), o_sent[1])
-        o_far, part = second_send(o_block, o_sent)
-        do_t = after(do_t, part)
+        mine = [own_cols(grad_h_bf, bits) for bits in range(cp_size)]
+        mine = [mine[0]] + [swap(mine[bits], bits) for bits in range(1, cp_size)]
+        do_t = dot_tt(w_o, grad_h_bf).astype(BF16)
 
         def kv_block(dkv):
             blocks = dkv.reshape((cp_size, 2) + dkv.shape[1:])
@@ -612,30 +616,37 @@
         kv0_far, part_kv = second_send(kv0_block, (after(kv0_sent[0], *parts_q), kv0_sent[1]))
         q0_far, part_q = second_send(q0_block, q0_sent)
         do_t = after(do_t, part_kv, part_q)
-        dq1_t, dkv1 = attn_backward(tab, q_t, do_t, o_f32, lse, kv_all, kv_heads, head_dim, 1)
-        kv1_block, q1_block = kv_block(dkv1), block_sum(x, dq1_t)
+        dq1_t, dkv1 = attn_backward(tab, q_t, do_t, o_f32, lse, kv_all, kv_heads, head_dim, 1, 0, 2)
+        q1_block = block_sum(x, dq1_t)
+        q1_sent, parts_q = first_sends(q1_block)
+        base_q = q0_block(0)
+        sum_o = sum(dot_tt(cols, rows_t) for cols, rows_t in zip(mine, (o_t, o_near, o_far, o_last))) * inv_count
+        q1_far, part_q = second_send(q1_block, (after(q1_sent[0], sum_o, base_q), q1_sent[1]))
+        do_t = after(do_t, part_q, *parts_q)
+        dq2_t, dkv1 = attn_backward(tab, q_t, do_t, o_f32, lse, kv_all, kv_heads, head_dim, 1, 1, 2, (dkv1,))
+        kv1_block, q2_block = kv_block(dkv1), block_sum(x, dq2_t)
         kv1_sent, parts_kv = first_sends(kv1_block)
-        q1_sent, parts_q = first_sends(q1_block)
+        q2_sent, parts_q = first_sends(q2_block)
         kv1_far, part_kv = second_send(kv1_block, (after(kv1_sent[0], *parts_q), kv1_sent[1]))
-        q1_far, part_q = second_send(q1_block, (after(q1_sent[0], part_kv), q1_sent[1]))
-        o_far = after(o_far, part_q)
-        base_o, base_q = o_block(0), q0_block(0)
-        sum_o = base_o + o_sent[1] + o_far
-        grad_oq = dp_reduce(jnp.concatenate([sum_o, base_q + q0_sent[1] + q0_far], axis=1))
+        q2_far, part_q = second_send(q2_block, (after(q2_sent[0], part_kv), q2_sent[1]))
+        q0_far = after(q0_far, part_q)
+        sum_q0 = base_q + q0_sent[1] + q0_far
+        grad_oq = dp_reduce(jnp.concatenate([sum_o, sum_q0], axis=1))
         kv0_own = (kv0_block(0) + kv0_sent[1] + after(kv0_far, part_q)).astype(BF16)
         kv1_own = (kv1_block(0) + kv1_sent[1] + after(kv1_far, kv0_own)).astype(BF16)
         dkv_t = jnp.concatenate([jnp.concatenate([part[0, which], part[1, which]], axis=1)
                                  for which in range(2) for part in (kv0_own, kv1_own)], axis=0)
         w_block = block_sum(x, dkv_t)
-        w_sent, parts = first_sends(w_block)
+        w_sent, _ = first_sends(w_block)
         w_far, part_w = second_send(w_block, w_sent)
-        later = after(jnp.concatenate([dq0_t, dq1_t], axis=0), part_w)
+        later = jnp.concatenate([after(dq0_t, part_w), dq1_t, dq2_t], axis=0)
         grad_x = dot_tt(later, w_q)
         grad_x = grad_h_bf + grad_x + dot_tt(after(dkv_t, part_w), w_kv)
-        sum_q1 = q1_block(0) + q1_sent[1] + q1_far
-        grad_qk = dp_reduce(jnp.concatenate([sum_q1, w_block(0) + w_sent[1] + w_far], axis=1))
+        sum_q1 = q1_block(0) + q1_sent[1] + after(q1_far, part_w)
+        sum_q2 = q2_block(0) + q2_sent[1] + after(q2_far, part_w)
+        grad_qk = dp_reduce(jnp.concatenate([sum_q1, sum_q2, w_block(0) + w_sent[1] + w_far], axis=1))
+        grad_w_down = jnp.concatenate(down_rows, axis=0)
         o_width = n_heads * head_dim
-        grad_w_down = jnp.concatenate(down_rows, axis=0)
 
         grad_w_q = jnp.concatenate([grad_oq[:, o_width:], grad_qk[:, :rows]], axis=1).reshape(own_rows, n_heads, head_dim)
         grad_w_k = grad_qk[:, rows:rows + kv_width].reshape(own_rows, kv_heads, head_dim)

time: 1270 us -> 1480 us (1.17)
  waiting for transfers between devices: 437 us -> 624 us
    reduce_scatter x6, waiting for transfers between devices: 0.03 us -> 176 us  [dp_reduce(): return lax.psum_scatter(grad, 'dp', scatter_dimension=0, tiled=True)]
    ppermute x37 -> x43, waiting for transfers between devices: 428 us -> 447 us  [swap(): lax.ppermute(values, 'cp', [(src, src ^ bits) for src in range(cp_size)])]
    pallas_call x2 -> x3, Pallas kernels: 119 us -> 127 us  [attn_backward(): pl.pallas_call(functools.partial(attn_bwd_kernel, heads, piece * heads, h...]
    dot_general x21 -> x25, matrix products: 107 us -> 115 us  [dot_tt(): lax.dot_general(lhs, rhs, (((0,), (1,)), ((), ())), preferred_element_typ...]
  transfers between devices with their start and end apart: 44 -> 50, of which waited for: 15 -> 19; matrix products, arithmetic and copies ran while one was open for 21% -> 18% of each run, Pallas kernels for 36% -> 31%
where the time goes in v6:
time: 1480 us; the launch traced here: 1470 us
  waiting for transfers between devices  624 us (42%)
  Pallas kernels  479 us (32%)
  matrix products  243 us (16%)
  local copies, waits for them, and re-layouts  43.2 us (3%)
  other arithmetic  29.6 us (2%)
  between operations  24.8 us (2%)
  starting transfers between devices  22.3 us (2%)
    ppermute x43, waiting for transfers between devices, swap(): lax.ppermute(values, 'cp', [(src, src ^ bits) for src in range(cp_size)])  447 us
    reduce_scatter x6, waiting for transfers between devices, dp_reduce(): return lax.psum_scatter(grad, 'dp', scatter_dimension=0, tiled=True)  176 us
    pallas_call x8, Pallas kernels, ff_forward(): pl.pallas_call(functools.partial(ff_kernel, FF_ROWS, copies, index * toke...  165 us
    pallas_call x3, Pallas kernels, attn_backward(): pl.pallas_call(functools.partial(attn_bwd_kernel, heads, piece * heads, h...  127 us
    dot_general x4, matrix products, dot_tn(): lax.dot_general(lhs, rhs, (((0,), (0,)), ((), ())), preferred_element_typ...  125 us
    dot_general x25, matrix products, dot_tt(): lax.dot_general(lhs, rhs, (((0,), (1,)), ((), ())), preferred_element_typ...  115 us
    pallas_call x6, Pallas kernels, grad_h_block(): pl.pallas_call(functools.partial(grad_h_kernel, len(up)), grid=(d_model /...  91.2 us
    pallas_call x1, Pallas kernels, attn_forward(): pl.pallas_call(functools.partial(attn_fwd_kernel, group, head_dim ** (-0....  67.3 us
  transfers between devices with their start and end apart: 50, of which 19 were waited for; matrix products, arithmetic and copies ran while one was open for 18% of the time, Pallas kernels for 31%

profile of v6, /device:TPU:0, one launch (start us, length us, event | category | flops | bytes accessed | tf_op | source)
XLA Modules:
  0.0 1466.4 jit_solution(14357535546719421666)
XLA Ops:
  26.4 21.0 %shard_map.135 = (bf16[2048,1280]{1,0:T(8,128)(2,1)}, bf16[2048,1536]{1,0:T(8,128)(2,1)}, bf16[1280,2048]{1,0:T(8,128)(2,1)}, bf16[1536,2048]{1,0:T(8,128)(2,1)}) custom-call(s32[3,8]{1,0:T(4,128)} %pad_add_fusion.1.idx_ref, bf16[2048,11008]{1,0:T(8,128)(2,1)} %refs_34_.1, bf16[2048,11008]{1,0:T(8,128)(2,1)} %refs_34_.1, bf16[2048,11008]{1,0:T(8,128)(2,1)} %refs_34_.1, ...), custom_call_target="tpu_custom_call" | custom-call | flops 46137344 | bytes 51904512 | tf_op jit(solution)/shard_map/pallas_call | solution.py:319
  50.6 14.0 convert_bitcast_fusion.1.q_ref
  64.6 67.3 %shard_map.136 = (f32[2048,1024]{1,0:T(8,128)}, bf16[2048,1024]{1,0:T(8,128)(2,1)}, f32[2,8,1024]{2,1,0:T(8,128)}) custom-call(s32[4,9]{1,0:T(4,128)} %pad_add_fusion.tab, bf16[2048,1024]{1,0:T(8,128)(2,1)} %convert_bitcast_fusion.1.q_ref, bf16[4096,512]{1,0:T(8,128)(2,1)} %all-gather.2.cloned.1.call-done.k_ref.v_ref, ...), custom_call_target="tpu_custom_call" | custom-call | flops 19327352832 | bytes 25165824 | tf_op jit(solution)/shard_map/pallas_call | solution.py:120
  132.0 14.1 add_convert_fusion.1.refs_0_
  148.0 19.3 %shard_map.137 = (bf16[4096,1280]{1,0:T(8,128)(2,1)}, bf16[4096,1280]{1,0:T(8,128)(2,1)}, bf16[4096,2048]{1,0:T(8,128)(2,1)}, bf16[4096,2048]{1,0:T(8,128)(2,1)}) custom-call(bf16[1024,2048]{1,0:T(8,128)(2,1)} %add_convert_fusion.1.refs_0_, bf16[1024,2048]{1,0:T(8,128)(2,1)} %bitcast.28.refs_1_.refs_4_, ...), custom_call_target="tpu_custom_call" | custom-call | flops 10737418240 | bytes 27262976 | tf_op jit(solution)/shard_map/pallas_call | solution.py:397
  167.8 19.2 %shard_map.138 = (bf16[4096,1280]{1,0:T(8,128)(2,1)}, bf16[4096,1280]{1,0:T(8,128)(2,1)}, bf16[4096,2048]{1,0:T(8,128)(2,1)}, bf16[4096,2048]{1,0:T(8,128)(2,1)}) custom-call(bf16[1024,2048]{1,0:T(8,128)(2,1)} %collective-permute-done.2.refs_0_, ...), custom_call_target="tpu_custom_call", output_to_operand_aliasing={{0}: (4, {}), {1}: (5, {}), {2}: (6, {}), {3}: (7, {})} | custom-call | flops 10737418240 | bytes 27262976 | tf_op jit(solution)/shard_map/pallas_call | solution.py:397
  187.1 21.8 %shard_map.139 = (bf16[4096,1536]{1,0:T(8,128)(2,1)}, bf16[4096,1536]{1,0:T(8,128)(2,1)}) custom-call(bf16[1024,2048]{1,0:T(8,128)(2,1)} %add_convert_fusion.1.refs_0_, bf16[1024,2048]{1,0:T(8,128)(2,1)} %bitcast.28.refs_1_.refs_4_, bf16[2048,1536]{1,0:T(8,128)(2,1)} %get-tuple-element.92.refs_2_.refs_4_.refs_3_, ...), custom_call_target="tpu_custom_call" | custom-call | flops 12884901888 | bytes 29360128 | tf_op jit(solution)/shard_map/pallas_call | solution.py:397
  208.9 6.5 collective-permute-done.1.refs_0_
  220.8 19.2 %shard_map.140 = (bf16[4096,1280]{1,0:T(8,128)(2,1)}, bf16[4096,1280]{1,0:T(8,128)(2,1)}, bf16[4096,2048]{1,0:T(8,128)(2,1)}, bf16[4096,2048]{1,0:T(8,128)(2,1)}) custom-call(bf16[512,2048]{1,0:T(8,128)(2,1)} %collective-permute-done.1.refs_0_, ...), custom_call_target="tpu_custom_call", output_to_operand_aliasing={{0}: (6, {}), {1}: (7, {}), {2}: (8, {}), {3}: (9, {})} | custom-call | flops 10737418240 | bytes 27262976 | tf_op jit(solution)/shard_map/pallas_call | solution.py:397
  240.1 22.0 %shard_map.141 = (bf16[4096,1536]{1,0:T(8,128)(2,1)}, bf16[4096,1536]{1,0:T(8,128)(2,1)}) custom-call(bf16[512,2048]{1,0:T(8,128)(2,1)} %collective-permute-done.1.refs_0_, bf16[1024,2048]{1,0:T(8,128)(2,1)} %collective-permute-done.4.refs_1_, bf16[512,2048]{1,0:T(8,128)(2,1)} %collective-permute-done.5.refs_2_, ...), custom_call_target="tpu_custom_call", output_to_operand_aliasing={{0}: (6, {}), {1}: (7, {})} | custom-call | flops 12884901888 | bytes 29360128 | tf_op jit(solution)/shard_map/pallas_call | solution.py:397
  272.3 19.2 %shard_map.142 = (bf16[4096,1280]{1,0:T(8,128)(2,1)}, bf16[4096,1280]{1,0:T(8,128)(2,1)}, bf16[4096,2048]{1,0:T(8,128)(2,1)}, bf16[4096,2048]{1,0:T(8,128)(2,1)}) custom-call(bf16[512,2048]{1,0:T(8,128)(2,1)} %copy-done.4, ...), custom_call_target="tpu_custom_call", output_to_operand_aliasing={{0}: (6, {}), {1}: (7, {}), {2}: (8, {}), {3}: (9, {})} | custom-call | flops 10737418240 | bytes 27262976 | tf_op jit(solution)/shard_map/pallas_call | solution.py:397
  291.5 29.6 %convolution_multiply_fusion.1 = f32[2048,1280]{1,0:T(8,128)} fusion(bf16[4096,2048]{1,0:T(8,128)(2,1)} %get-tuple-element.112, bf16[4096,1280]{1,0:T(8,128)(2,1)} %get-tuple-element.110.refs_0_), kind=kOutput, calls=%fused_computation.6 | convolution fusion | flops 21477457920 | bytes 37748736 | tf_op jit(solution)/shard_map/dot_general | solution.py:34
  321.2 12.1 shard_map.143
  333.5 22.1 %shard_map.144 = (bf16[4096,1536]{1,0:T(8,128)(2,1)}, bf16[4096,1536]{1,0:T(8,128)(2,1)}) custom-call(bf16[512,2048]{1,0:T(8,128)(2,1)} %copy-done.4, bf16[1024,2048]{1,0:T(8,128)(2,1)} %collective-permute-done.4.refs_1_, bf16[512,2048]{1,0:T(8,128)(2,1)} %copy-done.5, bf16[1024,2048]{1,0:T(8,128)(2,1)} %copy-done.2, ...), custom_call_target="tpu_custom_call", output_to_operand_aliasing={{0}: (6, {}), {1}: (7, {})} | custom-call | flops 12884901888 | bytes 29360128 | tf_op jit(solution)/shard_map/pallas_call | solution.py:397
  355.6 13.8 shard_map.145
  369.4 22.2 %shard_map.146 = (bf16[4096,1536]{1,0:T(8,128)(2,1)}, bf16[4096,1536]{1,0:T(8,128)(2,1)}) custom-call(bf16[1024,2048]{1,0:T(8,128)(2,1)} %collective-permute-done.2.refs_0_, bf16[1024,2048]{1,0:T(8,128)(2,1)} %collective-permute-done.3.refs_1_, ...), custom_call_target="tpu_custom_call", output_to_operand_aliasing={{0}: (4, {}), {1}: (5, {})} | custom-call | flops 12884901888 | bytes 29360128 | tf_op jit(solution)/shard_map/pallas_call | solution.py:397
  391.6 13.0 shard_map.147
  405.8 34.9 %fusion.7 = f32[2048,1472]{1,0:T(8,128)} fusion(bf16[4096,2048]{1,0:T(8,128)(2,1)} %get-tuple-element.112, bf16[4096,1536]{1,0:T(8,128)(2,1)} %get-tuple-element.129.refs_2_), kind=kOutput, calls=%fused_computation.7 | convolution fusion | flops 24699076608 | bytes 41418752 | tf_op jit(solution)/shard_map/dot_general | solution.py:34
  440.8 14.8 %shard_map.148 = f32[512,2048]{1,0:T(8,128)} custom-call(bf16[4096,1280]{1,0:T(8,128)(2,1)} %get-tuple-element.110.refs_0_, bf16[2048,1280]{1,0:T(8,128)(2,1)} %get-tuple-element.80.refs_2_.refs_4_.refs_1_, bf16[4096,1536]{1,0:T(8,128)(2,1)} %get-tuple-element.129.refs_2_, bf16[2048,1536]{1,0:T(8,128)(2,1)} %get-tuple-element.92.refs_2_.refs_4_.refs_3_, ...), custom_call_target="tpu_custom_call" | custom-call | flops 5905580032 | bytes 18612224 | tf_op jit(solution)/shard_map/pallas_call | solution.py:433
  455.6 26.3 %convolution_multiply_fusion = f32[1280,2048]{1,0:T(8,128)} fusion(bf16[4096,1280]{1,0:T(8,128)(2,1)S(1)} %bitcast.192, bf16[4096,2048]{1,0:T(8,128)(2,1)} %get-tuple-element.126), kind=kOutput, calls=%fused_computation.5 | convolution fusion | flops 21477457920 | bytes 37748736 | tf_op jit(solution)/shard_map/dot_general | solution.py:34
  484.4 17.6 %shard_map.149 = f32[1024,2048]{1,0:T(8,128)} custom-call(bf16[4096,1280]{1,0:T(8,128)(2,1)} %get-tuple-element.110.refs_0_, bf16[2048,1280]{1,0:T(8,128)(2,1)S(1)} %copy-done, bf16[4096,1536]{1,0:T(8,128)(2,1)} %get-tuple-element.129.refs_2_, bf16[2048,1536]{1,0:T(8,128)(2,1)} %get-tuple-element.92.refs_2_.refs_4_.refs_3_), custom_call_target="tpu_custom_call" | custom-call | flops 11811160064 | bytes 25690112 | tf_op jit(solution)/shard_map/pallas_call | solution.py:433
  508.2 87.5 %collective-permute-done.21 = bf16[2048,1024]{1,0:T(8,128)(2,1)} collective-permute-done((bf16[2048,1024]{1,0:T(8,128)(2,1)}, bf16[2048,1024]{1,0:T(8,128)(2,1)}, u32[]{:S(2)}, u32[]{:S(2)}) %collective-permute-start.21) | collective-permute-done | bytes 4194336 | tf_op jit(solution)/shard_map/ppermute | solution.py:473
  595.9 34.7 %fusion.4 = f32[1472,2048]{1,0:T(8,128)} fusion(bf16[4096,2048]{1,0:T(8,128)(2,1)} %get-tuple-element.126, bf16[4096,1536]{1,0:T(8,128)(2,1)} %get-tuple-element.128), kind=kOutput, calls=%fused_computation.4 | convolution fusion | flops 24699076608 | bytes 41418752 | tf_op jit(solution)/shard_map/dot_general | solution.py:34
  630.5 55.1 %collective-permute-done.11.refs_6_ = f32[512,2048]{1,0:T(8,128)} collective-permute-done((f32[512,2048]{1,0:T(8,128)}, f32[512,2048]{1,0:T(8,128)}, u32[]{:S(2)}, u32[]{:S(2)}) %collective-permute-start.11) | collective-permute-done | bytes 4194336 | tf_op jit(solution)/shard_map/ppermute | solution.py:473
  685.7 89.4 %collective-permute-done.12.refs_7_ = f32[512,2048]{1,0:T(8,128)} collective-permute-done((f32[512,2048]{1,0:T(8,128)}, f32[512,2048]{1,0:T(8,128)}, u32[]{:S(2)}, u32[]{:S(2)}) %collective-permute-start.12) | collective-permute-done | bytes 4194336 | tf_op jit(solution)/shard_map/ppermute | solution.py:473
  775.1 19.9 %shard_map.150 = bf16[1024,2048]{1,0:T(8,128)(2,1)S(1)} custom-call(bf16[4096,1280]{1,0:T(8,128)(2,1)} %get-tuple-element.110.refs_0_, bf16[2048,1280]{1,0:T(8,128)(2,1)} %get-tuple-element.80.refs_2_.refs_4_.refs_1_, bf16[4096,1536]{1,0:T(8,128)(2,1)} %get-tuple-element.129.refs_2_, bf16[2048,1536]{1,0:T(8,128)(2,1)} %get-tuple-element.92.refs_2_.refs_4_.refs_3_, ...), custom_call_target="tpu_custom_call" | custom-call | flops 11811160064 | bytes 25690112 | tf_op jit(solution)/shard_map/pallas_call | solution.py:433
  795.0 14.3 convert_bitcast_fusion.do_ref
  809.3 59.7 %shard_map.151 = (bf16[1024,1024]{1,0:T(8,128)(2,1)}, f32[8,2,128,512]{3,2,1,0:T(8,128)}) custom-call(s32[4,9]{1,0:T(4,128)} %pad_add_fusion.tab, bf16[2048,1024]{1,0:T(8,128)(2,1)} %convert_bitcast_fusion.1.q_ref, bf16[2048,1024]{1,0:T(8,128)(2,1)} %convert_bitcast_fusion.do_ref, f32[2048,1024]{1,0:T(8,128)} %get-tuple-element.131.of_ref, ...), custom_call_target="tpu_custom_call" | custom-call | flops 24159191040 | bytes 12582912 | tf_op jit(solution)/shard_map/pallas_call | solution.py:209
  886.8 12.6 collective-permute-done.20
  899.4 6.5 fusion.64
  906.0 6.9 fusion.63
  915.6 33.1 %shard_map.152 = (bf16[512,1024]{1,0:T(8,128)(2,1)}, f32[8,2,128,512]{3,2,1,0:T(8,128)}) custom-call(s32[4,9]{1,0:T(4,128)} %pad_add_fusion.tab, bf16[2048,1024]{1,0:T(8,128)(2,1)} %convert_bitcast_fusion.1.q_ref, bf16[2048,1024]{1,0:T(8,128)(2,1)} %convert_bitcast_fusion.do_ref, f32[2048,1024]{1,0:T(8,128)} %get-tuple-element.131.of_ref, ...), custom_call_target="tpu_custom_call" | custom-call | flops 12079595520 | bytes 6291456 | tf_op jit(solution)/shard_map/pallas_call | solution.py:209
  951.6 8.3 add_multiply_fusion
  964.1 34.5 %shard_map.153 = (bf16[512,1024]{1,0:T(8,128)(2,1)}, f32[8,2,128,512]{3,2,1,0:T(8,128)}) custom-call(s32[4,9]{1,0:T(4,128)} %pad_add_fusion.tab, bf16[2048,1024]{1,0:T(8,128)(2,1)} %convert_bitcast_fusion.1.q_ref, bf16[2048,1024]{1,0:T(8,128)(2,1)} %convert_bitcast_fusion.do_ref, f32[2048,1024]{1,0:T(8,128)} %get-tuple-element.131.of_ref, ...), custom_call_target="tpu_custom_call" | custom-call | flops 12079595520 | bytes 6291456 | tf_op jit(solution)/shard_map/pallas_call | solution.py:209
  1013.9 14.4 collective-permute-done.15
  1030.5 19.7 %collective-permute-done.27 = f32[2,2,128,512]{3,2,1,0:T(8,128)} collective-permute-done((f32[2,2,128,512]{3,2,1,0:T(8,128)}, f32[2,2,128,512]{3,2,1,0:T(8,128)}, u32[]{:S(2)}, u32[]{:S(2)}) %collective-permute-start.27) | collective-permute-done | bytes 1048608 | tf_op jit(solution)/shard_map/ppermute | solution.py:473
  1057.9 21.8 %collective-permute-done.34 = f32[512,512]{1,0:T(8,128)S(1)} collective-permute-done((f32[512,512]{1,0:T(8,128)S(1)}, f32[512,512]{1,0:T(8,128)S(1)}, u32[]{:S(2)}, u32[]{:S(2)}) %collective-permute-start.34) | collective-permute-done | bytes 1048608 | tf_op jit(solution)/shard_map/ppermute | solution.py:473
  1081.4 20.7 %collective-permute-done.32 = f32[512,512]{1,0:T(8,128)S(1)} collective-permute-done((f32[512,512]{1,0:T(8,128)S(1)}, f32[512,512]{1,0:T(8,128)S(1)}, u32[]{:S(2)}, u32[]{:S(2)}) %collective-permute-start.32) | collective-permute-done | bytes 1048608 | tf_op jit(solution)/shard_map/ppermute | solution.py:473
  1103.8 20.3 %collective-permute-done.36 = f32[512,512]{1,0:T(8,128)S(1)} collective-permute-done((f32[512,512]{1,0:T(8,128)S(1)}, f32[512,512]{1,0:T(8,128)S(1)}, u32[]{:S(2)}, u32[]{:S(2)}) %collective-permute-start.36) | collective-permute-done | bytes 1048608 | tf_op jit(solution)/shard_map/ppermute | solution.py:473
  1130.0 45.6 %collective-permute-done.30 = f32[512,1024]{1,0:T(8,128)S(1)} collective-permute-done((f32[512,1024]{1,0:T(8,128)}, f32[512,1024]{1,0:T(8,128)S(1)}, u32[]{:S(2)}, u32[]{:S(2)}) %collective-permute-start.30) | collective-permute-done | bytes 2097184 | tf_op jit(solution)/shard_map/ppermute | solution.py:473
  1183.3 14.9 %collective-permute-done.39 = f32[128,1280]{1,0:T(8,128)S(1)} collective-permute-done((f32[128,1280]{1,0:T(8,128)S(1)}, f32[128,1280]{1,0:T(8,128)S(1)}, u32[]{:S(2)}, u32[]{:S(2)}) %collective-permute-start.39) | collective-permute-done | bytes 655392 | tf_op jit(solution)/shard_map/ppermute | solution.py:473
  1198.2 14.3 collective-permute-done.38
  1228.4 16.8 %fusion.22 = bf16[1,1024,2048]{2,1,0:T(8,128)(2,1)} fusion(f32[1024,2048]{1,0:T(8,128)} %fusion.65, bf16[1024,2048]{1,0:T(8,128)(2,1)} %copy-done.1, bf16[256,8,16,128]{3,2,1,0:T(8,128)(2,1)} %bitcast.215, bf16[512,1024]{1,0:T(8,128)(2,1)} %get-tuple-element.142, bf16[512,1024]{1,0:T(8,128)(2,1)} %get-tuple-element.137, ...), kind=kOutput, calls=%fused_computation.24 | convolution fusion | flops 8610906112 | bytes 29360128 | tf_op jit(solution)/shard_map/dot_general | solution.py:38
  1245.5 14.3 collective-permute-done.41
  1264.5 6.9 shard_map.154
  1273.8 112.5 %reduce-scatter.17.cloned.1.call-done = f32[368,2048]{1,0:T(8,128)} async-done(((f32[1472,2048]{1,0:T(8,128)}), f32[368,2048]{1,0:T(8,128)}) %reduce-scatter.17.cloned.1.call-update) | async-done | bytes 3014672 | tf_op jit(solution)/shard_map/reduce_scatter | solution.py:476
  1386.4 5.8 pad_maximum_fusion.1
  1392.2 63.4 %reduce-scatter.7.cloned.1.call-done = f32[128,3072]{1,0:T(8,128)} async-done(((f32[512,3072]{1,0:T(8,128)}), f32[128,3072]{1,0:T(8,128)}) %reduce-scatter.7.cloned.1.call-update) | async-done | bytes 1572880 | tf_op jit(solution)/shard_map/reduce_scatter | solution.py:476
  (290 shorter events, 137.2 us)
Async XLA Ops:
  7.2 57.5 %all-gather.2.cloned.1.call-start = ((), (), s32[]{:S(2)}) async-start(), calls=%async_computation.6 | async-start | bytes 5242880 | tf_op jit(solution)/shard_map/all_gather | solution.py:508
  14.8 1164.6 %reduce-scatter.11.cloned.1.call-start = ((), (), s32[]{:S(2)}) async-start(), calls=%async_computation.9 | async-start | bytes 13107200 | tf_op jit(solution)/shard_map/reduce_scatter | solution.py:476
  14.9 152.9 %collective-permute-start.3 = (bf16[1024,2048]{1,0:T(8,128)(2,1)}, bf16[1024,2048]{1,0:T(8,128)(2,1)}, u32[]{:S(2)}, u32[]{:S(2)}) collective-permute-start(bf16[1024,2048]{1,0:T(8,128)(2,1)} %bitcast.28.refs_1_.refs_4_), channel_id=1, source_target_pairs={{0,1},{1,0},{2,3},{3,2},{4,5},{5,4},{6,7},{7,6},{8,9},{9,8},{10,11... | collective-permute-start | bytes 12582920 | tf_op jit(solution)/shard_map/ppermute | solution.py:473
  47.4 120.1 %collective-permute-start.4 = (bf16[1024,2048]{1,0:T(8,128)(2,1)}, bf16[1024,2048]{1,0:T(8,128)(2,1)}, u32[]{:S(2)}, u32[]{:S(2)}) collective-permute-start(bf16[1024,2048]{1,0:T(8,128)(2,1)} %bitcast.28.refs_1_.refs_4_), channel_id=1, source_target_pairs={{0,2},{1,3},{2,0},{3,1},{4,6},{5,7},{6,4},{7,5},{8,10},{9,11},{10,... | collective-permute-start | bytes 12582920 | tf_op jit(solution)/shard_map/ppermute | solution.py:473
  146.1 21.7 %collective-permute-start.2 = (bf16[1024,2048]{1,0:T(8,128)(2,1)}, bf16[1024,2048]{1,0:T(8,128)(2,1)}, u32[]{:S(2)}, u32[]{:S(2)}) collective-permute-start(bf16[1024,2048]{1,0:T(8,128)(2,1)} %add_convert_fusion.1.refs_0_), channel_id=1, source_target_pairs={{0,1},{1,0},{2,3},{3,2},{4,5},{5,4},{6,7},{7,6},{8,9},{9,8},{10,11... | collective-permute-start | bytes 12582920 | tf_op jit(solution)/shard_map/ppermute | solution.py:473
  167.2 48.2 %collective-permute-start.1 = (bf16[512,2048]{1,0:T(8,128)(2,1)S(1)}, bf16[512,2048]{1,0:T(8,128)(2,1)}, u32[]{:S(2)}, u32[]{:S(2)}) collective-permute-start(bf16[512,2048]{1,0:T(8,128)(2,1)S(1)} %slice.88), channel_id=1, source_target_pairs={{0,2},{1,3},{2,0},{3,1},{4,6},{5,7},{6,4},{7,5},{8,10},{9,11},{10,... | collective-permute-start | bytes 6291464 | tf_op jit(solution)/shard_map/ppermute | solution.py:473
  167.5 51.3 %collective-permute-start.6 = (bf16[1024,2048]{1,0:T(8,128)(2,1)}, bf16[1024,2048]{1,0:T(8,128)(2,1)S(1)}, u32[]{:S(2)}, u32[]{:S(2)}) collective-permute-start(bf16[1024,2048]{1,0:T(8,128)(2,1)} %collective-permute-done.4.refs_1_), channel_id=1, source_target_pairs={{0,1},{1,0},{2,3},{3,2},{4,5},{5,4},{6,7},{7,6},{8,9},{9,8},{10,11... | collective-permute-start | bytes 12582920 | tf_op jit(solution)/shard_map/ppermute | solution.py:473
  215.4 4.5 collective-permute-start.5
  218.6 48.3 %collective-permute-start = (bf16[512,2048]{1,0:T(8,128)(2,1)}, bf16[512,2048]{1,0:T(8,128)(2,1)S(1)}, u32[]{:S(2)}, u32[]{:S(2)}) collective-permute-start(bf16[512,2048]{1,0:T(8,128)(2,1)} %slice.71), channel_id=1, source_target_pairs={{0,2},{1,3},{2,0},{3,1},{4,6},{5,7},{6,4},{7,5},{8,10},{9,11},{10,... | collective-permute-start | bytes 6291464 | tf_op jit(solution)/shard_map/ppermute | solution.py:473
  321.1 899.6 %reduce-scatter.13.cloned.1.call-start = ((), (), s32[]{:S(2)}) async-start(), calls=%async_computation.10 | async-start | bytes 15728640 | tf_op jit(solution)/shard_map/reduce_scatter | solution.py:476
  333.2 22.3 %collective-permute-start.8 = (f32[512,2048]{1,0:T(8,128)S(1)}, f32[512,2048]{1,0:T(8,128)}, u32[]{:S(2)}, u32[]{:S(2)}) collective-permute-start(f32[512,2048]{1,0:T(8,128)S(1)} %shard_map.143), channel_id=1, source_target_pairs={{0,1},{1,0},{2,3},{3,2},{4,5},{5,4},{6,7},{7,6},{8,9},{9,8},{10,11... | collective-permute-start | bytes 12582920 | tf_op jit(solution)/shard_map/ppermute | solution.py:473
  404.5 36.2 %collective-permute-start.9 = (f32[512,2048]{1,0:T(8,128)}, f32[512,2048]{1,0:T(8,128)}, u32[]{:S(2)}, u32[]{:S(2)}) collective-permute-start(f32[512,2048]{1,0:T(8,128)} %shard_map.147), channel_id=1, source_target_pairs={{0,1},{1,0},{2,3},{3,2},{4,5},{5,4},{6,7},{7,6},{8,9},{9,8},{10,11... | collective-permute-start | bytes 12582920 | tf_op jit(solution)/shard_map/ppermute | solution.py:473
  502.0 273.1 %collective-permute-start.10 = (f32[1024,2048]{1,0:T(8,128)}, f32[1024,2048]{1,0:T(8,128)}, u32[]{:S(2)}, u32[]{:S(2)}) collective-permute-start(f32[1024,2048]{1,0:T(8,128)} %shard_map.149), channel_id=1, source_target_pairs={{0,1},{1,0},{2,3},{3,2},{4,5},{5,4},{6,7},{7,6},{8,9},{9,8},{10,11... | collective-permute-start | bytes 25165832 | tf_op jit(solution)/shard_map/ppermute | solution.py:473
  502.0 93.8 %collective-permute-start.21 = (bf16[2048,1024]{1,0:T(8,128)(2,1)}, bf16[2048,1024]{1,0:T(8,128)(2,1)}, u32[]{:S(2)}, u32[]{:S(2)}) collective-permute-start(bf16[2048,1024]{1,0:T(8,128)(2,1)} %get-tuple-element.138), channel_id=1, source_target_pairs={{0,2},{1,3},{2,0},{3,1},{4,6},{5,7},{6,4},{7,5},{8,10},{9,11},{10,... | collective-permute-start | bytes 12582920 | tf_op jit(solution)/shard_map/ppermute | solution.py:473
  502.0 183.6 %collective-permute-start.11 = (f32[512,2048]{1,0:T(8,128)}, f32[512,2048]{1,0:T(8,128)}, u32[]{:S(2)}, u32[]{:S(2)}) collective-permute-start(f32[512,2048]{1,0:T(8,128)} %shard_map.145), channel_id=1, source_target_pairs={{0,2},{1,3},{2,0},{3,1},{4,6},{5,7},{6,4},{7,5},{8,10},{9,11},{10,... | collective-permute-start | bytes 12582920 | tf_op jit(solution)/shard_map/ppermute | solution.py:473
  504.0 271.0 %collective-permute-start.12 = (f32[512,2048]{1,0:T(8,128)}, f32[512,2048]{1,0:T(8,128)}, u32[]{:S(2)}, u32[]{:S(2)}) collective-permute-start(f32[512,2048]{1,0:T(8,128)} %shard_map.148), channel_id=1, source_target_pairs={{0,2},{1,3},{2,0},{3,1},{4,6},{5,7},{6,4},{7,5},{8,10},{9,11},{10,... | collective-permute-start | bytes 12582920 | tf_op jit(solution)/shard_map/ppermute | solution.py:473
  508.2 397.8 %collective-permute-start.19 = (bf16[2048,1024]{1,0:T(8,128)(2,1)}, bf16[2048,1024]{1,0:T(8,128)(2,1)}, u32[]{:S(2)}, u32[]{:S(2)}) collective-permute-start(bf16[2048,1024]{1,0:T(8,128)(2,1)} %get-tuple-element.138), channel_id=1, source_target_pairs={{0,1},{1,0},{2,3},{3,2},{4,5},{5,4},{6,7},{7,6},{8,9},{9,8},{10,11... | collective-permute-start | bytes 12582920 | tf_op jit(solution)/shard_map/ppermute | solution.py:473
  595.8 355.8 %collective-permute-start.23 = (bf16[2048,1024]{1,0:T(8,128)(2,1)}, bf16[2048,1024]{1,0:T(8,128)(2,1)}, u32[]{:S(2)}, u32[]{:S(2)}) collective-permute-start(bf16[2048,1024]{1,0:T(8,128)(2,1)} %collective-permute-done.21), channel_id=1, source_target_pairs={{0,1},{1,0},{2,3},{3,2},{4,5},{5,4},{6,7},{7,6},{8,9},{9,8},{10,11... | collective-permute-start | bytes 12582920 | tf_op jit(solution)/shard_map/ppermute | solution.py:473
  595.8 675.6 %reduce-scatter.9.cloned.1.call-start = ((), (), s32[]{:S(2)}) async-start(), calls=%async_computation.8 | async-start | bytes 3932160 | tf_op jit(solution)/shard_map/reduce_scatter | solution.py:476
  871.0 10.8 collective-permute-start.14
  872.6 40.3 %collective-permute-start.16 = (f32[512,1024]{1,0:T(8,128)S(1)}, f32[512,1024]{1,0:T(8,128)S(1)}, u32[]{:S(2)}, u32[]{:S(2)}) collective-permute-start(f32[512,1024]{1,0:T(8,128)S(1)} %convolution_multiply_fusion.4), channel_id=1, source_target_pairs={{0,1},{1,0},{2,3},{3,2},{4,5},{5,4},{6,7},{7,6},{8,9},{9,8},{10,11... | collective-permute-start | bytes 6291464 | tf_op jit(solution)/shard_map/ppermute | solution.py:473
  874.1 25.3 %collective-permute-start.20 = (bf16[1024,512]{1,0:T(8,128)(2,1)S(1)}, bf16[1024,512]{1,0:T(8,128)(2,1)S(1)}, u32[]{:S(2)}, u32[]{:S(2)}) collective-permute-start(bf16[1024,512]{1,0:T(8,128)(2,1)S(1)} %pad_maximum_fusion.9), channel_id=1, source_target_pairs={{0,2},{1,3},{2,0},{3,1},{4,6},{5,7},{6,4},{7,5},{8,10},{9,11},{10,... | collective-permute-start | bytes 3145736 | tf_op jit(solution)/shard_map/ppermute | solution.py:473
  881.8 24.1 %collective-permute-start.18 = (bf16[1024,512]{1,0:T(8,128)(2,1)S(1)}, bf16[1024,512]{1,0:T(8,128)(2,1)S(1)}, u32[]{:S(2)}, u32[]{:S(2)}) collective-permute-start(bf16[1024,512]{1,0:T(8,128)(2,1)S(1)} %pad_maximum_fusion.8), channel_id=1, source_target_pairs={{0,1},{1,0},{2,3},{3,2},{4,5},{5,4},{6,7},{7,6},{8,9},{9,8},{10,11... | collective-permute-start | bytes 3145736 | tf_op jit(solution)/shard_map/ppermute | solution.py:473
  899.4 52.2 %collective-permute-start.22 = (bf16[1024,512]{1,0:T(8,128)(2,1)}, bf16[1024,512]{1,0:T(8,128)(2,1)}, u32[]{:S(2)}, u32[]{:S(2)}) collective-permute-start(bf16[1024,512]{1,0:T(8,128)(2,1)} %pad_maximum_fusion.10), channel_id=1, source_target_pairs={{0,3},{1,2},{2,1},{3,0},{4,7},{5,6},{6,5},{7,4},{8,11},{9,10},{10,... | collective-permute-start | bytes 3145736 | tf_op jit(solution)/shard_map/ppermute | solution.py:473
  951.2 11.7 collective-permute-start.17
  1001.4 5.9 collective-permute-start.25
  1001.8 26.5 %collective-permute-start.13 = (f32[2,2,128,512]{3,2,1,0:T(8,128)S(1)}, f32[2,2,128,512]{3,2,1,0:T(8,128)}, u32[]{:S(2)}, u32[]{:S(2)}) collective-permute-start(f32[2,2,128,512]{3,2,1,0:T(8,128)S(1)} %get-tuple-element.155), channel_id=1, source_target_pairs={{0,1},{1,0},{2,3},{3,2},{4,5},{5,4},{6,7},{7,6},{8,9},{9,8},{10,11... | collective-permute-start | bytes 3145736 | tf_op jit(solution)/shard_map/ppermute | solution.py:473
  1002.0 26.3 %collective-permute-start.15 = (f32[2,2,128,512]{3,2,1,0:T(8,128)}, f32[2,2,128,512]{3,2,1,0:T(8,128)}, u32[]{:S(2)}, u32[]{:S(2)}) collective-permute-start(f32[2,2,128,512]{3,2,1,0:T(8,128)} %bitcast_add_fusion.2), channel_id=1, source_target_pairs={{0,2},{1,3},{2,0},{3,1},{4,6},{5,7},{6,4},{7,5},{8,10},{9,11},{10,... | collective-permute-start | bytes 3145736 | tf_op jit(solution)/shard_map/ppermute | solution.py:473
  1005.5 7.0 collective-permute-start.24
  1009.8 40.5 %collective-permute-start.27 = (f32[2,2,128,512]{3,2,1,0:T(8,128)}, f32[2,2,128,512]{3,2,1,0:T(8,128)}, u32[]{:S(2)}, u32[]{:S(2)}) collective-permute-start(f32[2,2,128,512]{3,2,1,0:T(8,128)} %bitcast_add_fusion.1), channel_id=1, source_target_pairs={{0,2},{1,3},{2,0},{3,1},{4,6},{5,7},{6,4},{7,5},{8,10},{9,11},{10,... | collective-permute-start | bytes 3145736 | tf_op jit(solution)/shard_map/ppermute | solution.py:473
  1010.1 40.2 %collective-permute-start.26 = (f32[2,2,128,512]{3,2,1,0:T(8,128)}, f32[2,2,128,512]{3,2,1,0:T(8,128)}, u32[]{:S(2)}, u32[]{:S(2)}) collective-permute-start(f32[2,2,128,512]{3,2,1,0:T(8,128)} %get-tuple-element.153), channel_id=1, source_target_pairs={{0,1},{1,0},{2,3},{3,2},{4,5},{5,4},{6,7},{7,6},{8,9},{9,8},{10,11... | collective-permute-start | bytes 3145736 | tf_op jit(solution)/shard_map/ppermute | solution.py:473
  1053.6 26.1 %collective-permute-start.34 = (f32[512,512]{1,0:T(8,128)S(1)}, f32[512,512]{1,0:T(8,128)S(1)}, u32[]{:S(2)}, u32[]{:S(2)}) collective-permute-start(f32[512,512]{1,0:T(8,128)S(1)} %add.438), channel_id=1, source_target_pairs={{0,2},{1,3},{2,0},{3,1},{4,6},{5,7},{6,4},{7,5},{8,10},{9,11},{10,... | collective-permute-start | bytes 3145736 | tf_op jit(solution)/shard_map/ppermute | solution.py:473
  1055.4 46.8 %collective-permute-start.32 = (f32[512,512]{1,0:T(8,128)S(1)}, f32[512,512]{1,0:T(8,128)S(1)}, u32[]{:S(2)}, u32[]{:S(2)}) collective-permute-start(f32[512,512]{1,0:T(8,128)S(1)} %copy-done.10), channel_id=1, source_target_pairs={{0,2},{1,3},{2,0},{3,1},{4,6},{5,7},{6,4},{7,5},{8,10},{9,11},{10,... | collective-permute-start | bytes 3145736 | tf_op jit(solution)/shard_map/ppermute | solution.py:473
  1055.6 46.5 %collective-permute-start.33 = (f32[512,512]{1,0:T(8,128)S(1)}, f32[512,512]{1,0:T(8,128)S(1)}, u32[]{:S(2)}, u32[]{:S(2)}) collective-permute-start(f32[512,512]{1,0:T(8,128)S(1)} %copy-done.54), channel_id=1, source_target_pairs={{0,1},{1,0},{2,3},{3,2},{4,5},{5,4},{6,7},{7,6},{8,9},{9,8},{10,11... | collective-permute-start | bytes 3145736 | tf_op jit(solution)/shard_map/ppermute | solution.py:473
  1055.7 47.3 %collective-permute-start.31 = (f32[512,512]{1,0:T(8,128)S(1)}, f32[512,512]{1,0:T(8,128)S(1)}, u32[]{:S(2)}, u32[]{:S(2)}) collective-permute-start(f32[512,512]{1,0:T(8,128)S(1)} %copy-done.53), channel_id=1, source_target_pairs={{0,1},{1,0},{2,3},{3,2},{4,5},{5,4},{6,7},{7,6},{8,9},{9,8},{10,11... | collective-permute-start | bytes 3145736 | tf_op jit(solution)/shard_map/ppermute | solution.py:473
  1057.0 46.7 %collective-permute-start.35 = (f32[512,512]{1,0:T(8,128)S(1)}, f32[512,512]{1,0:T(8,128)S(1)}, u32[]{:S(2)}, u32[]{:S(2)}) collective-permute-start(f32[512,512]{1,0:T(8,128)S(1)} %convolution_multiply_fusion.5), channel_id=1, source_target_pairs={{0,1},{1,0},{2,3},{3,2},{4,5},{5,4},{6,7},{7,6},{8,9},{9,8},{10,11... | collective-permute-start | bytes 3145736 | tf_op jit(solution)/shard_map/ppermute | solution.py:473
  1079.6 44.4 %collective-permute-start.36 = (f32[512,512]{1,0:T(8,128)S(1)}, f32[512,512]{1,0:T(8,128)S(1)}, u32[]{:S(2)}, u32[]{:S(2)}) collective-permute-start(f32[512,512]{1,0:T(8,128)S(1)} %fusion.38), channel_id=1, source_target_pairs={{0,2},{1,3},{2,0},{3,1},{4,6},{5,7},{6,4},{7,5},{8,10},{9,11},{10,... | collective-permute-start | bytes 3145736 | tf_op jit(solution)/shard_map/ppermute | solution.py:473
  1126.8 147.0 %reduce-scatter.15.cloned.1.call-start = ((), (), s32[]{:S(2)}) async-start(), calls=%async_computation.11 | async-start | bytes 13107200 | tf_op jit(solution)/shard_map/reduce_scatter | solution.py:476
  1127.4 259.0 %reduce-scatter.17.cloned.1.call-start = ((), (), s32[]{:S(2)}) async-start(), calls=%async_computation.12 | async-start | bytes 15073280 | tf_op jit(solution)/shard_map/reduce_scatter | solution.py:476
  1127.9 327.7 %reduce-scatter.7.cloned.1.call-start = ((), (), s32[]{:S(2)}) async-start(), calls=%async_computation.7 | async-start | bytes 7864320 | tf_op jit(solution)/shard_map/reduce_scatter | solution.py:476
  1128.2 47.4 %collective-permute-start.30 = (f32[512,1024]{1,0:T(8,128)}, f32[512,1024]{1,0:T(8,128)S(1)}, u32[]{:S(2)}, u32[]{:S(2)}) collective-permute-start(f32[512,1024]{1,0:T(8,128)} %multiply_add_fusion), channel_id=1, source_target_pairs={{0,2},{1,3},{2,0},{3,1},{4,6},{5,7},{6,4},{7,5},{8,10},{9,11},{10,... | collective-permute-start | bytes 6291464 | tf_op jit(solution)/shard_map/ppermute | solution.py:473
  1130.0 45.6 %collective-permute-start.29 = (f32[512,1024]{1,0:T(8,128)}, f32[512,1024]{1,0:T(8,128)S(1)}, u32[]{:S(2)}, u32[]{:S(2)}) collective-permute-start(f32[512,1024]{1,0:T(8,128)} %convolution_multiply_fusion.3), channel_id=1, source_target_pairs={{0,1},{1,0},{2,3},{3,2},{4,5},{5,4},{6,7},{7,6},{8,9},{9,8},{10,11... | collective-permute-start | bytes 6291464 | tf_op jit(solution)/shard_map/ppermute | solution.py:473
  1181.4 16.8 %collective-permute-start.39 = (f32[128,1280]{1,0:T(8,128)S(1)}, f32[128,1280]{1,0:T(8,128)S(1)}, u32[]{:S(2)}, u32[]{:S(2)}) collective-permute-start(f32[128,1280]{1,0:T(8,128)S(1)} %get-tuple-element.194), channel_id=1, source_target_pairs={{0,3},{1,2},{2,1},{3,0},{4,7},{5,6},{6,5},{7,4},{8,11},{9,10},{10,... | collective-permute-start | bytes 1966088 | tf_op jit(solution)/shard_map/ppermute | solution.py:473
  1181.5 31.0 %collective-permute-start.38 = (f32[128,1280]{1,0:T(8,128)S(1)}, f32[128,1280]{1,0:T(8,128)S(1)}, u32[]{:S(2)}, u32[]{:S(2)}) collective-permute-start(f32[128,1280]{1,0:T(8,128)S(1)} %get-tuple-element.195), channel_id=1, source_target_pairs={{0,2},{1,3},{2,0},{3,1},{4,6},{5,7},{6,4},{7,5},{8,10},{9,11},{10,... | collective-permute-start | bytes 1966088 | tf_op jit(solution)/shard_map/ppermute | solution.py:473
  1183.2 29.3 %collective-permute-start.37 = (f32[128,1280]{1,0:T(8,128)S(1)}, f32[128,1280]{1,0:T(8,128)S(1)}, u32[]{:S(2)}, u32[]{:S(2)}) collective-permute-start(f32[128,1280]{1,0:T(8,128)S(1)} %get-tuple-element.196), channel_id=1, source_target_pairs={{0,1},{1,0},{2,3},{3,2},{4,5},{5,4},{6,7},{7,6},{8,9},{9,8},{10,11... | collective-permute-start | bytes 1966088 | tf_op jit(solution)/shard_map/ppermute | solution.py:473
  1224.2 21.0 %collective-permute-start.42 = (f32[128,1472]{0,1:T(8,128)}, f32[128,1472]{0,1:T(8,128)S(1)}, u32[]{:S(2)}, u32[]{:S(2)}) collective-permute-start(f32[128,1472]{0,1:T(8,128)} %copy.49), channel_id=1, source_target_pairs={{0,3},{1,2},{2,1},{3,0},{4,7},{5,6},{6,5},{7,4},{8,11},{9,10},{10,... | collective-permute-start | bytes 2261000 | tf_op jit(solution)/shard_map/ppermute | solution.py:473
  1225.9 33.9 %collective-permute-start.41 = (f32[128,1472]{0,1:T(8,128)}, f32[128,1472]{0,1:T(8,128)}, u32[]{:S(2)}, u32[]{:S(2)}) collective-permute-start(f32[128,1472]{0,1:T(8,128)} %copy.47), channel_id=1, source_target_pairs={{0,2},{1,3},{2,0},{3,1},{4,6},{5,7},{6,4},{7,5},{8,10},{9,11},{10,... | collective-permute-start | bytes 2261000 | tf_op jit(solution)/shard_map/ppermute | solution.py:473
  1228.0 33.3 %collective-permute-start.40 = (f32[128,1472]{0,1:T(8,128)}, f32[128,1472]{0,1:T(8,128)}, u32[]{:S(2)}, u32[]{:S(2)}) collective-permute-start(f32[128,1472]{0,1:T(8,128)} %copy.45), channel_id=1, source_target_pairs={{0,1},{1,0},{2,3},{3,2},{4,5},{5,4},{6,7},{7,6},{8,9},{9,8},{10,11... | collective-permute-start | bytes 2261000 | tf_op jit(solution)/shard_map/ppermute | solution.py:473
  (66 other events, 2369.3 us)
Sparse Core Ops, SparseCore 0:
  14.9 35.3 all-gather.1
  321.2 99.9 reduce-scatter.10
  595.9 117.0 reduce-scatter.12
  1126.9 41.1 reduce-scatter.8
  1171.0 99.7 reduce-scatter.14
  1273.7 112.5 reduce-scatter.16
  1389.3 66.2 reduce-scatter.6

commit v7 on v6

--- a/solution.py
+++ b/solution.py
@@ -442,6 +442,27 @@
     )(*args, *extras)
 
 
+def head_grad_kernel(scale, n_pairs, *refs):
+    total = sum(dot_nn(refs[n_pairs + pair][...], refs[pair][...]) for pair in range(n_pairs))
+    refs[-1][...] = (scale * total).T
+
+
+def head_grad(scale, columns, heads_t):
+    n_pairs = len(columns)
+    rows, width, tokens = columns[0].shape[1], heads_t[0].shape[0], columns[0].shape[0]
+    tile = 512
+    return pl.pallas_call(
+        functools.partial(head_grad_kernel, scale, n_pairs),
+        grid=(width // tile,),
+        in_specs=[pl.BlockSpec((tokens, rows), lambda n: (0, 0))] * n_pairs + [pl.BlockSpec((tile, tokens), lambda n: (n, 0))] * n_pairs,
+        out_specs=pl.BlockSpec((rows, tile), lambda n: (0, n)),
+        out_shape=jax.ShapeDtypeStruct((rows, width), F32),
+        compiler_params=pltpu.CompilerParams(vmem_limit_bytes=48 * 2 ** 20),
+        cost_estimate=pl.CostEstimate(flops=2 * n_pairs * rows * width * tokens, bytes_accessed=2 * n_pairs * tokens * (rows + width) + 4 * rows * width,
+                                      transcendentals=0),
+    )(*columns, *heads_t)
+
+
 def spread_kernel(splits, idx_ref, *refs):
     got_refs, out_ref = refs[:-1], refs[-1]
     count = got_refs[0].shape[0]
@@ -579,13 +600,13 @@
         far0 = after(far0, part)
 
         own_rows = d_model // dev_count
-        up_got = []
-        for rows_of in up_rows:
+
+        def exchange(rows_of):
             blocks = [lax.dynamic_slice_in_dim(rows_of, (my_idx ^ bits) * own_rows, own_rows, axis=0) for bits in range(cp_size)]
-            up_got.append(jnp.stack([blocks[0]] + [row_major(swap(row_major(blocks[bits]), bits))
-                                                   for bits in range(1, cp_size)]))
+            return jnp.stack([blocks[0]] + [row_major(swap(row_major(blocks[bits]), bits)) for bits in range(1, cp_size)])
+
+        up_got = [exchange(up_rows[0])]
         grad_h_bf = grad_h(0, seq_len, part, [cot, side, far0, far1], BF16)
-        grad_w_up = spread_columns(my_idx, up_got, splits)
 
         def block_sum(left, right_t):
             def block(bits):
@@ -601,8 +622,7 @@
             part = block(2) + sent[0]
             return swap(part, 2), part
 
-        mine = [own_cols(grad_h_bf, bits) for bits in range(cp_size)]
-        mine = [mine[0]] + [swap(mine[bits], bits) for bits in range(1, cp_size)]
+        mine = [None] + [swap(own_cols(grad_h_bf, bits), bits) for bits in range(1, cp_size)]
         do_t = dot_tt(w_o, grad_h_bf).astype(BF16)
 
         def kv_block(dkv):
@@ -620,8 +640,7 @@
         q1_block = block_sum(x, dq1_t)
         q1_sent, parts_q = first_sends(q1_block)
         base_q = q0_block(0)
-        sum_o = sum(dot_tt(cols, rows_t) for cols, rows_t in zip(mine, (o_t, o_near, o_far, o_last))) * inv_count
-        q1_far, part_q = second_send(q1_block, (after(q1_sent[0], sum_o, base_q), q1_sent[1]))
+        q1_far, part_q = second_send(q1_block, (after(q1_sent[0], base_q), q1_sent[1]))
         do_t = after(do_t, part_q, *parts_q)
         dq2_t, dkv1 = attn_backward(tab, q_t, do_t, o_f32, lse, kv_all, kv_heads, head_dim, 1, 1, 2, (dkv1,))
         kv1_block, q2_block = kv_block(dkv1), block_sum(x, dq2_t)
@@ -629,16 +648,20 @@
         q2_sent, parts_q = first_sends(q2_block)
         kv1_far, part_kv = second_send(kv1_block, (after(kv1_sent[0], *parts_q), kv1_sent[1]))
         q2_far, part_q = second_send(q2_block, (after(q2_sent[0], part_kv), q2_sent[1]))
-        q0_far = after(q0_far, part_q)
+        mine[0] = own_cols(after(grad_h_bf, part_q), 0)
+        sum_o = head_grad(inv_count, mine, (o_t, o_near, o_far, o_last))
+        q0_far = after(q0_far, sum_o)
         sum_q0 = base_q + q0_sent[1] + q0_far
         grad_oq = dp_reduce(jnp.concatenate([sum_o, sum_q0], axis=1))
-        kv0_own = (kv0_block(0) + kv0_sent[1] + after(kv0_far, part_q)).astype(BF16)
+        kv0_own = (kv0_block(0) + kv0_sent[1] + after(kv0_far, sum_o)).astype(BF16)
         kv1_own = (kv1_block(0) + kv1_sent[1] + after(kv1_far, kv0_own)).astype(BF16)
         dkv_t = jnp.concatenate([jnp.concatenate([part[0, which], part[1, which]], axis=1)
                                  for which in range(2) for part in (kv0_own, kv1_own)], axis=0)
         w_block = block_sum(x, dkv_t)
         w_sent, _ = first_sends(w_block)
         w_far, part_w = second_send(w_block, w_sent)
+        up_got.append(exchange(after(up_rows[1], part_w)))
+        grad_w_up = spread_columns(my_idx, up_got, splits)
         later = jnp.concatenate([after(dq0_t, part_w), dq1_t, dq2_t], axis=0)
         grad_x = dot_tt(later, w_q)
         grad_x = grad_h_bf + grad_x + dot_tt(after(dkv_t, part_w), w_kv)

time: 1480 us -> 1400 us (0.946)
  waiting for transfers between devices: 624 us -> 553 us
  matrix products: 243 us -> 221 us
    ppermute x43, waiting for transfers between devices: 447 us -> 379 us  [swap(): lax.ppermute(values, 'cp', [(src, src ^ bits) for src in range(cp_size)])]
    dot_general x25 -> x21, matrix products: 115 us -> 92.7 us  [dot_tt(): lax.dot_general(lhs, rhs, (((0,), (1,)), ((), ())), preferred_element_typ...]
  transfers between devices with their start and end apart: 50 -> 50, of which waited for: 19 -> 19; matrix products, arithmetic and copies ran while one was open for 18% -> 18% of each run, Pallas kernels for 31% -> 34%
where the time goes in v7:
time: 1400 us; the launch traced here: 1390 us
  waiting for transfers between devices  553 us (40%)
  Pallas kernels  492 us (35%)
  matrix products  221 us (16%)
  local copies, waits for them, and re-layouts  50.9 us (4%)
  other arithmetic  27.8 us (2%)
  between operations  25 us (2%)
  starting transfers between devices  20.6 us (1%)
    ppermute x43, waiting for transfers between devices, swap(): lax.ppermute(values, 'cp', [(src, src ^ bits) for src in range(cp_size)])  379 us
    reduce_scatter x6, waiting for transfers between devices, dp_reduce(): return lax.psum_scatter(grad, 'dp', scatter_dimension=0, tiled=True)  174 us
    pallas_call x8, Pallas kernels, ff_forward(): pl.pallas_call(functools.partial(ff_kernel, FF_ROWS, copies, index * toke...  165 us
    pallas_call x3, Pallas kernels, attn_backward(): pl.pallas_call(functools.partial(attn_bwd_kernel, heads, piece * heads, h...  127 us
    dot_general x4, matrix products, dot_tn(): lax.dot_general(lhs, rhs, (((0,), (0,)), ((), ())), preferred_element_typ...  125 us
    dot_general x21, matrix products, dot_tt(): lax.dot_general(lhs, rhs, (((0,), (1,)), ((), ())), preferred_element_typ...  92.7 us
    pallas_call x6, Pallas kernels, grad_h_block(): pl.pallas_call(functools.partial(grad_h_kernel, len(up)), grid=(d_model /...  91.2 us
    pallas_call x1, Pallas kernels, attn_forward(): pl.pallas_call(functools.partial(attn_fwd_kernel, group, head_dim ** (-0....  67.3 us
  transfers between devices with their start and end apart: 50, of which 19 were waited for; matrix products, arithmetic and copies ran while one was open for 18% of the time, Pallas kernels for 34%

profile of v7, /device:TPU:0, one launch (start us, length us, event | category | flops | bytes accessed | tf_op | source)
XLA Modules:
  0.0 1391.4 jit_solution(9841532880561610173)
XLA Ops:
  26.4 21.0 %shard_map.135 = (bf16[2048,1280]{1,0:T(8,128)(2,1)}, bf16[2048,1536]{1,0:T(8,128)(2,1)}, bf16[1280,2048]{1,0:T(8,128)(2,1)}, bf16[1536,2048]{1,0:T(8,128)(2,1)}) custom-call(s32[3,8]{1,0:T(4,128)} %pad_add_fusion.1.idx_ref, bf16[2048,11008]{1,0:T(8,128)(2,1)} %refs_34_.1, bf16[2048,11008]{1,0:T(8,128)(2,1)} %refs_34_.1, bf16[2048,11008]{1,0:T(8,128)(2,1)} %refs_34_.1, ...), custom_call_target="tpu_custom_call" | custom-call | flops 46137344 | bytes 51904512 | tf_op jit(solution)/shard_map/pallas_call | solution.py:319
  50.6 14.0 %convert_bitcast_fusion.1.q_ref = bf16[2048,1024]{1,0:T(8,128)(2,1)} fusion(bf16[1024,2048]{1,0:T(8,128)(2,1)} %bitcast.186, bf16[256,8,16,128]{3,2,1,0:T(8,128)(2,1)} %bitcast.207), kind=kOutput, calls=%fused_computation.31 | convolution fusion | flops 8592031744 | bytes 16777216 | tf_op jit(solution)/shard_map/dot_general | solution.py:38
  64.6 67.3 %shard_map.136 = (f32[2048,1024]{1,0:T(8,128)}, bf16[2048,1024]{1,0:T(8,128)(2,1)}, f32[2,8,1024]{2,1,0:T(8,128)}) custom-call(s32[4,9]{1,0:T(4,128)} %pad_add_fusion.tab, bf16[2048,1024]{1,0:T(8,128)(2,1)} %convert_bitcast_fusion.1.q_ref, bf16[4096,512]{1,0:T(8,128)(2,1)} %all-gather.2.cloned.1.call-done.k_ref.v_ref, ...), custom_call_target="tpu_custom_call" | custom-call | flops 19327352832 | bytes 25165824 | tf_op jit(solution)/shard_map/pallas_call | solution.py:120
  131.9 14.0 %add_convert_fusion.1.refs_0_ = bf16[1024,2048]{1,0:T(8,128)(2,1)} fusion(bf16[2048,1024]{1,0:T(8,128)(2,1)} %get-tuple-element.148.refs_4_, bf16[256,8,16,128]{3,2,1,0:T(8,128)(2,1)} %bitcast.205, bf16[1,1024,2048]{2,1,0:T(8,128)(2,1)S(1)} %copy-done.7), kind=kOutput, calls=%fused_computation.17 | convolution fusion | flops 8596226048 | bytes 20971520 | tf_op jit(solution)/shard_map/dot_general | solution.py:38
  147.8 19.5 %shard_map.137 = (bf16[4096,1280]{1,0:T(8,128)(2,1)}, bf16[4096,1280]{1,0:T(8,128)(2,1)}, bf16[4096,2048]{1,0:T(8,128)(2,1)}, bf16[4096,2048]{1,0:T(8,128)(2,1)}) custom-call(bf16[1024,2048]{1,0:T(8,128)(2,1)} %add_convert_fusion.1.refs_0_, bf16[1024,2048]{1,0:T(8,128)(2,1)} %bitcast.28.refs_1_.refs_4_, ...), custom_call_target="tpu_custom_call" | custom-call | flops 10737418240 | bytes 27262976 | tf_op jit(solution)/shard_map/pallas_call | solution.py:397
  168.0 19.1 %shard_map.138 = (bf16[4096,1280]{1,0:T(8,128)(2,1)}, bf16[4096,1280]{1,0:T(8,128)(2,1)}, bf16[4096,2048]{1,0:T(8,128)(2,1)}, bf16[4096,2048]{1,0:T(8,128)(2,1)}) custom-call(bf16[1024,2048]{1,0:T(8,128)(2,1)} %collective-permute-done.2.refs_0_, ...), custom_call_target="tpu_custom_call", output_to_operand_aliasing={{0}: (4, {}), {1}: (5, {}), {2}: (6, {}), {3}: (7, {})} | custom-call | flops 10737418240 | bytes 27262976 | tf_op jit(solution)/shard_map/pallas_call | solution.py:397
  187.1 21.9 %shard_map.139 = (bf16[4096,1536]{1,0:T(8,128)(2,1)}, bf16[4096,1536]{1,0:T(8,128)(2,1)}) custom-call(bf16[1024,2048]{1,0:T(8,128)(2,1)} %add_convert_fusion.1.refs_0_, bf16[1024,2048]{1,0:T(8,128)(2,1)} %bitcast.28.refs_1_.refs_4_, bf16[2048,1536]{1,0:T(8,128)(2,1)} %get-tuple-element.94.refs_2_.refs_4_.refs_3_, ...), custom_call_target="tpu_custom_call" | custom-call | flops 12884901888 | bytes 29360128 | tf_op jit(solution)/shard_map/pallas_call | solution.py:397
  209.0 6.6 collective-permute-done.1.refs_0_
  220.9 19.2 %shard_map.140 = (bf16[4096,1280]{1,0:T(8,128)(2,1)}, bf16[4096,1280]{1,0:T(8,128)(2,1)}, bf16[4096,2048]{1,0:T(8,128)(2,1)}, bf16[4096,2048]{1,0:T(8,128)(2,1)}) custom-call(bf16[512,2048]{1,0:T(8,128)(2,1)} %collective-permute-done.1.refs_0_, ...), custom_call_target="tpu_custom_call", output_to_operand_aliasing={{0}: (6, {}), {1}: (7, {}), {2}: (8, {}), {3}: (9, {})} | custom-call | flops 10737418240 | bytes 27262976 | tf_op jit(solution)/shard_map/pallas_call | solution.py:397
  240.2 22.0 %shard_map.141 = (bf16[4096,1536]{1,0:T(8,128)(2,1)}, bf16[4096,1536]{1,0:T(8,128)(2,1)}) custom-call(bf16[512,2048]{1,0:T(8,128)(2,1)} %collective-permute-done.1.refs_0_, bf16[1024,2048]{1,0:T(8,128)(2,1)} %collective-permute-done.4.refs_1_, bf16[512,2048]{1,0:T(8,128)(2,1)} %collective-permute-done.5.refs_2_, ...), custom_call_target="tpu_custom_call", output_to_operand_aliasing={{0}: (6, {}), {1}: (7, {})} | custom-call | flops 12884901888 | bytes 29360128 | tf_op jit(solution)/shard_map/pallas_call | solution.py:397
  262.2 4.8 collective-permute-done.refs_0_
  272.5 19.2 %shard_map.142 = (bf16[4096,1280]{1,0:T(8,128)(2,1)}, bf16[4096,1280]{1,0:T(8,128)(2,1)}, bf16[4096,2048]{1,0:T(8,128)(2,1)}, bf16[4096,2048]{1,0:T(8,128)(2,1)}) custom-call(bf16[512,2048]{1,0:T(8,128)(2,1)} %copy-done.3, ...), custom_call_target="tpu_custom_call", output_to_operand_aliasing={{0}: (6, {}), {1}: (7, {}), {2}: (8, {}), {3}: (9, {})} | custom-call | flops 10737418240 | bytes 27262976 | tf_op jit(solution)/shard_map/pallas_call | solution.py:397
  291.7 29.6 %convolution_multiply_fusion.1 = f32[2048,1280]{1,0:T(8,128)} fusion(bf16[4096,2048]{1,0:T(8,128)(2,1)} %get-tuple-element.114, bf16[4096,1280]{1,0:T(8,128)(2,1)} %get-tuple-element.112.refs_0_), kind=kOutput, calls=%fused_computation.6 | convolution fusion | flops 21477457920 | bytes 37748736 | tf_op jit(solution)/shard_map/dot_general | solution.py:34
  321.4 11.9 shard_map.143
  333.5 22.1 %shard_map.144 = (bf16[4096,1536]{1,0:T(8,128)(2,1)}, bf16[4096,1536]{1,0:T(8,128)(2,1)}) custom-call(bf16[512,2048]{1,0:T(8,128)(2,1)} %copy-done.3, bf16[1024,2048]{1,0:T(8,128)(2,1)} %collective-permute-done.4.refs_1_, bf16[512,2048]{1,0:T(8,128)(2,1)} %copy-done.4, bf16[1024,2048]{1,0:T(8,128)(2,1)} %copy-done.2, ...), custom_call_target="tpu_custom_call", output_to_operand_aliasing={{0}: (6, {}), {1}: (7, {})} | custom-call | flops 12884901888 | bytes 29360128 | tf_op jit(solution)/shard_map/pallas_call | solution.py:397
  355.5 13.7 shard_map.145
  369.3 22.1 %shard_map.146 = (bf16[4096,1536]{1,0:T(8,128)(2,1)}, bf16[4096,1536]{1,0:T(8,128)(2,1)}) custom-call(bf16[1024,2048]{1,0:T(8,128)(2,1)} %collective-permute-done.2.refs_0_, bf16[1024,2048]{1,0:T(8,128)(2,1)} %collective-permute-done.3.refs_1_, ...), custom_call_target="tpu_custom_call", output_to_operand_aliasing={{0}: (4, {}), {1}: (5, {})} | custom-call | flops 12884901888 | bytes 29360128 | tf_op jit(solution)/shard_map/pallas_call | solution.py:397
  391.4 12.8 shard_map.147
  405.7 34.9 %fusion.7 = f32[2048,1472]{1,0:T(8,128)} fusion(bf16[4096,2048]{1,0:T(8,128)(2,1)} %get-tuple-element.114, bf16[4096,1536]{1,0:T(8,128)(2,1)} %get-tuple-element.131.refs_2_), kind=kOutput, calls=%fused_computation.7 | convolution fusion | flops 24699076608 | bytes 41418752 | tf_op jit(solution)/shard_map/dot_general | solution.py:34
  440.7 15.2 %shard_map.148 = f32[512,2048]{1,0:T(8,128)} custom-call(bf16[4096,1280]{1,0:T(8,128)(2,1)} %get-tuple-element.112.refs_0_, bf16[2048,1280]{1,0:T(8,128)(2,1)} %get-tuple-element.82.refs_2_.refs_4_.refs_1_, bf16[4096,1536]{1,0:T(8,128)(2,1)} %get-tuple-element.131.refs_2_, bf16[2048,1536]{1,0:T(8,128)(2,1)} %get-tuple-element.94.refs_2_.refs_4_.refs_3_, ...), custom_call_target="tpu_custom_call" | custom-call | flops 5905580032 | bytes 18612224 | tf_op jit(solution)/shard_map/pallas_call | solution.py:433
  455.9 26.3 %convolution_multiply_fusion = f32[1280,2048]{1,0:T(8,128)} fusion(bf16[4096,1280]{1,0:T(8,128)(2,1)S(1)} %bitcast.185, bf16[4096,2048]{1,0:T(8,128)(2,1)} %get-tuple-element.128), kind=kOutput, calls=%fused_computation.5 | convolution fusion | flops 21477457920 | bytes 37748736 | tf_op jit(solution)/shard_map/dot_general | solution.py:34
  484.7 17.7 %shard_map.149 = f32[1024,2048]{1,0:T(8,128)} custom-call(bf16[4096,1280]{1,0:T(8,128)(2,1)} %get-tuple-element.112.refs_0_, bf16[2048,1280]{1,0:T(8,128)(2,1)S(1)} %copy-done, bf16[4096,1536]{1,0:T(8,128)(2,1)} %get-tuple-element.131.refs_2_, bf16[2048,1536]{1,0:T(8,128)(2,1)} %get-tuple-element.94.refs_2_.refs_4_.refs_3_), custom_call_target="tpu_custom_call" | custom-call | flops 11811160064 | bytes 25690112 | tf_op jit(solution)/shard_map/pallas_call | solution.py:433
  508.7 34.6 %fusion.4 = f32[1472,2048]{1,0:T(8,128)} fusion(bf16[4096,2048]{1,0:T(8,128)(2,1)} %get-tuple-element.128, bf16[4096,1536]{1,0:T(8,128)(2,1)} %get-tuple-element.130), kind=kOutput, calls=%fused_computation.4 | convolution fusion | flops 24699076608 | bytes 41418752 | tf_op jit(solution)/shard_map/dot_general | solution.py:34
  543.3 52.9 %collective-permute-done.11.refs_6_ = f32[512,2048]{1,0:T(8,128)} collective-permute-done((f32[512,2048]{1,0:T(8,128)}, f32[512,2048]{1,0:T(8,128)}, u32[]{:S(2)}, u32[]{:S(2)}) %collective-permute-start.11) | collective-permute-done | bytes 4194336 | tf_op jit(solution)/shard_map/ppermute | solution.py:494
  596.2 89.9 %collective-permute-done.12.refs_7_ = f32[512,2048]{1,0:T(8,128)} collective-permute-done((f32[512,2048]{1,0:T(8,128)}, f32[512,2048]{1,0:T(8,128)}, u32[]{:S(2)}, u32[]{:S(2)}) %collective-permute-start.12) | collective-permute-done | bytes 4194336 | tf_op jit(solution)/shard_map/ppermute | solution.py:494
  686.1 19.9 %shard_map.150 = bf16[1024,2048]{1,0:T(8,128)(2,1)S(1)} custom-call(bf16[4096,1280]{1,0:T(8,128)(2,1)} %get-tuple-element.112.refs_0_, bf16[2048,1280]{1,0:T(8,128)(2,1)} %get-tuple-element.82.refs_2_.refs_4_.refs_1_, bf16[4096,1536]{1,0:T(8,128)(2,1)} %get-tuple-element.131.refs_2_, bf16[2048,1536]{1,0:T(8,128)(2,1)} %get-tuple-element.94.refs_2_.refs_4_.refs_3_, ...), custom_call_target="tpu_custom_call" | custom-call | flops 11811160064 | bytes 25690112 | tf_op jit(solution)/shard_map/pallas_call | solution.py:433
  706.0 14.3 %convert_bitcast_fusion.do_ref = bf16[2048,1024]{1,0:T(8,128)(2,1)} fusion(bf16[1024,2048]{1,0:T(8,128)(2,1)S(1)} %shard_map.150, bf16[256,8,16,128]{3,2,1,0:T(8,128)(2,1)} %bitcast.206), kind=kOutput, calls=%fused_computation.30 | convolution fusion | flops 8592031744 | bytes 16777216 | tf_op jit(solution)/shard_map/dot_general | solution.py:38
  720.3 59.6 %shard_map.151 = (bf16[1024,1024]{1,0:T(8,128)(2,1)}, f32[8,2,128,512]{3,2,1,0:T(8,128)}) custom-call(s32[4,9]{1,0:T(4,128)} %pad_add_fusion.tab, bf16[2048,1024]{1,0:T(8,128)(2,1)} %convert_bitcast_fusion.1.q_ref, bf16[2048,1024]{1,0:T(8,128)(2,1)} %convert_bitcast_fusion.do_ref, f32[2048,1024]{1,0:T(8,128)} %get-tuple-element.133.of_ref, ...), custom_call_target="tpu_custom_call" | custom-call | flops 24159191040 | bytes 12582912 | tf_op jit(solution)/shard_map/pallas_call | solution.py:209
  798.8 33.3 %shard_map.152 = (bf16[512,1024]{1,0:T(8,128)(2,1)}, f32[8,2,128,512]{3,2,1,0:T(8,128)}) custom-call(s32[4,9]{1,0:T(4,128)} %pad_add_fusion.tab, bf16[2048,1024]{1,0:T(8,128)(2,1)} %convert_bitcast_fusion.1.q_ref, bf16[2048,1024]{1,0:T(8,128)(2,1)} %convert_bitcast_fusion.do_ref, f32[2048,1024]{1,0:T(8,128)} %get-tuple-element.133.of_ref, ...), custom_call_target="tpu_custom_call" | custom-call | flops 12079595520 | bytes 6291456 | tf_op jit(solution)/shard_map/pallas_call | solution.py:209
  839.4 34.4 %shard_map.153 = (bf16[512,1024]{1,0:T(8,128)(2,1)}, f32[8,2,128,512]{3,2,1,0:T(8,128)}) custom-call(s32[4,9]{1,0:T(4,128)} %pad_add_fusion.tab, bf16[2048,1024]{1,0:T(8,128)(2,1)} %convert_bitcast_fusion.1.q_ref, bf16[2048,1024]{1,0:T(8,128)(2,1)} %convert_bitcast_fusion.do_ref, f32[2048,1024]{1,0:T(8,128)} %get-tuple-element.133.of_ref, ...), custom_call_target="tpu_custom_call" | custom-call | flops 12079595520 | bytes 6291456 | tf_op jit(solution)/shard_map/pallas_call | solution.py:209
  894.2 14.1 %collective-permute-done.21.refs_2_ = bf16[1024,512]{1,0:T(8,128)(2,1)S(1)} collective-permute-done((bf16[1024,512]{1,0:T(8,128)(2,1)S(1)}, bf16[1024,512]{1,0:T(8,128)(2,1)S(1)}, u32[]{:S(2)}, u32[]{:S(2)}) %collective-permute-start.21) | collective-permute-done | bytes 1048608 | tf_op jit(solution)/shard_map/ppermute | solution.py:494
  908.3 20.6 %collective-permute-done.22.refs_3_ = bf16[1024,512]{1,0:T(8,128)(2,1)S(1)} collective-permute-done((bf16[1024,512]{1,0:T(8,128)(2,1)S(1)}, bf16[1024,512]{1,0:T(8,128)(2,1)S(1)}, u32[]{:S(2)}, u32[]{:S(2)}) %collective-permute-start.22) | collective-permute-done | bytes 1048608 | tf_op jit(solution)/shard_map/ppermute | solution.py:494
  928.9 13.4 shard_map.154
  942.3 11.0 collective-permute-done.15
  955.5 19.4 %collective-permute-done.27 = f32[2,2,128,512]{3,2,1,0:T(8,128)} collective-permute-done((f32[2,2,128,512]{3,2,1,0:T(8,128)}, f32[2,2,128,512]{3,2,1,0:T(8,128)}, u32[]{:S(2)}, u32[]{:S(2)}) %collective-permute-start.27) | collective-permute-done | bytes 1048608 | tf_op jit(solution)/shard_map/ppermute | solution.py:494
  983.1 21.8 %collective-permute-done.34 = f32[512,512]{1,0:T(8,128)S(1)} collective-permute-done((f32[512,512]{1,0:T(8,128)S(1)}, f32[512,512]{1,0:T(8,128)S(1)}, u32[]{:S(2)}, u32[]{:S(2)}) %collective-permute-start.34) | collective-permute-done | bytes 1048608 | tf_op jit(solution)/shard_map/ppermute | solution.py:494
  1005.2 22.2 %collective-permute-done.32 = f32[512,512]{1,0:T(8,128)S(1)} collective-permute-done((f32[512,512]{1,0:T(8,128)S(1)}, f32[512,512]{1,0:T(8,128)S(1)}, u32[]{:S(2)}, u32[]{:S(2)}) %collective-permute-start.32) | collective-permute-done | bytes 1048608 | tf_op jit(solution)/shard_map/ppermute | solution.py:494
  1028.9 20.4 %collective-permute-done.36 = f32[512,512]{1,0:T(8,128)S(1)} collective-permute-done((f32[512,512]{1,0:T(8,128)S(1)}, f32[512,512]{1,0:T(8,128)S(1)}, u32[]{:S(2)}, u32[]{:S(2)}) %collective-permute-start.36) | collective-permute-done | bytes 1048608 | tf_op jit(solution)/shard_map/ppermute | solution.py:494
  1053.8 47.1 %collective-permute-done.30 = f32[512,1024]{1,0:T(8,128)S(1)} collective-permute-done((f32[512,1024]{1,0:T(8,128)}, f32[512,1024]{1,0:T(8,128)S(1)}, u32[]{:S(2)}, u32[]{:S(2)}) %collective-permute-start.30) | collective-permute-done | bytes 2097184 | tf_op jit(solution)/shard_map/ppermute | solution.py:494
  1110.2 15.2 %collective-permute-done.39 = f32[128,1280]{1,0:T(8,128)S(1)} collective-permute-done((f32[128,1280]{1,0:T(8,128)S(1)}, f32[128,1280]{1,0:T(8,128)S(1)}, u32[]{:S(2)}, u32[]{:S(2)}) %collective-permute-start.39) | collective-permute-done | bytes 655392 | tf_op jit(solution)/shard_map/ppermute | solution.py:494
  1125.4 13.7 collective-permute-done.38
  1142.0 5.6 fusion.54
  1155.3 16.9 %fusion.22 = bf16[1,1024,2048]{2,1,0:T(8,128)(2,1)} fusion(f32[1024,2048]{1,0:T(8,128)} %fusion.54, bf16[1024,2048]{1,0:T(8,128)(2,1)} %copy-done.1, bf16[256,8,16,128]{3,2,1,0:T(8,128)(2,1)} %bitcast.208, bf16[512,1024]{1,0:T(8,128)(2,1)} %get-tuple-element.143, bf16[512,1024]{1,0:T(8,128)(2,1)} %get-tuple-element.139, ...), kind=kOutput, calls=%fused_computation.24 | convolution fusion | flops 8610906112 | bytes 29360128 | tf_op jit(solution)/shard_map/dot_general | solution.py:38
  1172.5 13.9 collective-permute-done.41
  1191.2 6.9 shard_map.155
  1200.6 110.1 %reduce-scatter.17.cloned.1.call-done = f32[368,2048]{1,0:T(8,128)} async-done(((f32[1472,2048]{1,0:T(8,128)}), f32[368,2048]{1,0:T(8,128)}) %reduce-scatter.17.cloned.1.call-update) | async-done | bytes 3014672 | tf_op jit(solution)/shard_map/reduce_scatter | solution.py:497
  1310.7 5.8 pad_maximum_fusion.1
  1316.6 63.4 %reduce-scatter.7.cloned.1.call-done = f32[128,3072]{1,0:T(8,128)} async-done(((f32[512,3072]{1,0:T(8,128)}), f32[128,3072]{1,0:T(8,128)}) %reduce-scatter.7.cloned.1.call-update) | async-done | bytes 1572880 | tf_op jit(solution)/shard_map/reduce_scatter | solution.py:497
  (305 shorter events, 131.0 us)
Async XLA Ops:
  7.2 57.5 %all-gather.2.cloned.1.call-start = ((), (), s32[]{:S(2)}) async-start(), calls=%async_computation.6 | async-start | bytes 5242880 | tf_op jit(solution)/shard_map/all_gather | solution.py:529
  14.8 1091.4 %reduce-scatter.11.cloned.1.call-start = ((), (), s32[]{:S(2)}) async-start(), calls=%async_computation.9 | async-start | bytes 13107200 | tf_op jit(solution)/shard_map/reduce_scatter | solution.py:497
  14.9 153.1 %collective-permute-start.3 = (bf16[1024,2048]{1,0:T(8,128)(2,1)}, bf16[1024,2048]{1,0:T(8,128)(2,1)}, u32[]{:S(2)}, u32[]{:S(2)}) collective-permute-start(bf16[1024,2048]{1,0:T(8,128)(2,1)} %bitcast.28.refs_1_.refs_4_), channel_id=1, source_target_pairs={{0,1},{1,0},{2,3},{3,2},{4,5},{5,4},{6,7},{7,6},{8,9},{9,8},{10,11... | collective-permute-start | bytes 12582920 | tf_op jit(solution)/shard_map/ppermute | solution.py:494
  47.4 120.3 %collective-permute-start.4 = (bf16[1024,2048]{1,0:T(8,128)(2,1)}, bf16[1024,2048]{1,0:T(8,128)(2,1)}, u32[]{:S(2)}, u32[]{:S(2)}) collective-permute-start(bf16[1024,2048]{1,0:T(8,128)(2,1)} %bitcast.28.refs_1_.refs_4_), channel_id=1, source_target_pairs={{0,2},{1,3},{2,0},{3,1},{4,6},{5,7},{6,4},{7,5},{8,10},{9,11},{10,... | collective-permute-start | bytes 12582920 | tf_op jit(solution)/shard_map/ppermute | solution.py:494
  146.0 22.0 %collective-permute-start.2 = (bf16[1024,2048]{1,0:T(8,128)(2,1)}, bf16[1024,2048]{1,0:T(8,128)(2,1)}, u32[]{:S(2)}, u32[]{:S(2)}) collective-permute-start(bf16[1024,2048]{1,0:T(8,128)(2,1)} %add_convert_fusion.1.refs_0_), channel_id=1, source_target_pairs={{0,1},{1,0},{2,3},{3,2},{4,5},{5,4},{6,7},{7,6},{8,9},{9,8},{10,11... | collective-permute-start | bytes 12582920 | tf_op jit(solution)/shard_map/ppermute | solution.py:494
  167.4 48.2 %collective-permute-start.1 = (bf16[512,2048]{1,0:T(8,128)(2,1)S(1)}, bf16[512,2048]{1,0:T(8,128)(2,1)}, u32[]{:S(2)}, u32[]{:S(2)}) collective-permute-start(bf16[512,2048]{1,0:T(8,128)(2,1)S(1)} %slice.88), channel_id=1, source_target_pairs={{0,2},{1,3},{2,0},{3,1},{4,6},{5,7},{6,4},{7,5},{8,10},{9,11},{10,... | collective-permute-start | bytes 6291464 | tf_op jit(solution)/shard_map/ppermute | solution.py:494
  167.6 51.4 %collective-permute-start.6 = (bf16[1024,2048]{1,0:T(8,128)(2,1)}, bf16[1024,2048]{1,0:T(8,128)(2,1)S(1)}, u32[]{:S(2)}, u32[]{:S(2)}) collective-permute-start(bf16[1024,2048]{1,0:T(8,128)(2,1)} %collective-permute-done.4.refs_1_), channel_id=1, source_target_pairs={{0,1},{1,0},{2,3},{3,2},{4,5},{5,4},{6,7},{7,6},{8,9},{9,8},{10,11... | collective-permute-start | bytes 12582920 | tf_op jit(solution)/shard_map/ppermute | solution.py:494
  215.5 4.5 collective-permute-start.5
  218.7 48.3 %collective-permute-start = (bf16[512,2048]{1,0:T(8,128)(2,1)}, bf16[512,2048]{1,0:T(8,128)(2,1)S(1)}, u32[]{:S(2)}, u32[]{:S(2)}) collective-permute-start(bf16[512,2048]{1,0:T(8,128)(2,1)} %slice.71), channel_id=1, source_target_pairs={{0,2},{1,3},{2,0},{3,1},{4,6},{5,7},{6,4},{7,5},{8,10},{9,11},{10,... | collective-permute-start | bytes 6291464 | tf_op jit(solution)/shard_map/ppermute | solution.py:494
  267.0 4.2 collective-permute-start.7
  321.3 826.3 %reduce-scatter.13.cloned.1.call-start = ((), (), s32[]{:S(2)}) async-start(), calls=%async_computation.10 | async-start | bytes 15728640 | tf_op jit(solution)/shard_map/reduce_scatter | solution.py:497
  333.3 22.2 %collective-permute-start.8 = (f32[512,2048]{1,0:T(8,128)S(1)}, f32[512,2048]{1,0:T(8,128)}, u32[]{:S(2)}, u32[]{:S(2)}) collective-permute-start(f32[512,2048]{1,0:T(8,128)S(1)} %shard_map.143), channel_id=1, source_target_pairs={{0,1},{1,0},{2,3},{3,2},{4,5},{5,4},{6,7},{7,6},{8,9},{9,8},{10,11... | collective-permute-start | bytes 12582920 | tf_op jit(solution)/shard_map/ppermute | solution.py:494
  404.2 36.5 %collective-permute-start.9 = (f32[512,2048]{1,0:T(8,128)}, f32[512,2048]{1,0:T(8,128)}, u32[]{:S(2)}, u32[]{:S(2)}) collective-permute-start(f32[512,2048]{1,0:T(8,128)} %shard_map.147), channel_id=1, source_target_pairs={{0,1},{1,0},{2,3},{3,2},{4,5},{5,4},{6,7},{7,6},{8,9},{9,8},{10,11... | collective-permute-start | bytes 12582920 | tf_op jit(solution)/shard_map/ppermute | solution.py:494
  502.4 183.7 %collective-permute-start.10 = (f32[1024,2048]{1,0:T(8,128)}, f32[1024,2048]{1,0:T(8,128)}, u32[]{:S(2)}, u32[]{:S(2)}) collective-permute-start(f32[1024,2048]{1,0:T(8,128)} %shard_map.149), channel_id=1, source_target_pairs={{0,1},{1,0},{2,3},{3,2},{4,5},{5,4},{6,7},{7,6},{8,9},{9,8},{10,11... | collective-permute-start | bytes 25165832 | tf_op jit(solution)/shard_map/ppermute | solution.py:494
  502.4 93.8 %collective-permute-start.11 = (f32[512,2048]{1,0:T(8,128)}, f32[512,2048]{1,0:T(8,128)}, u32[]{:S(2)}, u32[]{:S(2)}) collective-permute-start(f32[512,2048]{1,0:T(8,128)} %shard_map.145), channel_id=1, source_target_pairs={{0,2},{1,3},{2,0},{3,1},{4,6},{5,7},{6,4},{7,5},{8,10},{9,11},{10,... | collective-permute-start | bytes 12582920 | tf_op jit(solution)/shard_map/ppermute | solution.py:494
  502.4 183.6 %collective-permute-start.12 = (f32[512,2048]{1,0:T(8,128)}, f32[512,2048]{1,0:T(8,128)}, u32[]{:S(2)}, u32[]{:S(2)}) collective-permute-start(f32[512,2048]{1,0:T(8,128)} %shard_map.148), channel_id=1, source_target_pairs={{0,2},{1,3},{2,0},{3,1},{4,6},{5,7},{6,4},{7,5},{8,10},{9,11},{10,... | collective-permute-start | bytes 12582920 | tf_op jit(solution)/shard_map/ppermute | solution.py:494
  504.5 693.7 %reduce-scatter.9.cloned.1.call-start = ((), (), s32[]{:S(2)}) async-start(), calls=%async_computation.8 | async-start | bytes 3932160 | tf_op jit(solution)/shard_map/reduce_scatter | solution.py:497
  508.6 326.2 %collective-permute-start.24 = (bf16[2048,1024]{1,0:T(8,128)(2,1)}, bf16[2048,1024]{1,0:T(8,128)(2,1)}, u32[]{:S(2)}, u32[]{:S(2)}) collective-permute-start(bf16[2048,1024]{1,0:T(8,128)(2,1)} %get-tuple-element.148.refs_4_), channel_id=1, source_target_pairs={{0,2},{1,3},{2,0},{3,1},{4,6},{5,7},{6,4},{7,5},{8,10},{9,11},{10,... | collective-permute-start | bytes 12582920 | tf_op jit(solution)/shard_map/ppermute | solution.py:494
  784.1 10.5 collective-permute-start.16
  786.8 5.1 collective-permute-start.14
  834.2 4.9 collective-permute-start.17
  834.3 57.3 %collective-permute-start.23 = (bf16[2048,1024]{1,0:T(8,128)(2,1)}, bf16[2048,1024]{1,0:T(8,128)(2,1)}, u32[]{:S(2)}, u32[]{:S(2)}) collective-permute-start(bf16[2048,1024]{1,0:T(8,128)(2,1)} %get-tuple-element.148.refs_4_), channel_id=1, source_target_pairs={{0,1},{1,0},{2,3},{3,2},{4,5},{5,4},{6,7},{7,6},{8,9},{9,8},{10,11... | collective-permute-start | bytes 12582920 | tf_op jit(solution)/shard_map/ppermute | solution.py:494
  834.8 57.7 %collective-permute-start.25 = (bf16[2048,1024]{1,0:T(8,128)(2,1)}, bf16[2048,1024]{1,0:T(8,128)(2,1)}, u32[]{:S(2)}, u32[]{:S(2)}) collective-permute-start(bf16[2048,1024]{1,0:T(8,128)(2,1)} %collective-permute-done.24.refs_6_), channel_id=1, source_target_pairs={{0,1},{1,0},{2,3},{3,2},{4,5},{5,4},{6,7},{7,6},{8,9},{9,8},{10,11... | collective-permute-start | bytes 12582920 | tf_op jit(solution)/shard_map/ppermute | solution.py:494
  876.9 5.3 collective-permute-start.19
  881.4 12.6 collective-permute-start.20
  882.2 26.1 %collective-permute-start.21 = (bf16[1024,512]{1,0:T(8,128)(2,1)S(1)}, bf16[1024,512]{1,0:T(8,128)(2,1)S(1)}, u32[]{:S(2)}, u32[]{:S(2)}) collective-permute-start(bf16[1024,512]{1,0:T(8,128)(2,1)S(1)} %pad_maximum_fusion.11), channel_id=1, source_target_pairs={{0,2},{1,3},{2,0},{3,1},{4,6},{5,7},{6,4},{7,5},{8,10},{9,11},{10,... | collective-permute-start | bytes 3145736 | tf_op jit(solution)/shard_map/ppermute | solution.py:494
  882.3 46.6 %collective-permute-start.22 = (bf16[1024,512]{1,0:T(8,128)(2,1)S(1)}, bf16[1024,512]{1,0:T(8,128)(2,1)S(1)}, u32[]{:S(2)}, u32[]{:S(2)}) collective-permute-start(bf16[1024,512]{1,0:T(8,128)(2,1)S(1)} %pad_maximum_fusion.12), channel_id=1, source_target_pairs={{0,3},{1,2},{2,1},{3,0},{4,7},{5,6},{6,5},{7,4},{8,11},{9,10},{10,... | collective-permute-start | bytes 3145736 | tf_op jit(solution)/shard_map/ppermute | solution.py:494
  891.6 61.7 %collective-permute-start.13 = (f32[2,2,128,512]{3,2,1,0:T(8,128)S(1)}, f32[2,2,128,512]{3,2,1,0:T(8,128)}, u32[]{:S(2)}, u32[]{:S(2)}) collective-permute-start(f32[2,2,128,512]{3,2,1,0:T(8,128)S(1)} %copy-done.10), channel_id=1, source_target_pairs={{0,1},{1,0},{2,3},{3,2},{4,5},{5,4},{6,7},{7,6},{8,9},{9,8},{10,11... | collective-permute-start | bytes 3145736 | tf_op jit(solution)/shard_map/ppermute | solution.py:494
  892.4 60.9 %collective-permute-start.15 = (f32[2,2,128,512]{3,2,1,0:T(8,128)S(1)}, f32[2,2,128,512]{3,2,1,0:T(8,128)}, u32[]{:S(2)}, u32[]{:S(2)}) collective-permute-start(f32[2,2,128,512]{3,2,1,0:T(8,128)S(1)} %copy-done.14), channel_id=1, source_target_pairs={{0,2},{1,3},{2,0},{3,1},{4,6},{5,7},{6,4},{7,5},{8,10},{9,11},{10,... | collective-permute-start | bytes 3145736 | tf_op jit(solution)/shard_map/ppermute | solution.py:494
  894.0 80.9 %collective-permute-start.26 = (f32[2,2,128,512]{3,2,1,0:T(8,128)S(1)}, f32[2,2,128,512]{3,2,1,0:T(8,128)}, u32[]{:S(2)}, u32[]{:S(2)}) collective-permute-start(f32[2,2,128,512]{3,2,1,0:T(8,128)S(1)} %copy-done.11), channel_id=1, source_target_pairs={{0,1},{1,0},{2,3},{3,2},{4,5},{5,4},{6,7},{7,6},{8,9},{9,8},{10,11... | collective-permute-start | bytes 3145736 | tf_op jit(solution)/shard_map/ppermute | solution.py:494
  908.3 66.6 %collective-permute-start.27 = (f32[2,2,128,512]{3,2,1,0:T(8,128)}, f32[2,2,128,512]{3,2,1,0:T(8,128)}, u32[]{:S(2)}, u32[]{:S(2)}) collective-permute-start(f32[2,2,128,512]{3,2,1,0:T(8,128)} %bitcast_add_fusion.1), channel_id=1, source_target_pairs={{0,2},{1,3},{2,0},{3,1},{4,6},{5,7},{6,4},{7,5},{8,10},{9,11},{10,... | collective-permute-start | bytes 3145736 | tf_op jit(solution)/shard_map/ppermute | solution.py:494
  978.8 26.1 %collective-permute-start.34 = (f32[512,512]{1,0:T(8,128)S(1)}, f32[512,512]{1,0:T(8,128)S(1)}, u32[]{:S(2)}, u32[]{:S(2)}) collective-permute-start(f32[512,512]{1,0:T(8,128)S(1)} %add.426), channel_id=1, source_target_pairs={{0,2},{1,3},{2,0},{3,1},{4,6},{5,7},{6,4},{7,5},{8,10},{9,11},{10,... | collective-permute-start | bytes 3145736 | tf_op jit(solution)/shard_map/ppermute | solution.py:494
  979.1 48.2 %collective-permute-start.32 = (f32[512,512]{1,0:T(8,128)S(1)}, f32[512,512]{1,0:T(8,128)S(1)}, u32[]{:S(2)}, u32[]{:S(2)}) collective-permute-start(f32[512,512]{1,0:T(8,128)S(1)} %add.424), channel_id=1, source_target_pairs={{0,2},{1,3},{2,0},{3,1},{4,6},{5,7},{6,4},{7,5},{8,10},{9,11},{10,... | collective-permute-start | bytes 3145736 | tf_op jit(solution)/shard_map/ppermute | solution.py:494
  980.9 46.5 %collective-permute-start.33 = (f32[512,512]{1,0:T(8,128)S(1)}, f32[512,512]{1,0:T(8,128)S(1)}, u32[]{:S(2)}, u32[]{:S(2)}) collective-permute-start(f32[512,512]{1,0:T(8,128)S(1)} %copy-done.60), channel_id=1, source_target_pairs={{0,1},{1,0},{2,3},{3,2},{4,5},{5,4},{6,7},{7,6},{8,9},{9,8},{10,11... | collective-permute-start | bytes 3145736 | tf_op jit(solution)/shard_map/ppermute | solution.py:494
  980.9 47.3 %collective-permute-start.31 = (f32[512,512]{1,0:T(8,128)S(1)}, f32[512,512]{1,0:T(8,128)S(1)}, u32[]{:S(2)}, u32[]{:S(2)}) collective-permute-start(f32[512,512]{1,0:T(8,128)S(1)} %copy-done.59), channel_id=1, source_target_pairs={{0,1},{1,0},{2,3},{3,2},{4,5},{5,4},{6,7},{7,6},{8,9},{9,8},{10,11... | collective-permute-start | bytes 3145736 | tf_op jit(solution)/shard_map/ppermute | solution.py:494
  982.2 46.7 %collective-permute-start.35 = (f32[512,512]{1,0:T(8,128)S(1)}, f32[512,512]{1,0:T(8,128)S(1)}, u32[]{:S(2)}, u32[]{:S(2)}) collective-permute-start(f32[512,512]{1,0:T(8,128)S(1)} %convolution_multiply_fusion.5), channel_id=1, source_target_pairs={{0,1},{1,0},{2,3},{3,2},{4,5},{5,4},{6,7},{7,6},{8,9},{9,8},{10,11... | collective-permute-start | bytes 3145736 | tf_op jit(solution)/shard_map/ppermute | solution.py:494
  1004.9 44.4 %collective-permute-start.36 = (f32[512,512]{1,0:T(8,128)S(1)}, f32[512,512]{1,0:T(8,128)S(1)}, u32[]{:S(2)}, u32[]{:S(2)}) collective-permute-start(f32[512,512]{1,0:T(8,128)S(1)} %fusion.38), channel_id=1, source_target_pairs={{0,2},{1,3},{2,0},{3,1},{4,6},{5,7},{6,4},{7,5},{8,10},{9,11},{10,... | collective-permute-start | bytes 3145736 | tf_op jit(solution)/shard_map/ppermute | solution.py:494
  1052.0 148.6 %reduce-scatter.15.cloned.1.call-start = ((), (), s32[]{:S(2)}) async-start(), calls=%async_computation.11 | async-start | bytes 13107200 | tf_op jit(solution)/shard_map/reduce_scatter | solution.py:497
  1052.6 258.2 %reduce-scatter.17.cloned.1.call-start = ((), (), s32[]{:S(2)}) async-start(), calls=%async_computation.12 | async-start | bytes 15073280 | tf_op jit(solution)/shard_map/reduce_scatter | solution.py:497
  1053.1 326.9 %reduce-scatter.7.cloned.1.call-start = ((), (), s32[]{:S(2)}) async-start(), calls=%async_computation.7 | async-start | bytes 7864320 | tf_op jit(solution)/shard_map/reduce_scatter | solution.py:497
  1053.4 47.4 %collective-permute-start.30 = (f32[512,1024]{1,0:T(8,128)}, f32[512,1024]{1,0:T(8,128)S(1)}, u32[]{:S(2)}, u32[]{:S(2)}) collective-permute-start(f32[512,1024]{1,0:T(8,128)} %multiply_add_fusion), channel_id=1, source_target_pairs={{0,2},{1,3},{2,0},{3,1},{4,6},{5,7},{6,4},{7,5},{8,10},{9,11},{10,... | collective-permute-start | bytes 6291464 | tf_op jit(solution)/shard_map/ppermute | solution.py:494
  1053.8 47.1 %collective-permute-start.29 = (f32[512,1024]{1,0:T(8,128)}, f32[512,1024]{1,0:T(8,128)S(1)}, u32[]{:S(2)}, u32[]{:S(2)}) collective-permute-start(f32[512,1024]{1,0:T(8,128)} %convolution_multiply_fusion.3), channel_id=1, source_target_pairs={{0,1},{1,0},{2,3},{3,2},{4,5},{5,4},{6,7},{7,6},{8,9},{9,8},{10,11... | collective-permute-start | bytes 6291464 | tf_op jit(solution)/shard_map/ppermute | solution.py:494
  1108.3 17.1 %collective-permute-start.39 = (f32[128,1280]{1,0:T(8,128)S(1)}, f32[128,1280]{1,0:T(8,128)S(1)}, u32[]{:S(2)}, u32[]{:S(2)}) collective-permute-start(f32[128,1280]{1,0:T(8,128)S(1)} %get-tuple-element.198), channel_id=1, source_target_pairs={{0,3},{1,2},{2,1},{3,0},{4,7},{5,6},{6,5},{7,4},{8,11},{9,10},{10,... | collective-permute-start | bytes 1966088 | tf_op jit(solution)/shard_map/ppermute | solution.py:494
  1108.3 30.8 %collective-permute-start.38 = (f32[128,1280]{1,0:T(8,128)S(1)}, f32[128,1280]{1,0:T(8,128)S(1)}, u32[]{:S(2)}, u32[]{:S(2)}) collective-permute-start(f32[128,1280]{1,0:T(8,128)S(1)} %get-tuple-element.199), channel_id=1, source_target_pairs={{0,2},{1,3},{2,0},{3,1},{4,6},{5,7},{6,4},{7,5},{8,10},{9,11},{10,... | collective-permute-start | bytes 1966088 | tf_op jit(solution)/shard_map/ppermute | solution.py:494
  1109.6 29.5 %collective-permute-start.37 = (f32[128,1280]{1,0:T(8,128)S(1)}, f32[128,1280]{1,0:T(8,128)S(1)}, u32[]{:S(2)}, u32[]{:S(2)}) collective-permute-start(f32[128,1280]{1,0:T(8,128)S(1)} %get-tuple-element.200), channel_id=1, source_target_pairs={{0,1},{1,0},{2,3},{3,2},{4,5},{5,4},{6,7},{7,6},{8,9},{9,8},{10,11... | collective-permute-start | bytes 1966088 | tf_op jit(solution)/shard_map/ppermute | solution.py:494
  1150.8 21.4 %collective-permute-start.42 = (f32[128,1472]{0,1:T(8,128)}, f32[128,1472]{0,1:T(8,128)S(1)}, u32[]{:S(2)}, u32[]{:S(2)}) collective-permute-start(f32[128,1472]{0,1:T(8,128)} %copy.49), channel_id=1, source_target_pairs={{0,3},{1,2},{2,1},{3,0},{4,7},{5,6},{6,5},{7,4},{8,11},{9,10},{10,... | collective-permute-start | bytes 2261000 | tf_op jit(solution)/shard_map/ppermute | solution.py:494
  1152.6 33.8 %collective-permute-start.41 = (f32[128,1472]{0,1:T(8,128)}, f32[128,1472]{0,1:T(8,128)}, u32[]{:S(2)}, u32[]{:S(2)}) collective-permute-start(f32[128,1472]{0,1:T(8,128)} %copy.47), channel_id=1, source_target_pairs={{0,2},{1,3},{2,0},{3,1},{4,6},{5,7},{6,4},{7,5},{8,10},{9,11},{10,... | collective-permute-start | bytes 2261000 | tf_op jit(solution)/shard_map/ppermute | solution.py:494
  1155.3 32.5 %collective-permute-start.40 = (f32[128,1472]{0,1:T(8,128)}, f32[128,1472]{0,1:T(8,128)}, u32[]{:S(2)}, u32[]{:S(2)}) collective-permute-start(f32[128,1472]{0,1:T(8,128)} %copy.45), channel_id=1, source_target_pairs={{0,1},{1,0},{2,3},{3,2},{4,5},{5,4},{6,7},{7,6},{8,9},{9,8},{10,11... | collective-permute-start | bytes 2261000 | tf_op jit(solution)/shard_map/ppermute | solution.py:494
  (74 other events, 3251.2 us)
Sparse Core Ops, SparseCore 0:
  14.9 35.3 all-gather.1
  321.4 99.9 reduce-scatter.10
  504.6 117.1 reduce-scatter.12
  1052.1 40.3 reduce-scatter.8
  1095.4 99.7 reduce-scatter.14
  1198.2 112.5 reduce-scatter.16
  1313.7 66.2 reduce-scatter.6

commit v8 on v7

--- a/solution.py
+++ b/solution.py
@@ -14,6 +14,7 @@
 LOG2E = math.log2(math.e)
 F32 = jnp.float32
 FF_TILE = 256
+VMEM_BYTES = 56 * 2 ** 20
 FF_ROWS = 512
 BF16 = jnp.bfloat16
 
@@ -130,7 +131,7 @@
             scratch_shapes=[pltpu.VMEM((group, half), F32), pltpu.VMEM((group, half), F32), pltpu.VMEM((rows, half), F32)]),
         out_shape=[jax.ShapeDtypeStruct((width, seq), F32), jax.ShapeDtypeStruct((width, seq), BF16),
                    jax.ShapeDtypeStruct((kv_heads, group, seq), F32)],
-        compiler_params=pltpu.CompilerParams(vmem_limit_bytes=56 * 2 ** 20),
+        compiler_params=pltpu.CompilerParams(vmem_limit_bytes=VMEM_BYTES),
         cost_estimate=pl.CostEstimate(flops=4 * width * half * half * n_pairs,
                                       bytes_accessed=12 * width * seq, transcendentals=width // head_dim * half * half * n_pairs),
     )(tab, q_t, kv_all, kv_all)
@@ -159,28 +160,19 @@
             keys = k_ref[slot_rows, :]
             vals = v_ref[slot_rows, :]
             keys_t = keys.T
-
-            def products(head):
+            for head in range(group):
                 rows = slice(head * dim, (head + 1) * dim)
-                scores = dot_nn(keys, q_ref[rows, cols])
+                q_head = q_ref[rows, cols]
+                do_head = do_ref[rows, cols]
+                scores = dot_nn(keys, q_head)
                 if masked:
                     scores = jnp.where(causal_keep(half), scores, NEG_BIG)
-                return scores, dot_nn(vals, do_ref[rows, cols])
-
-            following = products(0)
-            grad_v = grad_k = jnp.zeros((dim, half), F32)
-            for head in range(group):
-                scores, grad_p = following
-                if head + 1 < group:
-                    following = products(head + 1)
-                rows = slice(head * dim, (head + 1) * dim)
                 probs = jnp.exp2(scores * factor - lse_ref[0, first_head + head:first_head + head + 1, cols])
+                grad_p = dot_nn(vals, do_head)
                 grad_s = (probs * (grad_p - delta_ref[head:head + 1, :])).astype(BF16)
-                grad_v = grad_v + dot_nt(do_ref[rows, cols], probs.astype(BF16))
-                grad_k = grad_k + dot_nt(q_ref[rows, cols], grad_s)
+                dkv_ref[slot, 1] += dot_nt(do_head, probs.astype(BF16))
+                dkv_ref[slot, 0] += scale * dot_nt(q_head, grad_s)
                 acc_ref[rows, :] += dot_nn(keys_t, grad_s)
-            dkv_ref[slot, 1] += grad_v
-            dkv_ref[slot, 0] += scale * grad_k
 
         @pl.when(tab[2, pair] == 0)
         def _():
@@ -221,7 +213,7 @@
             scratch_shapes=[pltpu.VMEM((heads, half), F32), pltpu.VMEM((rows, half), F32)]),
         out_shape=[jax.ShapeDtypeStruct((rows, seq), BF16),
                    jax.ShapeDtypeStruct((n_slots, 2, head_dim, half), F32)],
-        compiler_params=pltpu.CompilerParams(vmem_limit_bytes=56 * 2 ** 20),
+        compiler_params=pltpu.CompilerParams(vmem_limit_bytes=VMEM_BYTES),
         cost_estimate=pl.CostEstimate(flops=10 * rows * half * half * n_pairs,
                                       bytes_accessed=12 * rows * seq, transcendentals=heads * half * half * n_pairs),
     )(tab, q_t, do_t, o_f32, lse, kv_all, kv_all, *carry)
@@ -328,7 +320,7 @@
                             pltpu.SemaphoreType.DMA((n_own,)), pltpu.SemaphoreType.DMA((n_own * len(parts) + len(parts),))]),
         out_shape=[jax.ShapeDtypeStruct((d_model, width), BF16) for width in widths]
         + [jax.ShapeDtypeStruct((width, d_model), BF16) for width in widths],
-        compiler_params=pltpu.CompilerParams(vmem_limit_bytes=56 * 2 ** 20),
+        compiler_params=pltpu.CompilerParams(vmem_limit_bytes=VMEM_BYTES),
         cost_estimate=pl.CostEstimate(flops=8 * d_model * sum(widths), bytes_accessed=9 * d_model * sum(widths), transcendentals=0),
     )(table, *([w_up] * len(in_specs)), w_down)
     return outs[:len(parts)], outs[len(parts):]
@@ -403,7 +395,7 @@
         out_shape=shapes,
         input_output_aliases={len(args) + 2 + pos: pos for pos in range(len(carry))},
         scratch_shapes=[pltpu.SemaphoreType.DMA((2 * len(pieces),))] if copies else [],
-        compiler_params=pltpu.CompilerParams(vmem_limit_bytes=56 * 2 ** 20),
+        compiler_params=pltpu.CompilerParams(vmem_limit_bytes=VMEM_BYTES),
         cost_estimate=pl.CostEstimate(flops=4 * tokens * d_model * width, bytes_accessed=4 * d_model * (width + 2 * tokens),
                                       transcendentals=tokens * width),
     )(*args, up, down, *carry)
@@ -436,31 +428,42 @@
         in_specs=in_specs + [pl.BlockSpec((extra.shape[0], tile), lambda n: (0, n)) for extra in extras],
         out_specs=pl.BlockSpec((tokens, tile), lambda n: (0, n)),
         out_shape=jax.ShapeDtypeStruct((tokens, d_model), dtype),
-        compiler_params=pltpu.CompilerParams(vmem_limit_bytes=48 * 2 ** 20),
+        compiler_params=pltpu.CompilerParams(vmem_limit_bytes=VMEM_BYTES),
         cost_estimate=pl.CostEstimate(flops=2 * tokens * d_model * width, bytes_accessed=2 * width * (d_model + tokens) + 4 * tokens * d_model,
                                       transcendentals=0),
     )(*args, *extras)
 
 
-def head_grad_kernel(scale, n_pairs, *refs):
-    total = sum(dot_nn(refs[n_pairs + pair][...], refs[pair][...]) for pair in range(n_pairs))
-    refs[-1][...] = (scale * total).T
-
-
-def head_grad(scale, columns, heads_t):
+def head_grad_kernel(scale, n_pairs, n_tiles, *refs):
+    step = pl.program_id(0)
+
+    @pl.when(step < n_tiles)
+    def _():
+        total = sum(dot_nn(refs[n_pairs + pair][...], refs[pair][...]) for pair in range(n_pairs))
+        refs[-1][...] = (scale * total).T
+
+    @pl.when(step >= n_tiles)
+    def _():
+        refs[-1][...] = sum(ref[...] for ref in refs[2 * n_pairs:-1])
+
+
+def head_grad(scale, columns, heads_t, terms):
     n_pairs = len(columns)
     rows, width, tokens = columns[0].shape[1], heads_t[0].shape[0], columns[0].shape[0]
-    tile = 512
+    tile = rows
+    n_tiles, n_more = width // tile, terms[0].shape[1] // tile
+    last = n_tiles - 1
     return pl.pallas_call(
-        functools.partial(head_grad_kernel, scale, n_pairs),
-        grid=(width // tile,),
-        in_specs=[pl.BlockSpec((tokens, rows), lambda n: (0, 0))] * n_pairs + [pl.BlockSpec((tile, tokens), lambda n: (n, 0))] * n_pairs,
+        functools.partial(head_grad_kernel, scale, n_pairs, n_tiles),
+        grid=(n_tiles + n_more,),
+        in_specs=[pl.BlockSpec((tokens, rows), lambda n: (0, 0))] * n_pairs
+        + [pl.BlockSpec((tile, tokens), lambda n: (jnp.minimum(n, last), 0))] * n_pairs
+        + [pl.BlockSpec((rows, tile), lambda n: (0, jnp.maximum(n - n_tiles, 0)))] * len(terms),
         out_specs=pl.BlockSpec((rows, tile), lambda n: (0, n)),
-        out_shape=jax.ShapeDtypeStruct((rows, width), F32),
-        compiler_params=pltpu.CompilerParams(vmem_limit_bytes=48 * 2 ** 20),
-        cost_estimate=pl.CostEstimate(flops=2 * n_pairs * rows * width * tokens, bytes_accessed=2 * n_pairs * tokens * (rows + width) + 4 * rows * width,
-                                      transcendentals=0),
-    )(*columns, *heads_t)
+        out_shape=jax.ShapeDtypeStruct((rows, width + n_more * tile), F32),
+        compiler_params=pltpu.CompilerParams(vmem_limit_bytes=VMEM_BYTES),
+        cost_estimate=pl.CostEstimate(flops=2 * n_pairs * rows * width * tokens, bytes_accessed=9 * tokens * (rows + width), transcendentals=0),
+    )(*columns, *heads_t, *terms)
 
 
 def spread_kernel(splits, idx_ref, *refs):
@@ -649,11 +652,9 @@
         kv1_far, part_kv = second_send(kv1_block, (after(kv1_sent[0], *parts_q), kv1_sent[1]))
         q2_far, part_q = second_send(q2_block, (after(q2_sent[0], part_kv), q2_sent[1]))
         mine[0] = own_cols(after(grad_h_bf, part_q), 0)
-        sum_o = head_grad(inv_count, mine, (o_t, o_near, o_far, o_last))
-        q0_far = after(q0_far, sum_o)
-        sum_q0 = base_q + q0_sent[1] + q0_far
-        grad_oq = dp_reduce(jnp.concatenate([sum_o, sum_q0], axis=1))
-        kv0_own = (kv0_block(0) + kv0_sent[1] + after(kv0_far, sum_o)).astype(BF16)
+        sum_oq = head_grad(inv_count, mine, (o_t, o_near, o_far, o_last), (base_q, q0_sent[1], q0_far))
+        grad_oq = dp_reduce(sum_oq)
+        kv0_own = (kv0_block(0) + kv0_sent[1] + after(kv0_far, sum_oq)).astype(BF16)
         kv1_own = (kv1_block(0) + kv1_sent[1] + after(kv1_far, kv0_own)).astype(BF16)
         dkv_t = jnp.concatenate([jnp.concatenate([part[0, which], part[1, which]], axis=1)
                                  for which in range(2) for part in (kv0_own, kv1_own)], axis=0)
@@ -662,12 +663,14 @@
         w_far, part_w = second_send(w_block, w_sent)
         up_got.append(exchange(after(up_rows[1], part_w)))
         grad_w_up = spread_columns(my_idx, up_got, splits)
-        later = jnp.concatenate([after(dq0_t, part_w), dq1_t, dq2_t], axis=0)
-        grad_x = dot_tt(later, w_q)
-        grad_x = grad_h_bf + grad_x + dot_tt(after(dkv_t, part_w), w_kv)
         sum_q1 = q1_block(0) + q1_sent[1] + after(q1_far, part_w)
         sum_q2 = q2_block(0) + q2_sent[1] + after(q2_far, part_w)
-        grad_qk = dp_reduce(jnp.concatenate([sum_q1, sum_q2, w_block(0) + w_sent[1] + w_far], axis=1))
+        sum_w = w_block(0) + w_sent[1] + w_far
+        sum_qk = jnp.concatenate([sum_q1, sum_q2, sum_w], axis=1)
+        grad_qk = dp_reduce(sum_qk)
+        later = jnp.concatenate([after(dq0_t, sum_qk), dq1_t, dq2_t], axis=0)
+        grad_x = dot_tt(later, w_q)
+        grad_x = grad_h_bf + grad_x + dot_tt(after(dkv_t, sum_qk), w_kv)
         grad_w_down = jnp.concatenate(down_rows, axis=0)
         o_width = n_heads * head_dim
 

time: 1400 us -> 1440 us (1.029)
  waiting for transfers between devices: 553 us -> 588 us
    reduce_scatter x6, waiting for transfers between devices: 174 us -> 227 us  [dp_reduce(): return lax.psum_scatter(grad, 'dp', scatter_dimension=0, tiled=True)]
    ppermute x43, waiting for transfers between devices: 379 us -> 359 us  [swap(): lax.ppermute(values, 'cp', [(src, src ^ bits) for src in range(cp_size)])]
  transfers between devices with their start and end apart: 50 -> 50, of which waited for: 19 -> 19; matrix products, arithmetic and copies ran while one was open for 18% -> 18% of each run, Pallas kernels for 34% -> 33%
where the time goes in v8:
time: 1440 us
  waiting for transfers between devices  588 us (41%)
  Pallas kernels  496 us (34%)
  matrix products  226 us (16%)
  local copies, waits for them, and re-layouts  49.9 us (3%)
  other arithmetic  29.3 us (2%)
  between operations  25 us (2%)
  starting transfers between devices  21.5 us (1%)
    ppermute x43, waiting for transfers between devices, swap(): lax.ppermute(values, 'cp', [(src, src ^ bits) for src in range(cp_size)])  359 us
    reduce_scatter x6, waiting for transfers between devices, dp_reduce(): return lax.psum_scatter(grad, 'dp', scatter_dimension=0, tiled=True)  227 us
    pallas_call x8, Pallas kernels, ff_forward(): pl.pallas_call(functools.partial(ff_kernel, FF_ROWS, copies, index * toke...  165 us
    dot_general x4, matrix products, dot_tn(): lax.dot_general(lhs, rhs, (((0,), (0,)), ((), ())), preferred_element_typ...  128 us
    pallas_call x3, Pallas kernels, attn_backward(): pl.pallas_call(functools.partial(attn_bwd_kernel, heads, piece * heads, h...  123 us
    dot_general x21, matrix products, dot_tt(): lax.dot_general(lhs, rhs, (((0,), (1,)), ((), ())), preferred_element_typ...  94.2 us
    pallas_call x6, Pallas kernels, grad_h_block(): pl.pallas_call(functools.partial(grad_h_kernel, len(up)), grid=(d_model /...  92.8 us
    pallas_call x1, Pallas kernels, attn_forward(): pl.pallas_call(functools.partial(attn_fwd_kernel, group, head_dim ** (-0....  67.3 us
  transfers between devices with their start and end apart: 50, of which 19 were waited for; matrix products, arithmetic and copies ran while one was open for 18% of the time, Pallas kernels for 33%

profile of v8, /device:TPU:0, one launch (start us, length us, event | category | flops | bytes accessed | tf_op | source)
XLA Modules:
  0.0 1435.2 jit_solution(16714824168411461949)
XLA Ops:
  26.4 21.0 %shard_map.135 = (bf16[2048,1280]{1,0:T(8,128)(2,1)}, bf16[2048,1536]{1,0:T(8,128)(2,1)}, bf16[1280,2048]{1,0:T(8,128)(2,1)}, bf16[1536,2048]{1,0:T(8,128)(2,1)}) custom-call(s32[3,8]{1,0:T(4,128)} %pad_add_fusion.1.idx_ref, bf16[2048,11008]{1,0:T(8,128)(2,1)} %refs_34_.1, bf16[2048,11008]{1,0:T(8,128)(2,1)} %refs_34_.1, bf16[2048,11008]{1,0:T(8,128)(2,1)} %refs_34_.1, ...), custom_call_target="tpu_custom_call" | custom-call | flops 46137344 | bytes 51904512 | tf_op jit(solution)/shard_map/pallas_call | solution.py:311
  50.6 14.0 convert_bitcast_fusion.1.q_ref
  64.6 67.3 %shard_map.136 = (f32[2048,1024]{1,0:T(8,128)}, bf16[2048,1024]{1,0:T(8,128)(2,1)}, f32[2,8,1024]{2,1,0:T(8,128)}) custom-call(s32[4,9]{1,0:T(4,128)} %pad_add_fusion.tab, bf16[2048,1024]{1,0:T(8,128)(2,1)} %convert_bitcast_fusion.1.q_ref, bf16[4096,512]{1,0:T(8,128)(2,1)} %all-gather.2.cloned.1.call-done.k_ref.v_ref, ...), custom_call_target="tpu_custom_call" | custom-call | flops 19327352832 | bytes 25165824 | tf_op jit(solution)/shard_map/pallas_call | solution.py:121
  131.9 14.0 add_convert_fusion.1.refs_0_
  147.8 19.5 %shard_map.137 = (bf16[4096,1280]{1,0:T(8,128)(2,1)}, bf16[4096,1280]{1,0:T(8,128)(2,1)}, bf16[4096,2048]{1,0:T(8,128)(2,1)}, bf16[4096,2048]{1,0:T(8,128)(2,1)}) custom-call(bf16[1024,2048]{1,0:T(8,128)(2,1)} %add_convert_fusion.1.refs_0_, bf16[1024,2048]{1,0:T(8,128)(2,1)} %bitcast.28.refs_1_.refs_4_, ...), custom_call_target="tpu_custom_call" | custom-call | flops 10737418240 | bytes 27262976 | tf_op jit(solution)/shard_map/pallas_call | solution.py:389
  167.9 19.1 %shard_map.138 = (bf16[4096,1280]{1,0:T(8,128)(2,1)}, bf16[4096,1280]{1,0:T(8,128)(2,1)}, bf16[4096,2048]{1,0:T(8,128)(2,1)}, bf16[4096,2048]{1,0:T(8,128)(2,1)}) custom-call(bf16[1024,2048]{1,0:T(8,128)(2,1)} %collective-permute-done.2.refs_0_, ...), custom_call_target="tpu_custom_call", output_to_operand_aliasing={{0}: (4, {}), {1}: (5, {}), {2}: (6, {}), {3}: (7, {})} | custom-call | flops 10737418240 | bytes 27262976 | tf_op jit(solution)/shard_map/pallas_call | solution.py:389
  187.0 21.8 %shard_map.139 = (bf16[4096,1536]{1,0:T(8,128)(2,1)}, bf16[4096,1536]{1,0:T(8,128)(2,1)}) custom-call(bf16[1024,2048]{1,0:T(8,128)(2,1)} %add_convert_fusion.1.refs_0_, bf16[1024,2048]{1,0:T(8,128)(2,1)} %bitcast.28.refs_1_.refs_4_, bf16[2048,1536]{1,0:T(8,128)(2,1)} %get-tuple-element.93.refs_2_.refs_4_.refs_3_, ...), custom_call_target="tpu_custom_call" | custom-call | flops 12884901888 | bytes 29360128 | tf_op jit(solution)/shard_map/pallas_call | solution.py:389
  208.8 6.7 collective-permute-done.1.refs_0_
  220.9 19.2 %shard_map.140 = (bf16[4096,1280]{1,0:T(8,128)(2,1)}, bf16[4096,1280]{1,0:T(8,128)(2,1)}, bf16[4096,2048]{1,0:T(8,128)(2,1)}, bf16[4096,2048]{1,0:T(8,128)(2,1)}) custom-call(bf16[512,2048]{1,0:T(8,128)(2,1)} %collective-permute-done.1.refs_0_, ...), custom_call_target="tpu_custom_call", output_to_operand_aliasing={{0}: (6, {}), {1}: (7, {}), {2}: (8, {}), {3}: (9, {})} | custom-call | flops 10737418240 | bytes 27262976 | tf_op jit(solution)/shard_map/pallas_call | solution.py:389
  240.1 22.0 %shard_map.141 = (bf16[4096,1536]{1,0:T(8,128)(2,1)}, bf16[4096,1536]{1,0:T(8,128)(2,1)}) custom-call(bf16[512,2048]{1,0:T(8,128)(2,1)} %collective-permute-done.1.refs_0_, bf16[1024,2048]{1,0:T(8,128)(2,1)} %collective-permute-done.4.refs_1_, bf16[512,2048]{1,0:T(8,128)(2,1)} %collective-permute-done.5.refs_2_, ...), custom_call_target="tpu_custom_call", output_to_operand_aliasing={{0}: (6, {}), {1}: (7, {})} | custom-call | flops 12884901888 | bytes 29360128 | tf_op jit(solution)/shard_map/pallas_call | solution.py:389
  262.1 4.7 collective-permute-done.refs_0_
  272.4 19.1 %shard_map.142 = (bf16[4096,1280]{1,0:T(8,128)(2,1)}, bf16[4096,1280]{1,0:T(8,128)(2,1)}, bf16[4096,2048]{1,0:T(8,128)(2,1)}, bf16[4096,2048]{1,0:T(8,128)(2,1)}) custom-call(bf16[512,2048]{1,0:T(8,128)(2,1)} %copy-done.2, ...), custom_call_target="tpu_custom_call", output_to_operand_aliasing={{0}: (6, {}), {1}: (7, {}), {2}: (8, {}), {3}: (9, {})} | custom-call | flops 10737418240 | bytes 27262976 | tf_op jit(solution)/shard_map/pallas_call | solution.py:389
  291.5 29.6 %convolution_multiply_fusion.1 = f32[2048,1280]{1,0:T(8,128)} fusion(bf16[4096,2048]{1,0:T(8,128)(2,1)} %get-tuple-element.113, bf16[4096,1280]{1,0:T(8,128)(2,1)} %get-tuple-element.111.refs_0_), kind=kOutput, calls=%fused_computation.6 | convolution fusion | flops 21477457920 | bytes 37748736 | tf_op jit(solution)/shard_map/dot_general | solution.py:35
  321.2 13.2 shard_map.143
  334.5 22.2 %shard_map.144 = (bf16[4096,1536]{1,0:T(8,128)(2,1)}, bf16[4096,1536]{1,0:T(8,128)(2,1)}) custom-call(bf16[512,2048]{1,0:T(8,128)(2,1)} %copy-done.2, bf16[1024,2048]{1,0:T(8,128)(2,1)} %collective-permute-done.4.refs_1_, bf16[512,2048]{1,0:T(8,128)(2,1)} %copy-done.3, bf16[1024,2048]{1,0:T(8,128)(2,1)} %copy-done, ...), custom_call_target="tpu_custom_call", output_to_operand_aliasing={{0}: (6, {}), {1}: (7, {})} | custom-call | flops 12884901888 | bytes 29360128 | tf_op jit(solution)/shard_map/pallas_call | solution.py:389
  358.8 13.7 shard_map.145
  372.5 21.9 %shard_map.146 = (bf16[4096,1536]{1,0:T(8,128)(2,1)}, bf16[4096,1536]{1,0:T(8,128)(2,1)}) custom-call(bf16[1024,2048]{1,0:T(8,128)(2,1)} %collective-permute-done.2.refs_0_, bf16[1024,2048]{1,0:T(8,128)(2,1)} %collective-permute-done.3.refs_1_, ...), custom_call_target="tpu_custom_call", output_to_operand_aliasing={{0}: (4, {}), {1}: (5, {})} | custom-call | flops 12884901888 | bytes 29360128 | tf_op jit(solution)/shard_map/pallas_call | solution.py:389
  394.5 12.7 shard_map.147
  408.9 34.7 %fusion.7 = f32[2048,1472]{1,0:T(8,128)} fusion(bf16[4096,2048]{1,0:T(8,128)(2,1)} %get-tuple-element.113, bf16[4096,1536]{1,0:T(8,128)(2,1)} %get-tuple-element.130.refs_2_), kind=kOutput, calls=%fused_computation.7 | convolution fusion | flops 24699076608 | bytes 41418752 | tf_op jit(solution)/shard_map/dot_general | solution.py:35
  443.6 14.1 shard_map.148
  457.7 29.4 %convolution_multiply_fusion = f32[1280,2048]{1,0:T(8,128)} fusion(bf16[4096,1280]{1,0:T(8,128)(2,1)} %get-tuple-element.126, bf16[4096,2048]{1,0:T(8,128)(2,1)} %get-tuple-element.127), kind=kOutput, calls=%fused_computation.5 | convolution fusion | flops 21477457920 | bytes 37748736 | tf_op jit(solution)/shard_map/dot_general | solution.py:35
  487.0 17.8 %shard_map.149 = f32[1024,2048]{1,0:T(8,128)} custom-call(bf16[4096,1280]{1,0:T(8,128)(2,1)} %get-tuple-element.111.refs_0_, bf16[2048,1280]{1,0:T(8,128)(2,1)} %get-tuple-element.81.refs_2_.refs_4_.refs_1_, bf16[4096,1536]{1,0:T(8,128)(2,1)} %get-tuple-element.130.refs_2_, bf16[2048,1536]{1,0:T(8,128)(2,1)} %get-tuple-element.93.refs_2_.refs_4_.refs_3_), custom_call_target="tpu_custom_call" | custom-call | flops 11811160064 | bytes 25690112 | tf_op jit(solution)/shard_map/pallas_call | solution.py:425
  511.2 34.7 %fusion.4 = f32[1472,2048]{1,0:T(8,128)} fusion(bf16[4096,2048]{1,0:T(8,128)(2,1)} %get-tuple-element.127, bf16[4096,1536]{1,0:T(8,128)(2,1)} %get-tuple-element.129), kind=kOutput, calls=%fused_computation.4 | convolution fusion | flops 24699076608 | bytes 41418752 | tf_op jit(solution)/shard_map/dot_general | solution.py:35
  545.9 52.8 %collective-permute-done.11.refs_6_ = f32[512,2048]{1,0:T(8,128)} collective-permute-done((f32[512,2048]{1,0:T(8,128)}, f32[512,2048]{1,0:T(8,128)}, u32[]{:S(2)}, u32[]{:S(2)}) %collective-permute-start.11) | collective-permute-done | bytes 4194336 | tf_op jit(solution)/shard_map/ppermute | solution.py:497
  598.7 89.9 %collective-permute-done.12.refs_7_ = f32[512,2048]{1,0:T(8,128)} collective-permute-done((f32[512,2048]{1,0:T(8,128)}, f32[512,2048]{1,0:T(8,128)}, u32[]{:S(2)}, u32[]{:S(2)}) %collective-permute-start.12) | collective-permute-done | bytes 4194336 | tf_op jit(solution)/shard_map/ppermute | solution.py:497
  688.6 21.1 %shard_map.150 = bf16[1024,2048]{1,0:T(8,128)(2,1)} custom-call(bf16[4096,1280]{1,0:T(8,128)(2,1)} %get-tuple-element.111.refs_0_, bf16[2048,1280]{1,0:T(8,128)(2,1)} %get-tuple-element.81.refs_2_.refs_4_.refs_1_, bf16[4096,1536]{1,0:T(8,128)(2,1)} %get-tuple-element.130.refs_2_, bf16[2048,1536]{1,0:T(8,128)(2,1)} %get-tuple-element.93.refs_2_.refs_4_.refs_3_, ...), custom_call_target="tpu_custom_call" | custom-call | flops 11811160064 | bytes 25690112 | tf_op jit(solution)/shard_map/pallas_call | solution.py:425
  709.7 14.1 convert_bitcast_fusion.do_ref
  723.8 57.9 %shard_map.151 = (bf16[1024,1024]{1,0:T(8,128)(2,1)}, f32[8,2,128,512]{3,2,1,0:T(8,128)}) custom-call(s32[4,9]{1,0:T(4,128)} %pad_add_fusion.tab, bf16[2048,1024]{1,0:T(8,128)(2,1)} %convert_bitcast_fusion.1.q_ref, bf16[2048,1024]{1,0:T(8,128)(2,1)} %convert_bitcast_fusion.do_ref, f32[2048,1024]{1,0:T(8,128)} %get-tuple-element.132.of_ref, ...), custom_call_target="tpu_custom_call" | custom-call | flops 24159191040 | bytes 12582912 | tf_op jit(solution)/shard_map/pallas_call | solution.py:201
  789.7 4.5 convolution_multiply_fusion.3
  801.2 32.2 %shard_map.152 = (bf16[512,1024]{1,0:T(8,128)(2,1)}, f32[8,2,128,512]{3,2,1,0:T(8,128)}) custom-call(s32[4,9]{1,0:T(4,128)} %pad_add_fusion.tab, bf16[2048,1024]{1,0:T(8,128)(2,1)} %convert_bitcast_fusion.1.q_ref, bf16[2048,1024]{1,0:T(8,128)(2,1)} %convert_bitcast_fusion.do_ref, f32[2048,1024]{1,0:T(8,128)} %get-tuple-element.132.of_ref, ...), custom_call_target="tpu_custom_call" | custom-call | flops 12079595520 | bytes 6291456 | tf_op jit(solution)/shard_map/pallas_call | solution.py:201
  841.5 33.3 %shard_map.153 = (bf16[512,1024]{1,0:T(8,128)(2,1)}, f32[8,2,128,512]{3,2,1,0:T(8,128)}) custom-call(s32[4,9]{1,0:T(4,128)} %pad_add_fusion.tab, bf16[2048,1024]{1,0:T(8,128)(2,1)} %convert_bitcast_fusion.1.q_ref, bf16[2048,1024]{1,0:T(8,128)(2,1)} %convert_bitcast_fusion.do_ref, f32[2048,1024]{1,0:T(8,128)} %get-tuple-element.132.of_ref, ...), custom_call_target="tpu_custom_call" | custom-call | flops 12079595520 | bytes 6291456 | tf_op jit(solution)/shard_map/pallas_call | solution.py:201
  897.4 54.3 %collective-permute-done.23.refs_2_ = bf16[1024,512]{1,0:T(8,128)(2,1)} collective-permute-done((bf16[1024,512]{1,0:T(8,128)(2,1)}, bf16[1024,512]{1,0:T(8,128)(2,1)}, u32[]{:S(2)}, u32[]{:S(2)}) %collective-permute-start.23) | collective-permute-done | bytes 1048608 | tf_op jit(solution)/shard_map/ppermute | solution.py:497
  954.1 18.2 %collective-permute-done.24.refs_3_ = bf16[1024,512]{1,0:T(8,128)(2,1)S(1)} collective-permute-done((bf16[1024,512]{1,0:T(8,128)(2,1)S(1)}, bf16[1024,512]{1,0:T(8,128)(2,1)S(1)}, u32[]{:S(2)}, u32[]{:S(2)}) %collective-permute-start.24) | collective-permute-done | bytes 1048608 | tf_op jit(solution)/shard_map/ppermute | solution.py:497
  975.2 19.3 %shard_map.154 = f32[512,3072]{1,0:T(8,128)} custom-call(bf16[1024,512]{1,0:T(8,128)(2,1)} %pad_maximum_fusion.8.refs_0_, bf16[1024,512]{1,0:T(8,128)(2,1)} %collective-permute-done.22.refs_1_, bf16[1024,512]{1,0:T(8,128)(2,1)} %collective-permute-done.23.refs_2_, bf16[1024,512]{1,0:T(8,128)(2,1)} %copy-done.11, ...), custom_call_target="tpu_custom_call" | custom-call | flops 8589934592 | bytes 23592960 | tf_op jit(solution)/shard_map/pallas_call | solution.py:456
  998.8 19.4 %collective-permute-done.31 = f32[2,2,128,512]{3,2,1,0:T(8,128)} collective-permute-done((f32[2,2,128,512]{3,2,1,0:T(8,128)}, f32[2,2,128,512]{3,2,1,0:T(8,128)}, u32[]{:S(2)}, u32[]{:S(2)}) %collective-permute-start.31) | collective-permute-done | bytes 1048608 | tf_op jit(solution)/shard_map/ppermute | solution.py:497
  1027.0 21.8 %collective-permute-done.34 = f32[512,512]{1,0:T(8,128)S(1)} collective-permute-done((f32[512,512]{1,0:T(8,128)S(1)}, f32[512,512]{1,0:T(8,128)S(1)}, u32[]{:S(2)}, u32[]{:S(2)}) %collective-permute-start.34) | collective-permute-done | bytes 1048608 | tf_op jit(solution)/shard_map/ppermute | solution.py:497
  1049.1 22.2 %collective-permute-done.17 = f32[512,512]{1,0:T(8,128)S(1)} collective-permute-done((f32[512,512]{1,0:T(8,128)S(1)}, f32[512,512]{1,0:T(8,128)S(1)}, u32[]{:S(2)}, u32[]{:S(2)}) %collective-permute-start.17) | collective-permute-done | bytes 1048608 | tf_op jit(solution)/shard_map/ppermute | solution.py:497
  1072.9 20.1 %collective-permute-done.36 = f32[512,512]{1,0:T(8,128)S(1)} collective-permute-done((f32[512,512]{1,0:T(8,128)S(1)}, f32[512,512]{1,0:T(8,128)S(1)}, u32[]{:S(2)}, u32[]{:S(2)}) %collective-permute-start.36) | collective-permute-done | bytes 1048608 | tf_op jit(solution)/shard_map/ppermute | solution.py:497
  1101.4 15.2 %collective-permute-done.39 = f32[128,1280]{1,0:T(8,128)S(1)} collective-permute-done((f32[128,1280]{1,0:T(8,128)S(1)}, f32[128,1280]{1,0:T(8,128)S(1)}, u32[]{:S(2)}, u32[]{:S(2)}) %collective-permute-start.39) | collective-permute-done | bytes 655392 | tf_op jit(solution)/shard_map/ppermute | solution.py:497
  1116.6 13.0 collective-permute-done.38
  1132.2 5.7 fusion.54
  1145.7 17.2 %fusion.22 = bf16[1,1024,2048]{2,1,0:T(8,128)(2,1)} fusion(f32[1024,2048]{1,0:T(8,128)} %fusion.54, bf16[1024,2048]{1,0:T(8,128)(2,1)} %shard_map.150, bf16[256,8,16,128]{3,2,1,0:T(8,128)(2,1)} %bitcast.206, bf16[512,1024]{1,0:T(8,128)(2,1)} %get-tuple-element.142, bf16[512,1024]{1,0:T(8,128)(2,1)} %get-tuple-element.138, ...), kind=kOutput, calls=%fused_computation.23 | convolution fusion | flops 8610906112 | bytes 29360128 | tf_op jit(solution)/shard_map/dot_general | solution.py:39
  1163.2 13.5 collective-permute-done.41
  1181.3 7.2 shard_map.155
  1190.9 48.0 %reduce-scatter.15.cloned.1.call-done = f32[320,2048]{1,0:T(8,128)} async-done(((f32[1280,2048]{1,0:T(8,128)}), f32[320,2048]{1,0:T(8,128)}) %reduce-scatter.15.cloned.1.call-update) | async-done | bytes 2621456 | tf_op jit(solution)/shard_map/reduce_scatter | solution.py:500
  1239.0 115.5 %reduce-scatter.17.cloned.1.call-done = f32[368,2048]{1,0:T(8,128)} async-done(((f32[1472,2048]{1,0:T(8,128)}), f32[368,2048]{1,0:T(8,128)}) %reduce-scatter.17.cloned.1.call-update) | async-done | bytes 3014672 | tf_op jit(solution)/shard_map/reduce_scatter | solution.py:500
  1354.5 5.8 pad_maximum_fusion
  1360.3 63.4 %reduce-scatter.7.cloned.1.call-done = f32[128,3072]{1,0:T(8,128)} async-done(((f32[512,3072]{1,0:T(8,128)}), f32[128,3072]{1,0:T(8,128)}) %reduce-scatter.7.cloned.1.call-update) | async-done | bytes 1572880 | tf_op jit(solution)/shard_map/reduce_scatter | solution.py:500
  (310 shorter events, 132.0 us)
Async XLA Ops:
  7.2 57.5 %all-gather.2.cloned.1.call-start = ((), (), s32[]{:S(2)}) async-start(), calls=%async_computation.6 | async-start | bytes 5242880 | tf_op jit(solution)/shard_map/all_gather | solution.py:532
  14.8 1082.8 %reduce-scatter.11.cloned.1.call-start = ((), (), s32[]{:S(2)}) async-start(), calls=%async_computation.9 | async-start | bytes 13107200 | tf_op jit(solution)/shard_map/reduce_scatter | solution.py:500
  14.9 153.0 %collective-permute-start.3 = (bf16[1024,2048]{1,0:T(8,128)(2,1)}, bf16[1024,2048]{1,0:T(8,128)(2,1)}, u32[]{:S(2)}, u32[]{:S(2)}) collective-permute-start(bf16[1024,2048]{1,0:T(8,128)(2,1)} %bitcast.28.refs_1_.refs_4_), channel_id=1, source_target_pairs={{0,1},{1,0},{2,3},{3,2},{4,5},{5,4},{6,7},{7,6},{8,9},{9,8},{10,11... | collective-permute-start | bytes 12582920 | tf_op jit(solution)/shard_map/ppermute | solution.py:497
  47.4 120.2 %collective-permute-start.4 = (bf16[1024,2048]{1,0:T(8,128)(2,1)}, bf16[1024,2048]{1,0:T(8,128)(2,1)}, u32[]{:S(2)}, u32[]{:S(2)}) collective-permute-start(bf16[1024,2048]{1,0:T(8,128)(2,1)} %bitcast.28.refs_1_.refs_4_), channel_id=1, source_target_pairs={{0,2},{1,3},{2,0},{3,1},{4,6},{5,7},{6,4},{7,5},{8,10},{9,11},{10,... | collective-permute-start | bytes 12582920 | tf_op jit(solution)/shard_map/ppermute | solution.py:497
  146.0 21.9 %collective-permute-start.2 = (bf16[1024,2048]{1,0:T(8,128)(2,1)}, bf16[1024,2048]{1,0:T(8,128)(2,1)}, u32[]{:S(2)}, u32[]{:S(2)}) collective-permute-start(bf16[1024,2048]{1,0:T(8,128)(2,1)} %add_convert_fusion.1.refs_0_), channel_id=1, source_target_pairs={{0,1},{1,0},{2,3},{3,2},{4,5},{5,4},{6,7},{7,6},{8,9},{9,8},{10,11... | collective-permute-start | bytes 12582920 | tf_op jit(solution)/shard_map/ppermute | solution.py:497
  167.3 48.1 %collective-permute-start.1 = (bf16[512,2048]{1,0:T(8,128)(2,1)S(1)}, bf16[512,2048]{1,0:T(8,128)(2,1)}, u32[]{:S(2)}, u32[]{:S(2)}) collective-permute-start(bf16[512,2048]{1,0:T(8,128)(2,1)S(1)} %slice.88), channel_id=1, source_target_pairs={{0,2},{1,3},{2,0},{3,1},{4,6},{5,7},{6,4},{7,5},{8,10},{9,11},{10,... | collective-permute-start | bytes 6291464 | tf_op jit(solution)/shard_map/ppermute | solution.py:497
  167.6 51.3 %collective-permute-start.6 = (bf16[1024,2048]{1,0:T(8,128)(2,1)}, bf16[1024,2048]{1,0:T(8,128)(2,1)S(1)}, u32[]{:S(2)}, u32[]{:S(2)}) collective-permute-start(bf16[1024,2048]{1,0:T(8,128)(2,1)} %collective-permute-done.4.refs_1_), channel_id=1, source_target_pairs={{0,1},{1,0},{2,3},{3,2},{4,5},{5,4},{6,7},{7,6},{8,9},{9,8},{10,11... | collective-permute-start | bytes 12582920 | tf_op jit(solution)/shard_map/ppermute | solution.py:497
  215.5 4.5 collective-permute-start.5
  218.6 48.3 %collective-permute-start = (bf16[512,2048]{1,0:T(8,128)(2,1)}, bf16[512,2048]{1,0:T(8,128)(2,1)S(1)}, u32[]{:S(2)}, u32[]{:S(2)}) collective-permute-start(bf16[512,2048]{1,0:T(8,128)(2,1)} %slice.71), channel_id=1, source_target_pairs={{0,2},{1,3},{2,0},{3,1},{4,6},{5,7},{6,4},{7,5},{8,10},{9,11},{10,... | collective-permute-start | bytes 6291464 | tf_op jit(solution)/shard_map/ppermute | solution.py:497
  321.1 816.7 %reduce-scatter.13.cloned.1.call-start = ((), (), s32[]{:S(2)}) async-start(), calls=%async_computation.10 | async-start | bytes 15728640 | tf_op jit(solution)/shard_map/reduce_scatter | solution.py:500
  334.4 22.3 %collective-permute-start.8 = (f32[512,2048]{1,0:T(8,128)}, f32[512,2048]{1,0:T(8,128)S(1)}, u32[]{:S(2)}, u32[]{:S(2)}) collective-permute-start(f32[512,2048]{1,0:T(8,128)} %shard_map.143), channel_id=1, source_target_pairs={{0,1},{1,0},{2,3},{3,2},{4,5},{5,4},{6,7},{7,6},{8,9},{9,8},{10,11... | collective-permute-start | bytes 12582920 | tf_op jit(solution)/shard_map/ppermute | solution.py:497
  407.2 36.4 %collective-permute-start.9 = (f32[512,2048]{1,0:T(8,128)}, f32[512,2048]{1,0:T(8,128)}, u32[]{:S(2)}, u32[]{:S(2)}) collective-permute-start(f32[512,2048]{1,0:T(8,128)} %shard_map.147), channel_id=1, source_target_pairs={{0,1},{1,0},{2,3},{3,2},{4,5},{5,4},{6,7},{7,6},{8,9},{9,8},{10,11... | collective-permute-start | bytes 12582920 | tf_op jit(solution)/shard_map/ppermute | solution.py:497
  504.9 183.7 %collective-permute-start.10 = (f32[1024,2048]{1,0:T(8,128)}, f32[1024,2048]{1,0:T(8,128)}, u32[]{:S(2)}, u32[]{:S(2)}) collective-permute-start(f32[1024,2048]{1,0:T(8,128)} %shard_map.149), channel_id=1, source_target_pairs={{0,1},{1,0},{2,3},{3,2},{4,5},{5,4},{6,7},{7,6},{8,9},{9,8},{10,11... | collective-permute-start | bytes 25165832 | tf_op jit(solution)/shard_map/ppermute | solution.py:497
  505.0 93.8 %collective-permute-start.11 = (f32[512,2048]{1,0:T(8,128)}, f32[512,2048]{1,0:T(8,128)}, u32[]{:S(2)}, u32[]{:S(2)}) collective-permute-start(f32[512,2048]{1,0:T(8,128)} %shard_map.145), channel_id=1, source_target_pairs={{0,2},{1,3},{2,0},{3,1},{4,6},{5,7},{6,4},{7,5},{8,10},{9,11},{10,... | collective-permute-start | bytes 12582920 | tf_op jit(solution)/shard_map/ppermute | solution.py:497
  505.0 183.6 %collective-permute-start.12 = (f32[512,2048]{1,0:T(8,128)}, f32[512,2048]{1,0:T(8,128)}, u32[]{:S(2)}, u32[]{:S(2)}) collective-permute-start(f32[512,2048]{1,0:T(8,128)} %shard_map.148), channel_id=1, source_target_pairs={{0,2},{1,3},{2,0},{3,1},{4,6},{5,7},{6,4},{7,5},{8,10},{9,11},{10,... | collective-permute-start | bytes 12582920 | tf_op jit(solution)/shard_map/ppermute | solution.py:497
  507.0 681.5 %reduce-scatter.9.cloned.1.call-start = ((), (), s32[]{:S(2)}) async-start(), calls=%async_computation.8 | async-start | bytes 3932160 | tf_op jit(solution)/shard_map/reduce_scatter | solution.py:500
  511.2 278.1 %collective-permute-start.26 = (bf16[2048,1024]{1,0:T(8,128)(2,1)}, bf16[2048,1024]{1,0:T(8,128)(2,1)}, u32[]{:S(2)}, u32[]{:S(2)}) collective-permute-start(bf16[2048,1024]{1,0:T(8,128)(2,1)} %get-tuple-element.147.refs_4_), channel_id=1, source_target_pairs={{0,2},{1,3},{2,0},{3,1},{4,6},{5,7},{6,4},{7,5},{8,10},{9,11},{10,... | collective-permute-start | bytes 12582920 | tf_op jit(solution)/shard_map/ppermute | solution.py:497
  786.0 10.9 collective-permute-start.14
  788.7 5.6 collective-permute-start.13
  789.2 91.2 %collective-permute-start.25 = (bf16[2048,1024]{1,0:T(8,128)(2,1)}, bf16[2048,1024]{1,0:T(8,128)(2,1)S(1)}, u32[]{:S(2)}, u32[]{:S(2)}) collective-permute-start(bf16[2048,1024]{1,0:T(8,128)(2,1)} %get-tuple-element.147.refs_4_), channel_id=1, source_target_pairs={{0,1},{1,0},{2,3},{3,2},{4,5},{5,4},{6,7},{7,6},{8,9},{9,8},{10,11... | collective-permute-start | bytes 12582920 | tf_op jit(solution)/shard_map/ppermute | solution.py:497
  789.2 94.6 %collective-permute-start.27 = (bf16[2048,1024]{1,0:T(8,128)(2,1)}, bf16[2048,1024]{1,0:T(8,128)(2,1)}, u32[]{:S(2)}, u32[]{:S(2)}) collective-permute-start(bf16[2048,1024]{1,0:T(8,128)(2,1)} %collective-permute-done.26.refs_6_), channel_id=1, source_target_pairs={{0,1},{1,0},{2,3},{3,2},{4,5},{5,4},{6,7},{7,6},{8,9},{9,8},{10,11... | collective-permute-start | bytes 12582920 | tf_op jit(solution)/shard_map/ppermute | solution.py:497
  835.6 5.7 collective-permute-start.16
  877.7 7.3 collective-permute-start.21
  879.9 8.8 collective-permute-start.20
  880.0 93.9 %collective-permute-start.28 = (f32[512,1024]{1,0:T(8,128)}, f32[512,1024]{1,0:T(8,128)S(1)}, u32[]{:S(2)}, u32[]{:S(2)}) collective-permute-start(f32[512,1024]{1,0:T(8,128)} %convolution_multiply_fusion.3), channel_id=1, source_target_pairs={{0,1},{1,0},{2,3},{3,2},{4,5},{5,4},{6,7},{7,6},{8,9},{9,8},{10,11... | collective-permute-start | bytes 6291464 | tf_op jit(solution)/shard_map/ppermute | solution.py:497
  880.4 93.5 %collective-permute-start.29 = (f32[512,1024]{1,0:T(8,128)}, f32[512,1024]{1,0:T(8,128)}, u32[]{:S(2)}, u32[]{:S(2)}) collective-permute-start(f32[512,1024]{1,0:T(8,128)} %multiply_add_fusion), channel_id=1, source_target_pairs={{0,2},{1,3},{2,0},{3,1},{4,6},{5,7},{6,4},{7,5},{8,10},{9,11},{10,... | collective-permute-start | bytes 6291464 | tf_op jit(solution)/shard_map/ppermute | solution.py:497
  883.8 13.3 collective-permute-start.22
  885.9 65.8 %collective-permute-start.23 = (bf16[1024,512]{1,0:T(8,128)(2,1)}, bf16[1024,512]{1,0:T(8,128)(2,1)}, u32[]{:S(2)}, u32[]{:S(2)}) collective-permute-start(bf16[1024,512]{1,0:T(8,128)(2,1)} %pad_maximum_fusion.10), channel_id=1, source_target_pairs={{0,2},{1,3},{2,0},{3,1},{4,6},{5,7},{6,4},{7,5},{8,10},{9,11},{10,... | collective-permute-start | bytes 3145736 | tf_op jit(solution)/shard_map/ppermute | solution.py:497
  888.7 83.5 %collective-permute-start.24 = (bf16[1024,512]{1,0:T(8,128)(2,1)S(1)}, bf16[1024,512]{1,0:T(8,128)(2,1)S(1)}, u32[]{:S(2)}, u32[]{:S(2)}) collective-permute-start(bf16[1024,512]{1,0:T(8,128)(2,1)S(1)} %pad_maximum_fusion.11), channel_id=1, source_target_pairs={{0,3},{1,2},{2,1},{3,0},{4,7},{5,6},{6,5},{7,4},{8,11},{9,10},{10,... | collective-permute-start | bytes 3145736 | tf_op jit(solution)/shard_map/ppermute | solution.py:497
  897.1 99.6 %collective-permute-start.18 = (f32[2,2,128,512]{3,2,1,0:T(8,128)}, f32[2,2,128,512]{3,2,1,0:T(8,128)}, u32[]{:S(2)}, u32[]{:S(2)}) collective-permute-start(f32[2,2,128,512]{3,2,1,0:T(8,128)} %get-tuple-element.157), channel_id=1, source_target_pairs={{0,1},{1,0},{2,3},{3,2},{4,5},{5,4},{6,7},{7,6},{8,9},{9,8},{10,11... | collective-permute-start | bytes 3145736 | tf_op jit(solution)/shard_map/ppermute | solution.py:497
  951.7 44.9 %collective-permute-start.19 = (f32[2,2,128,512]{3,2,1,0:T(8,128)}, f32[2,2,128,512]{3,2,1,0:T(8,128)}, u32[]{:S(2)}, u32[]{:S(2)}) collective-permute-start(f32[2,2,128,512]{3,2,1,0:T(8,128)} %bitcast_add_fusion.3), channel_id=1, source_target_pairs={{0,2},{1,3},{2,0},{3,1},{4,6},{5,7},{6,4},{7,5},{8,10},{9,11},{10,... | collective-permute-start | bytes 3145736 | tf_op jit(solution)/shard_map/ppermute | solution.py:497
  972.3 46.0 %collective-permute-start.30 = (f32[2,2,128,512]{3,2,1,0:T(8,128)}, f32[2,2,128,512]{3,2,1,0:T(8,128)}, u32[]{:S(2)}, u32[]{:S(2)}) collective-permute-start(f32[2,2,128,512]{3,2,1,0:T(8,128)} %get-tuple-element.155), channel_id=1, source_target_pairs={{0,1},{1,0},{2,3},{3,2},{4,5},{5,4},{6,7},{7,6},{8,9},{9,8},{10,11... | collective-permute-start | bytes 3145736 | tf_op jit(solution)/shard_map/ppermute | solution.py:497
  973.9 44.3 %collective-permute-start.31 = (f32[2,2,128,512]{3,2,1,0:T(8,128)}, f32[2,2,128,512]{3,2,1,0:T(8,128)}, u32[]{:S(2)}, u32[]{:S(2)}) collective-permute-start(f32[2,2,128,512]{3,2,1,0:T(8,128)} %bitcast_add_fusion.1), channel_id=1, source_target_pairs={{0,2},{1,3},{2,0},{3,1},{4,6},{5,7},{6,4},{7,5},{8,10},{9,11},{10,... | collective-permute-start | bytes 3145736 | tf_op jit(solution)/shard_map/ppermute | solution.py:497
  1022.8 26.0 %collective-permute-start.34 = (f32[512,512]{1,0:T(8,128)S(1)}, f32[512,512]{1,0:T(8,128)S(1)}, u32[]{:S(2)}, u32[]{:S(2)}) collective-permute-start(f32[512,512]{1,0:T(8,128)S(1)} %copy-done.10), channel_id=1, source_target_pairs={{0,2},{1,3},{2,0},{3,1},{4,6},{5,7},{6,4},{7,5},{8,10},{9,11},{10,... | collective-permute-start | bytes 3145736 | tf_op jit(solution)/shard_map/ppermute | solution.py:497
  1023.1 48.2 %collective-permute-start.17 = (f32[512,512]{1,0:T(8,128)S(1)}, f32[512,512]{1,0:T(8,128)S(1)}, u32[]{:S(2)}, u32[]{:S(2)}) collective-permute-start(f32[512,512]{1,0:T(8,128)S(1)} %add.418), channel_id=1, source_target_pairs={{0,2},{1,3},{2,0},{3,1},{4,6},{5,7},{6,4},{7,5},{8,10},{9,11},{10,... | collective-permute-start | bytes 3145736 | tf_op jit(solution)/shard_map/ppermute | solution.py:497
  1024.8 46.5 %collective-permute-start.33 = (f32[512,512]{1,0:T(8,128)S(1)}, f32[512,512]{1,0:T(8,128)S(1)}, u32[]{:S(2)}, u32[]{:S(2)}) collective-permute-start(f32[512,512]{1,0:T(8,128)S(1)} %copy-done.67), channel_id=1, source_target_pairs={{0,1},{1,0},{2,3},{3,2},{4,5},{5,4},{6,7},{7,6},{8,9},{9,8},{10,11... | collective-permute-start | bytes 3145736 | tf_op jit(solution)/shard_map/ppermute | solution.py:497
  1024.8 47.3 %collective-permute-start.15 = (f32[512,512]{1,0:T(8,128)S(1)}, f32[512,512]{1,0:T(8,128)S(1)}, u32[]{:S(2)}, u32[]{:S(2)}) collective-permute-start(f32[512,512]{1,0:T(8,128)S(1)} %copy-done.66), channel_id=1, source_target_pairs={{0,1},{1,0},{2,3},{3,2},{4,5},{5,4},{6,7},{7,6},{8,9},{9,8},{10,11... | collective-permute-start | bytes 3145736 | tf_op jit(solution)/shard_map/ppermute | solution.py:497
  1026.2 46.7 %collective-permute-start.35 = (f32[512,512]{1,0:T(8,128)S(1)}, f32[512,512]{1,0:T(8,128)S(1)}, u32[]{:S(2)}, u32[]{:S(2)}) collective-permute-start(f32[512,512]{1,0:T(8,128)S(1)} %convolution_multiply_fusion.5), channel_id=1, source_target_pairs={{0,1},{1,0},{2,3},{3,2},{4,5},{5,4},{6,7},{7,6},{8,9},{9,8},{10,11... | collective-permute-start | bytes 3145736 | tf_op jit(solution)/shard_map/ppermute | solution.py:497
  1048.8 44.1 %collective-permute-start.36 = (f32[512,512]{1,0:T(8,128)S(1)}, f32[512,512]{1,0:T(8,128)S(1)}, u32[]{:S(2)}, u32[]{:S(2)}) collective-permute-start(f32[512,512]{1,0:T(8,128)S(1)} %fusion.41), channel_id=1, source_target_pairs={{0,2},{1,3},{2,0},{3,1},{4,6},{5,7},{6,4},{7,5},{8,10},{9,11},{10,... | collective-permute-start | bytes 3145736 | tf_op jit(solution)/shard_map/ppermute | solution.py:497
  1095.6 143.3 %reduce-scatter.15.cloned.1.call-start = ((), (), s32[]{:S(2)}) async-start(), calls=%async_computation.11 | async-start | bytes 13107200 | tf_op jit(solution)/shard_map/reduce_scatter | solution.py:500
  1096.2 258.3 %reduce-scatter.17.cloned.1.call-start = ((), (), s32[]{:S(2)}) async-start(), calls=%async_computation.12 | async-start | bytes 15073280 | tf_op jit(solution)/shard_map/reduce_scatter | solution.py:500
  1096.8 327.0 %reduce-scatter.7.cloned.1.call-start = ((), (), s32[]{:S(2)}) async-start(), calls=%async_computation.7 | async-start | bytes 7864320 | tf_op jit(solution)/shard_map/reduce_scatter | solution.py:500
  1099.5 17.1 %collective-permute-start.39 = (f32[128,1280]{1,0:T(8,128)S(1)}, f32[128,1280]{1,0:T(8,128)S(1)}, u32[]{:S(2)}, u32[]{:S(2)}) collective-permute-start(f32[128,1280]{1,0:T(8,128)S(1)} %get-tuple-element.196), channel_id=1, source_target_pairs={{0,3},{1,2},{2,1},{3,0},{4,7},{5,6},{6,5},{7,4},{8,11},{9,10},{10,... | collective-permute-start | bytes 1966088 | tf_op jit(solution)/shard_map/ppermute | solution.py:497
  1099.6 30.0 %collective-permute-start.38 = (f32[128,1280]{1,0:T(8,128)S(1)}, f32[128,1280]{1,0:T(8,128)S(1)}, u32[]{:S(2)}, u32[]{:S(2)}) collective-permute-start(f32[128,1280]{1,0:T(8,128)S(1)} %get-tuple-element.197), channel_id=1, source_target_pairs={{0,2},{1,3},{2,0},{3,1},{4,6},{5,7},{6,4},{7,5},{8,10},{9,11},{10,... | collective-permute-start | bytes 1966088 | tf_op jit(solution)/shard_map/ppermute | solution.py:497
  1100.5 29.1 %collective-permute-start.37 = (f32[128,1280]{1,0:T(8,128)S(1)}, f32[128,1280]{1,0:T(8,128)S(1)}, u32[]{:S(2)}, u32[]{:S(2)}) collective-permute-start(f32[128,1280]{1,0:T(8,128)S(1)} %get-tuple-element.198), channel_id=1, source_target_pairs={{0,1},{1,0},{2,3},{3,2},{4,5},{5,4},{6,7},{7,6},{8,9},{9,8},{10,11... | collective-permute-start | bytes 1966088 | tf_op jit(solution)/shard_map/ppermute | solution.py:497
  1141.1 21.8 %collective-permute-start.42 = (f32[128,1472]{0,1:T(8,128)}, f32[128,1472]{0,1:T(8,128)S(1)}, u32[]{:S(2)}, u32[]{:S(2)}) collective-permute-start(f32[128,1472]{0,1:T(8,128)} %copy.49), channel_id=1, source_target_pairs={{0,3},{1,2},{2,1},{3,0},{4,7},{5,6},{6,5},{7,4},{8,11},{9,10},{10,... | collective-permute-start | bytes 2261000 | tf_op jit(solution)/shard_map/ppermute | solution.py:497
  1143.0 33.7 %collective-permute-start.41 = (f32[128,1472]{0,1:T(8,128)}, f32[128,1472]{0,1:T(8,128)}, u32[]{:S(2)}, u32[]{:S(2)}) collective-permute-start(f32[128,1472]{0,1:T(8,128)} %copy.47), channel_id=1, source_target_pairs={{0,2},{1,3},{2,0},{3,1},{4,6},{5,7},{6,4},{7,5},{8,10},{9,11},{10,... | collective-permute-start | bytes 2261000 | tf_op jit(solution)/shard_map/ppermute | solution.py:497
  1145.7 32.4 %collective-permute-start.40 = (f32[128,1472]{0,1:T(8,128)}, f32[128,1472]{0,1:T(8,128)}, u32[]{:S(2)}, u32[]{:S(2)}) collective-permute-start(f32[128,1472]{0,1:T(8,128)} %copy.45), channel_id=1, source_target_pairs={{0,1},{1,0},{2,3},{3,2},{4,5},{5,4},{6,7},{7,6},{8,9},{9,8},{10,11... | collective-permute-start | bytes 2261000 | tf_op jit(solution)/shard_map/ppermute | solution.py:497
  (78 other events, 3547.9 us)
Sparse Core Ops, SparseCore 0:
  14.9 35.3 all-gather.1
  321.3 99.9 reduce-scatter.10
  507.1 117.2 reduce-scatter.12
  1095.7 40.5 reduce-scatter.8
  1139.2 99.7 reduce-scatter.14
  1241.9 112.5 reduce-scatter.16
  1357.5 66.2 reduce-scatter.6

commit v9 on v8

--- a/solution.py
+++ b/solution.py
@@ -625,8 +625,10 @@
             part = block(2) + sent[0]
             return swap(part, 2), part
 
-        mine = [None] + [swap(own_cols(grad_h_bf, bits), bits) for bits in range(1, cp_size)]
-        do_t = dot_tt(w_o, grad_h_bf).astype(BF16)
+        mine = [own_cols(grad_h_bf, bits) for bits in range(cp_size)]
+        later = after(grad_h_bf, mine[0])
+        mine[1:] = [swap(mine[bits], bits) for bits in range(1, cp_size)]
+        do_t = dot_tt(w_o, later).astype(BF16)
 
         def kv_block(dkv):
             blocks = dkv.reshape((cp_size, 2) + dkv.shape[1:])
@@ -650,11 +652,12 @@
         kv1_sent, parts_kv = first_sends(kv1_block)
         q2_sent, parts_q = first_sends(q2_block)
         kv1_far, part_kv = second_send(kv1_block, (after(kv1_sent[0], *parts_q), kv1_sent[1]))
-        q2_far, part_q = second_send(q2_block, (after(q2_sent[0], part_kv), q2_sent[1]))
-        mine[0] = own_cols(after(grad_h_bf, part_q), 0)
+        mine[0] = after(mine[0], part_kv)
         sum_oq = head_grad(inv_count, mine, (o_t, o_near, o_far, o_last), (base_q, q0_sent[1], q0_far))
         grad_oq = dp_reduce(sum_oq)
-        kv0_own = (kv0_block(0) + kv0_sent[1] + after(kv0_far, sum_oq)).astype(BF16)
+        q2_far, part_q = second_send(q2_block, (after(q2_sent[0], sum_oq), q2_sent[1]))
+        kv0_far = after(kv0_far, part_q)
+        kv0_own = (kv0_block(0) + kv0_sent[1] + kv0_far).astype(BF16)
         kv1_own = (kv1_block(0) + kv1_sent[1] + after(kv1_far, kv0_own)).astype(BF16)
         dkv_t = jnp.concatenate([jnp.concatenate([part[0, which], part[1, which]], axis=1)
                                  for which in range(2) for part in (kv0_own, kv1_own)], axis=0)

time: 1440 us -> 1450 us (level)
  transfers between devices with their start and end apart: 50 -> 50, of which waited for: 19 -> 18; matrix products, arithmetic and copies ran while one was open for 18% -> 18% of each run, Pallas kernels for 33% -> 33%
where the time goes in v9:
time: 1450 us; the launch traced here: 1440 us
  waiting for transfers between devices  591 us (41%)
  Pallas kernels  496 us (34%)
  matrix products  226 us (16%)
  local copies, waits for them, and re-layouts  49.8 us (3%)
  other arithmetic  28.5 us (2%)
  between operations  25 us (2%)
  starting transfers between devices  20.9 us (1%)
    ppermute x43, waiting for transfers between devices, swap(): lax.ppermute(values, 'cp', [(src, src ^ bits) for src in range(cp_size)])  363 us
    reduce_scatter x6, waiting for transfers between devices, dp_reduce(): return lax.psum_scatter(grad, 'dp', scatter_dimension=0, tiled=True)  226 us
    pallas_call x8, Pallas kernels, ff_forward(): pl.pallas_call(functools.partial(ff_kernel, FF_ROWS, copies, index * toke...  165 us
    dot_general x4, matrix products, dot_tn(): lax.dot_general(lhs, rhs, (((0,), (0,)), ((), ())), preferred_element_typ...  128 us
    pallas_call x3, Pallas kernels, attn_backward(): pl.pallas_call(functools.partial(attn_bwd_kernel, heads, piece * heads, h...  124 us
    dot_general x21, matrix products, dot_tt(): lax.dot_general(lhs, rhs, (((0,), (1,)), ((), ())), preferred_element_typ...  95.5 us
    pallas_call x6, Pallas kernels, grad_h_block(): pl.pallas_call(functools.partial(grad_h_kernel, len(up)), grid=(d_model /...  92.9 us
    pallas_call x1, Pallas kernels, attn_forward(): pl.pallas_call(functools.partial(attn_fwd_kernel, group, head_dim ** (-0....  67.3 us
  transfers between devices with their start and end apart: 50, of which 18 were waited for; matrix products, arithmetic and copies ran while one was open for 18% of the time, Pallas kernels for 33%

profile of v9, /device:TPU:0, one launch (start us, length us, event | category | flops | bytes accessed | tf_op | source)
XLA Modules:
  0.0 1437.8 jit_solution(12084814499441377154)
XLA Ops:
  26.4 21.0 %shard_map.135 = (bf16[2048,1280]{1,0:T(8,128)(2,1)}, bf16[2048,1536]{1,0:T(8,128)(2,1)}, bf16[1280,2048]{1,0:T(8,128)(2,1)}, bf16[1536,2048]{1,0:T(8,128)(2,1)}) custom-call(s32[3,8]{1,0:T(4,128)} %pad_add_fusion.1.idx_ref, bf16[2048,11008]{1,0:T(8,128)(2,1)} %refs_34_.1, bf16[2048,11008]{1,0:T(8,128)(2,1)} %refs_34_.1, bf16[2048,11008]{1,0:T(8,128)(2,1)} %refs_34_.1, ...), custom_call_target="tpu_custom_call" | custom-call | flops 46137344 | bytes 51904512 | tf_op jit(solution)/shard_map/pallas_call | solution.py:311
  50.6 14.0 convert_bitcast_fusion.1.q_ref
  64.6 67.3 %shard_map.136 = (f32[2048,1024]{1,0:T(8,128)}, bf16[2048,1024]{1,0:T(8,128)(2,1)}, f32[2,8,1024]{2,1,0:T(8,128)}) custom-call(s32[4,9]{1,0:T(4,128)} %pad_add_fusion.tab, bf16[2048,1024]{1,0:T(8,128)(2,1)} %convert_bitcast_fusion.1.q_ref, bf16[4096,512]{1,0:T(8,128)(2,1)} %all-gather.2.cloned.1.call-done.k_ref.v_ref, ...), custom_call_target="tpu_custom_call" | custom-call | flops 19327352832 | bytes 25165824 | tf_op jit(solution)/shard_map/pallas_call | solution.py:121
  131.9 14.0 add_convert_fusion.1.refs_0_
  147.8 19.5 %shard_map.137 = (bf16[4096,1280]{1,0:T(8,128)(2,1)}, bf16[4096,1280]{1,0:T(8,128)(2,1)}, bf16[4096,2048]{1,0:T(8,128)(2,1)}, bf16[4096,2048]{1,0:T(8,128)(2,1)}) custom-call(bf16[1024,2048]{1,0:T(8,128)(2,1)} %add_convert_fusion.1.refs_0_, bf16[1024,2048]{1,0:T(8,128)(2,1)} %bitcast.28.refs_1_.refs_4_, ...), custom_call_target="tpu_custom_call" | custom-call | flops 10737418240 | bytes 27262976 | tf_op jit(solution)/shard_map/pallas_call | solution.py:389
  167.9 19.2 %shard_map.138 = (bf16[4096,1280]{1,0:T(8,128)(2,1)}, bf16[4096,1280]{1,0:T(8,128)(2,1)}, bf16[4096,2048]{1,0:T(8,128)(2,1)}, bf16[4096,2048]{1,0:T(8,128)(2,1)}) custom-call(bf16[1024,2048]{1,0:T(8,128)(2,1)} %collective-permute-done.2.refs_0_, ...), custom_call_target="tpu_custom_call", output_to_operand_aliasing={{0}: (4, {}), {1}: (5, {}), {2}: (6, {}), {3}: (7, {})} | custom-call | flops 10737418240 | bytes 27262976 | tf_op jit(solution)/shard_map/pallas_call | solution.py:389
  187.1 22.0 %shard_map.139 = (bf16[4096,1536]{1,0:T(8,128)(2,1)}, bf16[4096,1536]{1,0:T(8,128)(2,1)}) custom-call(bf16[1024,2048]{1,0:T(8,128)(2,1)} %add_convert_fusion.1.refs_0_, bf16[1024,2048]{1,0:T(8,128)(2,1)} %bitcast.28.refs_1_.refs_4_, bf16[2048,1536]{1,0:T(8,128)(2,1)} %get-tuple-element.94.refs_2_.refs_4_.refs_3_, ...), custom_call_target="tpu_custom_call" | custom-call | flops 12884901888 | bytes 29360128 | tf_op jit(solution)/shard_map/pallas_call | solution.py:389
  209.0 6.4 collective-permute-done.1.refs_0_
  220.9 19.2 %shard_map.140 = (bf16[4096,1280]{1,0:T(8,128)(2,1)}, bf16[4096,1280]{1,0:T(8,128)(2,1)}, bf16[4096,2048]{1,0:T(8,128)(2,1)}, bf16[4096,2048]{1,0:T(8,128)(2,1)}) custom-call(bf16[512,2048]{1,0:T(8,128)(2,1)} %collective-permute-done.1.refs_0_, ...), custom_call_target="tpu_custom_call", output_to_operand_aliasing={{0}: (6, {}), {1}: (7, {}), {2}: (8, {}), {3}: (9, {})} | custom-call | flops 10737418240 | bytes 27262976 | tf_op jit(solution)/shard_map/pallas_call | solution.py:389
  240.1 22.1 %shard_map.141 = (bf16[4096,1536]{1,0:T(8,128)(2,1)}, bf16[4096,1536]{1,0:T(8,128)(2,1)}) custom-call(bf16[512,2048]{1,0:T(8,128)(2,1)} %collective-permute-done.1.refs_0_, bf16[1024,2048]{1,0:T(8,128)(2,1)} %collective-permute-done.4.refs_1_, bf16[512,2048]{1,0:T(8,128)(2,1)} %collective-permute-done.5.refs_2_, ...), custom_call_target="tpu_custom_call", output_to_operand_aliasing={{0}: (6, {}), {1}: (7, {})} | custom-call | flops 12884901888 | bytes 29360128 | tf_op jit(solution)/shard_map/pallas_call | solution.py:389
  262.2 4.7 collective-permute-done.refs_0_
  272.4 19.2 %shard_map.142 = (bf16[4096,1280]{1,0:T(8,128)(2,1)}, bf16[4096,1280]{1,0:T(8,128)(2,1)}, bf16[4096,2048]{1,0:T(8,128)(2,1)}, bf16[4096,2048]{1,0:T(8,128)(2,1)}) custom-call(bf16[512,2048]{1,0:T(8,128)(2,1)} %copy-done.2, ...), custom_call_target="tpu_custom_call", output_to_operand_aliasing={{0}: (6, {}), {1}: (7, {}), {2}: (8, {}), {3}: (9, {})} | custom-call | flops 10737418240 | bytes 27262976 | tf_op jit(solution)/shard_map/pallas_call | solution.py:389
  291.6 29.5 %convolution_multiply_fusion.1 = f32[2048,1280]{1,0:T(8,128)} fusion(bf16[4096,2048]{1,0:T(8,128)(2,1)} %get-tuple-element.114, bf16[4096,1280]{1,0:T(8,128)(2,1)} %get-tuple-element.112.refs_0_), kind=kOutput, calls=%fused_computation.6 | convolution fusion | flops 21477457920 | bytes 37748736 | tf_op jit(solution)/shard_map/dot_general | solution.py:35
  321.2 13.3 shard_map.143
  334.5 22.2 %shard_map.144 = (bf16[4096,1536]{1,0:T(8,128)(2,1)}, bf16[4096,1536]{1,0:T(8,128)(2,1)}) custom-call(bf16[512,2048]{1,0:T(8,128)(2,1)} %copy-done.2, bf16[1024,2048]{1,0:T(8,128)(2,1)} %collective-permute-done.4.refs_1_, bf16[512,2048]{1,0:T(8,128)(2,1)} %copy-done.3, bf16[1024,2048]{1,0:T(8,128)(2,1)} %copy-done, ...), custom_call_target="tpu_custom_call", output_to_operand_aliasing={{0}: (6, {}), {1}: (7, {})} | custom-call | flops 12884901888 | bytes 29360128 | tf_op jit(solution)/shard_map/pallas_call | solution.py:389
  358.7 13.8 shard_map.145
  372.5 22.0 %shard_map.146 = (bf16[4096,1536]{1,0:T(8,128)(2,1)}, bf16[4096,1536]{1,0:T(8,128)(2,1)}) custom-call(bf16[1024,2048]{1,0:T(8,128)(2,1)} %collective-permute-done.2.refs_0_, bf16[1024,2048]{1,0:T(8,128)(2,1)} %collective-permute-done.3.refs_1_, ...), custom_call_target="tpu_custom_call", output_to_operand_aliasing={{0}: (4, {}), {1}: (5, {})} | custom-call | flops 12884901888 | bytes 29360128 | tf_op jit(solution)/shard_map/pallas_call | solution.py:389
  394.5 12.7 shard_map.147
  408.9 34.7 %fusion.7 = f32[2048,1472]{1,0:T(8,128)} fusion(bf16[4096,2048]{1,0:T(8,128)(2,1)} %get-tuple-element.114, bf16[4096,1536]{1,0:T(8,128)(2,1)} %get-tuple-element.131.refs_2_), kind=kOutput, calls=%fused_computation.7 | convolution fusion | flops 24699076608 | bytes 41418752 | tf_op jit(solution)/shard_map/dot_general | solution.py:35
  443.6 14.1 shard_map.148
  457.7 29.4 %convolution_multiply_fusion = f32[1280,2048]{1,0:T(8,128)} fusion(bf16[4096,1280]{1,0:T(8,128)(2,1)} %get-tuple-element.127, bf16[4096,2048]{1,0:T(8,128)(2,1)} %get-tuple-element.128), kind=kOutput, calls=%fused_computation.5 | convolution fusion | flops 21477457920 | bytes 37748736 | tf_op jit(solution)/shard_map/dot_general | solution.py:35
  487.1 17.9 %shard_map.149 = f32[1024,2048]{1,0:T(8,128)} custom-call(bf16[4096,1280]{1,0:T(8,128)(2,1)} %get-tuple-element.112.refs_0_, bf16[2048,1280]{1,0:T(8,128)(2,1)} %get-tuple-element.82.refs_2_.refs_4_.refs_1_, bf16[4096,1536]{1,0:T(8,128)(2,1)} %get-tuple-element.131.refs_2_, bf16[2048,1536]{1,0:T(8,128)(2,1)} %get-tuple-element.94.refs_2_.refs_4_.refs_3_), custom_call_target="tpu_custom_call" | custom-call | flops 11811160064 | bytes 25690112 | tf_op jit(solution)/shard_map/pallas_call | solution.py:425
  511.3 34.0 %fusion.4 = f32[1472,2048]{1,0:T(8,128)} fusion(bf16[4096,2048]{1,0:T(8,128)(2,1)} %get-tuple-element.128, bf16[4096,1536]{1,0:T(8,128)(2,1)} %get-tuple-element.130), kind=kOutput, calls=%fused_computation.4 | convolution fusion | flops 24699076608 | bytes 41418752 | tf_op jit(solution)/shard_map/dot_general | solution.py:35
  545.3 53.5 %collective-permute-done.11.refs_6_ = f32[512,2048]{1,0:T(8,128)} collective-permute-done((f32[512,2048]{1,0:T(8,128)}, f32[512,2048]{1,0:T(8,128)}, u32[]{:S(2)}, u32[]{:S(2)}) %collective-permute-start.11) | collective-permute-done | bytes 4194336 | tf_op jit(solution)/shard_map/ppermute | solution.py:497
  598.8 89.9 %collective-permute-done.12.refs_7_ = f32[512,2048]{1,0:T(8,128)} collective-permute-done((f32[512,2048]{1,0:T(8,128)}, f32[512,2048]{1,0:T(8,128)}, u32[]{:S(2)}, u32[]{:S(2)}) %collective-permute-start.12) | collective-permute-done | bytes 4194336 | tf_op jit(solution)/shard_map/ppermute | solution.py:497
  688.7 21.1 %shard_map.150 = bf16[1024,2048]{1,0:T(8,128)(2,1)} custom-call(bf16[4096,1280]{1,0:T(8,128)(2,1)} %get-tuple-element.112.refs_0_, bf16[2048,1280]{1,0:T(8,128)(2,1)} %get-tuple-element.82.refs_2_.refs_4_.refs_1_, bf16[4096,1536]{1,0:T(8,128)(2,1)} %get-tuple-element.131.refs_2_, bf16[2048,1536]{1,0:T(8,128)(2,1)} %get-tuple-element.94.refs_2_.refs_4_.refs_3_, ...), custom_call_target="tpu_custom_call" | custom-call | flops 11811160064 | bytes 25690112 | tf_op jit(solution)/shard_map/pallas_call | solution.py:425
  715.1 13.0 convert_bitcast_fusion.do_ref
  728.1 58.0 %shard_map.151 = (bf16[1024,1024]{1,0:T(8,128)(2,1)}, f32[8,2,128,512]{3,2,1,0:T(8,128)}) custom-call(s32[4,9]{1,0:T(4,128)} %pad_add_fusion.tab, bf16[2048,1024]{1,0:T(8,128)(2,1)} %convert_bitcast_fusion.1.q_ref, bf16[2048,1024]{1,0:T(8,128)(2,1)} %convert_bitcast_fusion.do_ref, f32[2048,1024]{1,0:T(8,128)} %get-tuple-element.134.of_ref, ...), custom_call_target="tpu_custom_call" | custom-call | flops 24159191040 | bytes 12582912 | tf_op jit(solution)/shard_map/pallas_call | solution.py:201
  794.2 4.6 convolution_multiply_fusion.3
  805.7 32.3 %shard_map.152 = (bf16[512,1024]{1,0:T(8,128)(2,1)}, f32[8,2,128,512]{3,2,1,0:T(8,128)}) custom-call(s32[4,9]{1,0:T(4,128)} %pad_add_fusion.tab, bf16[2048,1024]{1,0:T(8,128)(2,1)} %convert_bitcast_fusion.1.q_ref, bf16[2048,1024]{1,0:T(8,128)(2,1)} %convert_bitcast_fusion.do_ref, f32[2048,1024]{1,0:T(8,128)} %get-tuple-element.134.of_ref, ...), custom_call_target="tpu_custom_call" | custom-call | flops 12079595520 | bytes 6291456 | tf_op jit(solution)/shard_map/pallas_call | solution.py:201
  846.1 33.3 %shard_map.153 = (bf16[512,1024]{1,0:T(8,128)(2,1)}, f32[8,2,128,512]{3,2,1,0:T(8,128)}) custom-call(s32[4,9]{1,0:T(4,128)} %pad_add_fusion.tab, bf16[2048,1024]{1,0:T(8,128)(2,1)} %convert_bitcast_fusion.1.q_ref, bf16[2048,1024]{1,0:T(8,128)(2,1)} %convert_bitcast_fusion.do_ref, f32[2048,1024]{1,0:T(8,128)} %get-tuple-element.134.of_ref, ...), custom_call_target="tpu_custom_call" | custom-call | flops 12079595520 | bytes 6291456 | tf_op jit(solution)/shard_map/pallas_call | solution.py:201
  896.6 57.4 %collective-permute-done.23.refs_2_ = bf16[1024,512]{1,0:T(8,128)(2,1)} collective-permute-done((bf16[1024,512]{1,0:T(8,128)(2,1)}, bf16[1024,512]{1,0:T(8,128)(2,1)}, u32[]{:S(2)}, u32[]{:S(2)}) %collective-permute-start.23) | collective-permute-done | bytes 1048608 | tf_op jit(solution)/shard_map/ppermute | solution.py:497
  954.0 21.4 %collective-permute-done.24.refs_3_ = bf16[1024,512]{1,0:T(8,128)(2,1)} collective-permute-done((bf16[1024,512]{1,0:T(8,128)(2,1)}, bf16[1024,512]{1,0:T(8,128)(2,1)}, u32[]{:S(2)}, u32[]{:S(2)}) %collective-permute-start.24) | collective-permute-done | bytes 1048608 | tf_op jit(solution)/shard_map/ppermute | solution.py:497
  980.1 19.1 %shard_map.154 = f32[512,3072]{1,0:T(8,128)} custom-call(bf16[1024,512]{1,0:T(8,128)(2,1)} %pad_maximum_fusion.4.refs_0_, bf16[1024,512]{1,0:T(8,128)(2,1)} %collective-permute-done.22.refs_1_, bf16[1024,512]{1,0:T(8,128)(2,1)} %collective-permute-done.23.refs_2_, bf16[1024,512]{1,0:T(8,128)(2,1)} %collective-permute-done.24.refs_3_, ...), custom_call_target="tpu_custom_call" | custom-call | flops 8589934592 | bytes 23592960 | tf_op jit(solution)/shard_map/pallas_call | solution.py:456
  1003.2 17.7 %collective-permute-done.31 = f32[2,2,128,512]{3,2,1,0:T(8,128)} collective-permute-done((f32[2,2,128,512]{3,2,1,0:T(8,128)}, f32[2,2,128,512]{3,2,1,0:T(8,128)}, u32[]{:S(2)}, u32[]{:S(2)}) %collective-permute-start.31) | collective-permute-done | bytes 1048608 | tf_op jit(solution)/shard_map/ppermute | solution.py:497
  1029.4 21.8 %collective-permute-done.34 = f32[512,512]{1,0:T(8,128)S(1)} collective-permute-done((f32[512,512]{1,0:T(8,128)S(1)}, f32[512,512]{1,0:T(8,128)S(1)}, u32[]{:S(2)}, u32[]{:S(2)}) %collective-permute-start.34) | collective-permute-done | bytes 1048608 | tf_op jit(solution)/shard_map/ppermute | solution.py:497
  1051.5 22.2 %collective-permute-done.17 = f32[512,512]{1,0:T(8,128)S(1)} collective-permute-done((f32[512,512]{1,0:T(8,128)S(1)}, f32[512,512]{1,0:T(8,128)S(1)}, u32[]{:S(2)}, u32[]{:S(2)}) %collective-permute-start.17) | collective-permute-done | bytes 1048608 | tf_op jit(solution)/shard_map/ppermute | solution.py:497
  1075.3 20.3 %collective-permute-done.36 = f32[512,512]{1,0:T(8,128)S(1)} collective-permute-done((f32[512,512]{1,0:T(8,128)S(1)}, f32[512,512]{1,0:T(8,128)S(1)}, u32[]{:S(2)}, u32[]{:S(2)}) %collective-permute-start.36) | collective-permute-done | bytes 1048608 | tf_op jit(solution)/shard_map/ppermute | solution.py:497
  1104.1 15.2 %collective-permute-done.39 = f32[128,1280]{1,0:T(8,128)S(1)} collective-permute-done((f32[128,1280]{1,0:T(8,128)S(1)}, f32[128,1280]{1,0:T(8,128)S(1)}, u32[]{:S(2)}, u32[]{:S(2)}) %collective-permute-start.39) | collective-permute-done | bytes 655392 | tf_op jit(solution)/shard_map/ppermute | solution.py:497
  1119.3 13.6 collective-permute-done.38
  1135.4 5.7 fusion.54
  1148.7 17.0 %fusion.22 = bf16[1,1024,2048]{2,1,0:T(8,128)(2,1)} fusion(f32[1024,2048]{1,0:T(8,128)} %fusion.54, bf16[1024,2048]{1,0:T(8,128)(2,1)} %shard_map.150, bf16[256,8,16,128]{3,2,1,0:T(8,128)(2,1)} %bitcast.206, bf16[512,1024]{1,0:T(8,128)(2,1)} %get-tuple-element.144, bf16[512,1024]{1,0:T(8,128)(2,1)} %get-tuple-element.140, ...), kind=kOutput, calls=%fused_computation.23 | convolution fusion | flops 8610906112 | bytes 29360128 | tf_op jit(solution)/shard_map/dot_general | solution.py:39
  1165.9 14.0 collective-permute-done.41
  1184.7 7.2 shard_map.155
  1194.4 47.2 %reduce-scatter.15.cloned.1.call-done = f32[320,2048]{1,0:T(8,128)} async-done(((f32[1280,2048]{1,0:T(8,128)}), f32[320,2048]{1,0:T(8,128)}) %reduce-scatter.15.cloned.1.call-update) | async-done | bytes 2621456 | tf_op jit(solution)/shard_map/reduce_scatter | solution.py:500
  1241.6 115.6 %reduce-scatter.17.cloned.1.call-done = f32[368,2048]{1,0:T(8,128)} async-done(((f32[1472,2048]{1,0:T(8,128)}), f32[368,2048]{1,0:T(8,128)}) %reduce-scatter.17.cloned.1.call-update) | async-done | bytes 3014672 | tf_op jit(solution)/shard_map/reduce_scatter | solution.py:500
  1357.2 5.8 pad_maximum_fusion
  1363.0 63.4 %reduce-scatter.7.cloned.1.call-done = f32[128,3072]{1,0:T(8,128)} async-done(((f32[512,3072]{1,0:T(8,128)}), f32[128,3072]{1,0:T(8,128)}) %reduce-scatter.7.cloned.1.call-update) | async-done | bytes 1572880 | tf_op jit(solution)/shard_map/reduce_scatter | solution.py:500
  (309 shorter events, 130.7 us)
Async XLA Ops:
  7.2 57.4 %all-gather.2.cloned.1.call-start = ((), (), s32[]{:S(2)}) async-start(), calls=%async_computation.6 | async-start | bytes 5242880 | tf_op jit(solution)/shard_map/all_gather | solution.py:532
  14.8 1085.4 %reduce-scatter.11.cloned.1.call-start = ((), (), s32[]{:S(2)}) async-start(), calls=%async_computation.9 | async-start | bytes 13107200 | tf_op jit(solution)/shard_map/reduce_scatter | solution.py:500
  14.9 153.0 %collective-permute-start.3 = (bf16[1024,2048]{1,0:T(8,128)(2,1)}, bf16[1024,2048]{1,0:T(8,128)(2,1)}, u32[]{:S(2)}, u32[]{:S(2)}) collective-permute-start(bf16[1024,2048]{1,0:T(8,128)(2,1)} %bitcast.28.refs_1_.refs_4_), channel_id=1, source_target_pairs={{0,1},{1,0},{2,3},{3,2},{4,5},{5,4},{6,7},{7,6},{8,9},{9,8},{10,11... | collective-permute-start | bytes 12582920 | tf_op jit(solution)/shard_map/ppermute | solution.py:497
  47.4 120.2 %collective-permute-start.4 = (bf16[1024,2048]{1,0:T(8,128)(2,1)}, bf16[1024,2048]{1,0:T(8,128)(2,1)}, u32[]{:S(2)}, u32[]{:S(2)}) collective-permute-start(bf16[1024,2048]{1,0:T(8,128)(2,1)} %bitcast.28.refs_1_.refs_4_), channel_id=1, source_target_pairs={{0,2},{1,3},{2,0},{3,1},{4,6},{5,7},{6,4},{7,5},{8,10},{9,11},{10,... | collective-permute-start | bytes 12582920 | tf_op jit(solution)/shard_map/ppermute | solution.py:497
  145.9 21.9 %collective-permute-start.2 = (bf16[1024,2048]{1,0:T(8,128)(2,1)}, bf16[1024,2048]{1,0:T(8,128)(2,1)}, u32[]{:S(2)}, u32[]{:S(2)}) collective-permute-start(bf16[1024,2048]{1,0:T(8,128)(2,1)} %add_convert_fusion.1.refs_0_), channel_id=1, source_target_pairs={{0,1},{1,0},{2,3},{3,2},{4,5},{5,4},{6,7},{7,6},{8,9},{9,8},{10,11... | collective-permute-start | bytes 12582920 | tf_op jit(solution)/shard_map/ppermute | solution.py:497
  167.3 48.1 %collective-permute-start.1 = (bf16[512,2048]{1,0:T(8,128)(2,1)S(1)}, bf16[512,2048]{1,0:T(8,128)(2,1)}, u32[]{:S(2)}, u32[]{:S(2)}) collective-permute-start(bf16[512,2048]{1,0:T(8,128)(2,1)S(1)} %slice.88), channel_id=1, source_target_pairs={{0,2},{1,3},{2,0},{3,1},{4,6},{5,7},{6,4},{7,5},{8,10},{9,11},{10,... | collective-permute-start | bytes 6291464 | tf_op jit(solution)/shard_map/ppermute | solution.py:497
  167.5 51.4 %collective-permute-start.6 = (bf16[1024,2048]{1,0:T(8,128)(2,1)}, bf16[1024,2048]{1,0:T(8,128)(2,1)S(1)}, u32[]{:S(2)}, u32[]{:S(2)}) collective-permute-start(bf16[1024,2048]{1,0:T(8,128)(2,1)} %collective-permute-done.4.refs_1_), channel_id=1, source_target_pairs={{0,1},{1,0},{2,3},{3,2},{4,5},{5,4},{6,7},{7,6},{8,9},{9,8},{10,11... | collective-permute-start | bytes 12582920 | tf_op jit(solution)/shard_map/ppermute | solution.py:497
  215.4 4.5 collective-permute-start.5
  218.6 48.3 %collective-permute-start = (bf16[512,2048]{1,0:T(8,128)(2,1)}, bf16[512,2048]{1,0:T(8,128)(2,1)S(1)}, u32[]{:S(2)}, u32[]{:S(2)}) collective-permute-start(bf16[512,2048]{1,0:T(8,128)(2,1)} %slice.71), channel_id=1, source_target_pairs={{0,2},{1,3},{2,0},{3,1},{4,6},{5,7},{6,4},{7,5},{8,10},{9,11},{10,... | collective-permute-start | bytes 6291464 | tf_op jit(solution)/shard_map/ppermute | solution.py:497
  321.1 820.0 %reduce-scatter.13.cloned.1.call-start = ((), (), s32[]{:S(2)}) async-start(), calls=%async_computation.10 | async-start | bytes 15728640 | tf_op jit(solution)/shard_map/reduce_scatter | solution.py:500
  334.4 22.3 %collective-permute-start.8 = (f32[512,2048]{1,0:T(8,128)}, f32[512,2048]{1,0:T(8,128)S(1)}, u32[]{:S(2)}, u32[]{:S(2)}) collective-permute-start(f32[512,2048]{1,0:T(8,128)} %shard_map.143), channel_id=1, source_target_pairs={{0,1},{1,0},{2,3},{3,2},{4,5},{5,4},{6,7},{7,6},{8,9},{9,8},{10,11... | collective-permute-start | bytes 12582920 | tf_op jit(solution)/shard_map/ppermute | solution.py:497
  407.3 36.3 %collective-permute-start.9 = (f32[512,2048]{1,0:T(8,128)}, f32[512,2048]{1,0:T(8,128)}, u32[]{:S(2)}, u32[]{:S(2)}) collective-permute-start(f32[512,2048]{1,0:T(8,128)} %shard_map.147), channel_id=1, source_target_pairs={{0,1},{1,0},{2,3},{3,2},{4,5},{5,4},{6,7},{7,6},{8,9},{9,8},{10,11... | collective-permute-start | bytes 12582920 | tf_op jit(solution)/shard_map/ppermute | solution.py:497
  505.0 183.7 %collective-permute-start.10 = (f32[1024,2048]{1,0:T(8,128)}, f32[1024,2048]{1,0:T(8,128)}, u32[]{:S(2)}, u32[]{:S(2)}) collective-permute-start(f32[1024,2048]{1,0:T(8,128)} %shard_map.149), channel_id=1, source_target_pairs={{0,1},{1,0},{2,3},{3,2},{4,5},{5,4},{6,7},{7,6},{8,9},{9,8},{10,11... | collective-permute-start | bytes 25165832 | tf_op jit(solution)/shard_map/ppermute | solution.py:497
  505.0 93.8 %collective-permute-start.11 = (f32[512,2048]{1,0:T(8,128)}, f32[512,2048]{1,0:T(8,128)}, u32[]{:S(2)}, u32[]{:S(2)}) collective-permute-start(f32[512,2048]{1,0:T(8,128)} %shard_map.145), channel_id=1, source_target_pairs={{0,2},{1,3},{2,0},{3,1},{4,6},{5,7},{6,4},{7,5},{8,10},{9,11},{10,... | collective-permute-start | bytes 12582920 | tf_op jit(solution)/shard_map/ppermute | solution.py:497
  505.0 183.6 %collective-permute-start.12 = (f32[512,2048]{1,0:T(8,128)}, f32[512,2048]{1,0:T(8,128)}, u32[]{:S(2)}, u32[]{:S(2)}) collective-permute-start(f32[512,2048]{1,0:T(8,128)} %shard_map.148), channel_id=1, source_target_pairs={{0,2},{1,3},{2,0},{3,1},{4,6},{5,7},{6,4},{7,5},{8,10},{9,11},{10,... | collective-permute-start | bytes 12582920 | tf_op jit(solution)/shard_map/ppermute | solution.py:497
  511.2 282.5 %collective-permute-start.26 = (bf16[2048,1024]{1,0:T(8,128)(2,1)}, bf16[2048,1024]{1,0:T(8,128)(2,1)}, u32[]{:S(2)}, u32[]{:S(2)}) collective-permute-start(bf16[2048,1024]{1,0:T(8,128)(2,1)} %get-tuple-element.148.refs_4_), channel_id=1, source_target_pairs={{0,2},{1,3},{2,0},{3,1},{4,6},{5,7},{6,4},{7,5},{8,10},{9,11},{10,... | collective-permute-start | bytes 12582920 | tf_op jit(solution)/shard_map/ppermute | solution.py:497
  511.3 680.6 %reduce-scatter.9.cloned.1.call-start = ((), (), s32[]{:S(2)}) async-start(), calls=%async_computation.8 | async-start | bytes 3932160 | tf_op jit(solution)/shard_map/reduce_scatter | solution.py:500
  790.4 11.0 collective-permute-start.14
  793.2 5.6 collective-permute-start.13
  793.7 91.4 %collective-permute-start.25 = (bf16[2048,1024]{1,0:T(8,128)(2,1)}, bf16[2048,1024]{1,0:T(8,128)(2,1)}, u32[]{:S(2)}, u32[]{:S(2)}) collective-permute-start(bf16[2048,1024]{1,0:T(8,128)(2,1)} %get-tuple-element.148.refs_4_), channel_id=1, source_target_pairs={{0,1},{1,0},{2,3},{3,2},{4,5},{5,4},{6,7},{7,6},{8,9},{9,8},{10,11... | collective-permute-start | bytes 12582920 | tf_op jit(solution)/shard_map/ppermute | solution.py:497
  793.7 92.9 %collective-permute-start.27 = (bf16[2048,1024]{1,0:T(8,128)(2,1)}, bf16[2048,1024]{1,0:T(8,128)(2,1)}, u32[]{:S(2)}, u32[]{:S(2)}) collective-permute-start(bf16[2048,1024]{1,0:T(8,128)(2,1)} %collective-permute-done.26.refs_6_), channel_id=1, source_target_pairs={{0,1},{1,0},{2,3},{3,2},{4,5},{5,4},{6,7},{7,6},{8,9},{9,8},{10,11... | collective-permute-start | bytes 12582920 | tf_op jit(solution)/shard_map/ppermute | solution.py:497
  840.1 5.7 collective-permute-start.16
  882.2 6.1 collective-permute-start.21
  882.7 96.1 %collective-permute-start.28 = (f32[512,1024]{1,0:T(8,128)}, f32[512,1024]{1,0:T(8,128)S(1)}, u32[]{:S(2)}, u32[]{:S(2)}) collective-permute-start(f32[512,1024]{1,0:T(8,128)} %convolution_multiply_fusion.3), channel_id=1, source_target_pairs={{0,1},{1,0},{2,3},{3,2},{4,5},{5,4},{6,7},{7,6},{8,9},{9,8},{10,11... | collective-permute-start | bytes 6291464 | tf_op jit(solution)/shard_map/ppermute | solution.py:497
  882.7 96.1 %collective-permute-start.29 = (f32[512,1024]{1,0:T(8,128)}, f32[512,1024]{1,0:T(8,128)}, u32[]{:S(2)}, u32[]{:S(2)}) collective-permute-start(f32[512,1024]{1,0:T(8,128)} %multiply_add_fusion), channel_id=1, source_target_pairs={{0,2},{1,3},{2,0},{3,1},{4,6},{5,7},{6,4},{7,5},{8,10},{9,11},{10,... | collective-permute-start | bytes 6291464 | tf_op jit(solution)/shard_map/ppermute | solution.py:497
  885.0 11.2 collective-permute-start.22
  886.5 67.5 %collective-permute-start.23 = (bf16[1024,512]{1,0:T(8,128)(2,1)}, bf16[1024,512]{1,0:T(8,128)(2,1)}, u32[]{:S(2)}, u32[]{:S(2)}) collective-permute-start(bf16[1024,512]{1,0:T(8,128)(2,1)} %pad_maximum_fusion.10), channel_id=1, source_target_pairs={{0,2},{1,3},{2,0},{3,1},{4,6},{5,7},{6,4},{7,5},{8,10},{9,11},{10,... | collective-permute-start | bytes 3145736 | tf_op jit(solution)/shard_map/ppermute | solution.py:497
  889.3 86.2 %collective-permute-start.24 = (bf16[1024,512]{1,0:T(8,128)(2,1)}, bf16[1024,512]{1,0:T(8,128)(2,1)}, u32[]{:S(2)}, u32[]{:S(2)}) collective-permute-start(bf16[1024,512]{1,0:T(8,128)(2,1)} %pad_maximum_fusion.11), channel_id=1, source_target_pairs={{0,3},{1,2},{2,1},{3,0},{4,7},{5,6},{6,5},{7,4},{8,11},{9,10},{10,... | collective-permute-start | bytes 3145736 | tf_op jit(solution)/shard_map/ppermute | solution.py:497
  896.2 104.7 %collective-permute-start.18 = (f32[2,2,128,512]{3,2,1,0:T(8,128)}, f32[2,2,128,512]{3,2,1,0:T(8,128)}, u32[]{:S(2)}, u32[]{:S(2)}) collective-permute-start(f32[2,2,128,512]{3,2,1,0:T(8,128)} %get-tuple-element.159), channel_id=1, source_target_pairs={{0,1},{1,0},{2,3},{3,2},{4,5},{5,4},{6,7},{7,6},{8,9},{9,8},{10,11... | collective-permute-start | bytes 3145736 | tf_op jit(solution)/shard_map/ppermute | solution.py:497
  954.0 46.9 %collective-permute-start.19 = (f32[2,2,128,512]{3,2,1,0:T(8,128)}, f32[2,2,128,512]{3,2,1,0:T(8,128)}, u32[]{:S(2)}, u32[]{:S(2)}) collective-permute-start(f32[2,2,128,512]{3,2,1,0:T(8,128)} %bitcast_add_fusion.3), channel_id=1, source_target_pairs={{0,2},{1,3},{2,0},{3,1},{4,6},{5,7},{6,4},{7,5},{8,10},{9,11},{10,... | collective-permute-start | bytes 3145736 | tf_op jit(solution)/shard_map/ppermute | solution.py:497
  975.4 23.8 %collective-permute-start.20 = (f32[512,512]{1,0:T(8,128)}, f32[512,512]{1,0:T(8,128)}, u32[]{:S(2)}, u32[]{:S(2)}) collective-permute-start(f32[512,512]{1,0:T(8,128)} %convolution_multiply_fusion.11), channel_id=1, source_target_pairs={{0,1},{1,0},{2,3},{3,2},{4,5},{5,4},{6,7},{7,6},{8,9},{9,8},{10,11... | collective-permute-start | bytes 3145736 | tf_op jit(solution)/shard_map/ppermute | solution.py:497
  978.8 42.1 %collective-permute-start.30 = (f32[2,2,128,512]{3,2,1,0:T(8,128)}, f32[2,2,128,512]{3,2,1,0:T(8,128)}, u32[]{:S(2)}, u32[]{:S(2)}) collective-permute-start(f32[2,2,128,512]{3,2,1,0:T(8,128)} %get-tuple-element.157), channel_id=1, source_target_pairs={{0,1},{1,0},{2,3},{3,2},{4,5},{5,4},{6,7},{7,6},{8,9},{9,8},{10,11... | collective-permute-start | bytes 3145736 | tf_op jit(solution)/shard_map/ppermute | solution.py:497
  978.8 42.1 %collective-permute-start.31 = (f32[2,2,128,512]{3,2,1,0:T(8,128)}, f32[2,2,128,512]{3,2,1,0:T(8,128)}, u32[]{:S(2)}, u32[]{:S(2)}) collective-permute-start(f32[2,2,128,512]{3,2,1,0:T(8,128)} %bitcast_add_fusion.1), channel_id=1, source_target_pairs={{0,2},{1,3},{2,0},{3,1},{4,6},{5,7},{6,4},{7,5},{8,10},{9,11},{10,... | collective-permute-start | bytes 3145736 | tf_op jit(solution)/shard_map/ppermute | solution.py:497
  1025.1 26.1 %collective-permute-start.34 = (f32[512,512]{1,0:T(8,128)S(1)}, f32[512,512]{1,0:T(8,128)S(1)}, u32[]{:S(2)}, u32[]{:S(2)}) collective-permute-start(f32[512,512]{1,0:T(8,128)S(1)} %add.421), channel_id=1, source_target_pairs={{0,2},{1,3},{2,0},{3,1},{4,6},{5,7},{6,4},{7,5},{8,10},{9,11},{10,... | collective-permute-start | bytes 3145736 | tf_op jit(solution)/shard_map/ppermute | solution.py:497
  1025.4 48.2 %collective-permute-start.17 = (f32[512,512]{1,0:T(8,128)S(1)}, f32[512,512]{1,0:T(8,128)S(1)}, u32[]{:S(2)}, u32[]{:S(2)}) collective-permute-start(f32[512,512]{1,0:T(8,128)S(1)} %add.418), channel_id=1, source_target_pairs={{0,2},{1,3},{2,0},{3,1},{4,6},{5,7},{6,4},{7,5},{8,10},{9,11},{10,... | collective-permute-start | bytes 3145736 | tf_op jit(solution)/shard_map/ppermute | solution.py:497
  1027.2 46.5 %collective-permute-start.33 = (f32[512,512]{1,0:T(8,128)S(1)}, f32[512,512]{1,0:T(8,128)S(1)}, u32[]{:S(2)}, u32[]{:S(2)}) collective-permute-start(f32[512,512]{1,0:T(8,128)S(1)} %copy-done.68), channel_id=1, source_target_pairs={{0,1},{1,0},{2,3},{3,2},{4,5},{5,4},{6,7},{7,6},{8,9},{9,8},{10,11... | collective-permute-start | bytes 3145736 | tf_op jit(solution)/shard_map/ppermute | solution.py:497
  1027.2 47.3 %collective-permute-start.15 = (f32[512,512]{1,0:T(8,128)S(1)}, f32[512,512]{1,0:T(8,128)S(1)}, u32[]{:S(2)}, u32[]{:S(2)}) collective-permute-start(f32[512,512]{1,0:T(8,128)S(1)} %copy-done.67), channel_id=1, source_target_pairs={{0,1},{1,0},{2,3},{3,2},{4,5},{5,4},{6,7},{7,6},{8,9},{9,8},{10,11... | collective-permute-start | bytes 3145736 | tf_op jit(solution)/shard_map/ppermute | solution.py:497
  1028.5 46.7 %collective-permute-start.35 = (f32[512,512]{1,0:T(8,128)S(1)}, f32[512,512]{1,0:T(8,128)S(1)}, u32[]{:S(2)}, u32[]{:S(2)}) collective-permute-start(f32[512,512]{1,0:T(8,128)S(1)} %convolution_multiply_fusion.5), channel_id=1, source_target_pairs={{0,1},{1,0},{2,3},{3,2},{4,5},{5,4},{6,7},{7,6},{8,9},{9,8},{10,11... | collective-permute-start | bytes 3145736 | tf_op jit(solution)/shard_map/ppermute | solution.py:497
  1051.2 44.4 %collective-permute-start.36 = (f32[512,512]{1,0:T(8,128)S(1)}, f32[512,512]{1,0:T(8,128)S(1)}, u32[]{:S(2)}, u32[]{:S(2)}) collective-permute-start(f32[512,512]{1,0:T(8,128)S(1)} %fusion.41), channel_id=1, source_target_pairs={{0,2},{1,3},{2,0},{3,1},{4,6},{5,7},{6,4},{7,5},{8,10},{9,11},{10,... | collective-permute-start | bytes 3145736 | tf_op jit(solution)/shard_map/ppermute | solution.py:497
  1098.3 143.3 %reduce-scatter.15.cloned.1.call-start = ((), (), s32[]{:S(2)}) async-start(), calls=%async_computation.11 | async-start | bytes 13107200 | tf_op jit(solution)/shard_map/reduce_scatter | solution.py:500
  1098.9 258.3 %reduce-scatter.17.cloned.1.call-start = ((), (), s32[]{:S(2)}) async-start(), calls=%async_computation.12 | async-start | bytes 15073280 | tf_op jit(solution)/shard_map/reduce_scatter | solution.py:500
  1099.5 327.0 %reduce-scatter.7.cloned.1.call-start = ((), (), s32[]{:S(2)}) async-start(), calls=%async_computation.7 | async-start | bytes 7864320 | tf_op jit(solution)/shard_map/reduce_scatter | solution.py:500
  1102.2 17.1 %collective-permute-start.39 = (f32[128,1280]{1,0:T(8,128)S(1)}, f32[128,1280]{1,0:T(8,128)S(1)}, u32[]{:S(2)}, u32[]{:S(2)}) collective-permute-start(f32[128,1280]{1,0:T(8,128)S(1)} %get-tuple-element.198), channel_id=1, source_target_pairs={{0,3},{1,2},{2,1},{3,0},{4,7},{5,6},{6,5},{7,4},{8,11},{9,10},{10,... | collective-permute-start | bytes 1966088 | tf_op jit(solution)/shard_map/ppermute | solution.py:497
  1102.2 30.6 %collective-permute-start.38 = (f32[128,1280]{1,0:T(8,128)S(1)}, f32[128,1280]{1,0:T(8,128)S(1)}, u32[]{:S(2)}, u32[]{:S(2)}) collective-permute-start(f32[128,1280]{1,0:T(8,128)S(1)} %get-tuple-element.199), channel_id=1, source_target_pairs={{0,2},{1,3},{2,0},{3,1},{4,6},{5,7},{6,4},{7,5},{8,10},{9,11},{10,... | collective-permute-start | bytes 1966088 | tf_op jit(solution)/shard_map/ppermute | solution.py:497
  1103.5 29.4 %collective-permute-start.37 = (f32[128,1280]{1,0:T(8,128)S(1)}, f32[128,1280]{1,0:T(8,128)S(1)}, u32[]{:S(2)}, u32[]{:S(2)}) collective-permute-start(f32[128,1280]{1,0:T(8,128)S(1)} %get-tuple-element.200), channel_id=1, source_target_pairs={{0,1},{1,0},{2,3},{3,2},{4,5},{5,4},{6,7},{7,6},{8,9},{9,8},{10,11... | collective-permute-start | bytes 1966088 | tf_op jit(solution)/shard_map/ppermute | solution.py:497
  1144.3 21.3 %collective-permute-start.42 = (f32[128,1472]{0,1:T(8,128)}, f32[128,1472]{0,1:T(8,128)S(1)}, u32[]{:S(2)}, u32[]{:S(2)}) collective-permute-start(f32[128,1472]{0,1:T(8,128)} %copy.49), channel_id=1, source_target_pairs={{0,3},{1,2},{2,1},{3,0},{4,7},{5,6},{6,5},{7,4},{8,11},{9,10},{10,... | collective-permute-start | bytes 2261000 | tf_op jit(solution)/shard_map/ppermute | solution.py:497
  1145.7 34.2 %collective-permute-start.41 = (f32[128,1472]{0,1:T(8,128)}, f32[128,1472]{0,1:T(8,128)}, u32[]{:S(2)}, u32[]{:S(2)}) collective-permute-start(f32[128,1472]{0,1:T(8,128)} %copy.47), channel_id=1, source_target_pairs={{0,2},{1,3},{2,0},{3,1},{4,6},{5,7},{6,4},{7,5},{8,10},{9,11},{10,... | collective-permute-start | bytes 2261000 | tf_op jit(solution)/shard_map/ppermute | solution.py:497
  1148.7 32.6 %collective-permute-start.40 = (f32[128,1472]{0,1:T(8,128)}, f32[128,1472]{0,1:T(8,128)}, u32[]{:S(2)}, u32[]{:S(2)}) collective-permute-start(f32[128,1472]{0,1:T(8,128)} %copy.45), channel_id=1, source_target_pairs={{0,1},{1,0},{2,3},{3,2},{4,5},{5,4},{6,7},{7,6},{8,9},{9,8},{10,11... | collective-permute-start | bytes 2261000 | tf_op jit(solution)/shard_map/ppermute | solution.py:497
  (78 other events, 3343.6 us)
Sparse Core Ops, SparseCore 0:
  14.9 35.3 all-gather.1
  321.2 99.9 reduce-scatter.10
  511.4 118.6 reduce-scatter.12
  1098.4 40.4 reduce-scatter.8
  1141.8 99.7 reduce-scatter.14
  1244.6 112.5 reduce-scatter.16
  1360.1 66.2 reduce-scatter.6
